TPU v7x, 128 devices: a whole 4x4x4 slice. The times are simulated.
128 devices in a mesh: lat: 2 (over x_lo), lon: 8 (over z_lo, x_hi, core), lev: 8 (over z_hi, y).
Axes of the slice: x: 4 (x_hi: 2, x_lo: 2; x = x_hi * 2 + x_lo), y: 4, z: 4 (z_hi: 2, z_lo: 2; z = z_hi * 2 + z_lo), core: 2. Of those that a mesh axis runs over, the one named last changes fastest.
Arguments:
- initial_state: float32 [16, 256, 512, 128], P('lat', 'lon', 'lev'), may hold values from 0.2 to 1.8
- scaled_diffusivity: float32 [16, 256, 512, 128], P('lat', 'lon', 'lev'), may hold values from 0.03 to 0.15
- scaled_forcing: float32 [16, 256, 512, 128], P('lat', 'lon', 'lev'), may hold values from -0.2 to 0.2
Outputs:
- cumulative_totals: float32 [16, 256, 512, 128], P('lat', 'lon', 'lev')
- temperature_end: float32 [16, 256, 512, 128], P('lat', 'lon', 'lev')
All inputs are finite; a program needn't handle non-finite values.
Results may differ from a plain program's by a relative error of at most 0.00002.
Values sent between devices are 32-bit elements; how exact they have to be, the bound alone decides.
No kernel may reach another device: no remote copies, remote signals or barrier semaphores. Data moves between devices by JAX's collectives and lax.ppermute only.
A program may use at most 128 MiB of HBM per device.

v0:
```python
import jax
import jax.numpy as jnp
from jax import lax
from jax.sharding import Mesh
from jax.sharding import PartitionSpec as P

STEPS = 4
LON = ("lon_0", "lon_1", "lon_2")


def with_halo(x, sides, width):
    edges = {}
    for axis, dim in sides:
        size, length = (lax.axis_size(axis), x.shape[dim])
        up = [(i, (i + 1) % size) for i in range(size - 1)]
        last = lax.slice_in_dim(x, length - width, length, axis=dim)
        initial = lax.slice_in_dim(x, 0, width, axis=dim)
        edges[dim] = (
            lax.ppermute(last, axis, up),
            lax.ppermute(initial, axis, [(b, a) for a, b in up]),
        )
    done = []
    for _, dim in sides:
        low, high = edges[dim]
        around = [(width, width) if d in done else (0, 0) for d in range(x.ndim)]
        x = jnp.concatenate([jnp.pad(low, around), x, jnp.pad(high, around)], axis=dim)
        done.append(dim)
    return x


def nothing_yet(x, identity):
    return jnp.broadcast_to(jnp.asarray(identity, x.dtype), x.shape)


def prefix_by_axis(x, axes, combine, identity):
    before = start = nothing_yet(x, identity)
    total = x
    for axis in reversed(axes):
        length, here = (lax.axis_size(axis), lax.axis_index(axis))
        pieces = lax.all_gather(total, axis)
        inside, total = (start, start)
        for k in range(length):
            passed = k < here
            total = combine(total, pieces[k])
            inside = jnp.where(passed, total, inside)
        before = combine(inside, before)
    return before


def strip_edges(values, dims):
    for dim in dims:
        values = lax.slice_in_dim(values, 1, values.shape[dim] - 1, axis=dim)
    return values


def neighbour(values, dim, start, dims):
    others = [other for other in dims if other != dim]
    values = strip_edges(values, others)
    return lax.slice_in_dim(values, start, start + values.shape[dim] - 2, axis=dim)


def explicit_update(haloed_values, scaled_diffusivity, scaled_forcing):
    middle = strip_edges(haloed_values, (0, 1, 2))
    lower = [neighbour(haloed_values, dim, 0, (0, 1, 2)) for dim in (0, 1, 2)]
    upper = [neighbour(haloed_values, dim, 2, (0, 1, 2)) for dim in (0, 1, 2)]
    spread = lower[0] + upper[0] + lower[1] + upper[1] + lower[2] + upper[2] - 6.0 * middle
    return middle + scaled_diffusivity * spread + scaled_forcing


def per_device(initial_state, scaled_diffusivity, scaled_forcing):
    for step in range(STEPS):
        haloed_values = with_halo(initial_state, (("lat", 0), (LON, 1), ("lev", 2)), 1)
        initial_state = explicit_update(haloed_values, scaled_diffusivity, scaled_forcing)
    present_layer = jnp.cumsum(initial_state, axis=1)
    total = lax.slice_in_dim(
        present_layer, present_layer.shape[1] - 1, present_layer.shape[1], axis=1
    )

    def add_pair(earlier_total, later_total):
        return earlier_total + later_total

    previous_plane = prefix_by_axis(total, LON, add_pair, jnp.zeros_like(total))
    cumulative_totals = (present_layer + previous_plane) / (
        initial_state.shape[1] * lax.axis_size(LON)
    )
    return (cumulative_totals, initial_state)


def solution(mesh):
    split = Mesh(
        mesh.devices.reshape(mesh.shape["lat"], 2, 2, 2, mesh.shape["lev"]),
        ("lat", "lon_0", "lon_1", "lon_2", "lev"),
    )
    return jax.shard_map(
        per_device,
        mesh=split,
        in_specs=(
            P("lat", LON, "lev", None),
            P("lat", LON, "lev", None),
            P("lat", LON, "lev", None),
        ),
        out_specs=(P("lat", LON, "lev", None), P("lat", LON, "lev", None)),
        check_vma=False,
    )
```

profile of v0, /device:TPU:98, one launch (start us, length us, event | category | flops | bytes accessed | tf_op | source)
XLA Modules:
  0.0 325.4 jit_solution(642423002292479463)
XLA Ops:
  0.6 0.0 copy-start
  0.6 1.8 fusion.59
  2.5 1.6 collective-permute-start
  4.0 4.7 %collective-permute-start.1 = (f32[1,32,64,128]{3,2,1,0:T(8,128)S(1)}, f32[1,32,64,128]{3,2,1,0:T(8,128)S(1)}, u32[]{:S(2)}, u32[]{:S(2)}) collective-permute-start(f32[1,32,64,128]{3,2,1,0:T(8,128)S(1)} %get-tuple-element.26), channel_id=1, source_target_pairs={{64,0},{65,1},{66,2},{67,3},{68,4},{69,5},{70,6},{71,7},{72,8},{73... | collective-permute-start | bytes 3145736 | tf_op jit(solution)/shard_map/ppermute | solution.py:20
  8.7 1.1 fusion.58
  9.8 1.9 collective-permute-start.2
  11.7 6.0 %collective-permute-start.3 = (f32[8,1,64,128]{3,2,1,0:T(8,128)S(1)}, f32[8,1,64,128]{3,2,1,0:T(8,128)S(1)}, u32[]{:S(2)}, u32[]{:S(2)}) collective-permute-start(f32[8,1,64,128]{3,2,1,0:T(8,128)S(1)} %get-tuple-element.25), channel_id=1, source_target_pairs={{8,0},{16,8},{24,16},{32,24},{40,32},{48,40},{56,48},{9,1},{17,9},... | collective-permute-start | bytes 786440 | tf_op jit(solution)/shard_map/ppermute | solution.py:20
  17.8 2.5 fusion.57
  20.2 3.5 %collective-permute-start.4 = (f32[8,32,1,128]{3,1,2,0:T(8,128)}, f32[8,32,1,128]{3,1,2,0:T(8,128)S(1)}, u32[]{:S(2)}, u32[]{:S(2)}) collective-permute-start(f32[8,32,1,128]{3,1,2,0:T(8,128)} %bitcast.22), channel_id=1, source_target_pairs={{0,1},{1,2},{2,3},{3,4},{4,5},{5,6},{6,7},{8,9},{9,10},{10,11},{11... | collective-permute-start | bytes 393224 | tf_op jit(solution)/shard_map/ppermute | solution.py:19
  23.7 13.7 %collective-permute-done.2 = f32[8,1,64,128]{3,2,1,0:T(8,128)S(1)} collective-permute-done((f32[8,1,64,128]{3,2,1,0:T(8,128)S(1)}, f32[8,1,64,128]{3,2,1,0:T(8,128)S(1)}, u32[]{:S(2)}, u32[]{:S(2)}) %collective-permute-start.2) | collective-permute-done | bytes 262176 | tf_op jit(solution)/shard_map/ppermute | solution.py:19
  37.4 4.6 %collective-permute-start.5 = (f32[8,32,1,128]{3,1,2,0:T(8,128)}, f32[8,32,1,128]{3,1,2,0:T(8,128)}, u32[]{:S(2)}, u32[]{:S(2)}) collective-permute-start(f32[8,32,1,128]{3,1,2,0:T(8,128)} %bitcast.24), channel_id=1, source_target_pairs={{1,0},{2,1},{3,2},{4,3},{5,4},{6,5},{7,6},{9,8},{10,9},{11,10},{12... | collective-permute-start | bytes 393224 | tf_op jit(solution)/shard_map/ppermute | solution.py:20
  42.0 0.0 collective-permute-done.3
  42.0 0.8 pad.51
  42.8 1.1 constant_dynamic-update-slice_fusion.2
  43.9 4.7 %constant_dynamic-update-slice_fusion.1 = f32[10,32,64,128]{3,2,1,0:T(8,128)} fusion(f32[10,32,64,128]{3,2,1,0:T(8,128)} %constant_dynamic-update-slice_fusion.2, f32[8,32,64,128]{3,2,1,0:T(8,128)S(1)} %copy-done), kind=kLoop, calls=%fused_computation.123 | loop fusion | bytes 16777216
  48.6 0.0 collective-permute-done.1
  48.6 1.0 copy-done.1
  49.6 1.1 constant_dynamic-update-slice_fusion
  50.6 0.0 collective-permute-done.4
  50.6 0.0 collective-permute-done.5
  50.7 30.1 %fusion.38 = f32[8,32,64,128]{3,2,1,0:T(8,128)} fusion(f32[8,32,64,128]{3,2,1,0:T(8,128)S(1)} %bitcast.43, f32[8,32,64,128]{3,2,1,0:T(8,128)} %param.3, f32[8,32,64,128]{3,2,1,0:T(8,128)} %param.4, f32[8,32,1,128]{3,2,1,0:T(1,128)} %bitcast.25, f32[10,1,64,128]{3,2,1,0:T(8,128)} %pad.51, f32[10,32,64,128]{3,2,1,0:T(8,128)} %constant_dynamic-update-slice_fusion, ...), kind=kLoop, calls=%fused_computation.93 | loop fusion | flops 54525952 | bytes 47054848 | tf_op jit(solution)/shard_map/add | solution.py:67
  80.8 1.7 fusion.55
  82.4 1.3 collective-permute-start.6
  83.7 4.7 %collective-permute-start.7 = (f32[1,32,64,128]{3,2,1,0:T(8,128)S(1)}, f32[1,32,64,128]{3,2,1,0:T(8,128)S(1)}, u32[]{:S(2)}, u32[]{:S(2)}) collective-permute-start(f32[1,32,64,128]{3,2,1,0:T(8,128)S(1)} %get-tuple-element.19), channel_id=1, source_target_pairs={{64,0},{65,1},{66,2},{67,3},{68,4},{69,5},{70,6},{71,7},{72,8},{73... | collective-permute-start | bytes 3145736 | tf_op jit(solution)/shard_map/ppermute | solution.py:20
  88.4 1.1 fusion.56
  89.5 1.9 collective-permute-start.8
  91.4 6.0 %collective-permute-start.9 = (f32[8,1,64,128]{3,2,1,0:T(8,128)S(1)}, f32[8,1,64,128]{3,2,1,0:T(8,128)S(1)}, u32[]{:S(2)}, u32[]{:S(2)}) collective-permute-start(f32[8,1,64,128]{3,2,1,0:T(8,128)S(1)} %get-tuple-element.21), channel_id=1, source_target_pairs={{8,0},{16,8},{24,16},{32,24},{40,32},{48,40},{56,48},{9,1},{17,9},... | collective-permute-start | bytes 786440 | tf_op jit(solution)/shard_map/ppermute | solution.py:20
  97.5 1.8 fusion.54
  99.2 1.9 collective-permute-start.10
  101.2 13.0 %collective-permute-done.8 = f32[8,1,64,128]{3,2,1,0:T(8,128)S(1)} collective-permute-done((f32[8,1,64,128]{3,2,1,0:T(8,128)S(1)}, f32[8,1,64,128]{3,2,1,0:T(8,128)S(1)}, u32[]{:S(2)}, u32[]{:S(2)}) %collective-permute-start.8) | collective-permute-done | bytes 262176 | tf_op jit(solution)/shard_map/ppermute | solution.py:19
  114.1 6.5 %collective-permute-start.11 = (f32[8,32,1,128]{3,1,2,0:T(8,128)S(1)}, f32[8,32,1,128]{3,1,2,0:T(8,128)S(1)}, u32[]{:S(2)}, u32[]{:S(2)}) collective-permute-start(f32[8,32,1,128]{3,1,2,0:T(8,128)S(1)} %bitcast.53), channel_id=1, source_target_pairs={{1,0},{2,1},{3,2},{4,3},{5,4},{6,5},{7,6},{9,8},{10,9},{11,10},{12... | collective-permute-start | bytes 393224 | tf_op jit(solution)/shard_map/ppermute | solution.py:20
  120.7 2.4 collective-permute-done.11
  123.1 28.3 %fusion.27 = f32[8,32,64,128]{3,2,1,0:T(8,128)} fusion(f32[8,32,64,128]{3,2,1,0:T(8,128)} %param.5, f32[8,32,64,128]{3,2,1,0:T(8,128)} %fusion.38, f32[8,32,64,128]{3,2,1,0:T(8,128)} %param.4, f32[8,32,1,128]{3,2,1,0:T(1,128)S(1)} %bitcast.51, f32[10,1,64,128]{3,2,1,0:T(8,128)S(1)} %pad.55, f32[10,1,64,128]{3,2,1,0:T(8,128)S(1)} %pad.54, ...), kind=kLoop, calls=%fused_computation.64 | loop fusion | flops 71303168 | bytes 36569088 | tf_op jit(solution)/shard_map/add | solution.py:67
  151.5 1.7 fusion.52
  153.1 1.3 collective-permute-start.12
  154.4 4.7 %collective-permute-start.13 = (f32[1,32,64,128]{3,2,1,0:T(8,128)S(1)}, f32[1,32,64,128]{3,2,1,0:T(8,128)S(1)}, u32[]{:S(2)}, u32[]{:S(2)}) collective-permute-start(f32[1,32,64,128]{3,2,1,0:T(8,128)S(1)} %get-tuple-element.13), channel_id=1, source_target_pairs={{64,0},{65,1},{66,2},{67,3},{68,4},{69,5},{70,6},{71,7},{72,8},{73... | collective-permute-start | bytes 3145736 | tf_op jit(solution)/shard_map/ppermute | solution.py:20
  159.1 1.1 fusion.53
  160.2 1.9 collective-permute-start.14
  162.1 6.0 %collective-permute-start.15 = (f32[8,1,64,128]{3,2,1,0:T(8,128)S(1)}, f32[8,1,64,128]{3,2,1,0:T(8,128)S(1)}, u32[]{:S(2)}, u32[]{:S(2)}) collective-permute-start(f32[8,1,64,128]{3,2,1,0:T(8,128)S(1)} %get-tuple-element.15), channel_id=1, source_target_pairs={{8,0},{16,8},{24,16},{32,24},{40,32},{48,40},{56,48},{9,1},{17,9},... | collective-permute-start | bytes 786440 | tf_op jit(solution)/shard_map/ppermute | solution.py:20
  168.2 1.8 fusion.51
  170.0 2.9 collective-permute-start.16
  172.9 8.0 %collective-permute-done.14 = f32[8,1,64,128]{3,2,1,0:T(8,128)S(1)} collective-permute-done((f32[8,1,64,128]{3,2,1,0:T(8,128)S(1)}, f32[8,1,64,128]{3,2,1,0:T(8,128)S(1)}, u32[]{:S(2)}, u32[]{:S(2)}) %collective-permute-start.14) | collective-permute-done | bytes 262176 | tf_op jit(solution)/shard_map/ppermute | solution.py:19
  180.9 6.2 %collective-permute-start.17 = (f32[8,32,1,128]{3,1,2,0:T(8,128)S(1)}, f32[8,32,1,128]{3,1,2,0:T(8,128)S(1)}, u32[]{:S(2)}, u32[]{:S(2)}) collective-permute-start(f32[8,32,1,128]{3,1,2,0:T(8,128)S(1)} %bitcast.54), channel_id=1, source_target_pairs={{1,0},{2,1},{3,2},{4,3},{5,4},{6,5},{7,6},{9,8},{10,9},{11,10},{12... | collective-permute-start | bytes 393224 | tf_op jit(solution)/shard_map/ppermute | solution.py:20
  187.2 2.2 collective-permute-done.17
  189.5 28.4 %fusion.16 = f32[8,32,64,128]{3,2,1,0:T(8,128)} fusion(f32[8,32,64,128]{3,2,1,0:T(8,128)} %param.5, f32[8,32,64,128]{3,2,1,0:T(8,128)} %fusion.27, f32[8,32,64,128]{3,2,1,0:T(8,128)} %param.4, f32[8,32,1,128]{3,2,1,0:T(1,128)S(1)} %bitcast.52, f32[10,1,64,128]{3,2,1,0:T(8,128)S(1)} %pad.59, f32[10,1,64,128]{3,2,1,0:T(8,128)S(1)} %pad.58, ...), kind=kLoop, calls=%fused_computation.35 | loop fusion | flops 71303168 | bytes 36569088 | tf_op jit(solution)/shard_map/add | solution.py:67
  217.9 2.7 fusion.49
  220.6 1.3 collective-permute-start.18
  221.8 4.7 %collective-permute-start.19 = (f32[1,32,64,128]{3,2,1,0:T(8,128)S(1)}, f32[1,32,64,128]{3,2,1,0:T(8,128)S(1)}, u32[]{:S(2)}, u32[]{:S(2)}) collective-permute-start(f32[1,32,64,128]{3,2,1,0:T(8,128)S(1)} %get-tuple-element.7), channel_id=1, source_target_pairs={{64,0},{65,1},{66,2},{67,3},{68,4},{69,5},{70,6},{71,7},{72,8},{73... | collective-permute-start | bytes 3145736 | tf_op jit(solution)/shard_map/ppermute | solution.py:20
  226.5 1.8 fusion.50
  228.3 1.9 collective-permute-start.20
  230.2 6.0 %collective-permute-start.21 = (f32[8,1,64,128]{3,2,1,0:T(8,128)}, f32[8,1,64,128]{3,2,1,0:T(8,128)S(1)}, u32[]{:S(2)}, u32[]{:S(2)}) collective-permute-start(f32[8,1,64,128]{3,2,1,0:T(8,128)} %get-tuple-element.9), channel_id=1, source_target_pairs={{8,0},{16,8},{24,16},{32,24},{40,32},{48,40},{56,48},{9,1},{17,9},... | collective-permute-start | bytes 786440 | tf_op jit(solution)/shard_map/ppermute | solution.py:20
  236.3 2.5 fusion.48
  238.7 8.0 %collective-permute-start.23 = (f32[8,32,1,128]{3,1,2,0:T(8,128)}, f32[8,32,1,128]{3,1,2,0:T(8,128)S(1)}, u32[]{:S(2)}, u32[]{:S(2)}) collective-permute-start(f32[8,32,1,128]{3,1,2,0:T(8,128)} %bitcast.10), channel_id=1, source_target_pairs={{1,0},{2,1},{3,2},{4,3},{5,4},{6,5},{7,6},{9,8},{10,9},{11,10},{12... | collective-permute-start | bytes 393224 | tf_op jit(solution)/shard_map/ppermute | solution.py:20
  246.7 1.9 collective-permute-start.22
  248.7 1.0 pad.62
  249.7 8.0 %collective-permute-done.22 = f32[8,32,1,128]{3,1,2,0:T(8,128)} collective-permute-done((f32[8,32,1,128]{3,1,2,0:T(8,128)}, f32[8,32,1,128]{3,1,2,0:T(8,128)}, u32[]{:S(2)}, u32[]{:S(2)}) %collective-permute-start.22) | collective-permute-done | bytes 131104 | tf_op jit(solution)/shard_map/ppermute | solution.py:19
  257.7 28.4 %fusion.5 = f32[8,32,64,128]{3,2,1,0:T(8,128)} fusion(f32[8,32,64,128]{3,2,1,0:T(8,128)} %param.5, f32[8,32,64,128]{3,2,1,0:T(8,128)} %fusion.16, f32[8,32,64,128]{3,2,1,0:T(8,128)} %param.4, f32[8,32,1,128]{3,2,1,0:T(1,128)S(1)} %bitcast.47, f32[10,1,64,128]{3,2,1,0:T(8,128)S(1)} %pad.63, f32[10,1,64,128]{3,2,1,0:T(8,128)S(1)} %pad.62, ...), kind=kLoop, calls=%fused_computation.6 | loop fusion | flops 71303168 | bytes 36569088 | tf_op jit(solution)/shard_map/add | solution.py:67
  286.1 8.4 %fusion.60 = f32[8,32,64,128]{3,2,1,0:T(8,128)} fusion(f32[8,32,64,128]{3,2,1,0:T(8,128)} %fusion.5), kind=kOutput, calls=%fused_computation.137 | output fusion | flops 65011712 | bytes 16777216 | tf_op jit(solution)/shard_map/jit(cumsum)/reduce_window_sum | solution.py:74
  294.6 1.0 slice.398
  295.5 2.2 all-gather
  297.7 10.5 %all-gather.1 = f32[16,1,64,128]{3,2,1,0:T(8,128)S(1)} all-gather(f32[8,1,64,128]{3,2,1,0:T(8,128)S(1)} %slice_add_fusion.2), channel_id=3, replica_groups=mesh['lat'=2,'lon_0'=2,'lon_1'=2,'lon_2'=2,'lev'=8] {'lon_1'}, dimensions={0}, use_global_device_ids=true | all-gather | bytes 786432 | tf_op jit(solution)/shard_map/all_gather | solution.py:40
  308.3 8.2 %all_gather.17 = f32[2,8,1,64,128]{4,3,2,1,0:T(8,128)S(1)} all-gather(f32[1,8,1,64,128]{4,3,2,1,0:T(8,128)S(1)} %fusion.47), channel_id=1, replica_groups=mesh['lat'=2,'lon_0'=2,'lon_1'=2,'lon_2'=2,'lev'=8] {'lon_0'}, dimensions={0}, use_global_device_ids=true | all-gather | bytes 786432 | tf_op jit(solution)/shard_map/all_gather | solution.py:40
  316.4 0.1 fusion.46
  316.6 8.8 %add_multiply_fusion = f32[8,32,64,128]{3,2,1,0:T(8,128)} fusion(f32[8,32,64,128]{3,2,1,0:T(8,128)} %fusion.60, f32[8,64,128]{2,1,0:T(8,128)S(1)} %fusion.46), kind=kLoop, calls=%fused_computation.110 | loop fusion | flops 4194304 | bytes 17039360 | tf_op jit(solution)/shard_map/div | solution.py:83
  (29 shorter events, 0.2 us)
Async XLA Ops:
  0.6 43.3 %copy-start = (f32[8,32,64,128]{3,2,1,0:T(8,128)S(1)}, f32[8,32,64,128]{3,2,1,0:T(8,128)}, u32[]{:S(2)}) copy-start(f32[8,32,64,128]{3,2,1,0:T(8,128)} %param.3) | copy-start | bytes 25165828
  2.5 40.4 %collective-permute-start = (f32[1,32,64,128]{3,2,1,0:T(8,128)S(1)}, f32[1,32,64,128]{3,2,1,0:T(8,128)S(1)}, u32[]{:S(2)}, u32[]{:S(2)}) collective-permute-start(f32[1,32,64,128]{3,2,1,0:T(8,128)S(1)} %get-tuple-element.27), channel_id=1, source_target_pairs={{0,64},{1,65},{2,66},{3,67},{4,68},{5,69},{6,70},{7,71},{8,72},{9,... | collective-permute-start | bytes 3145736 | tf_op jit(solution)/shard_map/ppermute | solution.py:19
  4.0 44.6 %collective-permute-start.1 = (f32[1,32,64,128]{3,2,1,0:T(8,128)S(1)}, f32[1,32,64,128]{3,2,1,0:T(8,128)S(1)}, u32[]{:S(2)}, u32[]{:S(2)}) collective-permute-start(f32[1,32,64,128]{3,2,1,0:T(8,128)S(1)} %get-tuple-element.26), channel_id=1, source_target_pairs={{64,0},{65,1},{66,2},{67,3},{68,4},{69,5},{70,6},{71,7},{72,8},{73... | collective-permute-start | bytes 3145736 | tf_op jit(solution)/shard_map/ppermute | solution.py:20
  9.8 27.6 %collective-permute-start.2 = (f32[8,1,64,128]{3,2,1,0:T(8,128)S(1)}, f32[8,1,64,128]{3,2,1,0:T(8,128)S(1)}, u32[]{:S(2)}, u32[]{:S(2)}) collective-permute-start(f32[8,1,64,128]{3,2,1,0:T(8,128)S(1)} %get-tuple-element.24), channel_id=1, source_target_pairs={{0,8},{8,16},{16,24},{24,32},{32,40},{40,48},{48,56},{1,9},{9,17},... | collective-permute-start | bytes 786440 | tf_op jit(solution)/shard_map/ppermute | solution.py:19
  11.7 30.3 %collective-permute-start.3 = (f32[8,1,64,128]{3,2,1,0:T(8,128)S(1)}, f32[8,1,64,128]{3,2,1,0:T(8,128)S(1)}, u32[]{:S(2)}, u32[]{:S(2)}) collective-permute-start(f32[8,1,64,128]{3,2,1,0:T(8,128)S(1)} %get-tuple-element.25), channel_id=1, source_target_pairs={{8,0},{16,8},{24,16},{32,24},{40,32},{48,40},{56,48},{9,1},{17,9},... | collective-permute-start | bytes 786440 | tf_op jit(solution)/shard_map/ppermute | solution.py:20
  20.2 30.4 %collective-permute-start.4 = (f32[8,32,1,128]{3,1,2,0:T(8,128)}, f32[8,32,1,128]{3,1,2,0:T(8,128)S(1)}, u32[]{:S(2)}, u32[]{:S(2)}) collective-permute-start(f32[8,32,1,128]{3,1,2,0:T(8,128)} %bitcast.22), channel_id=1, source_target_pairs={{0,1},{1,2},{2,3},{3,4},{4,5},{5,6},{6,7},{8,9},{9,10},{10,11},{11... | collective-permute-start | bytes 393224 | tf_op jit(solution)/shard_map/ppermute | solution.py:19
  37.4 13.3 %collective-permute-start.5 = (f32[8,32,1,128]{3,1,2,0:T(8,128)}, f32[8,32,1,128]{3,1,2,0:T(8,128)}, u32[]{:S(2)}, u32[]{:S(2)}) collective-permute-start(f32[8,32,1,128]{3,1,2,0:T(8,128)} %bitcast.24), channel_id=1, source_target_pairs={{1,0},{2,1},{3,2},{4,3},{5,4},{6,5},{7,6},{9,8},{10,9},{11,10},{12... | collective-permute-start | bytes 393224 | tf_op jit(solution)/shard_map/ppermute | solution.py:20
  42.8 7.8 %slice-start = ((s8[8388608]{0:T(1024)(128)(4,1)}), s8[4194304]{0:T(1024)(128)(4,1)S(1)}, s32[]{:S(2)}) async-start(s8[8388608]{0:T(1024)(128)(4,1)} %bitcast.42), calls=%async_computation | async-start | bytes 8388608
  43.9 6.7 %slice-start.1 = ((s8[8388608]{0:T(1024)(128)(4,1)}), s8[4194304]{0:T(1024)(128)(4,1)S(1)}, s32[]{:S(2)}) async-start(s8[8388608]{0:T(1024)(128)(4,1)} %bitcast.42), calls=%async_computation.1 | async-start | bytes 8388608
  48.6 1.0 copy-start.1
  82.4 40.7 %collective-permute-start.6 = (f32[1,32,64,128]{3,2,1,0:T(8,128)S(1)}, f32[1,32,64,128]{3,2,1,0:T(8,128)S(1)}, u32[]{:S(2)}, u32[]{:S(2)}) collective-permute-start(f32[1,32,64,128]{3,2,1,0:T(8,128)S(1)} %get-tuple-element.18), channel_id=1, source_target_pairs={{0,64},{1,65},{2,66},{3,67},{4,68},{5,69},{6,70},{7,71},{8,72},{9,... | collective-permute-start | bytes 3145736 | tf_op jit(solution)/shard_map/ppermute | solution.py:19
  83.7 39.4 %collective-permute-start.7 = (f32[1,32,64,128]{3,2,1,0:T(8,128)S(1)}, f32[1,32,64,128]{3,2,1,0:T(8,128)S(1)}, u32[]{:S(2)}, u32[]{:S(2)}) collective-permute-start(f32[1,32,64,128]{3,2,1,0:T(8,128)S(1)} %get-tuple-element.19), channel_id=1, source_target_pairs={{64,0},{65,1},{66,2},{67,3},{68,4},{69,5},{70,6},{71,7},{72,8},{73... | collective-permute-start | bytes 3145736 | tf_op jit(solution)/shard_map/ppermute | solution.py:20
  89.5 24.6 %collective-permute-start.8 = (f32[8,1,64,128]{3,2,1,0:T(8,128)S(1)}, f32[8,1,64,128]{3,2,1,0:T(8,128)S(1)}, u32[]{:S(2)}, u32[]{:S(2)}) collective-permute-start(f32[8,1,64,128]{3,2,1,0:T(8,128)S(1)} %get-tuple-element.20), channel_id=1, source_target_pairs={{0,8},{8,16},{16,24},{24,32},{32,40},{40,48},{48,56},{1,9},{9,17},... | collective-permute-start | bytes 786440 | tf_op jit(solution)/shard_map/ppermute | solution.py:19
  91.4 29.2 %collective-permute-start.9 = (f32[8,1,64,128]{3,2,1,0:T(8,128)S(1)}, f32[8,1,64,128]{3,2,1,0:T(8,128)S(1)}, u32[]{:S(2)}, u32[]{:S(2)}) collective-permute-start(f32[8,1,64,128]{3,2,1,0:T(8,128)S(1)} %get-tuple-element.21), channel_id=1, source_target_pairs={{8,0},{16,8},{24,16},{32,24},{40,32},{48,40},{56,48},{9,1},{17,9},... | collective-permute-start | bytes 786440 | tf_op jit(solution)/shard_map/ppermute | solution.py:20
  99.2 21.5 %collective-permute-start.10 = (f32[8,32,1,128]{3,1,2,0:T(8,128)S(1)}, f32[8,32,1,128]{3,1,2,0:T(8,128)S(1)}, u32[]{:S(2)}, u32[]{:S(2)}) collective-permute-start(f32[8,32,1,128]{3,1,2,0:T(8,128)S(1)} %bitcast.55), channel_id=1, source_target_pairs={{0,1},{1,2},{2,3},{3,4},{4,5},{5,6},{6,7},{8,9},{9,10},{10,11},{11... | collective-permute-start | bytes 393224 | tf_op jit(solution)/shard_map/ppermute | solution.py:19
  114.1 9.0 %collective-permute-start.11 = (f32[8,32,1,128]{3,1,2,0:T(8,128)S(1)}, f32[8,32,1,128]{3,1,2,0:T(8,128)S(1)}, u32[]{:S(2)}, u32[]{:S(2)}) collective-permute-start(f32[8,32,1,128]{3,1,2,0:T(8,128)S(1)} %bitcast.53), channel_id=1, source_target_pairs={{1,0},{2,1},{3,2},{4,3},{5,4},{6,5},{7,6},{9,8},{10,9},{11,10},{12... | collective-permute-start | bytes 393224 | tf_op jit(solution)/shard_map/ppermute | solution.py:20
  153.1 36.3 %collective-permute-start.12 = (f32[1,32,64,128]{3,2,1,0:T(8,128)S(1)}, f32[1,32,64,128]{3,2,1,0:T(8,128)S(1)}, u32[]{:S(2)}, u32[]{:S(2)}) collective-permute-start(f32[1,32,64,128]{3,2,1,0:T(8,128)S(1)} %get-tuple-element.12), channel_id=1, source_target_pairs={{0,64},{1,65},{2,66},{3,67},{4,68},{5,69},{6,70},{7,71},{8,72},{9,... | collective-permute-start | bytes 3145736 | tf_op jit(solution)/shard_map/ppermute | solution.py:19
  154.4 35.0 %collective-permute-start.13 = (f32[1,32,64,128]{3,2,1,0:T(8,128)S(1)}, f32[1,32,64,128]{3,2,1,0:T(8,128)S(1)}, u32[]{:S(2)}, u32[]{:S(2)}) collective-permute-start(f32[1,32,64,128]{3,2,1,0:T(8,128)S(1)} %get-tuple-element.13), channel_id=1, source_target_pairs={{64,0},{65,1},{66,2},{67,3},{68,4},{69,5},{70,6},{71,7},{72,8},{73... | collective-permute-start | bytes 3145736 | tf_op jit(solution)/shard_map/ppermute | solution.py:20
  160.2 20.7 %collective-permute-start.14 = (f32[8,1,64,128]{3,2,1,0:T(8,128)S(1)}, f32[8,1,64,128]{3,2,1,0:T(8,128)S(1)}, u32[]{:S(2)}, u32[]{:S(2)}) collective-permute-start(f32[8,1,64,128]{3,2,1,0:T(8,128)S(1)} %get-tuple-element.14), channel_id=1, source_target_pairs={{0,8},{8,16},{16,24},{24,32},{32,40},{40,48},{48,56},{1,9},{9,17},... | collective-permute-start | bytes 786440 | tf_op jit(solution)/shard_map/ppermute | solution.py:19
  162.1 25.1 %collective-permute-start.15 = (f32[8,1,64,128]{3,2,1,0:T(8,128)S(1)}, f32[8,1,64,128]{3,2,1,0:T(8,128)S(1)}, u32[]{:S(2)}, u32[]{:S(2)}) collective-permute-start(f32[8,1,64,128]{3,2,1,0:T(8,128)S(1)} %get-tuple-element.15), channel_id=1, source_target_pairs={{8,0},{16,8},{24,16},{32,24},{40,32},{48,40},{56,48},{9,1},{17,9},... | collective-permute-start | bytes 786440 | tf_op jit(solution)/shard_map/ppermute | solution.py:20
  170.0 17.3 %collective-permute-start.16 = (f32[8,32,1,128]{3,1,2,0:T(8,128)S(1)}, f32[8,32,1,128]{3,1,2,0:T(8,128)S(1)}, u32[]{:S(2)}, u32[]{:S(2)}) collective-permute-start(f32[8,32,1,128]{3,1,2,0:T(8,128)S(1)} %bitcast.56), channel_id=1, source_target_pairs={{0,1},{1,2},{2,3},{3,4},{4,5},{5,6},{6,7},{8,9},{9,10},{10,11},{11... | collective-permute-start | bytes 393224 | tf_op jit(solution)/shard_map/ppermute | solution.py:19
  180.9 8.6 %collective-permute-start.17 = (f32[8,32,1,128]{3,1,2,0:T(8,128)S(1)}, f32[8,32,1,128]{3,1,2,0:T(8,128)S(1)}, u32[]{:S(2)}, u32[]{:S(2)}) collective-permute-start(f32[8,32,1,128]{3,1,2,0:T(8,128)S(1)} %bitcast.54), channel_id=1, source_target_pairs={{1,0},{2,1},{3,2},{4,3},{5,4},{6,5},{7,6},{9,8},{10,9},{11,10},{12... | collective-permute-start | bytes 393224 | tf_op jit(solution)/shard_map/ppermute | solution.py:20
  220.6 37.2 %collective-permute-start.18 = (f32[1,32,64,128]{3,2,1,0:T(8,128)}, f32[1,32,64,128]{3,2,1,0:T(8,128)S(1)}, u32[]{:S(2)}, u32[]{:S(2)}) collective-permute-start(f32[1,32,64,128]{3,2,1,0:T(8,128)} %get-tuple-element.6), channel_id=1, source_target_pairs={{0,64},{1,65},{2,66},{3,67},{4,68},{5,69},{6,70},{7,71},{8,72},{9,... | collective-permute-start | bytes 3145736 | tf_op jit(solution)/shard_map/ppermute | solution.py:19
  221.8 35.9 %collective-permute-start.19 = (f32[1,32,64,128]{3,2,1,0:T(8,128)S(1)}, f32[1,32,64,128]{3,2,1,0:T(8,128)S(1)}, u32[]{:S(2)}, u32[]{:S(2)}) collective-permute-start(f32[1,32,64,128]{3,2,1,0:T(8,128)S(1)} %get-tuple-element.7), channel_id=1, source_target_pairs={{64,0},{65,1},{66,2},{67,3},{68,4},{69,5},{70,6},{71,7},{72,8},{73... | collective-permute-start | bytes 3145736 | tf_op jit(solution)/shard_map/ppermute | solution.py:20
  228.3 18.4 %collective-permute-start.20 = (f32[8,1,64,128]{3,2,1,0:T(8,128)S(1)}, f32[8,1,64,128]{3,2,1,0:T(8,128)}, u32[]{:S(2)}, u32[]{:S(2)}) collective-permute-start(f32[8,1,64,128]{3,2,1,0:T(8,128)S(1)} %get-tuple-element.8), channel_id=1, source_target_pairs={{0,8},{8,16},{16,24},{24,32},{32,40},{40,48},{48,56},{1,9},{9,17},... | collective-permute-start | bytes 786440 | tf_op jit(solution)/shard_map/ppermute | solution.py:19
  230.2 19.4 %collective-permute-start.21 = (f32[8,1,64,128]{3,2,1,0:T(8,128)}, f32[8,1,64,128]{3,2,1,0:T(8,128)S(1)}, u32[]{:S(2)}, u32[]{:S(2)}) collective-permute-start(f32[8,1,64,128]{3,2,1,0:T(8,128)} %get-tuple-element.9), channel_id=1, source_target_pairs={{8,0},{16,8},{24,16},{32,24},{40,32},{48,40},{56,48},{9,1},{17,9},... | collective-permute-start | bytes 786440 | tf_op jit(solution)/shard_map/ppermute | solution.py:20
  238.7 10.9 %collective-permute-start.23 = (f32[8,32,1,128]{3,1,2,0:T(8,128)}, f32[8,32,1,128]{3,1,2,0:T(8,128)S(1)}, u32[]{:S(2)}, u32[]{:S(2)}) collective-permute-start(f32[8,32,1,128]{3,1,2,0:T(8,128)} %bitcast.10), channel_id=1, source_target_pairs={{1,0},{2,1},{3,2},{4,3},{5,4},{6,5},{7,6},{9,8},{10,9},{11,10},{12... | collective-permute-start | bytes 393224 | tf_op jit(solution)/shard_map/ppermute | solution.py:20
  246.7 11.0 %collective-permute-start.22 = (f32[8,32,1,128]{3,1,2,0:T(8,128)}, f32[8,32,1,128]{3,1,2,0:T(8,128)}, u32[]{:S(2)}, u32[]{:S(2)}) collective-permute-start(f32[8,32,1,128]{3,1,2,0:T(8,128)} %bitcast.8), channel_id=1, source_target_pairs={{0,1},{1,2},{2,3},{3,4},{4,5},{5,6},{6,7},{8,9},{9,10},{10,11},{11... | collective-permute-start | bytes 393224 | tf_op jit(solution)/shard_map/ppermute | solution.py:19
where the time goes:
time: 326 us; the launch traced here: 325 us
  other arithmetic  133 us (41%)
  starting transfers between devices  91.5 us (28%)
  waiting for transfers between devices  47.4 us (15%)
  local copies, waits for them, and re-layouts  32 us (10%)
  blocking collectives  20.8 us (6%)
    add x4, other arithmetic, explicit_update(): return middle + scaled_diffusivity * spread + scaled_forcing  115 us
    ppermute x12, starting transfers between devices, with_halo(): lax.ppermute(initial, axis, [(b, a) for a, b in up])  68.2 us
    ppermute x12, waiting for transfers between devices, with_halo(): lax.ppermute(last, axis, up)  42.7 us
    ppermute x12, starting transfers between devices, with_halo(): lax.ppermute(last, axis, up)  23.3 us
    all_gather x3, blocking collectives, prefix_by_axis(): pieces = lax.all_gather(total, axis)  20.8 us
    slice x11, local copies, waits for them, and re-layouts, with_halo(): last = lax.slice_in_dim(x, length - width, length, axis=dim)  19.5 us
    div x1, other arithmetic, per_device(): (present_layer + previous_plane) / (initial_state.shape[1] * lax.axis_siz...  8.81 us
    another operation x1, other arithmetic, per_device(): present_layer = jnp.cumsum(initial_state, axis=1)  8.42 us
  transfers between devices with their start and end apart: 24, of which 6 were waited for; matrix products, arithmetic and copies ran while one was open for 7% of the time, Pallas kernels for 0%

commit v1 on v0

v1 whole, which is shorter than its diff:
```python
import functools

import jax
import jax.numpy as jnp
from jax import lax
from jax.experimental import pallas as pl
from jax.experimental.pallas import tpu as pltpu
from jax.sharding import PartitionSpec as P


STEPS = 4
BLOCK = 4
VMEM = pl.BlockSpec(memory_space=pltpu.VMEM)
HBM = pl.BlockSpec(memory_space=pltpu.HBM)
ANY = pl.BlockSpec(memory_space=pl.ANY)


def in_vmem(x):
    return pltpu.with_memory_space_constraint(x, pltpu.VMEM)


def in_hbm(x):
    return pltpu.with_memory_space_constraint(x, pltpu.HBM)


def new_rows(c, im, ip, nb, klo, khi, d, f):
    km = jnp.concatenate([klo, c[:-1]], axis=0)
    kp = jnp.concatenate([c[1:], khi], axis=0)
    spread = (im + ip) + nb + (km + kp) - 6.0 * c
    return c + d * spread + f


def sweep(lo, hi, row, below, above, nb, klo, khi, d, f, put, carry=None):
    def block(first, bottom, top, carry):
        rows = [bottom() if bottom else row(first - 1)]
        rows += [row(first + r) for r in range(BLOCK)]
        rows += [top() if top else row(first + BLOCK)]
        for r in range(BLOCK):
            i = first + r
            new = new_rows(rows[r + 1], rows[r], rows[r + 2], nb(i), klo(i), khi(i), d(i), f(i))
            carry = put(i, new, carry)
        return carry

    carry = block(lo, below, None, carry)

    def body(b, carry):
        return block(lo + b * BLOCK, None, None, carry)

    n = (hi - lo) // BLOCK
    carry = lax.fori_loop(1, n - 1, body, carry)
    return block(hi - BLOCK, None, above, carry)


def plane_at(depth, n):
    low = lax.axis_index("lat") == 0
    return jnp.where(low, n - 1 - depth, depth)


def faces_kernel(u, lon_lo, lon_hi, lev_lo, lev_hi):
    nj, ni, nk, _ = u.shape
    for j in range(nj):
        lon_lo[j] = u[j, 0]
        lon_hi[j] = u[j, ni - 1]
        lev_lo[j] = u[j, :, 0, :]
        lev_hi[j] = u[j, :, nk - 1, :]


def load_kernel(u_in, d_in, f_in, u, d_edge, f_edge, lon_lo, lon_hi, lev_lo, lev_hi, sem):
    nj = u.shape[0]
    pj = plane_at(0, nj)
    copies = [pltpu.make_async_copy(u_in.at[j], u.at[j], sem.at[j]) for j in range(nj)]
    copies += [
        pltpu.make_async_copy(d_in.at[pj], d_edge, sem.at[nj]),
        pltpu.make_async_copy(f_in.at[pj], f_edge, sem.at[nj + 1]),
    ]
    for copy in copies:
        copy.start()
    for copy in copies:
        copy.wait()
    faces_kernel(u, lon_lo, lon_hi, lev_lo, lev_hi)


def edge_kernel(part, u, pa, pb, lat, lon_lo, lon_hi, lev_lo, lev_hi, d, f, *rest):
    nj, ni, nk, _ = u.shape
    half = ni // 2
    pj, pn = plane_at(0, nj), plane_at(1, nj)
    mine = (pa, pb)[part]
    base = part * half
    if part == 0:
        (out,) = rest
        below = lambda: lon_lo[pj]
        above = lambda: pb[0]
    else:
        nu, npa, out, s_lon_lo, s_lon_hi, s_lev_lo, s_lev_hi = rest
        below = lambda: pa[half - 1]
        above = lambda: lon_hi[pj]

    def put(i, new, carry):
        out[i] = new
        return carry

    sweep(
        0,
        half,
        lambda i: mine[i],
        below,
        above,
        lambda i: u[pn, base + i] + lat[i],
        lambda i: lev_lo[pj, pl.ds(base + i, 1), :],
        lambda i: lev_hi[pj, pl.ds(base + i, 1), :],
        lambda i: d[base + i],
        lambda i: f[base + i],
        put,
        jnp.int32(0),
    )
    if part == 1:
        faces_kernel(nu, s_lon_lo, s_lon_hi, s_lev_lo, s_lev_hi)
        s_lon_lo[pj] = npa[0]
        s_lon_hi[pj] = out[half - 1]
        s_lev_lo[pj, :half] = npa[:, 0, :]
        s_lev_lo[pj, half:] = out[:, 0, :]
        s_lev_hi[pj, :half] = npa[:, nk - 1, :]
        s_lev_hi[pj, half:] = out[:, nk - 1, :]


def bulk_planes(u, pa, pb, lon_lo, lon_hi, lev_lo, lev_hi, d, f, put, start, finish):
    nj, ni, _, _ = u.shape
    half = ni // 2

    def run(j, lo, hi, nb, carry):
        return sweep(
            lo,
            hi,
            lambda i: u[j, i],
            (lambda: lon_lo[j]) if lo == 0 else None,
            (lambda: lon_hi[j]) if hi == ni else None,
            nb,
            lambda i: lev_lo[j, pl.ds(i, 1), :],
            lambda i: lev_hi[j, pl.ds(i, 1), :],
            lambda i: d[j, i],
            lambda i: f[j, i],
            functools.partial(put, j),
            carry,
        )

    j, inner = plane_at(1, nj), plane_at(2, nj)
    start(j, 1)
    carry = run(j, 0, half, lambda i: u[inner, i] + pa[i], zero_carry(u))
    carry = run(j, half, ni, lambda i: u[inner, i] + pb[i - half], carry)
    finish(j, 1, carry)

    def body(depth, _):
        j, outer, inner = plane_at(depth, nj), plane_at(depth - 1, nj), plane_at(depth + 1, nj)
        start(j, depth)
        carry = run(j, 0, ni, lambda i: u[outer, i] + u[inner, i], zero_carry(u))
        finish(j, depth, carry)
        return 0

    lax.fori_loop(2, nj - 1, body, 0)
    j, outer = plane_at(nj - 1, nj), plane_at(nj - 2, nj)
    start(j, nj - 1)
    carry = run(j, 0, ni, lambda i: u[outer, i], zero_carry(u))
    finish(j, nj - 1, carry)


def zero_carry(u):
    return jnp.zeros(u.shape[2:], u.dtype)


def nothing(*_):
    pass


def plain_put(out):
    def put(j, i, new, carry):
        out[j, i] = new
        return carry

    return put


def first_bulk_kernel(u, pa, pb, lon_lo, lon_hi, lev_lo, lev_hi, d_in, f_in, after, out, d, f, sem):
    del after
    nj = u.shape[0]

    def copies(j, depth):
        return (
            pltpu.make_async_copy(d_in.at[j], d.at[j], sem.at[0, depth]),
            pltpu.make_async_copy(f_in.at[j], f.at[j], sem.at[1, depth]),
        )

    for depth in range(1, nj):
        for copy in copies(plane_at(depth, nj), depth):
            copy.start()

    def start(j, depth):
        for copy in copies(j, depth):
            copy.wait()

    bulk_planes(u, pa, pb, lon_lo, lon_hi, lev_lo, lev_hi, d, f, plain_put(out), start, nothing)


def bulk_kernel(u, pa, pb, lon_lo, lon_hi, lev_lo, lev_hi, d, f, after, out):
    del after
    bulk_planes(u, pa, pb, lon_lo, lon_hi, lev_lo, lev_hi, d, f, plain_put(out), nothing, nothing)


def last_bulk_kernel(u, pa, pb, lon_lo, lon_hi, lev_lo, lev_hi, d_in, f_in, end, d, f, total, sem):
    del d_in, f_in
    nj = u.shape[0]

    def copy_out(j, depth):
        return pltpu.make_async_copy(f.at[j], end.at[j], sem.at[depth])

    def put(j, i, new, carry):
        f[j, i] = new
        carry = carry + new
        d[j, i] = carry
        return carry

    def finish(j, depth, carry):
        total[j] = carry
        copy_out(j, depth).start()

    bulk_planes(u, pa, pb, lon_lo, lon_hi, lev_lo, lev_hi, d, f, put, nothing, finish)
    pj = plane_at(0, nj)
    total[pj] = jnp.zeros(total.shape[1:], total.dtype)
    for depth in range(1, nj):
        copy_out(plane_at(depth, nj), depth).wait()


def last_edge_kernel(u, pa, pb, lata, latb, lon_lo, lon_hi, lev_lo, lev_hi, d, f, end_in, end, sums, total, stage, sem):
    del end_in
    nj, ni, nk, nm = u.shape
    half = ni // 2
    pj, pn = plane_at(0, nj), plane_at(1, nj)
    carry = jnp.zeros((nk, nm), u.dtype)
    for part in (0, 1):
        mine, lat, base = (pa, pb)[part], (lata, latb)[part], part * half

        def put(i, new, carry):
            stage[base + i] = new
            carry = carry + new
            sums[base + i] = carry
            return carry

        carry = sweep(
            0,
            half,
            lambda i: mine[i],
            (lambda: lon_lo[pj]) if part == 0 else (lambda: pa[half - 1]),
            (lambda: pb[0]) if part == 0 else (lambda: lon_hi[pj]),
            lambda i: u[pn, base + i] + lat[i],
            lambda i: lev_lo[pj, pl.ds(base + i, 1), :],
            lambda i: lev_hi[pj, pl.ds(base + i, 1), :],
            lambda i: d[base + i],
            lambda i: f[base + i],
            put,
            carry,
        )
    total[...] = carry
    copy = pltpu.make_async_copy(stage, end.at[pj], sem)
    copy.start()
    copy.wait()


def earlier(others):
    lon = lax.axis_index("lon")
    before = 0.0
    for bit, other in enumerate(others):
        before += jnp.where(lon & (1 << bit) != 0, other, 0.0)
    return before


def totals_kernel(scale, sums, *rest):
    *others, out, stage, sem = rest
    nj, ni = sums.shape[:2]

    def copy_out(j, depth):
        slot = depth % 2
        return pltpu.make_async_copy(stage.at[slot], out.at[j], sem.at[slot])

    def body(depth, _):
        j, slot = plane_at(depth, nj), depth % 2

        @pl.when(depth > 2)
        def _():
            copy_out(j, depth).wait()

        b = earlier([other[j] for other in others])

        def row(r, _):
            for q in range(BLOCK):
                i = r * BLOCK + q
                stage[slot, i] = (sums[j, i] + b) * scale
            return 0

        lax.fori_loop(0, ni // BLOCK, row, 0)
        copy_out(j, depth).start()
        return 0

    lax.fori_loop(1, nj, body, 0)
    copy_out(0, 0).wait()
    copy_out(0, 1).wait()


def last_totals_kernel(scale, sums, *rest):
    *others, _, out, stage, sem = rest
    ni = sums.shape[0]
    nj = out.shape[0]
    b = earlier([other[...] for other in others])

    def row(r, _):
        for q in range(BLOCK):
            i = r * BLOCK + q
            stage[i] = (sums[i] + b) * scale
        return 0

    lax.fori_loop(0, ni // BLOCK, row, 0)
    copy = pltpu.make_async_copy(stage, out.at[plane_at(0, nj)], sem)
    copy.start()
    copy.wait()


def call(kernel, out_shape, out_specs, in_specs, limit=2, scratch=(), aliases=None, flops=0):
    return pl.pallas_call(
        kernel,
        out_shape=out_shape,
        in_specs=in_specs,
        out_specs=out_specs,
        scratch_shapes=scratch,
        input_output_aliases=aliases or {},
        compiler_params=pltpu.CompilerParams(vmem_limit_bytes=limit * 2**20),
        cost_estimate=pl.CostEstimate(flops=flops, transcendentals=0, bytes_accessed=0),
    )


def per_device(lon_size, lev_size, initial_state, scaled_diffusivity, scaled_forcing):
    dtype = initial_state.dtype
    nj, ni, nk, nm = initial_state.shape
    half = ni // 2
    V = lambda *shape: pltpu.VMEM(shape, dtype)
    H = lambda *shape: pltpu.HBM(shape, dtype)

    swap = [(0, 1), (1, 0)]
    lon_up = [(i, i + 1) for i in range(lon_size - 1)]
    lev_up = [(i, i + 1) for i in range(lev_size - 1)]
    down = lambda pairs: [(b, a) for a, b in pairs]

    faces_out = (V(nj, nk, nm), V(nj, nk, nm), V(nj, ni, nm), V(nj, ni, nm))

    def exchange(faces):
        lon_lo, lon_hi, lev_lo, lev_hi = faces
        return (
            lax.ppermute(lon_hi, "lon", lon_up),
            lax.ppermute(lon_lo, "lon", down(lon_up)),
            lax.ppermute(lev_hi, "lev", lev_up),
            lax.ppermute(lev_lo, "lev", down(lev_up)),
        )

    pj = jnp.where(lax.axis_index("lat") == 0, nj - 1, 0)
    pa = lax.dynamic_slice(initial_state, (pj, 0, 0, 0), (1, half, nk, nm))[0]
    pb = lax.dynamic_slice(initial_state, (pj, half, 0, 0), (1, half, nk, nm))[0]
    lat_a = lax.ppermute(pa, "lat", swap)
    lat_b = lax.ppermute(pb, "lat", swap)

    u, d_edge, f_edge, *faces = call(
        load_kernel,
        (V(nj, ni, nk, nm), V(ni, nk, nm), V(ni, nk, nm)) + faces_out,
        (VMEM,) * 7,
        (HBM,) * 3,
        scratch=(pltpu.SemaphoreType.DMA((nj + 2,)),),
        flops=10**6,
    )(*map(in_hbm, (initial_state, scaled_diffusivity, scaled_forcing)))
    halo = exchange(faces)
    d_edge, f_edge = in_vmem(d_edge), in_vmem(f_edge)
    d, f = in_hbm(scaled_diffusivity), in_hbm(scaled_forcing)

    for step in range(STEPS - 1):
        halo = tuple(map(in_vmem, halo))
        u, pa, pb = map(in_vmem, (u, pa, pb))
        n_pa = call(
            functools.partial(edge_kernel, 0), V(half, nk, nm), VMEM, (VMEM,) * 10, flops=10**6
        )(u, pa, pb, in_vmem(lat_a), *halo, d_edge, f_edge)
        n_lat_a = lax.ppermute(n_pa, "lat", swap)
        if step == 0:
            n_u, d, f = call(
                first_bulk_kernel,
                (V(nj, ni, nk, nm),) * 3,
                (VMEM,) * 3,
                (VMEM,) * 7 + (HBM,) * 2 + (ANY,),
                scratch=(pltpu.SemaphoreType.DMA((2, nj)),),
                flops=2 * 10**7,
            )(u, pa, pb, *halo, d, f, n_pa)
        else:
            n_u = call(
                bulk_kernel, V(nj, ni, nk, nm), VMEM, (VMEM,) * 9 + (ANY,), flops=2 * 10**7
            )(u, pa, pb, *halo, in_vmem(d), in_vmem(f), n_pa)
        n_pb, *faces = call(
            functools.partial(edge_kernel, 1),
            (V(half, nk, nm),) + faces_out,
            (VMEM,) * 5,
            (VMEM,) * 12,
            flops=10**6,
        )(u, pa, pb, in_vmem(lat_b), *halo, d_edge, f_edge, in_vmem(n_u), in_vmem(n_pa))
        lat_b = lax.ppermute(n_pb, "lat", swap)
        halo = exchange(faces)
        u, pa, pb, lat_a = n_u, n_pa, n_pb, n_lat_a

    halo = tuple(map(in_vmem, halo))
    u, pa, pb = map(in_vmem, (u, pa, pb))
    end, sums, _, total = call(
        last_bulk_kernel,
        (H(nj, ni, nk, nm), V(nj, ni, nk, nm), V(nj, ni, nk, nm), V(nj, nk, nm)),
        (HBM, VMEM, VMEM, VMEM),
        (VMEM,) * 9,
        scratch=(pltpu.SemaphoreType.DMA((nj,)),),
        aliases={7: 1, 8: 2},
        flops=2 * 10**7,
    )(u, pa, pb, *halo, in_vmem(d), in_vmem(f))

    def partners(total):
        others = []
        for bit in range(lon_size.bit_length() - 1):
            pairs = [(i, i ^ (1 << bit)) for i in range(lon_size)]
            if others:
                total = total + others[-1]
            if 2 << bit == lon_size:
                pairs = [(a, b) for a, b in pairs if a < b]
            others.append(lax.ppermute(total, "lon", pairs))
        return tuple(map(in_vmem, others))

    scale = 1.0 / (ni * lon_size)
    out = call(
        functools.partial(totals_kernel, scale),
        H(nj, ni, nk, nm),
        HBM,
        (VMEM,) * lon_size.bit_length(),
        limit=4,
        scratch=(V(2, ni, nk, nm), pltpu.SemaphoreType.DMA((2,))),
        flops=10**6,
    )(in_vmem(sums), *partners(total))

    end, edge_sums, edge_total = call(
        last_edge_kernel,
        (H(nj, ni, nk, nm), V(ni, nk, nm), V(nk, nm)),
        (HBM, VMEM, VMEM),
        (VMEM,) * 11 + (HBM,),
        limit=4,
        scratch=(V(ni, nk, nm), pltpu.SemaphoreType.DMA),
        aliases={11: 0},
        flops=2 * 10**6,
    )(u, pa, pb, in_vmem(lat_a), in_vmem(lat_b), *halo, d_edge, f_edge, in_hbm(end))
    out = call(
        functools.partial(last_totals_kernel, scale),
        H(nj, ni, nk, nm),
        HBM,
        (VMEM,) * lon_size.bit_length() + (HBM,),
        limit=4,
        scratch=(V(ni, nk, nm), pltpu.SemaphoreType.DMA),
        aliases={lon_size.bit_length(): 0},
        flops=10**6,
    )(in_vmem(edge_sums), *partners(edge_total), in_hbm(out))
    return out, end


def solution(mesh):
    spec = P("lat", "lon", "lev", None)
    return jax.shard_map(
        functools.partial(per_device, mesh.shape["lon"], mesh.shape["lev"]),
        mesh=mesh,
        in_specs=(spec, spec, spec),
        out_specs=(spec, spec),
        check_vma=False,
    )
```

time: 326 us -> 178 us (0.55)
  the two profiles are of different devices: /device:TPU:98 before, /device:TPU:30 now
where the time goes in v1:
time: 178 us
  starting transfers between devices  72.1 us (41%)
  waiting for transfers between devices  70.8 us (40%)
  Pallas kernels  32.3 us (18%)
    ppermute x4, waiting for transfers between devices, exchange(): lax.ppermute(lev_lo, 'lev', down(lev_up))  34.4 us
    ppermute x6, waiting for transfers between devices, partners(): others.append(lax.ppermute(total, 'lon', pairs))  34.1 us
    ppermute x4, starting transfers between devices, exchange(): lax.ppermute(lev_hi, 'lev', lev_up)  17.4 us
    ppermute x4, starting transfers between devices, exchange(): lax.ppermute(lon_lo, 'lon', down(lon_up))  15.7 us
    ppermute x4, starting transfers between devices, exchange(): lax.ppermute(lon_hi, 'lon', lon_up)  14.1 us
    ppermute x6, starting transfers between devices, partners(): others.append(lax.ppermute(total, 'lon', pairs))  8.63 us
    pallas_call x2, Pallas kernels, per_device(): call(bulk_kernel, V(nj, ni, nk, nm), VMEM, (VMEM,) * 9 + (ANY,), flops=2...  7.77 us
    ppermute x4, starting transfers between devices, exchange(): lax.ppermute(lev_lo, 'lev', down(lev_up))  7.68 us
  transfers between devices with their start and end apart: 30, of which 8 were waited for; matrix products, arithmetic and copies ran while one was open for 0% of the time, Pallas kernels for 14%

profile of v1, /device:TPU:30, one launch (start us, length us, event | category | flops | bytes accessed | tf_op | source)
XLA Modules:
  0.0 177.6 jit_solution(8998223818858383337)
XLA Ops:
  0.6 1.3 dynamic-slice_bitcast_fusion
  1.9 0.9 collective-permute-start.4
  2.9 1.2 collective-permute-start.5
  4.1 4.3 %shard_map.50 = (f32[8,32,64,128]{3,2,1,0:T(8,128)S(1)}, f32[32,64,128]{2,1,0:T(8,128)S(1)}, f32[32,64,128]{2,1,0:T(8,128)S(1)}, f32[8,64,128]{2,1,0:T(8,128)S(1...) custom-call(f32[8,32,64,128]{3,2,1,0:T(8,128)} %u_in.1, ...), custom_call_target="tpu_custom_call" | custom-call | flops 1000000 | tf_op jit(solution)/shard_map/pallas_call | solution.py:367
  8.3 5.4 %collective-permute-start.2 = (f32[8,32,128]{2,1,0:T(8,128)S(1)}, f32[8,32,128]{2,1,0:T(8,128)S(1)}, u32[]{:S(2)}, u32[]{:S(2)}) collective-permute-start(f32[8,32,128]{2,1,0:T(8,128)S(1)} %get-tuple-element.36), channel_id=1, source_target_pairs={{0,1},{1,2},{2,3},{3,4},{4,5},{5,6},{6,7},{8,9},{9,10},{10,11},{11... | collective-permute-start | bytes 393224 | tf_op jit(solution)/shard_map/ppermute | solution.py:357
  13.8 1.9 %collective-permute-start = (f32[8,64,128]{2,1,0:T(8,128)S(1)}, f32[8,64,128]{2,1,0:T(8,128)S(1)}, u32[]{:S(2)}, u32[]{:S(2)}) collective-permute-start(f32[8,64,128]{2,1,0:T(8,128)S(1)} %get-tuple-element.34), channel_id=1, source_target_pairs={{0,8},{8,16},{16,24},{24,32},{32,40},{40,48},{48,56},{1,9},{9,17},... | collective-permute-start | bytes 786440 | tf_op jit(solution)/shard_map/ppermute | solution.py:355
  15.7 5.1 %collective-permute-start.1 = (f32[8,64,128]{2,1,0:T(8,128)S(1)}, f32[8,64,128]{2,1,0:T(8,128)S(1)}, u32[]{:S(2)}, u32[]{:S(2)}) collective-permute-start(f32[8,64,128]{2,1,0:T(8,128)S(1)} %get-tuple-element.35), channel_id=1, source_target_pairs={{8,0},{16,8},{24,16},{32,24},{40,32},{48,40},{56,48},{9,1},{17,9},... | collective-permute-start | bytes 786440 | tf_op jit(solution)/shard_map/ppermute | solution.py:356
  20.9 0.0 collective-permute-done.2.lev_lo
  20.9 1.9 %collective-permute-start.3 = (f32[8,32,128]{2,1,0:T(8,128)S(1)}, f32[8,32,128]{2,1,0:T(8,128)S(1)}, u32[]{:S(2)}, u32[]{:S(2)}) collective-permute-start(f32[8,32,128]{2,1,0:T(8,128)S(1)} %get-tuple-element.37), channel_id=1, source_target_pairs={{1,0},{2,1},{3,2},{4,3},{5,4},{6,5},{7,6},{9,8},{10,9},{11,10},{12... | collective-permute-start | bytes 393224 | tf_op jit(solution)/shard_map/ppermute | solution.py:358
  22.8 8.5 %collective-permute-done.3.lev_hi = f32[8,32,128]{2,1,0:T(8,128)S(1)} collective-permute-done((f32[8,32,128]{2,1,0:T(8,128)S(1)}, f32[8,32,128]{2,1,0:T(8,128)S(1)}, u32[]{:S(2)}, u32[]{:S(2)}) %collective-permute-start.3) | collective-permute-done | bytes 131104 | tf_op jit(solution)/shard_map/ppermute | solution.py:358
  31.3 0.0 collective-permute-done.lon_lo
  31.3 0.0 collective-permute-done.1.lon_hi
  31.3 0.0 collective-permute-done.4.lat
  31.4 0.3 shard_map.51.after.rest_1_.pa
  31.6 0.9 collective-permute-start.10
  32.5 5.8 %shard_map.52 = (f32[8,32,64,128]{3,2,1,0:T(8,128)S(1)}, f32[8,32,64,128]{3,2,1,0:T(8,128)S(1)}, f32[8,32,64,128]{3,2,1,0:T(8,128)S(1)}) custom-call(f32[8,32,64,128]{3,2,1,0:T(8,128)S(1)} %get-tuple-element.33.u, f32[16,64,128]{2,1,0:T(8,128)S(1)} %get-tuple-element.65.pa, f32[16,64,128]{2,1,0:T(8,128)S(1)} %get-tuple-element.64.pb, ...), custom_call_target="tpu_custom_call" | custom-call | flops 20000000 | tf_op jit(solution)/shard_map/pallas_call | solution.py:387
  38.4 0.0 copy-start
  38.4 0.0 collective-permute-done.5.lat
  38.4 0.5 shard_map.53
  38.9 1.3 collective-permute-start.11
  40.1 5.0 %collective-permute-start.8 = (f32[8,32,128]{2,1,0:T(8,128)S(1)}, f32[8,32,128]{2,1,0:T(8,128)S(1)}, u32[]{:S(2)}, u32[]{:S(2)}) collective-permute-start(f32[8,32,128]{2,1,0:T(8,128)S(1)} %get-tuple-element.44), channel_id=1, source_target_pairs={{0,1},{1,2},{2,3},{3,4},{4,5},{5,6},{6,7},{8,9},{9,10},{10,11},{11... | collective-permute-start | bytes 393224 | tf_op jit(solution)/shard_map/ppermute | solution.py:357
  45.1 3.5 %collective-permute-start.6 = (f32[8,64,128]{2,1,0:T(8,128)S(1)}, f32[8,64,128]{2,1,0:T(8,128)S(1)}, u32[]{:S(2)}, u32[]{:S(2)}) collective-permute-start(f32[8,64,128]{2,1,0:T(8,128)S(1)} %get-tuple-element.42), channel_id=1, source_target_pairs={{0,8},{8,16},{16,24},{24,32},{32,40},{40,48},{48,56},{1,9},{9,17},... | collective-permute-start | bytes 786440 | tf_op jit(solution)/shard_map/ppermute | solution.py:355
  48.6 3.6 %collective-permute-start.7 = (f32[8,64,128]{2,1,0:T(8,128)S(1)}, f32[8,64,128]{2,1,0:T(8,128)S(1)}, u32[]{:S(2)}, u32[]{:S(2)}) collective-permute-start(f32[8,64,128]{2,1,0:T(8,128)S(1)} %get-tuple-element.43), channel_id=1, source_target_pairs={{8,0},{16,8},{24,16},{32,24},{40,32},{48,40},{56,48},{9,1},{17,9},... | collective-permute-start | bytes 786440 | tf_op jit(solution)/shard_map/ppermute | solution.py:356
  52.2 1.9 %collective-permute-start.9 = (f32[8,32,128]{2,1,0:T(8,128)S(1)}, f32[8,32,128]{2,1,0:T(8,128)S(1)}, u32[]{:S(2)}, u32[]{:S(2)}) collective-permute-start(f32[8,32,128]{2,1,0:T(8,128)S(1)} %get-tuple-element.45), channel_id=1, source_target_pairs={{1,0},{2,1},{3,2},{4,3},{5,4},{6,5},{7,6},{9,8},{10,9},{11,10},{12... | collective-permute-start | bytes 393224 | tf_op jit(solution)/shard_map/ppermute | solution.py:358
  54.1 9.0 %collective-permute-done.9.lev_hi = f32[8,32,128]{2,1,0:T(8,128)S(1)} collective-permute-done((f32[8,32,128]{2,1,0:T(8,128)S(1)}, f32[8,32,128]{2,1,0:T(8,128)S(1)}, u32[]{:S(2)}, u32[]{:S(2)}) %collective-permute-start.9) | collective-permute-done | bytes 131104 | tf_op jit(solution)/shard_map/ppermute | solution.py:358
  63.1 0.0 collective-permute-done.6.lon_lo
  63.1 0.0 collective-permute-done.7.lon_hi
  63.1 0.0 collective-permute-done.10.lat
  63.2 0.3 shard_map.54.after.rest_1_.pa
  63.4 1.3 collective-permute-start.16
  64.7 3.8 %shard_map.55.rest_0_.u = f32[8,32,64,128]{3,2,1,0:T(8,128)S(1)} custom-call(f32[8,32,64,128]{3,2,1,0:T(8,128)S(1)} %get-tuple-element.40.rest_0_.u, f32[16,64,128]{2,1,0:T(8,128)S(1)} %shard_map.51.after.rest_1_.pa, f32[16,64,128]{2,1,0:T(8,128)S(1)} %get-tuple-element.41.pb, f32[8,64,128]{2,1,0:T(8,128)S(1)} %collective-permute-done.6.lon_lo, ...), custom_call_target="tpu_custom_call" | custom-call | flops 20000000 | tf_op jit(solution)/shard_map/pallas_call | solution.py:396
  68.5 0.0 collective-permute-done.11.lat
  68.6 0.5 shard_map.56
  69.0 0.0 copy-start.1
  69.0 0.9 collective-permute-start.17
  69.9 3.0 %collective-permute-start.14 = (f32[8,32,128]{2,1,0:T(8,128)S(1)}, f32[8,32,128]{2,1,0:T(8,128)S(1)}, u32[]{:S(2)}, u32[]{:S(2)}) collective-permute-start(f32[8,32,128]{2,1,0:T(8,128)S(1)} %get-tuple-element.51), channel_id=1, source_target_pairs={{0,1},{1,2},{2,3},{3,4},{4,5},{5,6},{6,7},{8,9},{9,10},{10,11},{11... | collective-permute-start | bytes 393224 | tf_op jit(solution)/shard_map/ppermute | solution.py:357
  72.9 6.6 %collective-permute-start.12 = (f32[8,64,128]{2,1,0:T(8,128)S(1)}, f32[8,64,128]{2,1,0:T(8,128)S(1)}, u32[]{:S(2)}, u32[]{:S(2)}) collective-permute-start(f32[8,64,128]{2,1,0:T(8,128)S(1)} %get-tuple-element.49), channel_id=1, source_target_pairs={{0,8},{8,16},{16,24},{24,32},{32,40},{40,48},{48,56},{1,9},{9,17},... | collective-permute-start | bytes 786440 | tf_op jit(solution)/shard_map/ppermute | solution.py:355
  79.5 1.9 %collective-permute-start.13 = (f32[8,64,128]{2,1,0:T(8,128)S(1)}, f32[8,64,128]{2,1,0:T(8,128)S(1)}, u32[]{:S(2)}, u32[]{:S(2)}) collective-permute-start(f32[8,64,128]{2,1,0:T(8,128)S(1)} %get-tuple-element.50), channel_id=1, source_target_pairs={{8,0},{16,8},{24,16},{32,24},{40,32},{48,40},{56,48},{9,1},{17,9},... | collective-permute-start | bytes 786440 | tf_op jit(solution)/shard_map/ppermute | solution.py:356
  81.5 1.9 %collective-permute-start.15 = (f32[8,32,128]{2,1,0:T(8,128)S(1)}, f32[8,32,128]{2,1,0:T(8,128)S(1)}, u32[]{:S(2)}, u32[]{:S(2)}) collective-permute-start(f32[8,32,128]{2,1,0:T(8,128)S(1)} %get-tuple-element.52), channel_id=1, source_target_pairs={{1,0},{2,1},{3,2},{4,3},{5,4},{6,5},{7,6},{9,8},{10,9},{11,10},{12... | collective-permute-start | bytes 393224 | tf_op jit(solution)/shard_map/ppermute | solution.py:358
  83.4 9.9 %collective-permute-done.15.lev_hi = f32[8,32,128]{2,1,0:T(8,128)S(1)} collective-permute-done((f32[8,32,128]{2,1,0:T(8,128)S(1)}, f32[8,32,128]{2,1,0:T(8,128)S(1)}, u32[]{:S(2)}, u32[]{:S(2)}) %collective-permute-start.15) | collective-permute-done | bytes 131104 | tf_op jit(solution)/shard_map/ppermute | solution.py:358
  93.3 0.3 shard_map.57.after.rest_1_.pa
  93.6 4.0 %shard_map.58.rest_0_.u = f32[8,32,64,128]{3,2,1,0:T(8,128)S(1)} custom-call(f32[8,32,64,128]{3,2,1,0:T(8,128)S(1)} %shard_map.55.rest_0_.u, f32[16,64,128]{2,1,0:T(8,128)S(1)} %shard_map.54.after.rest_1_.pa, f32[16,64,128]{2,1,0:T(8,128)S(1)} %get-tuple-element.48.pb, f32[8,64,128]{2,1,0:T(8,128)S(1)} %collective-permute-done.12.lon_lo, ...), custom_call_target="tpu_custom_call" | custom-call | flops 20000000 | tf_op jit(solution)/shard_map/pallas_call | solution.py:396
  97.5 0.4 shard_map.59
  98.0 2.1 %collective-permute-start.20 = (f32[8,64,128]{2,1,0:T(8,128)S(1)}, f32[8,64,128]{2,1,0:T(8,128)S(1)}, u32[]{:S(2)}, u32[]{:S(2)}) collective-permute-start(f32[8,64,128]{2,1,0:T(8,128)S(1)} %get-tuple-element.54), channel_id=1, source_target_pairs={{0,8},{8,16},{16,24},{24,32},{32,40},{40,48},{48,56},{1,9},{9,17},... | collective-permute-start | bytes 786440 | tf_op jit(solution)/shard_map/ppermute | solution.py:355
  100.1 5.1 %collective-permute-start.21 = (f32[8,64,128]{2,1,0:T(8,128)S(1)}, f32[8,64,128]{2,1,0:T(8,128)S(1)}, u32[]{:S(2)}, u32[]{:S(2)}) collective-permute-start(f32[8,64,128]{2,1,0:T(8,128)S(1)} %get-tuple-element.55), channel_id=1, source_target_pairs={{8,0},{16,8},{24,16},{32,24},{40,32},{48,40},{56,48},{9,1},{17,9},... | collective-permute-start | bytes 786440 | tf_op jit(solution)/shard_map/ppermute | solution.py:356
  105.2 4.0 %collective-permute-start.22 = (f32[8,32,128]{2,1,0:T(8,128)S(1)}, f32[8,32,128]{2,1,0:T(8,128)S(1)}, u32[]{:S(2)}, u32[]{:S(2)}) collective-permute-start(f32[8,32,128]{2,1,0:T(8,128)S(1)} %get-tuple-element.56), channel_id=1, source_target_pairs={{0,1},{1,2},{2,3},{3,4},{4,5},{5,6},{6,7},{8,9},{9,10},{10,11},{11... | collective-permute-start | bytes 393224 | tf_op jit(solution)/shard_map/ppermute | solution.py:357
  109.2 1.9 %collective-permute-start.23 = (f32[8,32,128]{2,1,0:T(8,128)S(1)}, f32[8,32,128]{2,1,0:T(8,128)S(1)}, u32[]{:S(2)}, u32[]{:S(2)}) collective-permute-start(f32[8,32,128]{2,1,0:T(8,128)S(1)} %get-tuple-element.57), channel_id=1, source_target_pairs={{1,0},{2,1},{3,2},{4,3},{5,4},{6,5},{7,6},{9,8},{10,9},{11,10},{12... | collective-permute-start | bytes 393224 | tf_op jit(solution)/shard_map/ppermute | solution.py:358
  111.1 2.3 %collective-permute-done.22.lev_lo = f32[8,32,128]{2,1,0:T(8,128)S(1)} collective-permute-done((f32[8,32,128]{2,1,0:T(8,128)S(1)}, f32[8,32,128]{2,1,0:T(8,128)S(1)}, u32[]{:S(2)}, u32[]{:S(2)}) %collective-permute-start.22) | collective-permute-done | bytes 131104 | tf_op jit(solution)/shard_map/ppermute | solution.py:357
  113.4 6.9 %collective-permute-done.23.lev_hi = f32[8,32,128]{2,1,0:T(8,128)S(1)} collective-permute-done((f32[8,32,128]{2,1,0:T(8,128)S(1)}, f32[8,32,128]{2,1,0:T(8,128)S(1)}, u32[]{:S(2)}, u32[]{:S(2)}) %collective-permute-start.23) | collective-permute-done | bytes 131104 | tf_op jit(solution)/shard_map/ppermute | solution.py:358
  120.4 5.2 %shard_map.60 = (f32[8,32,64,128]{3,2,1,0:T(8,128)}, f32[8,32,64,128]{3,2,1,0:T(8,128)S(1)}, f32[8,32,64,128]{3,2,1,0:T(8,128)S(1)}, f32[8,64,128]{2,1,0:T(8,128)S(1)}) custom-call(f32[8,32,64,128]{3,2,1,0:T(8,128)S(1)} %shard_map.58.rest_0_.u, f32[16,64,128]{2,1,0:T(8,128)S(1)} %shard_map.57.after.rest_1_.pa, ...), custom_call_target="tpu_custom_call", output_to_operand_aliasing={{1}: (7, {}), {2}: (8, {})} | custom-call | flops 20000000 | tf_op jit(solution)/shard_map/pallas_call | solution.py:412
  125.6 0.1 collective-permute-start.27
  125.7 1.4 collective-permute-start.19
  127.0 0.7 collective-permute-start.18
  127.8 0.1 collective-permute-start.28
  127.9 27.8 %collective-permute-done.28.rest_1_ = f32[8,64,128]{2,1,0:T(8,128)S(1)} collective-permute-done((f32[8,64,128]{2,1,0:T(8,128)S(1)}, f32[8,64,128]{2,1,0:T(8,128)S(1)}, u32[]{:S(2)}, u32[]{:S(2)}) %collective-permute-start.28) | collective-permute-done | bytes 262176 | tf_op jit(solution)/shard_map/ppermute | solution.py:430
  155.7 6.8 %collective-permute-start.29 = (f32[8,64,128]{2,1,0:T(8,128)S(1)}, f32[8,64,128]{2,1,0:T(8,128)S(1)}, u32[]{:S(2)}, u32[]{:S(2)}) collective-permute-start(f32[8,64,128]{2,1,0:T(8,128)S(1)} %add.17), channel_id=1, source_target_pairs={{0,32},{8,40},{16,48},{24,56},{1,33},{9,41},{17,49},{25,57},{2,34}... | collective-permute-start | bytes 786440 | tf_op jit(solution)/shard_map/ppermute | solution.py:430
  162.5 1.5 shard_map.61
  164.1 0.1 collective-permute-start.24
  164.2 1.2 collective-permute-done.24.rest_0_
  165.4 0.3 collective-permute-start.25
  165.6 5.1 %collective-permute-done.25.rest_1_ = f32[64,128]{1,0:T(8,128)S(1)} collective-permute-done((f32[64,128]{1,0:T(8,128)S(1)}, f32[64,128]{1,0:T(8,128)S(1)}, u32[]{:S(2)}, u32[]{:S(2)}) %collective-permute-start.25) | collective-permute-done | bytes 32800 | tf_op jit(solution)/shard_map/ppermute | solution.py:430
  170.8 1.3 collective-permute-start.26
  172.1 4.4 %shard_map.62.rest_3_ = f32[8,32,64,128]{3,2,1,0:T(8,128)} custom-call(f32[8,32,64,128]{3,2,1,0:T(8,128)S(1)} %get-tuple-element.61.sums, f32[8,64,128]{2,1,0:T(8,128)S(1)} %collective-permute-done.27.rest_0_, f32[8,64,128]{2,1,0:T(8,128)S(1)} %collective-permute-done.28.rest_1_, f32[8,64,128]{2,1,0:T(8,128)S(1)} %collective-permute-done.29.rest_2_), custom_call_target="tpu_custom_call" | custom-call | flops 1000000 | tf_op jit(solution)/shard_map/pallas_call | solution.py:434
  176.5 1.1 shard_map.63
  (19 shorter events, 0.1 us)
Async XLA Ops:
  1.9 29.4 %collective-permute-start.4 = (f32[16,64,128]{2,1,0:T(8,128)S(1)}, f32[16,64,128]{2,1,0:T(8,128)S(1)}, u32[]{:S(2)}, u32[]{:S(2)}) collective-permute-start(f32[16,64,128]{2,1,0:T(8,128)S(1)} %get-tuple-element.65.pa), channel_id=1, source_target_pairs={{0,64},{64,0},{1,65},{65,1},{2,66},{66,2},{3,67},{67,3},{4,68},{68... | collective-permute-start | bytes 1572872 | tf_op jit(solution)/shard_map/ppermute | solution.py:364
  2.9 35.5 %collective-permute-start.5 = (f32[16,64,128]{2,1,0:T(8,128)S(1)}, f32[16,64,128]{2,1,0:T(8,128)S(1)}, u32[]{:S(2)}, u32[]{:S(2)}) collective-permute-start(f32[16,64,128]{2,1,0:T(8,128)S(1)} %get-tuple-element.64.pb), channel_id=1, source_target_pairs={{0,64},{64,0},{1,65},{65,1},{2,66},{66,2},{3,67},{67,3},{4,68},{68... | collective-permute-start | bytes 1572872 | tf_op jit(solution)/shard_map/ppermute | solution.py:365
  8.3 12.5 %collective-permute-start.2 = (f32[8,32,128]{2,1,0:T(8,128)S(1)}, f32[8,32,128]{2,1,0:T(8,128)S(1)}, u32[]{:S(2)}, u32[]{:S(2)}) collective-permute-start(f32[8,32,128]{2,1,0:T(8,128)S(1)} %get-tuple-element.36), channel_id=1, source_target_pairs={{0,1},{1,2},{2,3},{3,4},{4,5},{5,6},{6,7},{8,9},{9,10},{10,11},{11... | collective-permute-start | bytes 393224 | tf_op jit(solution)/shard_map/ppermute | solution.py:357
  13.8 17.6 %collective-permute-start = (f32[8,64,128]{2,1,0:T(8,128)S(1)}, f32[8,64,128]{2,1,0:T(8,128)S(1)}, u32[]{:S(2)}, u32[]{:S(2)}) collective-permute-start(f32[8,64,128]{2,1,0:T(8,128)S(1)} %get-tuple-element.34), channel_id=1, source_target_pairs={{0,8},{8,16},{16,24},{24,32},{32,40},{40,48},{48,56},{1,9},{9,17},... | collective-permute-start | bytes 786440 | tf_op jit(solution)/shard_map/ppermute | solution.py:355
  15.7 15.6 %collective-permute-start.1 = (f32[8,64,128]{2,1,0:T(8,128)S(1)}, f32[8,64,128]{2,1,0:T(8,128)S(1)}, u32[]{:S(2)}, u32[]{:S(2)}) collective-permute-start(f32[8,64,128]{2,1,0:T(8,128)S(1)} %get-tuple-element.35), channel_id=1, source_target_pairs={{8,0},{16,8},{24,16},{32,24},{40,32},{48,40},{56,48},{9,1},{17,9},... | collective-permute-start | bytes 786440 | tf_op jit(solution)/shard_map/ppermute | solution.py:356
  20.9 10.5 %collective-permute-start.3 = (f32[8,32,128]{2,1,0:T(8,128)S(1)}, f32[8,32,128]{2,1,0:T(8,128)S(1)}, u32[]{:S(2)}, u32[]{:S(2)}) collective-permute-start(f32[8,32,128]{2,1,0:T(8,128)S(1)} %get-tuple-element.37), channel_id=1, source_target_pairs={{1,0},{2,1},{3,2},{4,3},{5,4},{6,5},{7,6},{9,8},{10,9},{11,10},{12... | collective-permute-start | bytes 393224 | tf_op jit(solution)/shard_map/ppermute | solution.py:358
  31.6 31.5 %collective-permute-start.10 = (f32[16,64,128]{2,1,0:T(8,128)S(1)}, f32[16,64,128]{2,1,0:T(8,128)S(1)}, u32[]{:S(2)}, u32[]{:S(2)}) collective-permute-start(f32[16,64,128]{2,1,0:T(8,128)S(1)} %shard_map.51.after.rest_1_.pa), channel_id=1, source_target_pairs={{0,64},{64,0},{1,65},{65,1},{2,66},{66,2},{3,67},{67,3},{4,68},{68... | collective-permute-start | bytes 1572872 | tf_op jit(solution)/shard_map/ppermute | solution.py:385
  38.4 26.3 %copy-start = (f32[8,32,64,128]{3,2,1,0:T(8,128)}, f32[8,32,64,128]{3,2,1,0:T(8,128)S(1)}, u32[]{:S(2)}) copy-start(f32[8,32,64,128]{3,2,1,0:T(8,128)S(1)} %get-tuple-element.47.f.f_in) | copy-start | bytes 25165828
  38.9 29.7 %collective-permute-start.11 = (f32[16,64,128]{2,1,0:T(8,128)S(1)}, f32[16,64,128]{2,1,0:T(8,128)S(1)}, u32[]{:S(2)}, u32[]{:S(2)}) collective-permute-start(f32[16,64,128]{2,1,0:T(8,128)S(1)} %get-tuple-element.41.pb), channel_id=1, source_target_pairs={{0,64},{64,0},{1,65},{65,1},{2,66},{66,2},{3,67},{67,3},{4,68},{68... | collective-permute-start | bytes 1572872 | tf_op jit(solution)/shard_map/ppermute | solution.py:406
  40.1 12.1 %collective-permute-start.8 = (f32[8,32,128]{2,1,0:T(8,128)S(1)}, f32[8,32,128]{2,1,0:T(8,128)S(1)}, u32[]{:S(2)}, u32[]{:S(2)}) collective-permute-start(f32[8,32,128]{2,1,0:T(8,128)S(1)} %get-tuple-element.44), channel_id=1, source_target_pairs={{0,1},{1,2},{2,3},{3,4},{4,5},{5,6},{6,7},{8,9},{9,10},{10,11},{11... | collective-permute-start | bytes 393224 | tf_op jit(solution)/shard_map/ppermute | solution.py:357
  45.1 18.0 %collective-permute-start.6 = (f32[8,64,128]{2,1,0:T(8,128)S(1)}, f32[8,64,128]{2,1,0:T(8,128)S(1)}, u32[]{:S(2)}, u32[]{:S(2)}) collective-permute-start(f32[8,64,128]{2,1,0:T(8,128)S(1)} %get-tuple-element.42), channel_id=1, source_target_pairs={{0,8},{8,16},{16,24},{24,32},{32,40},{40,48},{48,56},{1,9},{9,17},... | collective-permute-start | bytes 786440 | tf_op jit(solution)/shard_map/ppermute | solution.py:355
  48.6 14.5 %collective-permute-start.7 = (f32[8,64,128]{2,1,0:T(8,128)S(1)}, f32[8,64,128]{2,1,0:T(8,128)S(1)}, u32[]{:S(2)}, u32[]{:S(2)}) collective-permute-start(f32[8,64,128]{2,1,0:T(8,128)S(1)} %get-tuple-element.43), channel_id=1, source_target_pairs={{8,0},{16,8},{24,16},{32,24},{40,32},{48,40},{56,48},{9,1},{17,9},... | collective-permute-start | bytes 786440 | tf_op jit(solution)/shard_map/ppermute | solution.py:356
  52.2 10.9 %collective-permute-start.9 = (f32[8,32,128]{2,1,0:T(8,128)S(1)}, f32[8,32,128]{2,1,0:T(8,128)S(1)}, u32[]{:S(2)}, u32[]{:S(2)}) collective-permute-start(f32[8,32,128]{2,1,0:T(8,128)S(1)} %get-tuple-element.45), channel_id=1, source_target_pairs={{1,0},{2,1},{3,2},{4,3},{5,4},{6,5},{7,6},{9,8},{10,9},{11,10},{12... | collective-permute-start | bytes 393224 | tf_op jit(solution)/shard_map/ppermute | solution.py:358
  63.4 29.8 %collective-permute-start.16 = (f32[16,64,128]{2,1,0:T(8,128)S(1)}, f32[16,64,128]{2,1,0:T(8,128)S(1)}, u32[]{:S(2)}, u32[]{:S(2)}) collective-permute-start(f32[16,64,128]{2,1,0:T(8,128)S(1)} %shard_map.54.after.rest_1_.pa), channel_id=1, source_target_pairs={{0,64},{64,0},{1,65},{65,1},{2,66},{66,2},{3,67},{67,3},{4,68},{68... | collective-permute-start | bytes 1572872 | tf_op jit(solution)/shard_map/ppermute | solution.py:385
  69.0 24.5 %copy-start.1 = (f32[8,32,64,128]{3,2,1,0:T(8,128)S(1)}, f32[8,32,64,128]{3,2,1,0:T(8,128)}, u32[]{:S(2)}) copy-start(f32[8,32,64,128]{3,2,1,0:T(8,128)} %copy-done) | copy-start | bytes 25165828
  69.0 28.5 %collective-permute-start.17 = (f32[16,64,128]{2,1,0:T(8,128)S(1)}, f32[16,64,128]{2,1,0:T(8,128)S(1)}, u32[]{:S(2)}, u32[]{:S(2)}) collective-permute-start(f32[16,64,128]{2,1,0:T(8,128)S(1)} %get-tuple-element.48.pb), channel_id=1, source_target_pairs={{0,64},{64,0},{1,65},{65,1},{2,66},{66,2},{3,67},{67,3},{4,68},{68... | collective-permute-start | bytes 1572872 | tf_op jit(solution)/shard_map/ppermute | solution.py:406
  69.9 11.5 %collective-permute-start.14 = (f32[8,32,128]{2,1,0:T(8,128)S(1)}, f32[8,32,128]{2,1,0:T(8,128)S(1)}, u32[]{:S(2)}, u32[]{:S(2)}) collective-permute-start(f32[8,32,128]{2,1,0:T(8,128)S(1)} %get-tuple-element.51), channel_id=1, source_target_pairs={{0,1},{1,2},{2,3},{3,4},{4,5},{5,6},{6,7},{8,9},{9,10},{10,11},{11... | collective-permute-start | bytes 393224 | tf_op jit(solution)/shard_map/ppermute | solution.py:357
  72.9 20.3 %collective-permute-start.12 = (f32[8,64,128]{2,1,0:T(8,128)S(1)}, f32[8,64,128]{2,1,0:T(8,128)S(1)}, u32[]{:S(2)}, u32[]{:S(2)}) collective-permute-start(f32[8,64,128]{2,1,0:T(8,128)S(1)} %get-tuple-element.49), channel_id=1, source_target_pairs={{0,8},{8,16},{16,24},{24,32},{32,40},{40,48},{48,56},{1,9},{9,17},... | collective-permute-start | bytes 786440 | tf_op jit(solution)/shard_map/ppermute | solution.py:355
  79.5 13.8 %collective-permute-start.13 = (f32[8,64,128]{2,1,0:T(8,128)S(1)}, f32[8,64,128]{2,1,0:T(8,128)S(1)}, u32[]{:S(2)}, u32[]{:S(2)}) collective-permute-start(f32[8,64,128]{2,1,0:T(8,128)S(1)} %get-tuple-element.50), channel_id=1, source_target_pairs={{8,0},{16,8},{24,16},{32,24},{40,32},{48,40},{56,48},{9,1},{17,9},... | collective-permute-start | bytes 786440 | tf_op jit(solution)/shard_map/ppermute | solution.py:356
  81.5 11.8 %collective-permute-start.15 = (f32[8,32,128]{2,1,0:T(8,128)S(1)}, f32[8,32,128]{2,1,0:T(8,128)S(1)}, u32[]{:S(2)}, u32[]{:S(2)}) collective-permute-start(f32[8,32,128]{2,1,0:T(8,128)S(1)} %get-tuple-element.52), channel_id=1, source_target_pairs={{1,0},{2,1},{3,2},{4,3},{5,4},{6,5},{7,6},{9,8},{10,9},{11,10},{12... | collective-permute-start | bytes 393224 | tf_op jit(solution)/shard_map/ppermute | solution.py:358
  98.0 22.4 %collective-permute-start.20 = (f32[8,64,128]{2,1,0:T(8,128)S(1)}, f32[8,64,128]{2,1,0:T(8,128)S(1)}, u32[]{:S(2)}, u32[]{:S(2)}) collective-permute-start(f32[8,64,128]{2,1,0:T(8,128)S(1)} %get-tuple-element.54), channel_id=1, source_target_pairs={{0,8},{8,16},{16,24},{24,32},{32,40},{40,48},{48,56},{1,9},{9,17},... | collective-permute-start | bytes 786440 | tf_op jit(solution)/shard_map/ppermute | solution.py:355
  100.1 20.2 %collective-permute-start.21 = (f32[8,64,128]{2,1,0:T(8,128)S(1)}, f32[8,64,128]{2,1,0:T(8,128)S(1)}, u32[]{:S(2)}, u32[]{:S(2)}) collective-permute-start(f32[8,64,128]{2,1,0:T(8,128)S(1)} %get-tuple-element.55), channel_id=1, source_target_pairs={{8,0},{16,8},{24,16},{32,24},{40,32},{48,40},{56,48},{9,1},{17,9},... | collective-permute-start | bytes 786440 | tf_op jit(solution)/shard_map/ppermute | solution.py:356
  105.2 8.2 %collective-permute-start.22 = (f32[8,32,128]{2,1,0:T(8,128)S(1)}, f32[8,32,128]{2,1,0:T(8,128)S(1)}, u32[]{:S(2)}, u32[]{:S(2)}) collective-permute-start(f32[8,32,128]{2,1,0:T(8,128)S(1)} %get-tuple-element.56), channel_id=1, source_target_pairs={{0,1},{1,2},{2,3},{3,4},{4,5},{5,6},{6,7},{8,9},{9,10},{10,11},{11... | collective-permute-start | bytes 393224 | tf_op jit(solution)/shard_map/ppermute | solution.py:357
  109.2 11.1 %collective-permute-start.23 = (f32[8,32,128]{2,1,0:T(8,128)S(1)}, f32[8,32,128]{2,1,0:T(8,128)S(1)}, u32[]{:S(2)}, u32[]{:S(2)}) collective-permute-start(f32[8,32,128]{2,1,0:T(8,128)S(1)} %get-tuple-element.57), channel_id=1, source_target_pairs={{1,0},{2,1},{3,2},{4,3},{5,4},{6,5},{7,6},{9,8},{10,9},{11,10},{12... | collective-permute-start | bytes 393224 | tf_op jit(solution)/shard_map/ppermute | solution.py:358
  125.6 2.2 %collective-permute-start.27 = (f32[8,64,128]{2,1,0:T(8,128)S(1)}, f32[8,64,128]{2,1,0:T(8,128)S(1)}, u32[]{:S(2)}, u32[]{:S(2)}) collective-permute-start(f32[8,64,128]{2,1,0:T(8,128)S(1)} %get-tuple-element.62), channel_id=1, source_target_pairs={{0,8},{8,0},{16,24},{24,16},{32,40},{40,32},{48,56},{56,48},{1,9},... | collective-permute-start | bytes 786440 | tf_op jit(solution)/shard_map/ppermute | solution.py:430
  125.7 36.8 %collective-permute-start.19 = (f32[16,64,128]{2,1,0:T(8,128)S(1)}, f32[16,64,128]{2,1,0:T(8,128)S(1)}, u32[]{:S(2)}, u32[]{:S(2)}) collective-permute-start(f32[16,64,128]{2,1,0:T(8,128)S(1)} %get-tuple-element.53.pb), channel_id=1, source_target_pairs={{0,64},{64,0},{1,65},{65,1},{2,66},{66,2},{3,67},{67,3},{4,68},{68... | collective-permute-start | bytes 1572872 | tf_op jit(solution)/shard_map/ppermute | solution.py:406
  127.0 35.5 %collective-permute-start.18 = (f32[16,64,128]{2,1,0:T(8,128)S(1)}, f32[16,64,128]{2,1,0:T(8,128)S(1)}, u32[]{:S(2)}, u32[]{:S(2)}) collective-permute-start(f32[16,64,128]{2,1,0:T(8,128)S(1)} %shard_map.57.after.rest_1_.pa), channel_id=1, source_target_pairs={{0,64},{64,0},{1,65},{65,1},{2,66},{66,2},{3,67},{67,3},{4,68},{68... | collective-permute-start | bytes 1572872 | tf_op jit(solution)/shard_map/ppermute | solution.py:385
  127.8 27.8 %collective-permute-start.28 = (f32[8,64,128]{2,1,0:T(8,128)S(1)}, f32[8,64,128]{2,1,0:T(8,128)S(1)}, u32[]{:S(2)}, u32[]{:S(2)}) collective-permute-start(f32[8,64,128]{2,1,0:T(8,128)S(1)} %add.16), channel_id=1, source_target_pairs={{0,16},{8,24},{16,0},{24,8},{32,48},{40,56},{48,32},{56,40},{1,17}... | collective-permute-start | bytes 786440 | tf_op jit(solution)/shard_map/ppermute | solution.py:430
  155.7 16.4 %collective-permute-start.29 = (f32[8,64,128]{2,1,0:T(8,128)S(1)}, f32[8,64,128]{2,1,0:T(8,128)S(1)}, u32[]{:S(2)}, u32[]{:S(2)}) collective-permute-start(f32[8,64,128]{2,1,0:T(8,128)S(1)} %add.17), channel_id=1, source_target_pairs={{0,32},{8,40},{16,48},{24,56},{1,33},{9,41},{17,49},{25,57},{2,34}... | collective-permute-start | bytes 786440 | tf_op jit(solution)/shard_map/ppermute | solution.py:430
  164.1 1.3 collective-permute-start.24
  165.4 5.4 %collective-permute-start.25 = (f32[64,128]{1,0:T(8,128)S(1)}, f32[64,128]{1,0:T(8,128)S(1)}, u32[]{:S(2)}, u32[]{:S(2)}) collective-permute-start(f32[64,128]{1,0:T(8,128)S(1)} %add.14), channel_id=1, source_target_pairs={{0,16},{8,24},{16,0},{24,8},{32,48},{40,56},{48,32},{56,40},{1,17}... | collective-permute-start | bytes 98312 | tf_op jit(solution)/shard_map/ppermute | solution.py:430
  170.8 5.7 %collective-permute-start.26 = (f32[64,128]{1,0:T(8,128)S(1)}, f32[64,128]{1,0:T(8,128)S(1)}, u32[]{:S(2)}, u32[]{:S(2)}) collective-permute-start(f32[64,128]{1,0:T(8,128)S(1)} %add.15), channel_id=1, source_target_pairs={{0,32},{8,40},{16,48},{24,56},{1,33},{9,41},{17,49},{25,57},{2,34}... | collective-permute-start | bytes 98312 | tf_op jit(solution)/shard_map/ppermute | solution.py:430

commit v2 on v1

v2 whole, which is shorter than its diff:
```python
import functools

import jax
import jax.numpy as jnp
from jax import lax
from jax.experimental import pallas as pl
from jax.experimental.pallas import tpu as pltpu
from jax.sharding import PartitionSpec as P


STEPS = 4
BLOCK = 4
VMEM = pl.BlockSpec(memory_space=pltpu.VMEM)
HBM = pl.BlockSpec(memory_space=pltpu.HBM)
ANY = pl.BlockSpec(memory_space=pl.ANY)


def in_vmem(x):
    return pltpu.with_memory_space_constraint(x, pltpu.VMEM)


def in_hbm(x):
    return pltpu.with_memory_space_constraint(x, pltpu.HBM)


def new_rows(c, im, ip, nb, klo, khi, d, f):
    km = jnp.concatenate([klo, c[:-1]], axis=0)
    kp = jnp.concatenate([c[1:], khi], axis=0)
    spread = (im + ip) + nb + (km + kp) - 6.0 * c
    return c + d * spread + f


def sweep(lo, hi, row, below, above, nb, klo, khi, d, f, put, carry=None):
    def block(first, bottom, top, carry):
        rows = [bottom() if bottom else row(first - 1)]
        rows += [row(first + r) for r in range(BLOCK)]
        rows += [top() if top else row(first + BLOCK)]
        for r in range(BLOCK):
            i = first + r
            new = new_rows(rows[r + 1], rows[r], rows[r + 2], nb(i), klo(i), khi(i), d(i), f(i))
            carry = put(i, new, carry)
        return carry

    carry = block(lo, below, None, carry)

    def body(b, carry):
        return block(lo + b * BLOCK, None, None, carry)

    n = (hi - lo) // BLOCK
    carry = lax.fori_loop(1, n - 1, body, carry)
    return block(hi - BLOCK, None, above, carry)


def plane_at(depth, n):
    low = lax.axis_index("lat") == 0
    return jnp.where(low, n - 1 - depth, depth)


def faces_kernel(u, lon_lo, lon_hi, lev_lo, lev_hi):
    nj, ni, nk, _ = u.shape
    for j in range(nj):
        lon_lo[j] = u[j, 0]
        lon_hi[j] = u[j, ni - 1]
        lev_lo[j] = u[j, :, 0, :]
        lev_hi[j] = u[j, :, nk - 1, :]


def load_kernel(u_in, d_in, f_in, u, pb, d_edge, f_edge, lon_lo, lon_hi, lev_lo, lev_hi, sem):
    nj, ni = u.shape[:2]
    q = ni // 4
    pj = plane_at(0, nj)
    copies = [pltpu.make_async_copy(u_in.at[j], u.at[j], sem.at[j]) for j in range(nj)]
    copies += [
        pltpu.make_async_copy(d_in.at[pj], d_edge, sem.at[nj]),
        pltpu.make_async_copy(f_in.at[pj], f_edge, sem.at[nj + 1]),
        pltpu.make_async_copy(u_in.at[pj, pl.ds(0, q)], pb.at[pl.ds(0, q)], sem.at[nj + 2]),
        pltpu.make_async_copy(u_in.at[pj, pl.ds(ni - q, q)], pb.at[pl.ds(q, q)], sem.at[nj + 3]),
    ]
    for copy in copies:
        copy.start()
    for copy in copies:
        copy.wait()
    faces_kernel(u, lon_lo, lon_hi, lev_lo, lev_hi)


def edge_rows(lo, hi, base, mine, below, above, u, lat, lev_lo, lev_hi, d, f, put):
    nj = u.shape[0]
    pj, pn = plane_at(0, nj), plane_at(1, nj)
    sweep(
        lo,
        hi,
        lambda i: mine[i],
        below,
        above,
        lambda i: u[pn, base + i] + lat[i],
        lambda i: lev_lo[pj, pl.ds(base + i, 1), :],
        lambda i: lev_hi[pj, pl.ds(base + i, 1), :],
        lambda i: d[base + i],
        lambda i: f[base + i],
        put,
        jnp.int32(0),
    )


def edge_a_kernel(u, pa, pb, lat, lev_lo, lev_hi, d, f, out):
    def put(i, new, carry):
        out[i] = new
        return carry

    n = pa.shape[0]
    edge_rows(0, n, n // 2, pa, lambda: pb[n // 2 - 1], lambda: pb[n // 2], u, lat, lev_lo, lev_hi, d, f, put)


def edge_b_kernel(u, pa, pb, lat, lon_lo, lon_hi, lev_lo, lev_hi, d, f, *rest):
    nj, ni, nk, _ = u.shape
    q = ni // 4
    pj = plane_at(0, nj)
    out = rest[2] if len(rest) > 1 else rest[0]

    def put(i, new, carry):
        out[i] = new
        return carry

    args = (u, lat, lev_lo, lev_hi, d, f, put)
    edge_rows(0, q, 0, pb, lambda: lon_lo[pj], lambda: pa[0], *args)
    edge_rows(q, 2 * q, 2 * q, pb, lambda: pa[2 * q - 1], lambda: lon_hi[pj], *args)
    if len(rest) > 1:
        nu, npa, _, s_lon_lo, s_lon_hi, s_lev_lo, s_lev_hi = rest
        faces_kernel(nu, s_lon_lo, s_lon_hi, s_lev_lo, s_lev_hi)
        s_lon_lo[pj] = out[0]
        s_lon_hi[pj] = out[2 * q - 1]
        for s_lev, k in ((s_lev_lo, 0), (s_lev_hi, nk - 1)):
            s_lev[pj, :q] = out[:q, k, :]
            s_lev[pj, q : 3 * q] = npa[:, k, :]
            s_lev[pj, 3 * q :] = out[q:, k, :]


def bulk_planes(u, pa, pb, lon_lo, lon_hi, lev_lo, lev_hi, d, f, put, start, finish):
    nj, ni, _, _ = u.shape
    q = ni // 4

    def run(j, lo, hi, nb, carry):
        return sweep(
            lo,
            hi,
            lambda i: u[j, i],
            (lambda: lon_lo[j]) if lo == 0 else None,
            (lambda: lon_hi[j]) if hi == ni else None,
            nb,
            lambda i: lev_lo[j, pl.ds(i, 1), :],
            lambda i: lev_hi[j, pl.ds(i, 1), :],
            lambda i: d[j, i],
            lambda i: f[j, i],
            functools.partial(put, j),
            carry,
        )

    j, inner = plane_at(1, nj), plane_at(2, nj)
    start(j, 1)
    carry = run(j, 0, q, lambda i: u[inner, i] + pb[i], zero_carry(u))
    carry = run(j, q, 3 * q, lambda i: u[inner, i] + pa[i - q], carry)
    carry = run(j, 3 * q, ni, lambda i: u[inner, i] + pb[i - 2 * q], carry)
    finish(j, 1, carry)

    def body(depth, _):
        j, outer, inner = plane_at(depth, nj), plane_at(depth - 1, nj), plane_at(depth + 1, nj)
        start(j, depth)
        carry = run(j, 0, ni, lambda i: u[outer, i] + u[inner, i], zero_carry(u))
        finish(j, depth, carry)
        return 0

    lax.fori_loop(2, nj - 1, body, 0)
    j, outer = plane_at(nj - 1, nj), plane_at(nj - 2, nj)
    start(j, nj - 1)
    carry = run(j, 0, ni, lambda i: u[outer, i], zero_carry(u))
    finish(j, nj - 1, carry)


def zero_carry(u):
    return jnp.zeros(u.shape[2:], u.dtype)


def nothing(*_):
    pass


def plain_put(out):
    def put(j, i, new, carry):
        out[j, i] = new
        return carry

    return put


def first_bulk_kernel(u, pa, pb, lon_lo, lon_hi, lev_lo, lev_hi, d_in, f_in, after, out, d, f, sem):
    del after
    nj = u.shape[0]

    def copies(j, depth):
        return (
            pltpu.make_async_copy(d_in.at[j], d.at[j], sem.at[0, depth]),
            pltpu.make_async_copy(f_in.at[j], f.at[j], sem.at[1, depth]),
        )

    for depth in range(1, nj):
        for copy in copies(plane_at(depth, nj), depth):
            copy.start()

    def start(j, depth):
        for copy in copies(j, depth):
            copy.wait()

    bulk_planes(u, pa, pb, lon_lo, lon_hi, lev_lo, lev_hi, d, f, plain_put(out), start, nothing)


def bulk_kernel(u, pa, pb, lon_lo, lon_hi, lev_lo, lev_hi, d, f, after, out):
    del after
    bulk_planes(u, pa, pb, lon_lo, lon_hi, lev_lo, lev_hi, d, f, plain_put(out), nothing, nothing)


def last_bulk_kernel(u, pa, pb, lon_lo, lon_hi, lev_lo, lev_hi, d_in, f_in, after, end, d, f, total, sem):
    del d_in, f_in, after
    nj = u.shape[0]

    def copy_out(j, depth):
        return pltpu.make_async_copy(f.at[j], end.at[j], sem.at[depth])

    def put(j, i, new, carry):
        f[j, i] = new
        carry = carry + new
        d[j, i] = carry
        return carry

    def finish(j, depth, carry):
        total[depth - 1] = carry
        copy_out(j, depth).start()

    bulk_planes(u, pa, pb, lon_lo, lon_hi, lev_lo, lev_hi, d, f, put, nothing, finish)
    for depth in range(1, nj):
        copy_out(plane_at(depth, nj), depth).wait()


def last_edge_kernel(u, pa, pb, lat, lon_lo, lon_hi, lev_lo, lev_hi, d, f, npa, npb, sums, total):
    edge_b_kernel(u, pa, pb, lat, lon_lo, lon_hi, lev_lo, lev_hi, d, f, npb)
    ni = sums.shape[0]
    q = ni // 4
    carry = zero_carry(u)
    for part, lo, n, base in ((npb, 0, q, 0), (npa, 0, 2 * q, q), (npb, q, q, 3 * q)):

        def row(r, carry):
            carry = carry + part[lo + r]
            sums[base + r] = carry
            return carry

        carry = lax.fori_loop(0, n, row, carry, unroll=4)
    total[...] = carry


def earlier(others):
    lon = lax.axis_index("lon")
    before = 0.0
    for bit, other in enumerate(others):
        before += jnp.where(lon & (1 << bit) != 0, other, 0.0)
    return before


def totals_kernel(scale, sums, *rest):
    *others, out, stage, sem = rest
    nj, ni = sums.shape[:2]

    def copy_out(j, depth):
        slot = depth % 2
        return pltpu.make_async_copy(stage.at[slot], out.at[j], sem.at[slot])

    def body(depth, _):
        j, slot = plane_at(depth, nj), depth % 2

        @pl.when(depth > 2)
        def _():
            copy_out(j, depth).wait()

        b = earlier([other[depth - 1] for other in others])

        def row(r, _):
            for q in range(BLOCK):
                i = r * BLOCK + q
                stage[slot, i] = (sums[j, i] + b) * scale
            return 0

        lax.fori_loop(0, ni // BLOCK, row, 0)
        copy_out(j, depth).start()
        return 0

    lax.fori_loop(1, nj, body, 0)
    copy_out(0, 0).wait()
    copy_out(0, 1).wait()


def last_totals_kernel(scale, sums, npa, npb, *rest):
    *others, _, _, end, out, stage, sem = rest
    ni = sums.shape[0]
    nj = out.shape[0]
    q = ni // 4
    pj = plane_at(0, nj)
    copies = [
        pltpu.make_async_copy(npb.at[pl.ds(0, q)], end.at[pj, pl.ds(0, q)], sem.at[0]),
        pltpu.make_async_copy(npa, end.at[pj, pl.ds(q, 2 * q)], sem.at[1]),
        pltpu.make_async_copy(npb.at[pl.ds(q, q)], end.at[pj, pl.ds(3 * q, q)], sem.at[2]),
    ]
    for copy in copies:
        copy.start()
    b = earlier([other[...] for other in others])

    def row(r, _):
        for p in range(BLOCK):
            i = r * BLOCK + p
            stage[i] = (sums[i] + b) * scale
        return 0

    for half in range(2):
        lax.fori_loop(half * ni // 2 // BLOCK, (half + 1) * ni // 2 // BLOCK, row, 0)
        rows = pl.ds(half * ni // 2, ni // 2)
        copies.append(pltpu.make_async_copy(stage.at[rows], out.at[pj, rows], sem.at[3 + half]))
        copies[-1].start()
    for copy in copies:
        copy.wait()


def call(kernel, out_shape, out_specs, in_specs, limit=2, scratch=(), aliases=None, flops=0):
    return pl.pallas_call(
        kernel,
        out_shape=out_shape,
        in_specs=in_specs,
        out_specs=out_specs,
        scratch_shapes=scratch,
        input_output_aliases=aliases or {},
        compiler_params=pltpu.CompilerParams(vmem_limit_bytes=limit * 2**20),
        cost_estimate=pl.CostEstimate(flops=flops, transcendentals=0, bytes_accessed=0),
    )


def per_device(lon_size, lev_size, initial_state, scaled_diffusivity, scaled_forcing):
    dtype = initial_state.dtype
    nj, ni, nk, nm = initial_state.shape
    half = ni // 2
    V = lambda *shape: pltpu.VMEM(shape, dtype)
    H = lambda *shape: pltpu.HBM(shape, dtype)

    swap = [(0, 1), (1, 0)]
    lon_up = [(i, i + 1) for i in range(lon_size - 1)]
    lev_up = [(i, i + 1) for i in range(lev_size - 1)]
    down = lambda pairs: [(b, a) for a, b in pairs]

    faces_out = (V(nj, nk, nm), V(nj, nk, nm), V(nj, ni, nm), V(nj, ni, nm))

    def lon_exchange(lon_lo, lon_hi):
        return lax.ppermute(lon_hi, "lon", lon_up), lax.ppermute(lon_lo, "lon", down(lon_up))

    def lev_exchange(lev_lo, lev_hi):
        return lax.ppermute(lev_hi, "lev", lev_up), lax.ppermute(lev_lo, "lev", down(lev_up))

    def partners(total):
        others = []
        for bit in range(lon_size.bit_length() - 1):
            pairs = [(i, i ^ (1 << bit)) for i in range(lon_size)]
            if others:
                total = total + others[-1]
            if 2 << bit == lon_size:
                pairs = [(a, b) for a, b in pairs if a < b]
            others.append(lax.ppermute(total, "lon", pairs))
        return tuple(map(in_vmem, others))

    pj = jnp.where(lax.axis_index("lat") == 0, nj - 1, 0)
    pa = lax.dynamic_slice(initial_state, (pj, ni // 4, 0, 0), (1, half, nk, nm))[0]
    lat_a = lax.ppermute(pa, "lat", swap)
    u, pb, d_edge, f_edge, *faces = call(
        load_kernel,
        (V(nj, ni, nk, nm), V(half, nk, nm), V(ni, nk, nm), V(ni, nk, nm)) + faces_out,
        (VMEM,) * 8,
        (HBM,) * 3,
        scratch=(pltpu.SemaphoreType.DMA((nj + 4,)),),
        flops=10**6,
    )(*map(in_hbm, (initial_state, scaled_diffusivity, scaled_forcing)))
    lon = lon_exchange(*faces[:2])
    lat_b = lax.ppermute(pb, "lat", swap)
    lev = lev_exchange(*faces[2:])
    d_edge, f_edge = in_vmem(d_edge), in_vmem(f_edge)
    d, f = in_hbm(scaled_diffusivity), in_hbm(scaled_forcing)

    for step in range(STEPS):
        last = step == STEPS - 1
        u, pa, pb, lat_a, lat_b = map(in_vmem, (u, pa, pb, lat_a, lat_b))
        lon, lev = tuple(map(in_vmem, lon)), tuple(map(in_vmem, lev))
        n_pa = call(edge_a_kernel, V(half, nk, nm), VMEM, (VMEM,) * 8, flops=10**6)(
            u, pa, pb, lat_a, *lev, d_edge, f_edge
        )
        if last:
            break
        lat_a = lax.ppermute(n_pa, "lat", swap)
        if step == 0:
            n_u, d, f = call(
                first_bulk_kernel,
                (V(nj, ni, nk, nm),) * 3,
                (VMEM,) * 3,
                (VMEM,) * 7 + (HBM,) * 2 + (ANY,),
                scratch=(pltpu.SemaphoreType.DMA((2, nj)),),
                flops=2 * 10**7,
            )(u, pa, pb, *lon, *lev, d, f, n_pa)
        else:
            n_u = call(
                bulk_kernel, V(nj, ni, nk, nm), VMEM, (VMEM,) * 9 + (ANY,), flops=2 * 10**7
            )(u, pa, pb, *lon, *lev, in_vmem(d), in_vmem(f), n_pa)
        n_pb, *faces = call(
            edge_b_kernel, (V(half, nk, nm),) + faces_out, (VMEM,) * 5, (VMEM,) * 12, flops=10**6
        )(u, pa, pb, lat_b, *lon, *lev, d_edge, f_edge, in_vmem(n_u), in_vmem(n_pa))
        lon = lon_exchange(*faces[:2])
        lat_b = lax.ppermute(n_pb, "lat", swap)
        lev = lev_exchange(*faces[2:])
        u, pa, pb = n_u, n_pa, n_pb

    scale = 1.0 / (ni * lon_size)
    n = lon_size.bit_length()
    end, sums, _, total = call(
        last_bulk_kernel,
        (H(nj, ni, nk, nm), V(nj, ni, nk, nm), V(nj, ni, nk, nm), V(nj - 1, nk, nm)),
        (HBM, VMEM, VMEM, VMEM),
        (VMEM,) * 9 + (ANY,),
        scratch=(pltpu.SemaphoreType.DMA((nj,)),),
        aliases={7: 1, 8: 2},
        flops=2 * 10**7,
    )(u, pa, pb, *lon, *lev, in_vmem(d), in_vmem(f), n_pa)
    others = partners(total)
    out = call(
        functools.partial(totals_kernel, scale),
        H(nj, ni, nk, nm),
        HBM,
        (VMEM,) * n,
        limit=4,
        scratch=(V(2, ni, nk, nm), pltpu.SemaphoreType.DMA((2,))),
        flops=10**6,
    )(in_vmem(sums), *others)
    n_pa = in_vmem(n_pa)
    n_pb, edge_sums, edge_total = call(
        last_edge_kernel, (V(half, nk, nm), V(ni, nk, nm), V(nk, nm)), (VMEM,) * 3, (VMEM,) * 11, flops=2 * 10**6
    )(u, pa, pb, lat_b, *lon, *lev, d_edge, f_edge, n_pa)
    others = partners(edge_total)
    end, out = call(
        functools.partial(last_totals_kernel, scale),
        (H(nj, ni, nk, nm),) * 2,
        (HBM, HBM),
        (VMEM,) * (n + 2) + (HBM, HBM),
        scratch=(V(ni, nk, nm), pltpu.SemaphoreType.DMA((5,))),
        limit=4,
        aliases={n + 2: 0, n + 3: 1},
        flops=10**6,
    )(in_vmem(edge_sums), n_pa, in_vmem(n_pb), *others, in_hbm(end), in_hbm(out))
    return out, end


def solution(mesh):
    spec = P("lat", "lon", "lev", None)
    return jax.shard_map(
        functools.partial(per_device, mesh.shape["lon"], mesh.shape["lev"]),
        mesh=mesh,
        in_specs=(spec, spec, spec),
        out_specs=(spec, spec),
        check_vma=False,
    )
```

time: 178 us -> 166 us (0.933)
  waiting for transfers between devices: 70.8 us -> 46.9 us
  starting transfers between devices: 72.1 us -> 84.1 us
    ppermute x19, waiting for transfers between devices: 36.7 us -> 23.5 us  [the longest x4 11.5 us: lev_exchange(): lax.ppermute(lev_lo, 'lev', down(lev_up))]
    ppermute x19, starting transfers between devices: 57.8 us -> 70.5 us  [the longest x4 28.3 us: lev_exchange(): lax.ppermute(lev_hi, 'lev', lev_up)]
    ppermute x6, waiting for transfers between devices: 34.1 us -> 23.4 us  [partners(): others.append(lax.ppermute(total, 'lon', pairs))]
    pallas_call x9 -> x10, Pallas kernels: 9.08 us -> 8.61 us  [the longest x1 4.37 us: per_device(): call(load_kernel, (V(nj, ni, nk, nm), V(half, nk, nm), V(ni, nk, nm), V(n...]
  transfers between devices with their start and end apart: 30 -> 30, of which waited for: 8 -> 13; matrix products, arithmetic and copies ran while one was open for 0% -> 0% of each run, Pallas kernels for 14% -> 15%
where the time goes in v2:
time: 166 us; the launch traced here: 165 us
  starting transfers between devices  84.1 us (51%)
  waiting for transfers between devices  46.9 us (28%)
  Pallas kernels  31.7 us (19%)
    ppermute x4, starting transfers between devices, lev_exchange(): lax.ppermute(lev_hi, 'lev', lev_up)  28.3 us
    ppermute x6, waiting for transfers between devices, partners(): others.append(lax.ppermute(total, 'lon', pairs))  23.4 us
    ppermute x4, starting transfers between devices, lon_exchange(): lax.ppermute(lon_hi, 'lon', lon_up)  18.8 us
    ppermute x4, starting transfers between devices, lon_exchange(): lax.ppermute(lon_lo, 'lon', down(lon_up))  12.5 us
    ppermute x4, waiting for transfers between devices, lev_exchange(): lax.ppermute(lev_lo, 'lev', down(lev_up))  11.5 us
    pallas_call x2, Pallas kernels, per_device(): call(bulk_kernel, V(nj, ni, nk, nm), VMEM, (VMEM,) * 9 + (ANY,), flops=2...  7.71 us
    ppermute x4, starting transfers between devices, lev_exchange(): lax.ppermute(lev_lo, 'lev', down(lev_up))  7.68 us
    ppermute x6, starting transfers between devices, partners(): others.append(lax.ppermute(total, 'lon', pairs))  7.65 us
  transfers between devices with their start and end apart: 30, of which 13 were waited for; matrix products, arithmetic and copies ran while one was open for 0% of the time, Pallas kernels for 15%

profile of v2, /device:TPU:30, one launch (start us, length us, event | category | flops | bytes accessed | tf_op | source)
XLA Modules:
  0.0 164.9 jit_solution(15577893124367196290)
XLA Ops:
  0.6 1.1 dynamic-slice_bitcast_fusion.pa
  1.7 0.9 collective-permute-start.4
  2.6 4.4 %shard_map.50 = (f32[8,32,64,128]{3,2,1,0:T(8,128)S(1)}, f32[16,64,128]{2,1,0:T(8,128)S(1)}, f32[32,64,128]{2,1,0:T(8,128)S(1)}, f32[32,64,128]{2,1,0:T(8,128)S(...) custom-call(f32[8,32,64,128]{3,2,1,0:T(8,128)} %u_in.1, ...), custom_call_target="tpu_custom_call" | custom-call | flops 1000000 | tf_op jit(solution)/shard_map/pallas_call | solution.py:376
  7.0 1.3 collective-permute-start.5
  8.3 5.4 %collective-permute-start.2 = (f32[8,32,128]{2,1,0:T(8,128)S(1)}, f32[8,32,128]{2,1,0:T(8,128)S(1)}, u32[]{:S(2)}, u32[]{:S(2)}) collective-permute-start(f32[8,32,128]{2,1,0:T(8,128)S(1)} %get-tuple-element.40), channel_id=1, source_target_pairs={{0,1},{1,2},{2,3},{3,4},{4,5},{5,6},{6,7},{8,9},{9,10},{10,11},{11... | collective-permute-start | bytes 393224 | tf_op jit(solution)/shard_map/ppermute | solution.py:360
  13.7 1.9 %collective-permute-start.3 = (f32[8,32,128]{2,1,0:T(8,128)S(1)}, f32[8,32,128]{2,1,0:T(8,128)S(1)}, u32[]{:S(2)}, u32[]{:S(2)}) collective-permute-start(f32[8,32,128]{2,1,0:T(8,128)S(1)} %get-tuple-element.41), channel_id=1, source_target_pairs={{1,0},{2,1},{3,2},{4,3},{5,4},{6,5},{7,6},{9,8},{10,9},{11,10},{12... | collective-permute-start | bytes 393224 | tf_op jit(solution)/shard_map/ppermute | solution.py:360
  15.7 1.9 %collective-permute-start = (f32[8,64,128]{2,1,0:T(8,128)S(1)}, f32[8,64,128]{2,1,0:T(8,128)S(1)}, u32[]{:S(2)}, u32[]{:S(2)}) collective-permute-start(f32[8,64,128]{2,1,0:T(8,128)S(1)} %get-tuple-element.38), channel_id=1, source_target_pairs={{0,8},{8,16},{16,24},{24,32},{32,40},{40,48},{48,56},{1,9},{9,17},... | collective-permute-start | bytes 786440 | tf_op jit(solution)/shard_map/ppermute | solution.py:357
  17.6 0.0 collective-permute-done.2.lev_lo
  17.6 5.1 %collective-permute-start.1 = (f32[8,64,128]{2,1,0:T(8,128)S(1)}, f32[8,64,128]{2,1,0:T(8,128)S(1)}, u32[]{:S(2)}, u32[]{:S(2)}) collective-permute-start(f32[8,64,128]{2,1,0:T(8,128)S(1)} %get-tuple-element.39), channel_id=1, source_target_pairs={{8,0},{16,8},{24,16},{32,24},{40,32},{48,40},{56,48},{9,1},{17,9},... | collective-permute-start | bytes 786440 | tf_op jit(solution)/shard_map/ppermute | solution.py:357
  22.8 1.5 collective-permute-done.3.lev_hi
  24.2 0.0 collective-permute-done.4.lat
  24.2 0.3 shard_map.51.after.rest_1_.pa
  24.5 0.9 collective-permute-start.10
  25.4 5.4 %collective-permute-done.lon_lo = f32[8,64,128]{2,1,0:T(8,128)S(1)} collective-permute-done((f32[8,64,128]{2,1,0:T(8,128)S(1)}, f32[8,64,128]{2,1,0:T(8,128)S(1)}, u32[]{:S(2)}, u32[]{:S(2)}) %collective-permute-start) | collective-permute-done | bytes 262176 | tf_op jit(solution)/shard_map/ppermute | solution.py:357
  30.8 1.0 collective-permute-done.1.lon_hi
  31.8 5.8 %shard_map.52 = (f32[8,32,64,128]{3,2,1,0:T(8,128)S(1)}, f32[8,32,64,128]{3,2,1,0:T(8,128)S(1)}, f32[8,32,64,128]{3,2,1,0:T(8,128)S(1)}) custom-call(f32[8,32,64,128]{3,2,1,0:T(8,128)S(1)} %get-tuple-element.36.u, f32[16,64,128]{2,1,0:T(8,128)S(1)} %dynamic-slice_bitcast_fusion.pa, f32[16,64,128]{2,1,0:T(8,128)S(1)} %get-tuple-element.37.pb, ...), custom_call_target="tpu_custom_call" | custom-call | flops 20000000 | tf_op jit(solution)/shard_map/pallas_call | solution.py:401
  37.6 0.0 copy-start
  37.7 0.0 collective-permute-done.5.lat
  37.7 0.4 shard_map.53
  38.1 1.3 collective-permute-start.11
  39.4 5.4 %collective-permute-start.8 = (f32[8,32,128]{2,1,0:T(8,128)S(1)}, f32[8,32,128]{2,1,0:T(8,128)S(1)}, u32[]{:S(2)}, u32[]{:S(2)}) collective-permute-start(f32[8,32,128]{2,1,0:T(8,128)S(1)} %get-tuple-element.48), channel_id=1, source_target_pairs={{0,1},{1,2},{2,3},{3,4},{4,5},{5,6},{6,7},{8,9},{9,10},{10,11},{11... | collective-permute-start | bytes 393224 | tf_op jit(solution)/shard_map/ppermute | solution.py:360
  44.8 1.9 %collective-permute-start.9 = (f32[8,32,128]{2,1,0:T(8,128)S(1)}, f32[8,32,128]{2,1,0:T(8,128)S(1)}, u32[]{:S(2)}, u32[]{:S(2)}) collective-permute-start(f32[8,32,128]{2,1,0:T(8,128)S(1)} %get-tuple-element.49), channel_id=1, source_target_pairs={{1,0},{2,1},{3,2},{4,3},{5,4},{6,5},{7,6},{9,8},{10,9},{11,10},{12... | collective-permute-start | bytes 393224 | tf_op jit(solution)/shard_map/ppermute | solution.py:360
  46.8 3.8 %collective-permute-start.6 = (f32[8,64,128]{2,1,0:T(8,128)S(1)}, f32[8,64,128]{2,1,0:T(8,128)S(1)}, u32[]{:S(2)}, u32[]{:S(2)}) collective-permute-start(f32[8,64,128]{2,1,0:T(8,128)S(1)} %get-tuple-element.46), channel_id=1, source_target_pairs={{0,8},{8,16},{16,24},{24,32},{32,40},{40,48},{48,56},{1,9},{9,17},... | collective-permute-start | bytes 786440 | tf_op jit(solution)/shard_map/ppermute | solution.py:357
  50.6 0.0 collective-permute-done.8.lev_lo
  50.6 3.5 %collective-permute-start.7 = (f32[8,64,128]{2,1,0:T(8,128)S(1)}, f32[8,64,128]{2,1,0:T(8,128)S(1)}, u32[]{:S(2)}, u32[]{:S(2)}) collective-permute-start(f32[8,64,128]{2,1,0:T(8,128)S(1)} %get-tuple-element.47), channel_id=1, source_target_pairs={{8,0},{16,8},{24,16},{32,24},{40,32},{48,40},{56,48},{9,1},{17,9},... | collective-permute-start | bytes 786440 | tf_op jit(solution)/shard_map/ppermute | solution.py:357
  54.1 1.7 %collective-permute-done.9.lev_hi = f32[8,32,128]{2,1,0:T(8,128)S(1)} collective-permute-done((f32[8,32,128]{2,1,0:T(8,128)S(1)}, f32[8,32,128]{2,1,0:T(8,128)S(1)}, u32[]{:S(2)}, u32[]{:S(2)}) %collective-permute-start.9) | collective-permute-done | bytes 131104 | tf_op jit(solution)/shard_map/ppermute | solution.py:360
  55.8 0.3 shard_map.54.after.rest_1_.pa
  56.1 0.4 collective-permute-start.16
  56.5 2.7 %collective-permute-done.7.lon_hi = f32[8,64,128]{2,1,0:T(8,128)S(1)} collective-permute-done((f32[8,64,128]{2,1,0:T(8,128)S(1)}, f32[8,64,128]{2,1,0:T(8,128)S(1)}, u32[]{:S(2)}, u32[]{:S(2)}) %collective-permute-start.7) | collective-permute-done | bytes 262176 | tf_op jit(solution)/shard_map/ppermute | solution.py:357
  59.2 3.8 %shard_map.55.rest_0_.u = f32[8,32,64,128]{3,2,1,0:T(8,128)S(1)} custom-call(f32[8,32,64,128]{3,2,1,0:T(8,128)S(1)} %get-tuple-element.44.rest_0_.u, f32[16,64,128]{2,1,0:T(8,128)S(1)} %shard_map.51.after.rest_1_.pa, f32[16,64,128]{2,1,0:T(8,128)S(1)} %get-tuple-element.45.pb, f32[8,64,128]{2,1,0:T(8,128)S(1)} %collective-permute-done.6.lon_lo, ...), custom_call_target="tpu_custom_call" | custom-call | flops 20000000 | tf_op jit(solution)/shard_map/pallas_call | solution.py:410
  63.1 0.4 shard_map.56
  63.5 0.0 copy-start.1
  63.5 1.7 %collective-permute-start.17 = (f32[16,64,128]{2,1,0:T(8,128)S(1)}, f32[16,64,128]{2,1,0:T(8,128)S(1)}, u32[]{:S(2)}, u32[]{:S(2)}) collective-permute-start(f32[16,64,128]{2,1,0:T(8,128)S(1)} %get-tuple-element.52.pb), channel_id=1, source_target_pairs={{0,64},{64,0},{1,65},{65,1},{2,66},{66,2},{3,67},{67,3},{4,68},{68... | collective-permute-start | bytes 1572872 | tf_op jit(solution)/shard_map/ppermute | solution.py:417
  65.2 7.5 %collective-permute-start.14 = (f32[8,32,128]{2,1,0:T(8,128)S(1)}, f32[8,32,128]{2,1,0:T(8,128)S(1)}, u32[]{:S(2)}, u32[]{:S(2)}) collective-permute-start(f32[8,32,128]{2,1,0:T(8,128)S(1)} %get-tuple-element.55), channel_id=1, source_target_pairs={{0,1},{1,2},{2,3},{3,4},{4,5},{5,6},{6,7},{8,9},{9,10},{10,11},{11... | collective-permute-start | bytes 393224 | tf_op jit(solution)/shard_map/ppermute | solution.py:360
  72.8 1.9 %collective-permute-start.15 = (f32[8,32,128]{2,1,0:T(8,128)S(1)}, f32[8,32,128]{2,1,0:T(8,128)S(1)}, u32[]{:S(2)}, u32[]{:S(2)}) collective-permute-start(f32[8,32,128]{2,1,0:T(8,128)S(1)} %get-tuple-element.56), channel_id=1, source_target_pairs={{1,0},{2,1},{3,2},{4,3},{5,4},{6,5},{7,6},{9,8},{10,9},{11,10},{12... | collective-permute-start | bytes 393224 | tf_op jit(solution)/shard_map/ppermute | solution.py:360
  74.7 6.0 %collective-permute-start.12 = (f32[8,64,128]{2,1,0:T(8,128)S(1)}, f32[8,64,128]{2,1,0:T(8,128)S(1)}, u32[]{:S(2)}, u32[]{:S(2)}) collective-permute-start(f32[8,64,128]{2,1,0:T(8,128)S(1)} %get-tuple-element.53), channel_id=1, source_target_pairs={{0,8},{8,16},{16,24},{24,32},{32,40},{40,48},{48,56},{1,9},{9,17},... | collective-permute-start | bytes 786440 | tf_op jit(solution)/shard_map/ppermute | solution.py:357
  80.7 1.9 %collective-permute-start.13 = (f32[8,64,128]{2,1,0:T(8,128)S(1)}, f32[8,64,128]{2,1,0:T(8,128)S(1)}, u32[]{:S(2)}, u32[]{:S(2)}) collective-permute-start(f32[8,64,128]{2,1,0:T(8,128)S(1)} %get-tuple-element.54), channel_id=1, source_target_pairs={{8,0},{16,8},{24,16},{32,24},{40,32},{48,40},{56,48},{9,1},{17,9},... | collective-permute-start | bytes 786440 | tf_op jit(solution)/shard_map/ppermute | solution.py:357
  82.6 0.6 collective-permute-done.15.lev_hi
  83.2 0.3 shard_map.57.after.rest_1_.pa
  83.5 1.9 %collective-permute-start.23 = (f32[16,64,128]{2,1,0:T(8,128)S(1)}, f32[16,64,128]{2,1,0:T(8,128)S(1)}, u32[]{:S(2)}, u32[]{:S(2)}) collective-permute-start(f32[16,64,128]{2,1,0:T(8,128)S(1)} %shard_map.57.after.rest_1_.pa), channel_id=1, source_target_pairs={{0,64},{64,0},{1,65},{65,1},{2,66},{66,2},{3,67},{67,3},{4,68},{68... | collective-permute-start | bytes 1572872 | tf_op jit(solution)/shard_map/ppermute | solution.py:399
  85.4 1.4 collective-permute-done.13.lon_hi
  86.9 3.9 %shard_map.58.rest_0_.u = f32[8,32,64,128]{3,2,1,0:T(8,128)S(1)} custom-call(f32[8,32,64,128]{3,2,1,0:T(8,128)S(1)} %shard_map.55.rest_0_.u, f32[16,64,128]{2,1,0:T(8,128)S(1)} %shard_map.54.after.rest_1_.pa, f32[16,64,128]{2,1,0:T(8,128)S(1)} %get-tuple-element.52.pb, f32[8,64,128]{2,1,0:T(8,128)S(1)} %collective-permute-done.12.lon_lo, ...), custom_call_target="tpu_custom_call" | custom-call | flops 20000000 | tf_op jit(solution)/shard_map/pallas_call | solution.py:410
  90.8 0.5 shard_map.59
  91.2 7.1 %collective-permute-start.19 = (f32[8,64,128]{2,1,0:T(8,128)S(1)}, f32[8,64,128]{2,1,0:T(8,128)S(1)}, u32[]{:S(2)}, u32[]{:S(2)}) collective-permute-start(f32[8,64,128]{2,1,0:T(8,128)S(1)} %get-tuple-element.58), channel_id=1, source_target_pairs={{0,8},{8,16},{16,24},{24,32},{32,40},{40,48},{48,56},{1,9},{9,17},... | collective-permute-start | bytes 786440 | tf_op jit(solution)/shard_map/ppermute | solution.py:357
  98.3 1.9 %collective-permute-start.20 = (f32[8,64,128]{2,1,0:T(8,128)S(1)}, f32[8,64,128]{2,1,0:T(8,128)S(1)}, u32[]{:S(2)}, u32[]{:S(2)}) collective-permute-start(f32[8,64,128]{2,1,0:T(8,128)S(1)} %get-tuple-element.59), channel_id=1, source_target_pairs={{8,0},{16,8},{24,16},{32,24},{40,32},{48,40},{56,48},{9,1},{17,9},... | collective-permute-start | bytes 786440 | tf_op jit(solution)/shard_map/ppermute | solution.py:357
  100.3 9.9 %collective-permute-start.21 = (f32[8,32,128]{2,1,0:T(8,128)S(1)}, f32[8,32,128]{2,1,0:T(8,128)S(1)}, u32[]{:S(2)}, u32[]{:S(2)}) collective-permute-start(f32[8,32,128]{2,1,0:T(8,128)S(1)} %get-tuple-element.60), channel_id=1, source_target_pairs={{0,1},{1,2},{2,3},{3,4},{4,5},{5,6},{6,7},{8,9},{9,10},{10,11},{11... | collective-permute-start | bytes 393224 | tf_op jit(solution)/shard_map/ppermute | solution.py:360
  110.1 1.9 %collective-permute-start.22 = (f32[8,32,128]{2,1,0:T(8,128)S(1)}, f32[8,32,128]{2,1,0:T(8,128)S(1)}, u32[]{:S(2)}, u32[]{:S(2)}) collective-permute-start(f32[8,32,128]{2,1,0:T(8,128)S(1)} %get-tuple-element.61), channel_id=1, source_target_pairs={{1,0},{2,1},{3,2},{4,3},{5,4},{6,5},{7,6},{9,8},{10,9},{11,10},{12... | collective-permute-start | bytes 393224 | tf_op jit(solution)/shard_map/ppermute | solution.py:360
  112.1 1.5 collective-permute-done.21.lev_lo
  113.5 7.7 %collective-permute-done.22.lev_hi = f32[8,32,128]{2,1,0:T(8,128)S(1)} collective-permute-done((f32[8,32,128]{2,1,0:T(8,128)S(1)}, f32[8,32,128]{2,1,0:T(8,128)S(1)}, u32[]{:S(2)}, u32[]{:S(2)}) %collective-permute-start.22) | collective-permute-done | bytes 131104 | tf_op jit(solution)/shard_map/ppermute | solution.py:360
  121.3 0.3 shard_map.60.npa.after
  121.6 5.2 %shard_map.62 = (f32[8,32,64,128]{3,2,1,0:T(8,128)}, f32[8,32,64,128]{3,2,1,0:T(8,128)S(1)}, f32[8,32,64,128]{3,2,1,0:T(8,128)S(1)}, f32[7,64,128]{2,1,0:T(8,128)S(1)}) custom-call(f32[8,32,64,128]{3,2,1,0:T(8,128)S(1)} %shard_map.58.rest_0_.u, f32[16,64,128]{2,1,0:T(8,128)S(1)} %shard_map.57.after.rest_1_.pa, ...), custom_call_target="tpu_custom_call", output_to_operand_aliasing={{1}: (7, {}), {2}: (8, {})} | custom-call | flops 20000000 | tf_op jit(solution)/shard_map/pallas_call | solution.py:423
  126.8 0.1 collective-permute-start.27
  126.9 0.8 collective-permute-start.18
  127.7 0.7 collective-permute-done.27.rest_0_
  128.4 0.1 collective-permute-start.28
  128.5 16.1 %collective-permute-done.28.rest_1_ = f32[7,64,128]{2,1,0:T(8,128)S(1)} collective-permute-done((f32[7,64,128]{2,1,0:T(8,128)S(1)}, f32[7,64,128]{2,1,0:T(8,128)S(1)}, u32[]{:S(2)}, u32[]{:S(2)}) %collective-permute-start.28) | collective-permute-done | bytes 229408 | tf_op jit(solution)/shard_map/ppermute | solution.py:370
  144.6 6.1 %collective-permute-start.29 = (f32[7,64,128]{2,1,0:T(8,128)S(1)}, f32[7,64,128]{2,1,0:T(8,128)S(1)}, u32[]{:S(2)}, u32[]{:S(2)}) collective-permute-start(f32[7,64,128]{2,1,0:T(8,128)S(1)} %add.16), channel_id=1, source_target_pairs={{0,32},{8,40},{16,48},{24,56},{1,33},{9,41},{17,49},{25,57},{2,34}... | collective-permute-start | bytes 688136 | tf_op jit(solution)/shard_map/ppermute | solution.py:370
  150.8 0.4 shard_map.61
  151.1 0.1 collective-permute-start.24
  151.2 1.2 collective-permute-done.24.rest_0_
  152.4 5.4 %collective-permute-done.25.rest_1_ = f32[64,128]{1,0:T(8,128)S(1)} collective-permute-done((f32[64,128]{1,0:T(8,128)S(1)}, f32[64,128]{1,0:T(8,128)S(1)}, u32[]{:S(2)}, u32[]{:S(2)}) %collective-permute-start.25) | collective-permute-done | bytes 32800 | tf_op jit(solution)/shard_map/ppermute | solution.py:370
  157.9 1.3 collective-permute-start.26
  159.2 4.4 %shard_map.63.rest_4_ = f32[8,32,64,128]{3,2,1,0:T(8,128)} custom-call(f32[8,32,64,128]{3,2,1,0:T(8,128)S(1)} %get-tuple-element.66.sums, f32[7,64,128]{2,1,0:T(8,128)S(1)} %collective-permute-done.27.rest_0_, f32[7,64,128]{2,1,0:T(8,128)S(1)} %collective-permute-done.28.rest_1_, f32[7,64,128]{2,1,0:T(8,128)S(1)} %collective-permute-done.29.rest_2_), custom_call_target="tpu_custom_call" | custom-call | flops 1000000 | tf_op jit(solution)/shard_map/pallas_call | solution.py:433
  163.6 1.4 shard_map.64
  (20 shorter events, 0.1 us)
Async XLA Ops:
  1.7 22.5 %collective-permute-start.4 = (f32[16,64,128]{2,1,0:T(8,128)S(1)}, f32[16,64,128]{2,1,0:T(8,128)S(1)}, u32[]{:S(2)}, u32[]{:S(2)}) collective-permute-start(f32[16,64,128]{2,1,0:T(8,128)S(1)} %dynamic-slice_bitcast_fusion.pa), channel_id=1, source_target_pairs={{0,64},{64,0},{1,65},{65,1},{2,66},{66,2},{3,67},{67,3},{4,68},{68... | collective-permute-start | bytes 1572872 | tf_op jit(solution)/shard_map/ppermute | solution.py:375
  7.0 30.6 %collective-permute-start.5 = (f32[16,64,128]{2,1,0:T(8,128)S(1)}, f32[16,64,128]{2,1,0:T(8,128)S(1)}, u32[]{:S(2)}, u32[]{:S(2)}) collective-permute-start(f32[16,64,128]{2,1,0:T(8,128)S(1)} %get-tuple-element.37.pb), channel_id=1, source_target_pairs={{0,64},{64,0},{1,65},{65,1},{2,66},{66,2},{3,67},{67,3},{4,68},{68... | collective-permute-start | bytes 1572872 | tf_op jit(solution)/shard_map/ppermute | solution.py:385
  8.3 9.3 %collective-permute-start.2 = (f32[8,32,128]{2,1,0:T(8,128)S(1)}, f32[8,32,128]{2,1,0:T(8,128)S(1)}, u32[]{:S(2)}, u32[]{:S(2)}) collective-permute-start(f32[8,32,128]{2,1,0:T(8,128)S(1)} %get-tuple-element.40), channel_id=1, source_target_pairs={{0,1},{1,2},{2,3},{3,4},{4,5},{5,6},{6,7},{8,9},{9,10},{10,11},{11... | collective-permute-start | bytes 393224 | tf_op jit(solution)/shard_map/ppermute | solution.py:360
  13.7 10.5 %collective-permute-start.3 = (f32[8,32,128]{2,1,0:T(8,128)S(1)}, f32[8,32,128]{2,1,0:T(8,128)S(1)}, u32[]{:S(2)}, u32[]{:S(2)}) collective-permute-start(f32[8,32,128]{2,1,0:T(8,128)S(1)} %get-tuple-element.41), channel_id=1, source_target_pairs={{1,0},{2,1},{3,2},{4,3},{5,4},{6,5},{7,6},{9,8},{10,9},{11,10},{12... | collective-permute-start | bytes 393224 | tf_op jit(solution)/shard_map/ppermute | solution.py:360
  15.7 15.1 %collective-permute-start = (f32[8,64,128]{2,1,0:T(8,128)S(1)}, f32[8,64,128]{2,1,0:T(8,128)S(1)}, u32[]{:S(2)}, u32[]{:S(2)}) collective-permute-start(f32[8,64,128]{2,1,0:T(8,128)S(1)} %get-tuple-element.38), channel_id=1, source_target_pairs={{0,8},{8,16},{16,24},{24,32},{32,40},{40,48},{48,56},{1,9},{9,17},... | collective-permute-start | bytes 786440 | tf_op jit(solution)/shard_map/ppermute | solution.py:357
  17.6 14.2 %collective-permute-start.1 = (f32[8,64,128]{2,1,0:T(8,128)S(1)}, f32[8,64,128]{2,1,0:T(8,128)S(1)}, u32[]{:S(2)}, u32[]{:S(2)}) collective-permute-start(f32[8,64,128]{2,1,0:T(8,128)S(1)} %get-tuple-element.39), channel_id=1, source_target_pairs={{8,0},{16,8},{24,16},{32,24},{40,32},{48,40},{56,48},{9,1},{17,9},... | collective-permute-start | bytes 786440 | tf_op jit(solution)/shard_map/ppermute | solution.py:357
  24.5 31.3 %collective-permute-start.10 = (f32[16,64,128]{2,1,0:T(8,128)S(1)}, f32[16,64,128]{2,1,0:T(8,128)S(1)}, u32[]{:S(2)}, u32[]{:S(2)}) collective-permute-start(f32[16,64,128]{2,1,0:T(8,128)S(1)} %shard_map.51.after.rest_1_.pa), channel_id=1, source_target_pairs={{0,64},{64,0},{1,65},{65,1},{2,66},{66,2},{3,67},{67,3},{4,68},{68... | collective-permute-start | bytes 1572872 | tf_op jit(solution)/shard_map/ppermute | solution.py:399
  37.6 21.6 %copy-start = (f32[8,32,64,128]{3,2,1,0:T(8,128)}, f32[8,32,64,128]{3,2,1,0:T(8,128)S(1)}, u32[]{:S(2)}) copy-start(f32[8,32,64,128]{3,2,1,0:T(8,128)S(1)} %get-tuple-element.51.f.f_in) | copy-start | bytes 25165828
  38.1 24.9 %collective-permute-start.11 = (f32[16,64,128]{2,1,0:T(8,128)S(1)}, f32[16,64,128]{2,1,0:T(8,128)S(1)}, u32[]{:S(2)}, u32[]{:S(2)}) collective-permute-start(f32[16,64,128]{2,1,0:T(8,128)S(1)} %get-tuple-element.45.pb), channel_id=1, source_target_pairs={{0,64},{64,0},{1,65},{65,1},{2,66},{66,2},{3,67},{67,3},{4,68},{68... | collective-permute-start | bytes 1572872 | tf_op jit(solution)/shard_map/ppermute | solution.py:417
  39.4 11.2 %collective-permute-start.8 = (f32[8,32,128]{2,1,0:T(8,128)S(1)}, f32[8,32,128]{2,1,0:T(8,128)S(1)}, u32[]{:S(2)}, u32[]{:S(2)}) collective-permute-start(f32[8,32,128]{2,1,0:T(8,128)S(1)} %get-tuple-element.48), channel_id=1, source_target_pairs={{0,1},{1,2},{2,3},{3,4},{4,5},{5,6},{6,7},{8,9},{9,10},{10,11},{11... | collective-permute-start | bytes 393224 | tf_op jit(solution)/shard_map/ppermute | solution.py:360
  44.8 10.9 %collective-permute-start.9 = (f32[8,32,128]{2,1,0:T(8,128)S(1)}, f32[8,32,128]{2,1,0:T(8,128)S(1)}, u32[]{:S(2)}, u32[]{:S(2)}) collective-permute-start(f32[8,32,128]{2,1,0:T(8,128)S(1)} %get-tuple-element.49), channel_id=1, source_target_pairs={{1,0},{2,1},{3,2},{4,3},{5,4},{6,5},{7,6},{9,8},{10,9},{11,10},{12... | collective-permute-start | bytes 393224 | tf_op jit(solution)/shard_map/ppermute | solution.py:360
  46.8 9.8 %collective-permute-start.6 = (f32[8,64,128]{2,1,0:T(8,128)S(1)}, f32[8,64,128]{2,1,0:T(8,128)S(1)}, u32[]{:S(2)}, u32[]{:S(2)}) collective-permute-start(f32[8,64,128]{2,1,0:T(8,128)S(1)} %get-tuple-element.46), channel_id=1, source_target_pairs={{0,8},{8,16},{16,24},{24,32},{32,40},{40,48},{48,56},{1,9},{9,17},... | collective-permute-start | bytes 786440 | tf_op jit(solution)/shard_map/ppermute | solution.py:357
  50.6 8.6 %collective-permute-start.7 = (f32[8,64,128]{2,1,0:T(8,128)S(1)}, f32[8,64,128]{2,1,0:T(8,128)S(1)}, u32[]{:S(2)}, u32[]{:S(2)}) collective-permute-start(f32[8,64,128]{2,1,0:T(8,128)S(1)} %get-tuple-element.47), channel_id=1, source_target_pairs={{8,0},{16,8},{24,16},{32,24},{40,32},{48,40},{56,48},{9,1},{17,9},... | collective-permute-start | bytes 786440 | tf_op jit(solution)/shard_map/ppermute | solution.py:357
  56.1 27.1 %collective-permute-start.16 = (f32[16,64,128]{2,1,0:T(8,128)S(1)}, f32[16,64,128]{2,1,0:T(8,128)S(1)}, u32[]{:S(2)}, u32[]{:S(2)}) collective-permute-start(f32[16,64,128]{2,1,0:T(8,128)S(1)} %shard_map.54.after.rest_1_.pa), channel_id=1, source_target_pairs={{0,64},{64,0},{1,65},{65,1},{2,66},{66,2},{3,67},{67,3},{4,68},{68... | collective-permute-start | bytes 1572872 | tf_op jit(solution)/shard_map/ppermute | solution.py:399
  63.5 23.4 %copy-start.1 = (f32[8,32,64,128]{3,2,1,0:T(8,128)S(1)}, f32[8,32,64,128]{3,2,1,0:T(8,128)}, u32[]{:S(2)}) copy-start(f32[8,32,64,128]{3,2,1,0:T(8,128)} %copy-done) | copy-start | bytes 25165828
  63.5 27.3 %collective-permute-start.17 = (f32[16,64,128]{2,1,0:T(8,128)S(1)}, f32[16,64,128]{2,1,0:T(8,128)S(1)}, u32[]{:S(2)}, u32[]{:S(2)}) collective-permute-start(f32[16,64,128]{2,1,0:T(8,128)S(1)} %get-tuple-element.52.pb), channel_id=1, source_target_pairs={{0,64},{64,0},{1,65},{65,1},{2,66},{66,2},{3,67},{67,3},{4,68},{68... | collective-permute-start | bytes 1572872 | tf_op jit(solution)/shard_map/ppermute | solution.py:417
  65.2 15.5 %collective-permute-start.14 = (f32[8,32,128]{2,1,0:T(8,128)S(1)}, f32[8,32,128]{2,1,0:T(8,128)S(1)}, u32[]{:S(2)}, u32[]{:S(2)}) collective-permute-start(f32[8,32,128]{2,1,0:T(8,128)S(1)} %get-tuple-element.55), channel_id=1, source_target_pairs={{0,1},{1,2},{2,3},{3,4},{4,5},{5,6},{6,7},{8,9},{9,10},{10,11},{11... | collective-permute-start | bytes 393224 | tf_op jit(solution)/shard_map/ppermute | solution.py:360
  72.8 10.5 %collective-permute-start.15 = (f32[8,32,128]{2,1,0:T(8,128)S(1)}, f32[8,32,128]{2,1,0:T(8,128)S(1)}, u32[]{:S(2)}, u32[]{:S(2)}) collective-permute-start(f32[8,32,128]{2,1,0:T(8,128)S(1)} %get-tuple-element.56), channel_id=1, source_target_pairs={{1,0},{2,1},{3,2},{4,3},{5,4},{6,5},{7,6},{9,8},{10,9},{11,10},{12... | collective-permute-start | bytes 393224 | tf_op jit(solution)/shard_map/ppermute | solution.py:360
  74.7 10.7 %collective-permute-start.12 = (f32[8,64,128]{2,1,0:T(8,128)S(1)}, f32[8,64,128]{2,1,0:T(8,128)S(1)}, u32[]{:S(2)}, u32[]{:S(2)}) collective-permute-start(f32[8,64,128]{2,1,0:T(8,128)S(1)} %get-tuple-element.53), channel_id=1, source_target_pairs={{0,8},{8,16},{16,24},{24,32},{32,40},{40,48},{48,56},{1,9},{9,17},... | collective-permute-start | bytes 786440 | tf_op jit(solution)/shard_map/ppermute | solution.py:357
  80.7 6.2 %collective-permute-start.13 = (f32[8,64,128]{2,1,0:T(8,128)S(1)}, f32[8,64,128]{2,1,0:T(8,128)S(1)}, u32[]{:S(2)}, u32[]{:S(2)}) collective-permute-start(f32[8,64,128]{2,1,0:T(8,128)S(1)} %get-tuple-element.54), channel_id=1, source_target_pairs={{8,0},{16,8},{24,16},{32,24},{40,32},{48,40},{56,48},{9,1},{17,9},... | collective-permute-start | bytes 786440 | tf_op jit(solution)/shard_map/ppermute | solution.py:357
  83.5 37.7 %collective-permute-start.23 = (f32[16,64,128]{2,1,0:T(8,128)S(1)}, f32[16,64,128]{2,1,0:T(8,128)S(1)}, u32[]{:S(2)}, u32[]{:S(2)}) collective-permute-start(f32[16,64,128]{2,1,0:T(8,128)S(1)} %shard_map.57.after.rest_1_.pa), channel_id=1, source_target_pairs={{0,64},{64,0},{1,65},{65,1},{2,66},{66,2},{3,67},{67,3},{4,68},{68... | collective-permute-start | bytes 1572872 | tf_op jit(solution)/shard_map/ppermute | solution.py:399
  91.2 30.3 %collective-permute-start.19 = (f32[8,64,128]{2,1,0:T(8,128)S(1)}, f32[8,64,128]{2,1,0:T(8,128)S(1)}, u32[]{:S(2)}, u32[]{:S(2)}) collective-permute-start(f32[8,64,128]{2,1,0:T(8,128)S(1)} %get-tuple-element.58), channel_id=1, source_target_pairs={{0,8},{8,16},{16,24},{24,32},{32,40},{40,48},{48,56},{1,9},{9,17},... | collective-permute-start | bytes 786440 | tf_op jit(solution)/shard_map/ppermute | solution.py:357
  98.3 23.2 %collective-permute-start.20 = (f32[8,64,128]{2,1,0:T(8,128)S(1)}, f32[8,64,128]{2,1,0:T(8,128)S(1)}, u32[]{:S(2)}, u32[]{:S(2)}) collective-permute-start(f32[8,64,128]{2,1,0:T(8,128)S(1)} %get-tuple-element.59), channel_id=1, source_target_pairs={{8,0},{16,8},{24,16},{32,24},{40,32},{48,40},{56,48},{9,1},{17,9},... | collective-permute-start | bytes 786440 | tf_op jit(solution)/shard_map/ppermute | solution.py:357
  100.3 13.3 %collective-permute-start.21 = (f32[8,32,128]{2,1,0:T(8,128)S(1)}, f32[8,32,128]{2,1,0:T(8,128)S(1)}, u32[]{:S(2)}, u32[]{:S(2)}) collective-permute-start(f32[8,32,128]{2,1,0:T(8,128)S(1)} %get-tuple-element.60), channel_id=1, source_target_pairs={{0,1},{1,2},{2,3},{3,4},{4,5},{5,6},{6,7},{8,9},{9,10},{10,11},{11... | collective-permute-start | bytes 393224 | tf_op jit(solution)/shard_map/ppermute | solution.py:360
  110.1 11.1 %collective-permute-start.22 = (f32[8,32,128]{2,1,0:T(8,128)S(1)}, f32[8,32,128]{2,1,0:T(8,128)S(1)}, u32[]{:S(2)}, u32[]{:S(2)}) collective-permute-start(f32[8,32,128]{2,1,0:T(8,128)S(1)} %get-tuple-element.61), channel_id=1, source_target_pairs={{1,0},{2,1},{3,2},{4,3},{5,4},{6,5},{7,6},{9,8},{10,9},{11,10},{12... | collective-permute-start | bytes 393224 | tf_op jit(solution)/shard_map/ppermute | solution.py:360
  126.8 1.6 collective-permute-start.27
  126.9 23.9 %collective-permute-start.18 = (f32[16,64,128]{2,1,0:T(8,128)S(1)}, f32[16,64,128]{2,1,0:T(8,128)S(1)}, u32[]{:S(2)}, u32[]{:S(2)}) collective-permute-start(f32[16,64,128]{2,1,0:T(8,128)S(1)} %get-tuple-element.57.pb), channel_id=1, source_target_pairs={{0,64},{64,0},{1,65},{65,1},{2,66},{66,2},{3,67},{67,3},{4,68},{68... | collective-permute-start | bytes 1572872 | tf_op jit(solution)/shard_map/ppermute | solution.py:417
  128.4 16.2 %collective-permute-start.28 = (f32[7,64,128]{2,1,0:T(8,128)S(1)}, f32[7,64,128]{2,1,0:T(8,128)S(1)}, u32[]{:S(2)}, u32[]{:S(2)}) collective-permute-start(f32[7,64,128]{2,1,0:T(8,128)S(1)} %add.15), channel_id=1, source_target_pairs={{0,16},{8,24},{16,0},{24,8},{32,48},{40,56},{48,32},{56,40},{1,17}... | collective-permute-start | bytes 688136 | tf_op jit(solution)/shard_map/ppermute | solution.py:370
  144.6 14.5 %collective-permute-start.29 = (f32[7,64,128]{2,1,0:T(8,128)S(1)}, f32[7,64,128]{2,1,0:T(8,128)S(1)}, u32[]{:S(2)}, u32[]{:S(2)}) collective-permute-start(f32[7,64,128]{2,1,0:T(8,128)S(1)} %add.16), channel_id=1, source_target_pairs={{0,32},{8,40},{16,48},{24,56},{1,33},{9,41},{17,49},{25,57},{2,34}... | collective-permute-start | bytes 688136 | tf_op jit(solution)/shard_map/ppermute | solution.py:370
  151.1 1.3 collective-permute-start.24
  152.4 5.4 %collective-permute-start.25 = (f32[64,128]{1,0:T(8,128)S(1)}, f32[64,128]{1,0:T(8,128)S(1)}, u32[]{:S(2)}, u32[]{:S(2)}) collective-permute-start(f32[64,128]{1,0:T(8,128)S(1)} %add.13), channel_id=1, source_target_pairs={{0,16},{8,24},{16,0},{24,8},{32,48},{40,56},{48,32},{56,40},{1,17}... | collective-permute-start | bytes 98312 | tf_op jit(solution)/shard_map/ppermute | solution.py:370
  157.9 5.7 %collective-permute-start.26 = (f32[64,128]{1,0:T(8,128)S(1)}, f32[64,128]{1,0:T(8,128)S(1)}, u32[]{:S(2)}, u32[]{:S(2)}) collective-permute-start(f32[64,128]{1,0:T(8,128)S(1)} %add.14), channel_id=1, source_target_pairs={{0,32},{8,40},{16,48},{24,56},{1,33},{9,41},{17,49},{25,57},{2,34}... | collective-permute-start | bytes 98312 | tf_op jit(solution)/shard_map/ppermute | solution.py:370

commit v3 on v2

--- a/solution.py
+++ b/solution.py
@@ -56,16 +56,30 @@
     return jnp.where(low, n - 1 - depth, depth)
 
 
-def faces_kernel(u, lon_lo, lon_hi, lev_lo, lev_hi):
+def odd(axis):
+    return lax.axis_index(axis) % 2 == 1
+
+
+def lower(axis, e, o):
+    return jnp.where(odd(axis), e, o)
+
+
+def upper(axis, e, o):
+    return jnp.where(odd(axis), o, e)
+
+
+def faces_kernel(u, lon_e, lon_o, lev_e, lev_o):
     nj, ni, nk, _ = u.shape
+    at_e = jnp.where(odd("lon"), 0, ni - 1)
     for j in range(nj):
-        lon_lo[j] = u[j, 0]
-        lon_hi[j] = u[j, ni - 1]
-        lev_lo[j] = u[j, :, 0, :]
-        lev_hi[j] = u[j, :, nk - 1, :]
-
-
-def load_kernel(u_in, d_in, f_in, u, pb, d_edge, f_edge, lon_lo, lon_hi, lev_lo, lev_hi, sem):
+        lon_e[j] = u[j, at_e]
+        lon_o[j] = u[j, ni - 1 - at_e]
+        lo, hi = u[j, :, 0, :], u[j, :, nk - 1, :]
+        lev_e[j] = lower("lev", lo, hi)
+        lev_o[j] = upper("lev", lo, hi)
+
+
+def load_kernel(u_in, d_in, f_in, u, pb, d_edge, f_edge, lon_e, lon_o, lev_e, lev_o, sem):
     nj, ni = u.shape[:2]
     q = ni // 4
     pj = plane_at(0, nj)
@@ -80,10 +94,21 @@
         copy.start()
     for copy in copies:
         copy.wait()
-    faces_kernel(u, lon_lo, lon_hi, lev_lo, lev_hi)
-
-
-def edge_rows(lo, hi, base, mine, below, above, u, lat, lev_lo, lev_hi, d, f, put):
+    faces_kernel(u, lon_e, lon_o, lev_e, lev_o)
+
+
+def lev_rows(lev_e, lev_o, j, base):
+    def get(side):
+        def row(i):
+            at = pl.ds(base + i, 1)
+            return side("lev", lev_e[j, at, :], lev_o[j, at, :])
+
+        return row
+
+    return get(lower), get(upper)
+
+
+def edge_rows(lo, hi, base, mine, below, above, u, lat, lev_e, lev_o, d, f, put):
     nj = u.shape[0]
     pj, pn = plane_at(0, nj), plane_at(1, nj)
     sweep(
@@ -93,8 +118,7 @@
         below,
         above,
         lambda i: u[pn, base + i] + lat[i],
-        lambda i: lev_lo[pj, pl.ds(base + i, 1), :],
-        lambda i: lev_hi[pj, pl.ds(base + i, 1), :],
+        *lev_rows(lev_e, lev_o, pj, base),
         lambda i: d[base + i],
         lambda i: f[base + i],
         put,
@@ -102,16 +126,16 @@
     )
 
 
-def edge_a_kernel(u, pa, pb, lat, lev_lo, lev_hi, d, f, out):
+def edge_a_kernel(u, pa, pb, lat, lev_e, lev_o, d, f, out):
     def put(i, new, carry):
         out[i] = new
         return carry
 
     n = pa.shape[0]
-    edge_rows(0, n, n // 2, pa, lambda: pb[n // 2 - 1], lambda: pb[n // 2], u, lat, lev_lo, lev_hi, d, f, put)
-
-
-def edge_b_kernel(u, pa, pb, lat, lon_lo, lon_hi, lev_lo, lev_hi, d, f, *rest):
+    edge_rows(0, n, n // 2, pa, lambda: pb[n // 2 - 1], lambda: pb[n // 2], u, lat, lev_e, lev_o, d, f, put)
+
+
+def edge_b_kernel(u, pa, pb, lat, lon_e, lon_o, lev_e, lev_o, d, f, *rest):
     nj, ni, nk, _ = u.shape
     q = ni // 4
     pj = plane_at(0, nj)
@@ -121,21 +145,21 @@
         out[i] = new
         return carry
 
-    args = (u, lat, lev_lo, lev_hi, d, f, put)
-    edge_rows(0, q, 0, pb, lambda: lon_lo[pj], lambda: pa[0], *args)
-    edge_rows(q, 2 * q, 2 * q, pb, lambda: pa[2 * q - 1], lambda: lon_hi[pj], *args)
+    args = (u, lat, lev_e, lev_o, d, f, put)
+    edge_rows(0, q, 0, pb, lambda: lower("lon", lon_e[pj], lon_o[pj]), lambda: pa[0], *args)
+    edge_rows(q, 2 * q, 2 * q, pb, lambda: pa[2 * q - 1], lambda: upper("lon", lon_e[pj], lon_o[pj]), *args)
     if len(rest) > 1:
-        nu, npa, _, s_lon_lo, s_lon_hi, s_lev_lo, s_lev_hi = rest
-        faces_kernel(nu, s_lon_lo, s_lon_hi, s_lev_lo, s_lev_hi)
-        s_lon_lo[pj] = out[0]
-        s_lon_hi[pj] = out[2 * q - 1]
-        for s_lev, k in ((s_lev_lo, 0), (s_lev_hi, nk - 1)):
-            s_lev[pj, :q] = out[:q, k, :]
-            s_lev[pj, q : 3 * q] = npa[:, k, :]
-            s_lev[pj, 3 * q :] = out[q:, k, :]
-
-
-def bulk_planes(u, pa, pb, lon_lo, lon_hi, lev_lo, lev_hi, d, f, put, start, finish):
+        nu, npa, _, s_lon_e, s_lon_o, s_lev_e, s_lev_o = rest
+        faces_kernel(nu, s_lon_e, s_lon_o, s_lev_e, s_lev_o)
+        s_lon_e[pj] = lower("lon", out[0], out[2 * q - 1])
+        s_lon_o[pj] = upper("lon", out[0], out[2 * q - 1])
+        for s_lev, side in ((s_lev_e, lower), (s_lev_o, upper)):
+            s_lev[pj, :q] = side("lev", out[:q, 0, :], out[:q, nk - 1, :])
+            s_lev[pj, q : 3 * q] = side("lev", npa[:, 0, :], npa[:, nk - 1, :])
+            s_lev[pj, 3 * q :] = side("lev", out[q:, 0, :], out[q:, nk - 1, :])
+
+
+def bulk_planes(u, pa, pb, lon_e, lon_o, lev_e, lev_o, d, f, put, start, finish):
     nj, ni, _, _ = u.shape
     q = ni // 4
 
@@ -144,11 +168,10 @@
             lo,
             hi,
             lambda i: u[j, i],
-            (lambda: lon_lo[j]) if lo == 0 else None,
-            (lambda: lon_hi[j]) if hi == ni else None,
+            (lambda: lower("lon", lon_e[j], lon_o[j])) if lo == 0 else None,
+            (lambda: upper("lon", lon_e[j], lon_o[j])) if hi == ni else None,
             nb,
-            lambda i: lev_lo[j, pl.ds(i, 1), :],
-            lambda i: lev_hi[j, pl.ds(i, 1), :],
+            *lev_rows(lev_e, lev_o, j, 0),
             lambda i: d[j, i],
             lambda i: f[j, i],
             functools.partial(put, j),
@@ -192,7 +215,7 @@
     return put
 
 
-def first_bulk_kernel(u, pa, pb, lon_lo, lon_hi, lev_lo, lev_hi, d_in, f_in, after, out, d, f, sem):
+def first_bulk_kernel(u, pa, pb, lon_e, lon_o, lev_e, lev_o, d_in, f_in, after, out, d, f, sem):
     del after
     nj = u.shape[0]
 
@@ -210,15 +233,15 @@
         for copy in copies(j, depth):
             copy.wait()
 
-    bulk_planes(u, pa, pb, lon_lo, lon_hi, lev_lo, lev_hi, d, f, plain_put(out), start, nothing)
-
-
-def bulk_kernel(u, pa, pb, lon_lo, lon_hi, lev_lo, lev_hi, d, f, after, out):
+    bulk_planes(u, pa, pb, lon_e, lon_o, lev_e, lev_o, d, f, plain_put(out), start, nothing)
+
+
+def bulk_kernel(u, pa, pb, lon_e, lon_o, lev_e, lev_o, d, f, after, out):
     del after
-    bulk_planes(u, pa, pb, lon_lo, lon_hi, lev_lo, lev_hi, d, f, plain_put(out), nothing, nothing)
-
-
-def last_bulk_kernel(u, pa, pb, lon_lo, lon_hi, lev_lo, lev_hi, d_in, f_in, after, end, d, f, total, sem):
+    bulk_planes(u, pa, pb, lon_e, lon_o, lev_e, lev_o, d, f, plain_put(out), nothing, nothing)
+
+
+def last_bulk_kernel(u, pa, pb, lon_e, lon_o, lev_e, lev_o, d_in, f_in, after, end, d, f, total, sem):
     del d_in, f_in, after
     nj = u.shape[0]
 
@@ -235,13 +258,13 @@
         total[depth - 1] = carry
         copy_out(j, depth).start()
 
-    bulk_planes(u, pa, pb, lon_lo, lon_hi, lev_lo, lev_hi, d, f, put, nothing, finish)
+    bulk_planes(u, pa, pb, lon_e, lon_o, lev_e, lev_o, d, f, put, nothing, finish)
     for depth in range(1, nj):
         copy_out(plane_at(depth, nj), depth).wait()
 
 
-def last_edge_kernel(u, pa, pb, lat, lon_lo, lon_hi, lev_lo, lev_hi, d, f, npa, npb, sums, total):
-    edge_b_kernel(u, pa, pb, lat, lon_lo, lon_hi, lev_lo, lev_hi, d, f, npb)
+def last_edge_kernel(u, pa, pb, lat, lon_e, lon_o, lev_e, lev_o, d, f, npa, npb, sums, total):
+    edge_b_kernel(u, pa, pb, lat, lon_e, lon_o, lev_e, lev_o, d, f, npb)
     ni = sums.shape[0]
     q = ni // 4
     carry = zero_carry(u)
@@ -256,16 +279,28 @@
     total[...] = carry
 
 
-def earlier(others):
+def earlier(others, first=0):
     lon = lax.axis_index("lon")
     before = 0.0
     for bit, other in enumerate(others):
-        before += jnp.where(lon & (1 << bit) != 0, other, 0.0)
+        before += jnp.where(lon & (1 << (first + bit)) != 0, other, 0.0)
     return before
 
 
-def totals_kernel(scale, sums, *rest):
-    *others, out, stage, sem = rest
+def half_kernel(total, other, out):
+    n = out.shape[1]
+    at = pl.ds(pl.multiple_of(jnp.where(odd("lon"), n, 0), n), n)
+    for p in range(out.shape[0]):
+        out[p] = total[p, at] + other[p, at]
+
+
+def before_kernel(*refs):
+    *others, out = refs
+    for p in range(out.shape[0]):
+        out[p] = earlier([other[p] for other in others], 1)
+
+
+def totals_kernel(scale, sums, other, mine, partners, out, stage, sem):
     nj, ni = sums.shape[:2]
 
     def copy_out(j, depth):
@@ -279,7 +314,9 @@
         def _():
             copy_out(j, depth).wait()
 
-        b = earlier([other[depth - 1] for other in others])
+        a, b = mine[depth - 1], partners[depth - 1]
+        b = jnp.concatenate([jnp.where(odd("lon"), b, a), jnp.where(odd("lon"), a, b)], axis=0)
+        b += earlier([other[depth - 1]])
 
         def row(r, _):
             for q in range(BLOCK):
@@ -347,28 +384,27 @@
     H = lambda *shape: pltpu.HBM(shape, dtype)
 
     swap = [(0, 1), (1, 0)]
-    lon_up = [(i, i + 1) for i in range(lon_size - 1)]
-    lev_up = [(i, i + 1) for i in range(lev_size - 1)]
-    down = lambda pairs: [(b, a) for a, b in pairs]
-
     faces_out = (V(nj, nk, nm), V(nj, nk, nm), V(nj, ni, nm), V(nj, ni, nm))
 
-    def lon_exchange(lon_lo, lon_hi):
-        return lax.ppermute(lon_hi, "lon", lon_up), lax.ppermute(lon_lo, "lon", down(lon_up))
-
-    def lev_exchange(lev_lo, lev_hi):
-        return lax.ppermute(lev_hi, "lev", lev_up), lax.ppermute(lev_lo, "lev", down(lev_up))
-
-    def partners(total):
-        others = []
-        for bit in range(lon_size.bit_length() - 1):
-            pairs = [(i, i ^ (1 << bit)) for i in range(lon_size)]
-            if others:
-                total = total + others[-1]
-            if 2 << bit == lon_size:
-                pairs = [(a, b) for a, b in pairs if a < b]
-            others.append(lax.ppermute(total, "lon", pairs))
-        return tuple(map(in_vmem, others))
+    def exchange(axis, size, e, o):
+        def swaps(first):
+            return [(a, b) for i in range(first, size - 1, 2) for a, b in ((i, i + 1), (i + 1, i))]
+
+        return lax.ppermute(e, axis, swaps(0)), lax.ppermute(o, axis, swaps(1))
+
+    def lon_exchange(e, o):
+        return exchange("lon", lon_size, e, o)
+
+    def lev_exchange(e, o):
+        return exchange("lev", lev_size, e, o)
+
+    def partner(bit, total):
+        pairs = [(i, i ^ (1 << bit)) for i in range(lon_size)]
+        if 2 << bit == lon_size:
+            pairs = [(a, b) for a, b in pairs if a < b]
+        return lax.ppermute(total, "lon", pairs)
+
+    bits = lon_size.bit_length() - 1
 
     pj = jnp.where(lax.axis_index("lat") == 0, nj - 1, 0)
     pa = lax.dynamic_slice(initial_state, (pj, ni // 4, 0, 0), (1, half, nk, nm))[0]
@@ -381,9 +417,9 @@
         scratch=(pltpu.SemaphoreType.DMA((nj + 4,)),),
         flops=10**6,
     )(*map(in_hbm, (initial_state, scaled_diffusivity, scaled_forcing)))
+    lev = lev_exchange(*faces[2:])
     lon = lon_exchange(*faces[:2])
     lat_b = lax.ppermute(pb, "lat", swap)
-    lev = lev_exchange(*faces[2:])
     d_edge, f_edge = in_vmem(d_edge), in_vmem(f_edge)
     d, f = in_hbm(scaled_diffusivity), in_hbm(scaled_forcing)
 
@@ -419,7 +455,7 @@
         u, pa, pb = n_u, n_pa, n_pb
 
     scale = 1.0 / (ni * lon_size)
-    n = lon_size.bit_length()
+    n = bits + 1
     end, sums, _, total = call(
         last_bulk_kernel,
         (H(nj, ni, nk, nm), V(nj, ni, nk, nm), V(nj, ni, nk, nm), V(nj - 1, nk, nm)),
@@ -429,21 +465,32 @@
         aliases={7: 1, 8: 2},
         flops=2 * 10**7,
     )(u, pa, pb, *lon, *lev, in_vmem(d), in_vmem(f), n_pa)
-    others = partners(total)
+    other = partner(0, total)
+    mine = call(half_kernel, V(nj - 1, nk // 2, nm), VMEM, (VMEM,) * 2, flops=10**5)(in_vmem(total), in_vmem(other))
+    others = []
+    for bit in range(1, bits):
+        others.append(partner(bit, mine))
+        mine = mine + others[-1]
+    mine = call(before_kernel, V(nj - 1, nk // 2, nm), VMEM, (VMEM,) * (bits - 1), flops=10**5)(*map(in_vmem, others))
+    back = lax.ppermute(mine, "lon", [(i, i ^ 1) for i in range(lon_size)])
     out = call(
         functools.partial(totals_kernel, scale),
         H(nj, ni, nk, nm),
         HBM,
-        (VMEM,) * n,
+        (VMEM,) * 4,
         limit=4,
         scratch=(V(2, ni, nk, nm), pltpu.SemaphoreType.DMA((2,))),
         flops=10**6,
-    )(in_vmem(sums), *others)
+    )(*map(in_vmem, (sums, other, mine, back)))
     n_pa = in_vmem(n_pa)
     n_pb, edge_sums, edge_total = call(
         last_edge_kernel, (V(half, nk, nm), V(ni, nk, nm), V(nk, nm)), (VMEM,) * 3, (VMEM,) * 11, flops=2 * 10**6
     )(u, pa, pb, lat_b, *lon, *lev, d_edge, f_edge, n_pa)
-    others = partners(edge_total)
+    others = []
+    for bit in range(bits):
+        others.append(partner(bit, edge_total))
+        edge_total = edge_total + others[-1]
+    others = tuple(map(in_vmem, others))
     end, out = call(
         functools.partial(last_totals_kernel, scale),
         (H(nj, ni, nk, nm),) * 2,

time: 166 us -> 148 us (0.89)
  the two profiles are of different devices: /device:TPU:30 before, /device:TPU:64 now
where the time goes in v3:
time: 148 us
  starting transfers between devices  88.3 us (60%)
  Pallas kernels  32.1 us (22%)
  waiting for transfers between devices  25.2 us (17%)
    ppermute x16, starting transfers between devices, exchange(): return (lax.ppermute(e, axis, swaps(0)), lax.ppermute(o, axis, swaps(1)))  62.6 us
    ppermute x6, starting transfers between devices, partner(): return lax.ppermute(total, 'lon', pairs)  16.7 us
    ppermute x16, waiting for transfers between devices, exchange(): return (lax.ppermute(e, axis, swaps(0)), lax.ppermute(o, axis, swaps(1)))  14 us
    ppermute x6, waiting for transfers between devices, partner(): return lax.ppermute(total, 'lon', pairs)  11.2 us
    pallas_call x2, Pallas kernels, per_device(): call(bulk_kernel, V(nj, ni, nk, nm), VMEM, (VMEM,) * 9 + (ANY,), flops=2...  7.76 us
    pallas_call x1, Pallas kernels, per_device(): call(first_bulk_kernel, (V(nj, ni, nk, nm),) * 3, (VMEM,) * 3, (VMEM,) *...  5.85 us
    pallas_call x1, Pallas kernels, per_device(): call(last_bulk_kernel, (H(nj, ni, nk, nm), V(nj, ni, nk, nm), V(nj, ni, n...  5.24 us
    ppermute x3, starting transfers between devices, per_device(): lat_a = lax.ppermute(n_pa, 'lat', swap)  4.91 us
  transfers between devices with their start and end apart: 31, of which 9 were waited for; matrix products, arithmetic and copies ran while one was open for 0% of the time, Pallas kernels for 21%

profile of v3, /device:TPU:64, one launch (start us, length us, event | category | flops | bytes accessed | tf_op | source)
XLA Modules:
  0.0 147.8 jit_solution(10496597210953570786)
XLA Ops:
  0.6 1.1 dynamic-slice_bitcast_fusion.pa
  1.7 1.6 %collective-permute-start.4 = (f32[16,64,128]{2,1,0:T(8,128)S(1)}, f32[16,64,128]{2,1,0:T(8,128)S(1)}, u32[]{:S(2)}, u32[]{:S(2)}) collective-permute-start(f32[16,64,128]{2,1,0:T(8,128)S(1)} %dynamic-slice_bitcast_fusion.pa), channel_id=1, source_target_pairs={{0,64},{64,0},{1,65},{65,1},{2,66},{66,2},{3,67},{67,3},{4,68},{68... | collective-permute-start | bytes 1572872 | tf_op jit(solution)/shard_map/ppermute | solution.py:411
  3.3 4.4 %shard_map.50 = (f32[8,32,64,128]{3,2,1,0:T(8,128)S(1)}, f32[16,64,128]{2,1,0:T(8,128)S(1)}, f32[32,64,128]{2,1,0:T(8,128)S(1)}, f32[32,64,128]{2,1,0:T(8,128)S(...) custom-call(f32[8,32,64,128]{3,2,1,0:T(8,128)} %u_in.1, ...), custom_call_target="tpu_custom_call" | custom-call | flops 1000000 | tf_op jit(solution)/shard_map/pallas_call | solution.py:412
  7.7 0.6 collective-permute-start.5
  8.4 1.6 %collective-permute-start.2 = (f32[8,32,128]{2,1,0:T(8,128)S(1)}, f32[8,32,128]{2,1,0:T(8,128)S(1)}, u32[]{:S(2)}, u32[]{:S(2)}) collective-permute-start(f32[8,32,128]{2,1,0:T(8,128)S(1)} %get-tuple-element.40), channel_id=1, source_target_pairs={{0,1},{1,0},{2,3},{3,2},{4,5},{5,4},{6,7},{7,6},{8,9},{9,8},{10,11... | collective-permute-start | bytes 393224 | tf_op jit(solution)/shard_map/ppermute | solution.py:393
  9.9 3.2 %collective-permute-start.3 = (f32[8,32,128]{2,1,0:T(8,128)S(1)}, f32[8,32,128]{2,1,0:T(8,128)S(1)}, u32[]{:S(2)}, u32[]{:S(2)}) collective-permute-start(f32[8,32,128]{2,1,0:T(8,128)S(1)} %get-tuple-element.41), channel_id=1, source_target_pairs={{1,2},{2,1},{3,4},{4,3},{5,6},{6,5},{9,10},{10,9},{11,12},{12,11},... | collective-permute-start | bytes 393224 | tf_op jit(solution)/shard_map/ppermute | solution.py:393
  13.1 0.1 collective-permute-start
  13.2 0.1 collective-permute-done.2.lev_e
  13.3 0.7 collective-permute-start.1
  14.0 6.4 %collective-permute-done.3.lev_o = f32[8,32,128]{2,1,0:T(8,128)S(1)} collective-permute-done((f32[8,32,128]{2,1,0:T(8,128)S(1)}, f32[8,32,128]{2,1,0:T(8,128)S(1)}, u32[]{:S(2)}, u32[]{:S(2)}) %collective-permute-start.3) | collective-permute-done | bytes 131104 | tf_op jit(solution)/shard_map/ppermute | solution.py:393
  20.4 0.0 collective-permute-done.4.lat
  20.4 0.3 shard_map.51.after.rest_1_.pa
  20.7 1.6 %collective-permute-start.10 = (f32[16,64,128]{2,1,0:T(8,128)S(1)}, f32[16,64,128]{2,1,0:T(8,128)S(1)}, u32[]{:S(2)}, u32[]{:S(2)}) collective-permute-start(f32[16,64,128]{2,1,0:T(8,128)S(1)} %shard_map.51.after.rest_1_.pa), channel_id=1, source_target_pairs={{0,64},{64,0},{1,65},{65,1},{2,66},{66,2},{3,67},{67,3},{4,68},{68... | collective-permute-start | bytes 1572872 | tf_op jit(solution)/shard_map/ppermute | solution.py:435
  22.2 0.0 collective-permute-done.lon_e
  22.2 0.0 collective-permute-done.1.lon_o
  22.2 5.9 %shard_map.52 = (f32[8,32,64,128]{3,2,1,0:T(8,128)S(1)}, f32[8,32,64,128]{3,2,1,0:T(8,128)S(1)}, f32[8,32,64,128]{3,2,1,0:T(8,128)S(1)}) custom-call(f32[8,32,64,128]{3,2,1,0:T(8,128)S(1)} %get-tuple-element.36.u, f32[16,64,128]{2,1,0:T(8,128)S(1)} %dynamic-slice_bitcast_fusion.pa, f32[16,64,128]{2,1,0:T(8,128)S(1)} %get-tuple-element.37.pb, ...), custom_call_target="tpu_custom_call" | custom-call | flops 20000000 | tf_op jit(solution)/shard_map/pallas_call | solution.py:437
  28.1 0.0 copy-start
  28.1 0.5 shard_map.53
  28.7 1.3 collective-permute-start.11
  30.0 1.6 %collective-permute-start.8 = (f32[8,32,128]{2,1,0:T(8,128)S(1)}, f32[8,32,128]{2,1,0:T(8,128)S(1)}, u32[]{:S(2)}, u32[]{:S(2)}) collective-permute-start(f32[8,32,128]{2,1,0:T(8,128)S(1)} %get-tuple-element.48), channel_id=1, source_target_pairs={{0,1},{1,0},{2,3},{3,2},{4,5},{5,4},{6,7},{7,6},{8,9},{9,8},{10,11... | collective-permute-start | bytes 393224 | tf_op jit(solution)/shard_map/ppermute | solution.py:393
  31.5 3.2 %collective-permute-start.9 = (f32[8,32,128]{2,1,0:T(8,128)S(1)}, f32[8,32,128]{2,1,0:T(8,128)S(1)}, u32[]{:S(2)}, u32[]{:S(2)}) collective-permute-start(f32[8,32,128]{2,1,0:T(8,128)S(1)} %get-tuple-element.49), channel_id=1, source_target_pairs={{1,2},{2,1},{3,4},{4,3},{5,6},{6,5},{9,10},{10,9},{11,12},{12,11},... | collective-permute-start | bytes 393224 | tf_op jit(solution)/shard_map/ppermute | solution.py:393
  34.7 11.6 %collective-permute-start.6 = (f32[8,64,128]{2,1,0:T(8,128)S(1)}, f32[8,64,128]{2,1,0:T(8,128)S(1)}, u32[]{:S(2)}, u32[]{:S(2)}) collective-permute-start(f32[8,64,128]{2,1,0:T(8,128)S(1)} %get-tuple-element.46), channel_id=1, source_target_pairs={{0,8},{8,0},{16,24},{24,16},{32,40},{40,32},{48,56},{56,48},{1,9},... | collective-permute-start | bytes 786440 | tf_op jit(solution)/shard_map/ppermute | solution.py:393
  46.4 0.0 collective-permute-done.8.lev_e
  46.4 0.7 collective-permute-start.7
  47.0 0.0 collective-permute-done.10.lat
  47.1 0.3 shard_map.54.after.rest_1_.pa
  47.3 1.7 %collective-permute-start.16 = (f32[16,64,128]{2,1,0:T(8,128)S(1)}, f32[16,64,128]{2,1,0:T(8,128)S(1)}, u32[]{:S(2)}, u32[]{:S(2)}) collective-permute-start(f32[16,64,128]{2,1,0:T(8,128)S(1)} %shard_map.54.after.rest_1_.pa), channel_id=1, source_target_pairs={{0,64},{64,0},{1,65},{65,1},{2,66},{66,2},{3,67},{67,3},{4,68},{68... | collective-permute-start | bytes 1572872 | tf_op jit(solution)/shard_map/ppermute | solution.py:435
  49.1 3.9 %shard_map.55.rest_0_.u = f32[8,32,64,128]{3,2,1,0:T(8,128)S(1)} custom-call(f32[8,32,64,128]{3,2,1,0:T(8,128)S(1)} %get-tuple-element.44.rest_0_.u, f32[16,64,128]{2,1,0:T(8,128)S(1)} %shard_map.51.after.rest_1_.pa, f32[16,64,128]{2,1,0:T(8,128)S(1)} %get-tuple-element.45.pb, f32[8,64,128]{2,1,0:T(8,128)S(1)} %collective-permute-done.6.lon_e, ...), custom_call_target="tpu_custom_call" | custom-call | flops 20000000 | tf_op jit(solution)/shard_map/pallas_call | solution.py:446
  53.0 0.5 shard_map.56
  53.5 0.0 copy-start.1
  53.5 0.5 collective-permute-start.17
  54.0 1.6 %collective-permute-start.14 = (f32[8,32,128]{2,1,0:T(8,128)S(1)}, f32[8,32,128]{2,1,0:T(8,128)S(1)}, u32[]{:S(2)}, u32[]{:S(2)}) collective-permute-start(f32[8,32,128]{2,1,0:T(8,128)S(1)} %get-tuple-element.55), channel_id=1, source_target_pairs={{0,1},{1,0},{2,3},{3,2},{4,5},{5,4},{6,7},{7,6},{8,9},{9,8},{10,11... | collective-permute-start | bytes 393224 | tf_op jit(solution)/shard_map/ppermute | solution.py:393
  55.6 4.9 %collective-permute-start.15 = (f32[8,32,128]{2,1,0:T(8,128)S(1)}, f32[8,32,128]{2,1,0:T(8,128)S(1)}, u32[]{:S(2)}, u32[]{:S(2)}) collective-permute-start(f32[8,32,128]{2,1,0:T(8,128)S(1)} %get-tuple-element.56), channel_id=1, source_target_pairs={{1,2},{2,1},{3,4},{4,3},{5,6},{6,5},{9,10},{10,9},{11,12},{12,11},... | collective-permute-start | bytes 393224 | tf_op jit(solution)/shard_map/ppermute | solution.py:393
  60.5 11.0 %collective-permute-start.12 = (f32[8,64,128]{2,1,0:T(8,128)S(1)}, f32[8,64,128]{2,1,0:T(8,128)S(1)}, u32[]{:S(2)}, u32[]{:S(2)}) collective-permute-start(f32[8,64,128]{2,1,0:T(8,128)S(1)} %get-tuple-element.53), channel_id=1, source_target_pairs={{0,8},{8,0},{16,24},{24,16},{32,40},{40,32},{48,56},{56,48},{1,9},... | collective-permute-start | bytes 786440 | tf_op jit(solution)/shard_map/ppermute | solution.py:393
  71.5 0.0 collective-permute-done.14.lev_e
  71.5 0.7 collective-permute-start.13
  72.2 0.3 shard_map.57.after.rest_1_.pa
  72.5 1.6 %collective-permute-start.23 = (f32[16,64,128]{2,1,0:T(8,128)S(1)}, f32[16,64,128]{2,1,0:T(8,128)S(1)}, u32[]{:S(2)}, u32[]{:S(2)}) collective-permute-start(f32[16,64,128]{2,1,0:T(8,128)S(1)} %shard_map.57.after.rest_1_.pa), channel_id=1, source_target_pairs={{0,64},{64,0},{1,65},{65,1},{2,66},{66,2},{3,67},{67,3},{4,68},{68... | collective-permute-start | bytes 1572872 | tf_op jit(solution)/shard_map/ppermute | solution.py:435
  74.1 3.9 %shard_map.58.rest_0_.u = f32[8,32,64,128]{3,2,1,0:T(8,128)S(1)} custom-call(f32[8,32,64,128]{3,2,1,0:T(8,128)S(1)} %shard_map.55.rest_0_.u, f32[16,64,128]{2,1,0:T(8,128)S(1)} %shard_map.54.after.rest_1_.pa, f32[16,64,128]{2,1,0:T(8,128)S(1)} %get-tuple-element.52.pb, f32[8,64,128]{2,1,0:T(8,128)S(1)} %collective-permute-done.12.lon_e, ...), custom_call_target="tpu_custom_call" | custom-call | flops 20000000 | tf_op jit(solution)/shard_map/pallas_call | solution.py:446
  78.0 0.5 shard_map.59
  78.5 16.7 %collective-permute-start.19 = (f32[8,64,128]{2,1,0:T(8,128)S(1)}, f32[8,64,128]{2,1,0:T(8,128)S(1)}, u32[]{:S(2)}, u32[]{:S(2)}) collective-permute-start(f32[8,64,128]{2,1,0:T(8,128)S(1)} %get-tuple-element.58), channel_id=1, source_target_pairs={{0,8},{8,0},{16,24},{24,16},{32,40},{40,32},{48,56},{56,48},{1,9},... | collective-permute-start | bytes 786440 | tf_op jit(solution)/shard_map/ppermute | solution.py:393
  95.2 0.7 collective-permute-start.20
  95.9 1.7 %collective-permute-start.21 = (f32[8,32,128]{2,1,0:T(8,128)S(1)}, f32[8,32,128]{2,1,0:T(8,128)S(1)}, u32[]{:S(2)}, u32[]{:S(2)}) collective-permute-start(f32[8,32,128]{2,1,0:T(8,128)S(1)} %get-tuple-element.60), channel_id=1, source_target_pairs={{0,1},{1,0},{2,3},{3,2},{4,5},{5,4},{6,7},{7,6},{8,9},{9,8},{10,11... | collective-permute-start | bytes 393224 | tf_op jit(solution)/shard_map/ppermute | solution.py:393
  97.6 2.9 %collective-permute-start.22 = (f32[8,32,128]{2,1,0:T(8,128)S(1)}, f32[8,32,128]{2,1,0:T(8,128)S(1)}, u32[]{:S(2)}, u32[]{:S(2)}) collective-permute-start(f32[8,32,128]{2,1,0:T(8,128)S(1)} %get-tuple-element.61), channel_id=1, source_target_pairs={{1,2},{2,1},{3,4},{4,3},{5,6},{6,5},{9,10},{10,9},{11,12},{12,11},... | collective-permute-start | bytes 393224 | tf_op jit(solution)/shard_map/ppermute | solution.py:393
  100.4 0.5 collective-permute-done.21.lev_e
  101.0 0.2 collective-permute-start.18
  101.1 6.9 %collective-permute-done.22.lev_o = f32[8,32,128]{2,1,0:T(8,128)S(1)} collective-permute-done((f32[8,32,128]{2,1,0:T(8,128)S(1)}, f32[8,32,128]{2,1,0:T(8,128)S(1)}, u32[]{:S(2)}, u32[]{:S(2)}) %collective-permute-start.22) | collective-permute-done | bytes 131104 | tf_op jit(solution)/shard_map/ppermute | solution.py:393
  108.1 0.3 shard_map.60.npa.after
  108.3 5.2 %shard_map.62 = (f32[8,32,64,128]{3,2,1,0:T(8,128)}, f32[8,32,64,128]{3,2,1,0:T(8,128)S(1)}, f32[8,32,64,128]{3,2,1,0:T(8,128)S(1)}, f32[7,64,128]{2,1,0:T(8,128)S(1)}) custom-call(f32[8,32,64,128]{3,2,1,0:T(8,128)S(1)} %shard_map.58.rest_0_.u, f32[16,64,128]{2,1,0:T(8,128)S(1)} %shard_map.57.after.rest_1_.pa, ...), custom_call_target="tpu_custom_call", output_to_operand_aliasing={{1}: (7, {}), {2}: (8, {})} | custom-call | flops 20000000 | tf_op jit(solution)/shard_map/pallas_call | solution.py:459
  113.6 1.8 %collective-permute-start.27 = (f32[7,64,128]{2,1,0:T(8,128)S(1)}, f32[7,64,128]{2,1,0:T(8,128)S(1)}, u32[]{:S(2)}, u32[]{:S(2)}) collective-permute-start(f32[7,64,128]{2,1,0:T(8,128)S(1)} %get-tuple-element.67.total), channel_id=1, source_target_pairs={{0,8},{8,0},{16,24},{24,16},{32,40},{40,32},{48,56},{56,48},{1,9},... | collective-permute-start | bytes 688136 | tf_op jit(solution)/shard_map/ppermute | solution.py:405
  115.4 1.1 collective-permute-done.27.other
  116.5 4.4 %collective-permute-start.28 = (f32[7,32,128]{2,1,0:T(8,128)S(1)}, f32[7,32,128]{2,1,0:T(8,128)S(1)}, u32[]{:S(2)}, u32[]{:S(2)}) collective-permute-start(f32[7,32,128]{2,1,0:T(8,128)S(1)} %shard_map.63), channel_id=1, source_target_pairs={{0,16},{8,24},{16,0},{24,8},{32,48},{40,56},{48,32},{56,40},{1,17}... | collective-permute-start | bytes 344072 | tf_op jit(solution)/shard_map/ppermute | solution.py:405
  121.0 3.4 %collective-permute-done.28.refs_0_ = f32[7,32,128]{2,1,0:T(8,128)S(1)} collective-permute-done((f32[7,32,128]{2,1,0:T(8,128)S(1)}, f32[7,32,128]{2,1,0:T(8,128)S(1)}, u32[]{:S(2)}, u32[]{:S(2)}) %collective-permute-start.28) | collective-permute-done | bytes 114720 | tf_op jit(solution)/shard_map/ppermute | solution.py:405
  124.4 3.6 %collective-permute-start.29 = (f32[7,32,128]{2,1,0:T(8,128)S(1)}, f32[7,32,128]{2,1,0:T(8,128)S(1)}, u32[]{:S(2)}, u32[]{:S(2)}) collective-permute-start(f32[7,32,128]{2,1,0:T(8,128)S(1)} %add.12), channel_id=1, source_target_pairs={{0,32},{8,40},{16,48},{24,56},{1,33},{9,41},{17,49},{25,57},{2,34}... | collective-permute-start | bytes 344072 | tf_op jit(solution)/shard_map/ppermute | solution.py:405
  128.0 2.3 %collective-permute-done.29.refs_1_ = f32[7,32,128]{2,1,0:T(8,128)S(1)} collective-permute-done((f32[7,32,128]{2,1,0:T(8,128)S(1)}, f32[7,32,128]{2,1,0:T(8,128)S(1)}, u32[]{:S(2)}, u32[]{:S(2)}) %collective-permute-start.29) | collective-permute-done | bytes 114720 | tf_op jit(solution)/shard_map/ppermute | solution.py:405
  130.4 0.1 collective-permute-start.30
  130.5 0.4 shard_map.61
  130.9 0.6 collective-permute-start.24
  131.4 0.9 collective-permute-done.24.rest_0_
  132.3 1.9 %collective-permute-start.25 = (f32[64,128]{1,0:T(8,128)S(1)}, f32[64,128]{1,0:T(8,128)S(1)}, u32[]{:S(2)}, u32[]{:S(2)}) collective-permute-start(f32[64,128]{1,0:T(8,128)S(1)} %add.10), channel_id=1, source_target_pairs={{0,16},{8,24},{16,0},{24,8},{32,48},{40,56},{48,32},{56,40},{1,17}... | collective-permute-start | bytes 98312 | tf_op jit(solution)/shard_map/ppermute | solution.py:405
  134.2 3.5 %collective-permute-done.25.rest_1_ = f32[64,128]{1,0:T(8,128)S(1)} collective-permute-done((f32[64,128]{1,0:T(8,128)S(1)}, f32[64,128]{1,0:T(8,128)S(1)}, u32[]{:S(2)}, u32[]{:S(2)}) %collective-permute-start.25) | collective-permute-done | bytes 32800 | tf_op jit(solution)/shard_map/ppermute | solution.py:405
  137.7 4.3 %collective-permute-start.26 = (f32[64,128]{1,0:T(8,128)S(1)}, f32[64,128]{1,0:T(8,128)S(1)}, u32[]{:S(2)}, u32[]{:S(2)}) collective-permute-start(f32[64,128]{1,0:T(8,128)S(1)} %add.11), channel_id=1, source_target_pairs={{0,32},{8,40},{16,48},{24,56},{1,33},{9,41},{17,49},{25,57},{2,34}... | collective-permute-start | bytes 98312 | tf_op jit(solution)/shard_map/ppermute | solution.py:405
  142.1 4.4 %shard_map.65.rest_4_ = f32[8,32,64,128]{3,2,1,0:T(8,128)} custom-call(f32[8,32,64,128]{3,2,1,0:T(8,128)S(1)} %get-tuple-element.66.sums, f32[7,64,128]{2,1,0:T(8,128)S(1)} %collective-permute-done.27.other, f32[7,32,128]{2,1,0:T(8,128)S(1)} %shard_map.64.mine, f32[7,32,128]{2,1,0:T(8,128)S(1)} %collective-permute-done.30.partners), custom_call_target="tpu_custom_call" | custom-call | flops 1000000 | tf_op jit(solution)/shard_map/pallas_call | solution.py:476
  146.4 1.4 shard_map.66
  (23 shorter events, 0.1 us)
Async XLA Ops:
  1.7 18.7 %collective-permute-start.4 = (f32[16,64,128]{2,1,0:T(8,128)S(1)}, f32[16,64,128]{2,1,0:T(8,128)S(1)}, u32[]{:S(2)}, u32[]{:S(2)}) collective-permute-start(f32[16,64,128]{2,1,0:T(8,128)S(1)} %dynamic-slice_bitcast_fusion.pa), channel_id=1, source_target_pairs={{0,64},{64,0},{1,65},{65,1},{2,66},{66,2},{3,67},{67,3},{4,68},{68... | collective-permute-start | bytes 1572872 | tf_op jit(solution)/shard_map/ppermute | solution.py:411
  7.7 20.4 %collective-permute-start.5 = (f32[16,64,128]{2,1,0:T(8,128)S(1)}, f32[16,64,128]{2,1,0:T(8,128)S(1)}, u32[]{:S(2)}, u32[]{:S(2)}) collective-permute-start(f32[16,64,128]{2,1,0:T(8,128)S(1)} %get-tuple-element.37.pb), channel_id=1, source_target_pairs={{0,64},{64,0},{1,65},{65,1},{2,66},{66,2},{3,67},{67,3},{4,68},{68... | collective-permute-start | bytes 1572872 | tf_op jit(solution)/shard_map/ppermute | solution.py:422
  8.4 5.0 %collective-permute-start.2 = (f32[8,32,128]{2,1,0:T(8,128)S(1)}, f32[8,32,128]{2,1,0:T(8,128)S(1)}, u32[]{:S(2)}, u32[]{:S(2)}) collective-permute-start(f32[8,32,128]{2,1,0:T(8,128)S(1)} %get-tuple-element.40), channel_id=1, source_target_pairs={{0,1},{1,0},{2,3},{3,2},{4,5},{5,4},{6,7},{7,6},{8,9},{9,8},{10,11... | collective-permute-start | bytes 393224 | tf_op jit(solution)/shard_map/ppermute | solution.py:393
  9.9 10.5 %collective-permute-start.3 = (f32[8,32,128]{2,1,0:T(8,128)S(1)}, f32[8,32,128]{2,1,0:T(8,128)S(1)}, u32[]{:S(2)}, u32[]{:S(2)}) collective-permute-start(f32[8,32,128]{2,1,0:T(8,128)S(1)} %get-tuple-element.41), channel_id=1, source_target_pairs={{1,2},{2,1},{3,4},{4,3},{5,6},{6,5},{9,10},{10,9},{11,12},{12,11},... | collective-permute-start | bytes 393224 | tf_op jit(solution)/shard_map/ppermute | solution.py:393
  13.1 9.1 %collective-permute-start = (f32[8,64,128]{2,1,0:T(8,128)S(1)}, f32[8,64,128]{2,1,0:T(8,128)S(1)}, u32[]{:S(2)}, u32[]{:S(2)}) collective-permute-start(f32[8,64,128]{2,1,0:T(8,128)S(1)} %get-tuple-element.38), channel_id=1, source_target_pairs={{0,8},{8,0},{16,24},{24,16},{32,40},{40,32},{48,56},{56,48},{1,9},... | collective-permute-start | bytes 786440 | tf_op jit(solution)/shard_map/ppermute | solution.py:393
  13.3 8.9 %collective-permute-start.1 = (f32[8,64,128]{2,1,0:T(8,128)S(1)}, f32[8,64,128]{2,1,0:T(8,128)S(1)}, u32[]{:S(2)}, u32[]{:S(2)}) collective-permute-start(f32[8,64,128]{2,1,0:T(8,128)S(1)} %get-tuple-element.39), channel_id=1, source_target_pairs={{8,16},{16,8},{24,32},{32,24},{40,48},{48,40},{9,17},{17,9},{25,33... | collective-permute-start | bytes 786440 | tf_op jit(solution)/shard_map/ppermute | solution.py:393
  20.7 26.4 %collective-permute-start.10 = (f32[16,64,128]{2,1,0:T(8,128)S(1)}, f32[16,64,128]{2,1,0:T(8,128)S(1)}, u32[]{:S(2)}, u32[]{:S(2)}) collective-permute-start(f32[16,64,128]{2,1,0:T(8,128)S(1)} %shard_map.51.after.rest_1_.pa), channel_id=1, source_target_pairs={{0,64},{64,0},{1,65},{65,1},{2,66},{66,2},{3,67},{67,3},{4,68},{68... | collective-permute-start | bytes 1572872 | tf_op jit(solution)/shard_map/ppermute | solution.py:435
  28.1 21.0 %copy-start = (f32[8,32,64,128]{3,2,1,0:T(8,128)}, f32[8,32,64,128]{3,2,1,0:T(8,128)S(1)}, u32[]{:S(2)}) copy-start(f32[8,32,64,128]{3,2,1,0:T(8,128)S(1)} %get-tuple-element.51.f.f_in) | copy-start | bytes 25165828
  28.7 24.3 %collective-permute-start.11 = (f32[16,64,128]{2,1,0:T(8,128)S(1)}, f32[16,64,128]{2,1,0:T(8,128)S(1)}, u32[]{:S(2)}, u32[]{:S(2)}) collective-permute-start(f32[16,64,128]{2,1,0:T(8,128)S(1)} %get-tuple-element.45.pb), channel_id=1, source_target_pairs={{0,64},{64,0},{1,65},{65,1},{2,66},{66,2},{3,67},{67,3},{4,68},{68... | collective-permute-start | bytes 1572872 | tf_op jit(solution)/shard_map/ppermute | solution.py:453
  30.0 16.4 %collective-permute-start.8 = (f32[8,32,128]{2,1,0:T(8,128)S(1)}, f32[8,32,128]{2,1,0:T(8,128)S(1)}, u32[]{:S(2)}, u32[]{:S(2)}) collective-permute-start(f32[8,32,128]{2,1,0:T(8,128)S(1)} %get-tuple-element.48), channel_id=1, source_target_pairs={{0,1},{1,0},{2,3},{3,2},{4,5},{5,4},{6,7},{7,6},{8,9},{9,8},{10,11... | collective-permute-start | bytes 393224 | tf_op jit(solution)/shard_map/ppermute | solution.py:393
  31.5 15.5 %collective-permute-start.9 = (f32[8,32,128]{2,1,0:T(8,128)S(1)}, f32[8,32,128]{2,1,0:T(8,128)S(1)}, u32[]{:S(2)}, u32[]{:S(2)}) collective-permute-start(f32[8,32,128]{2,1,0:T(8,128)S(1)} %get-tuple-element.49), channel_id=1, source_target_pairs={{1,2},{2,1},{3,4},{4,3},{5,6},{6,5},{9,10},{10,9},{11,12},{12,11},... | collective-permute-start | bytes 393224 | tf_op jit(solution)/shard_map/ppermute | solution.py:393
  34.7 14.4 %collective-permute-start.6 = (f32[8,64,128]{2,1,0:T(8,128)S(1)}, f32[8,64,128]{2,1,0:T(8,128)S(1)}, u32[]{:S(2)}, u32[]{:S(2)}) collective-permute-start(f32[8,64,128]{2,1,0:T(8,128)S(1)} %get-tuple-element.46), channel_id=1, source_target_pairs={{0,8},{8,0},{16,24},{24,16},{32,40},{40,32},{48,56},{56,48},{1,9},... | collective-permute-start | bytes 786440 | tf_op jit(solution)/shard_map/ppermute | solution.py:393
  46.4 2.7 %collective-permute-start.7 = (f32[8,64,128]{2,1,0:T(8,128)S(1)}, f32[8,64,128]{2,1,0:T(8,128)S(1)}, u32[]{:S(2)}, u32[]{:S(2)}) collective-permute-start(f32[8,64,128]{2,1,0:T(8,128)S(1)} %get-tuple-element.47), channel_id=1, source_target_pairs={{8,16},{16,8},{24,32},{32,24},{40,48},{48,40},{9,17},{17,9},{25,33... | collective-permute-start | bytes 786440 | tf_op jit(solution)/shard_map/ppermute | solution.py:393
  47.3 24.8 %collective-permute-start.16 = (f32[16,64,128]{2,1,0:T(8,128)S(1)}, f32[16,64,128]{2,1,0:T(8,128)S(1)}, u32[]{:S(2)}, u32[]{:S(2)}) collective-permute-start(f32[16,64,128]{2,1,0:T(8,128)S(1)} %shard_map.54.after.rest_1_.pa), channel_id=1, source_target_pairs={{0,64},{64,0},{1,65},{65,1},{2,66},{66,2},{3,67},{67,3},{4,68},{68... | collective-permute-start | bytes 1572872 | tf_op jit(solution)/shard_map/ppermute | solution.py:435
  53.5 20.5 %copy-start.1 = (f32[8,32,64,128]{3,2,1,0:T(8,128)S(1)}, f32[8,32,64,128]{3,2,1,0:T(8,128)}, u32[]{:S(2)}) copy-start(f32[8,32,64,128]{3,2,1,0:T(8,128)} %copy-done) | copy-start | bytes 25165828
  53.5 24.4 %collective-permute-start.17 = (f32[16,64,128]{2,1,0:T(8,128)S(1)}, f32[16,64,128]{2,1,0:T(8,128)S(1)}, u32[]{:S(2)}, u32[]{:S(2)}) collective-permute-start(f32[16,64,128]{2,1,0:T(8,128)S(1)} %get-tuple-element.52.pb), channel_id=1, source_target_pairs={{0,64},{64,0},{1,65},{65,1},{2,66},{66,2},{3,67},{67,3},{4,68},{68... | collective-permute-start | bytes 1572872 | tf_op jit(solution)/shard_map/ppermute | solution.py:453
  54.0 17.5 %collective-permute-start.14 = (f32[8,32,128]{2,1,0:T(8,128)S(1)}, f32[8,32,128]{2,1,0:T(8,128)S(1)}, u32[]{:S(2)}, u32[]{:S(2)}) collective-permute-start(f32[8,32,128]{2,1,0:T(8,128)S(1)} %get-tuple-element.55), channel_id=1, source_target_pairs={{0,1},{1,0},{2,3},{3,2},{4,5},{5,4},{6,7},{7,6},{8,9},{9,8},{10,11... | collective-permute-start | bytes 393224 | tf_op jit(solution)/shard_map/ppermute | solution.py:393
  55.6 16.6 %collective-permute-start.15 = (f32[8,32,128]{2,1,0:T(8,128)S(1)}, f32[8,32,128]{2,1,0:T(8,128)S(1)}, u32[]{:S(2)}, u32[]{:S(2)}) collective-permute-start(f32[8,32,128]{2,1,0:T(8,128)S(1)} %get-tuple-element.56), channel_id=1, source_target_pairs={{1,2},{2,1},{3,4},{4,3},{5,6},{6,5},{9,10},{10,9},{11,12},{12,11},... | collective-permute-start | bytes 393224 | tf_op jit(solution)/shard_map/ppermute | solution.py:393
  60.5 13.5 %collective-permute-start.12 = (f32[8,64,128]{2,1,0:T(8,128)S(1)}, f32[8,64,128]{2,1,0:T(8,128)S(1)}, u32[]{:S(2)}, u32[]{:S(2)}) collective-permute-start(f32[8,64,128]{2,1,0:T(8,128)S(1)} %get-tuple-element.53), channel_id=1, source_target_pairs={{0,8},{8,0},{16,24},{24,16},{32,40},{40,32},{48,56},{56,48},{1,9},... | collective-permute-start | bytes 786440 | tf_op jit(solution)/shard_map/ppermute | solution.py:393
  71.5 2.6 %collective-permute-start.13 = (f32[8,64,128]{2,1,0:T(8,128)S(1)}, f32[8,64,128]{2,1,0:T(8,128)S(1)}, u32[]{:S(2)}, u32[]{:S(2)}) collective-permute-start(f32[8,64,128]{2,1,0:T(8,128)S(1)} %get-tuple-element.54), channel_id=1, source_target_pairs={{8,16},{16,8},{24,32},{32,24},{40,48},{48,40},{9,17},{17,9},{25,33... | collective-permute-start | bytes 786440 | tf_op jit(solution)/shard_map/ppermute | solution.py:393
  72.5 35.6 %collective-permute-start.23 = (f32[16,64,128]{2,1,0:T(8,128)S(1)}, f32[16,64,128]{2,1,0:T(8,128)S(1)}, u32[]{:S(2)}, u32[]{:S(2)}) collective-permute-start(f32[16,64,128]{2,1,0:T(8,128)S(1)} %shard_map.57.after.rest_1_.pa), channel_id=1, source_target_pairs={{0,64},{64,0},{1,65},{65,1},{2,66},{66,2},{3,67},{67,3},{4,68},{68... | collective-permute-start | bytes 1572872 | tf_op jit(solution)/shard_map/ppermute | solution.py:435
  78.5 29.8 %collective-permute-start.19 = (f32[8,64,128]{2,1,0:T(8,128)S(1)}, f32[8,64,128]{2,1,0:T(8,128)S(1)}, u32[]{:S(2)}, u32[]{:S(2)}) collective-permute-start(f32[8,64,128]{2,1,0:T(8,128)S(1)} %get-tuple-element.58), channel_id=1, source_target_pairs={{0,8},{8,0},{16,24},{24,16},{32,40},{40,32},{48,56},{56,48},{1,9},... | collective-permute-start | bytes 786440 | tf_op jit(solution)/shard_map/ppermute | solution.py:393
  95.2 13.1 %collective-permute-start.20 = (f32[8,64,128]{2,1,0:T(8,128)S(1)}, f32[8,64,128]{2,1,0:T(8,128)S(1)}, u32[]{:S(2)}, u32[]{:S(2)}) collective-permute-start(f32[8,64,128]{2,1,0:T(8,128)S(1)} %get-tuple-element.59), channel_id=1, source_target_pairs={{8,16},{16,8},{24,32},{32,24},{40,48},{48,40},{9,17},{17,9},{25,33... | collective-permute-start | bytes 786440 | tf_op jit(solution)/shard_map/ppermute | solution.py:393
  95.9 5.0 %collective-permute-start.21 = (f32[8,32,128]{2,1,0:T(8,128)S(1)}, f32[8,32,128]{2,1,0:T(8,128)S(1)}, u32[]{:S(2)}, u32[]{:S(2)}) collective-permute-start(f32[8,32,128]{2,1,0:T(8,128)S(1)} %get-tuple-element.60), channel_id=1, source_target_pairs={{0,1},{1,0},{2,3},{3,2},{4,5},{5,4},{6,7},{7,6},{8,9},{9,8},{10,11... | collective-permute-start | bytes 393224 | tf_op jit(solution)/shard_map/ppermute | solution.py:393
  97.6 10.5 %collective-permute-start.22 = (f32[8,32,128]{2,1,0:T(8,128)S(1)}, f32[8,32,128]{2,1,0:T(8,128)S(1)}, u32[]{:S(2)}, u32[]{:S(2)}) collective-permute-start(f32[8,32,128]{2,1,0:T(8,128)S(1)} %get-tuple-element.61), channel_id=1, source_target_pairs={{1,2},{2,1},{3,4},{4,3},{5,6},{6,5},{9,10},{10,9},{11,12},{12,11},... | collective-permute-start | bytes 393224 | tf_op jit(solution)/shard_map/ppermute | solution.py:393
  101.0 29.5 %collective-permute-start.18 = (f32[16,64,128]{2,1,0:T(8,128)S(1)}, f32[16,64,128]{2,1,0:T(8,128)S(1)}, u32[]{:S(2)}, u32[]{:S(2)}) collective-permute-start(f32[16,64,128]{2,1,0:T(8,128)S(1)} %get-tuple-element.57.pb), channel_id=1, source_target_pairs={{0,64},{64,0},{1,65},{65,1},{2,66},{66,2},{3,67},{67,3},{4,68},{68... | collective-permute-start | bytes 1572872 | tf_op jit(solution)/shard_map/ppermute | solution.py:453
  113.6 2.9 %collective-permute-start.27 = (f32[7,64,128]{2,1,0:T(8,128)S(1)}, f32[7,64,128]{2,1,0:T(8,128)S(1)}, u32[]{:S(2)}, u32[]{:S(2)}) collective-permute-start(f32[7,64,128]{2,1,0:T(8,128)S(1)} %get-tuple-element.67.total), channel_id=1, source_target_pairs={{0,8},{8,0},{16,24},{24,16},{32,40},{40,32},{48,56},{56,48},{1,9},... | collective-permute-start | bytes 688136 | tf_op jit(solution)/shard_map/ppermute | solution.py:405
  116.5 7.9 %collective-permute-start.28 = (f32[7,32,128]{2,1,0:T(8,128)S(1)}, f32[7,32,128]{2,1,0:T(8,128)S(1)}, u32[]{:S(2)}, u32[]{:S(2)}) collective-permute-start(f32[7,32,128]{2,1,0:T(8,128)S(1)} %shard_map.63), channel_id=1, source_target_pairs={{0,16},{8,24},{16,0},{24,8},{32,48},{40,56},{48,32},{56,40},{1,17}... | collective-permute-start | bytes 344072 | tf_op jit(solution)/shard_map/ppermute | solution.py:405
  124.4 5.9 %collective-permute-start.29 = (f32[7,32,128]{2,1,0:T(8,128)S(1)}, f32[7,32,128]{2,1,0:T(8,128)S(1)}, u32[]{:S(2)}, u32[]{:S(2)}) collective-permute-start(f32[7,32,128]{2,1,0:T(8,128)S(1)} %add.12), channel_id=1, source_target_pairs={{0,32},{8,40},{16,48},{24,56},{1,33},{9,41},{17,49},{25,57},{2,34}... | collective-permute-start | bytes 344072 | tf_op jit(solution)/shard_map/ppermute | solution.py:405
  130.4 11.7 %collective-permute-start.30 = (f32[7,32,128]{2,1,0:T(8,128)S(1)}, f32[7,32,128]{2,1,0:T(8,128)S(1)}, u32[]{:S(2)}, u32[]{:S(2)}) collective-permute-start(f32[7,32,128]{2,1,0:T(8,128)S(1)} %shard_map.64.mine), channel_id=1, source_target_pairs={{0,8},{8,0},{16,24},{24,16},{32,40},{40,32},{48,56},{56,48},{1,9},... | collective-permute-start | bytes 344072 | tf_op jit(solution)/shard_map/ppermute | solution.py:475
  130.9 1.4 collective-permute-start.24
  132.3 5.4 %collective-permute-start.25 = (f32[64,128]{1,0:T(8,128)S(1)}, f32[64,128]{1,0:T(8,128)S(1)}, u32[]{:S(2)}, u32[]{:S(2)}) collective-permute-start(f32[64,128]{1,0:T(8,128)S(1)} %add.10), channel_id=1, source_target_pairs={{0,16},{8,24},{16,0},{24,8},{32,48},{40,56},{48,32},{56,40},{1,17}... | collective-permute-start | bytes 98312 | tf_op jit(solution)/shard_map/ppermute | solution.py:405
  137.7 8.7 %collective-permute-start.26 = (f32[64,128]{1,0:T(8,128)S(1)}, f32[64,128]{1,0:T(8,128)S(1)}, u32[]{:S(2)}, u32[]{:S(2)}) collective-permute-start(f32[64,128]{1,0:T(8,128)S(1)} %add.11), channel_id=1, source_target_pairs={{0,32},{8,40},{16,48},{24,56},{1,33},{9,41},{17,49},{25,57},{2,34}... | collective-permute-start | bytes 98312 | tf_op jit(solution)/shard_map/ppermute | solution.py:405

commit v4 on v3

--- a/solution.py
+++ b/solution.py
@@ -108,7 +108,7 @@
     return get(lower), get(upper)
 
 
-def edge_rows(lo, hi, base, mine, below, above, u, lat, lev_e, lev_o, d, f, put):
+def edge_rows(lo, hi, base, mine, lat, below, above, u, lev_e, lev_o, d, f, put):
     nj = u.shape[0]
     pj, pn = plane_at(0, nj), plane_at(1, nj)
     sweep(
@@ -117,7 +117,7 @@
         lambda i: mine[i],
         below,
         above,
-        lambda i: u[pn, base + i] + lat[i],
+        lambda i: u[pn, base + i] + lat(i),
         *lev_rows(lev_e, lev_o, pj, base),
         lambda i: d[base + i],
         lambda i: f[base + i],
@@ -126,13 +126,31 @@
     )
 
 
-def edge_a_kernel(u, pa, pb, lat, lev_e, lev_o, d, f, out):
+def edge_a_kernel(parts, u, pa, pb, *rest):
+    lats, (lev_e, lev_o, d, f, out) = rest[:parts], rest[parts:]
+
     def put(i, new, carry):
         out[i] = new
         return carry
 
     n = pa.shape[0]
-    edge_rows(0, n, n // 2, pa, lambda: pb[n // 2 - 1], lambda: pb[n // 2], u, lat, lev_e, lev_o, d, f, put)
+    m = n // parts
+    for part, lat in enumerate(lats):
+        edge_rows(
+            part * m,
+            (part + 1) * m,
+            n // 2,
+            pa,
+            lambda i: lat[i - part * m],
+            (lambda: pb[n // 2 - 1]) if part == 0 else None,
+            (lambda: pb[n // 2]) if part == parts - 1 else None,
+            u,
+            lev_e,
+            lev_o,
+            d,
+            f,
+            put,
+        )
 
 
 def edge_b_kernel(u, pa, pb, lat, lon_e, lon_o, lev_e, lev_o, d, f, *rest):
@@ -145,9 +163,11 @@
         out[i] = new
         return carry
 
-    args = (u, lat, lev_e, lev_o, d, f, put)
-    edge_rows(0, q, 0, pb, lambda: lower("lon", lon_e[pj], lon_o[pj]), lambda: pa[0], *args)
-    edge_rows(q, 2 * q, 2 * q, pb, lambda: pa[2 * q - 1], lambda: upper("lon", lon_e[pj], lon_o[pj]), *args)
+    lat_lo, lat_hi = lat if isinstance(lat, tuple) else (lat, lat.at[pl.ds(q, q)])
+    args = (u, lev_e, lev_o, d, f, put)
+    edge_rows(0, q, 0, pb, lambda i: lat_lo[i], lambda: lower("lon", lon_e[pj], lon_o[pj]), lambda: pa[0], *args)
+    above = lambda: upper("lon", lon_e[pj], lon_o[pj])
+    edge_rows(q, 2 * q, 2 * q, pb, lambda i: lat_hi[i - q], lambda: pa[2 * q - 1], above, *args)
     if len(rest) > 1:
         nu, npa, _, s_lon_e, s_lon_o, s_lev_e, s_lev_o = rest
         faces_kernel(nu, s_lon_e, s_lon_o, s_lev_e, s_lev_o)
@@ -241,8 +261,8 @@
     bulk_planes(u, pa, pb, lon_e, lon_o, lev_e, lev_o, d, f, plain_put(out), nothing, nothing)
 
 
-def last_bulk_kernel(u, pa, pb, lon_e, lon_o, lev_e, lev_o, d_in, f_in, after, end, d, f, total, sem):
-    del d_in, f_in, after
+def last_bulk_kernel(u, pa, pb, lon_e, lon_o, lev_e, lev_o, d_in, f_in, end, d, f, total, sem):
+    del d_in, f_in
     nj = u.shape[0]
 
     def copy_out(j, depth):
@@ -263,8 +283,8 @@
         copy_out(plane_at(depth, nj), depth).wait()
 
 
-def last_edge_kernel(u, pa, pb, lat, lon_e, lon_o, lev_e, lev_o, d, f, npa, npb, sums, total):
-    edge_b_kernel(u, pa, pb, lat, lon_e, lon_o, lev_e, lev_o, d, f, npb)
+def last_edge_kernel(u, pa, pb, lat_lo, lat_hi, lon_e, lon_o, lev_e, lev_o, d, f, npa, npb, sums, total):
+    edge_b_kernel(u, pa, pb, (lat_lo, lat_hi), lon_e, lon_o, lev_e, lev_o, d, f, npb)
     ni = sums.shape[0]
     q = ni // 4
     carry = zero_carry(u)
@@ -423,16 +443,19 @@
     d_edge, f_edge = in_vmem(d_edge), in_vmem(f_edge)
     d, f = in_hbm(scaled_diffusivity), in_hbm(scaled_forcing)
 
+    lat_a = (lat_a,)
     for step in range(STEPS):
-        last = step == STEPS - 1
-        u, pa, pb, lat_a, lat_b = map(in_vmem, (u, pa, pb, lat_a, lat_b))
+        next_is_last = step == STEPS - 2
+        u, pa, pb = map(in_vmem, (u, pa, pb))
+        lat_a = tuple(map(in_vmem, lat_a))
         lon, lev = tuple(map(in_vmem, lon)), tuple(map(in_vmem, lev))
-        n_pa = call(edge_a_kernel, V(half, nk, nm), VMEM, (VMEM,) * 8, flops=10**6)(
-            u, pa, pb, lat_a, *lev, d_edge, f_edge
-        )
-        if last:
+        parts = len(lat_a)
+        n_pa = call(
+            functools.partial(edge_a_kernel, parts), V(half, nk, nm), VMEM, (VMEM,) * (7 + parts), flops=10**6
+        )(u, pa, pb, *lat_a, *lev, d_edge, f_edge)
+        if step == STEPS - 1:
             break
-        lat_a = lax.ppermute(n_pa, "lat", swap)
+        lat_a = (lax.ppermute(n_pa[: half // 2] if next_is_last else n_pa, "lat", swap),)
         if step == 0:
             n_u, d, f = call(
                 first_bulk_kernel,
@@ -448,23 +471,29 @@
             )(u, pa, pb, *lon, *lev, in_vmem(d), in_vmem(f), n_pa)
         n_pb, *faces = call(
             edge_b_kernel, (V(half, nk, nm),) + faces_out, (VMEM,) * 5, (VMEM,) * 12, flops=10**6
-        )(u, pa, pb, lat_b, *lon, *lev, d_edge, f_edge, in_vmem(n_u), in_vmem(n_pa))
+        )(u, pa, pb, in_vmem(lat_b), *lon, *lev, d_edge, f_edge, in_vmem(n_u), in_vmem(n_pa))
         lon = lon_exchange(*faces[:2])
-        lat_b = lax.ppermute(n_pb, "lat", swap)
+        if next_is_last:
+            lat_a += (lax.ppermute(n_pa[half // 2 :], "lat", swap),)
+            lat_b = lax.ppermute(n_pb[: half // 2], "lat", swap)
+            final = n_pb[half // 2 :]
+        else:
+            lat_b = lax.ppermute(n_pb, "lat", swap)
         lev = lev_exchange(*faces[2:])
         u, pa, pb = n_u, n_pa, n_pb
 
     scale = 1.0 / (ni * lon_size)
     n = bits + 1
+    lat_c = lax.ppermute(final, "lat", swap)
     end, sums, _, total = call(
         last_bulk_kernel,
         (H(nj, ni, nk, nm), V(nj, ni, nk, nm), V(nj, ni, nk, nm), V(nj - 1, nk, nm)),
         (HBM, VMEM, VMEM, VMEM),
-        (VMEM,) * 9 + (ANY,),
+        (VMEM,) * 9,
         scratch=(pltpu.SemaphoreType.DMA((nj,)),),
         aliases={7: 1, 8: 2},
         flops=2 * 10**7,
-    )(u, pa, pb, *lon, *lev, in_vmem(d), in_vmem(f), n_pa)
+    )(u, pa, pb, *lon, *lev, in_vmem(d), in_vmem(f))
     other = partner(0, total)
     mine = call(half_kernel, V(nj - 1, nk // 2, nm), VMEM, (VMEM,) * 2, flops=10**5)(in_vmem(total), in_vmem(other))
     others = []
@@ -484,8 +513,8 @@
     )(*map(in_vmem, (sums, other, mine, back)))
     n_pa = in_vmem(n_pa)
     n_pb, edge_sums, edge_total = call(
-        last_edge_kernel, (V(half, nk, nm), V(ni, nk, nm), V(nk, nm)), (VMEM,) * 3, (VMEM,) * 11, flops=2 * 10**6
-    )(u, pa, pb, lat_b, *lon, *lev, d_edge, f_edge, n_pa)
+        last_edge_kernel, (V(half, nk, nm), V(ni, nk, nm), V(nk, nm)), (VMEM,) * 3, (VMEM,) * 12, flops=2 * 10**6
+    )(u, pa, pb, in_vmem(lat_b), in_vmem(lat_c), *lon, *lev, d_edge, f_edge, n_pa)
     others = []
     for bit in range(bits):
         others.append(partner(bit, edge_total))

time: 148 us -> 164 us (1.11)
  waiting for transfers between devices: 25.2 us -> 58.1 us
  starting transfers between devices: 88.3 us -> 70.7 us
    ppermute x16, waiting for transfers between devices: 14 us -> 32.3 us  [exchange(): return (lax.ppermute(e, axis, swaps(0)), lax.ppermute(o, axis, swaps(1)))]
    ppermute x16, starting transfers between devices: 62.6 us -> 46.6 us  [exchange(): return (lax.ppermute(e, axis, swaps(0)), lax.ppermute(o, axis, swaps(1)))]
    ppermute x6, waiting for transfers between devices: 11.2 us -> 25.8 us  [partner(): return lax.ppermute(total, 'lon', pairs)]
    ppermute x6, starting transfers between devices: 16.7 us -> 14.8 us  [partner(): return lax.ppermute(total, 'lon', pairs)]
    ppermute x3 -> x6, starting transfers between devices: 4.91 us -> 6.45 us  [the longest x3 4.07 us: per_device(): lax.ppermute(n_pa[:half // 2] if next_is_last else n_pa, 'lat', swap)]
  transfers between devices with their start and end apart: 31 -> 33, of which waited for: 9 -> 10; matrix products, arithmetic and copies ran while one was open for 0% -> 0% of each run, Pallas kernels for 21% -> 19%
where the time goes in v4:
time: 164 us; the launch traced here: 163 us
  starting transfers between devices  70.7 us (43%)
  waiting for transfers between devices  58.1 us (35%)
  Pallas kernels  32.1 us (20%)
    ppermute x16, starting transfers between devices, exchange(): return (lax.ppermute(e, axis, swaps(0)), lax.ppermute(o, axis, swaps(1)))  46.6 us
    ppermute x16, waiting for transfers between devices, exchange(): return (lax.ppermute(e, axis, swaps(0)), lax.ppermute(o, axis, swaps(1)))  32.3 us
    ppermute x6, waiting for transfers between devices, partner(): return lax.ppermute(total, 'lon', pairs)  25.8 us
    ppermute x6, starting transfers between devices, partner(): return lax.ppermute(total, 'lon', pairs)  14.8 us
    pallas_call x2, Pallas kernels, per_device(): call(bulk_kernel, V(nj, ni, nk, nm), VMEM, (VMEM,) * 9 + (ANY,), flops=2...  7.76 us
    pallas_call x1, Pallas kernels, per_device(): call(first_bulk_kernel, (V(nj, ni, nk, nm),) * 3, (VMEM,) * 3, (VMEM,) *...  5.85 us
    pallas_call x1, Pallas kernels, per_device(): call(last_bulk_kernel, (H(nj, ni, nk, nm), V(nj, ni, nk, nm), V(nj, ni, n...  5.23 us
    pallas_call x1, Pallas kernels, per_device(): call(load_kernel, (V(nj, ni, nk, nm), V(half, nk, nm), V(ni, nk, nm), V(n...  4.43 us
  transfers between devices with their start and end apart: 33, of which 10 were waited for; matrix products, arithmetic and copies ran while one was open for 0% of the time, Pallas kernels for 19%

profile of v4, /device:TPU:64, one launch (start us, length us, event | category | flops | bytes accessed | tf_op | source)
XLA Modules:
  0.0 163.2 jit_solution(4587537473051011261)
XLA Ops:
  0.6 1.1 dynamic-slice_bitcast_fusion.pa
  1.7 1.6 collective-permute-start.4
  3.3 4.4 %shard_map.50 = (f32[8,32,64,128]{3,2,1,0:T(8,128)S(1)}, f32[16,64,128]{2,1,0:T(8,128)S(1)}, f32[32,64,128]{2,1,0:T(8,128)S(1)}, f32[32,64,128]{2,1,0:T(8,128)S(...) custom-call(f32[8,32,64,128]{3,2,1,0:T(8,128)} %u_in.1, ...), custom_call_target="tpu_custom_call" | custom-call | flops 1000000 | tf_op jit(solution)/shard_map/pallas_call | solution.py:432
  7.7 0.6 collective-permute-start.5
  8.4 1.6 collective-permute-start.2
  9.9 0.7 collective-permute-start.1
  10.6 2.7 %collective-permute-done.2.rest_1_.lev_e = f32[8,32,128]{2,1,0:T(8,128)S(1)} collective-permute-done((f32[8,32,128]{2,1,0:T(8,128)S(1)}, f32[8,32,128]{2,1,0:T(8,128)S(1)}, u32[]{:S(2)}, u32[]{:S(2)}) %collective-permute-start.2) | collective-permute-done | bytes 131104 | tf_op jit(solution)/shard_map/ppermute | solution.py:413
  13.3 4.0 %collective-permute-start.3 = (f32[8,32,128]{2,1,0:T(8,128)S(1)}, f32[8,32,128]{2,1,0:T(8,128)S(1)}, u32[]{:S(2)}, u32[]{:S(2)}) collective-permute-start(f32[8,32,128]{2,1,0:T(8,128)S(1)} %get-tuple-element.41), channel_id=1, source_target_pairs={{1,2},{2,1},{3,4},{4,3},{5,6},{6,5},{9,10},{10,9},{11,12},{12,11},... | collective-permute-start | bytes 393224 | tf_op jit(solution)/shard_map/ppermute | solution.py:413
  17.3 7.2 %collective-permute-done.3.rest_2_.lev_o = f32[8,32,128]{2,1,0:T(8,128)S(1)} collective-permute-done((f32[8,32,128]{2,1,0:T(8,128)S(1)}, f32[8,32,128]{2,1,0:T(8,128)S(1)}, u32[]{:S(2)}, u32[]{:S(2)}) %collective-permute-start.3) | collective-permute-done | bytes 131104 | tf_op jit(solution)/shard_map/ppermute | solution.py:413
  24.5 0.0 collective-permute-done.4.rest_0_
  24.5 0.3 shard_map.51.after.rest_1_.pa
  24.8 2.1 %collective-permute-start.10 = (f32[16,64,128]{2,1,0:T(8,128)S(1)}, f32[16,64,128]{2,1,0:T(8,128)S(1)}, u32[]{:S(2)}, u32[]{:S(2)}) collective-permute-start(f32[16,64,128]{2,1,0:T(8,128)S(1)} %shard_map.51.after.rest_1_.pa), channel_id=1, source_target_pairs={{0,64},{64,0},{1,65},{65,1},{2,66},{66,2},{3,67},{67,3},{4,68},{68... | collective-permute-start | bytes 1572872 | tf_op jit(solution)/shard_map/ppermute | solution.py:458
  26.8 0.0 collective-permute-done.lon_e
  26.9 0.0 collective-permute-done.1.lon_o
  26.9 5.9 %shard_map.52 = (f32[8,32,64,128]{3,2,1,0:T(8,128)S(1)}, f32[8,32,64,128]{3,2,1,0:T(8,128)S(1)}, f32[8,32,64,128]{3,2,1,0:T(8,128)S(1)}) custom-call(f32[8,32,64,128]{3,2,1,0:T(8,128)S(1)} %get-tuple-element.36.u, f32[16,64,128]{2,1,0:T(8,128)S(1)} %dynamic-slice_bitcast_fusion.pa, f32[16,64,128]{2,1,0:T(8,128)S(1)} %get-tuple-element.37.pb, ...), custom_call_target="tpu_custom_call" | custom-call | flops 20000000 | tf_op jit(solution)/shard_map/pallas_call | solution.py:460
  32.7 0.0 copy-start
  32.7 0.0 collective-permute-done.5.lat
  32.7 0.5 shard_map.53
  33.3 0.1 collective-permute-start.11
  33.4 0.1 collective-permute-start.8
  33.5 9.9 %collective-permute-start.6 = (f32[8,64,128]{2,1,0:T(8,128)S(1)}, f32[8,64,128]{2,1,0:T(8,128)S(1)}, u32[]{:S(2)}, u32[]{:S(2)}) collective-permute-start(f32[8,64,128]{2,1,0:T(8,128)S(1)} %get-tuple-element.46), channel_id=1, source_target_pairs={{0,8},{8,0},{16,24},{24,16},{32,40},{40,32},{48,56},{56,48},{1,9},... | collective-permute-start | bytes 786440 | tf_op jit(solution)/shard_map/ppermute | solution.py:413
  43.4 0.7 collective-permute-start.7
  44.1 3.2 %collective-permute-start.9 = (f32[8,32,128]{2,1,0:T(8,128)S(1)}, f32[8,32,128]{2,1,0:T(8,128)S(1)}, u32[]{:S(2)}, u32[]{:S(2)}) collective-permute-start(f32[8,32,128]{2,1,0:T(8,128)S(1)} %get-tuple-element.49), channel_id=1, source_target_pairs={{1,2},{2,1},{3,4},{4,3},{5,6},{6,5},{9,10},{10,9},{11,12},{12,11},... | collective-permute-start | bytes 393224 | tf_op jit(solution)/shard_map/ppermute | solution.py:413
  47.3 7.3 %collective-permute-done.9.rest_2_.lev_o = f32[8,32,128]{2,1,0:T(8,128)S(1)} collective-permute-done((f32[8,32,128]{2,1,0:T(8,128)S(1)}, f32[8,32,128]{2,1,0:T(8,128)S(1)}, u32[]{:S(2)}, u32[]{:S(2)}) %collective-permute-start.9) | collective-permute-done | bytes 131104 | tf_op jit(solution)/shard_map/ppermute | solution.py:413
  54.5 0.3 shard_map.54.after.rest_1_.pa
  54.8 1.7 %collective-permute-start.16 = (f32[16,64,128]{2,1,0:T(8,128)S(1)}, f32[16,64,128]{2,1,0:T(8,128)S(1)}, u32[]{:S(2)}, u32[]{:S(2)}) collective-permute-start(f32[16,64,128]{2,1,0:T(8,128)S(1)} %shard_map.54.after.rest_1_.pa), channel_id=1, source_target_pairs={{0,64},{64,0},{1,65},{65,1},{2,66},{66,2},{3,67},{67,3},{4,68},{68... | collective-permute-start | bytes 1572872 | tf_op jit(solution)/shard_map/ppermute | solution.py:458
  56.6 0.0 collective-permute-done.6.lon_e
  56.6 3.9 %shard_map.55.rest_0_.u = f32[8,32,64,128]{3,2,1,0:T(8,128)S(1)} custom-call(f32[8,32,64,128]{3,2,1,0:T(8,128)S(1)} %get-tuple-element.44.rest_0_.u, f32[16,64,128]{2,1,0:T(8,128)S(1)} %shard_map.51.after.rest_1_.pa, f32[16,64,128]{2,1,0:T(8,128)S(1)} %get-tuple-element.45.pb, f32[8,64,128]{2,1,0:T(8,128)S(1)} %collective-permute-done.6.lon_e, ...), custom_call_target="tpu_custom_call" | custom-call | flops 20000000 | tf_op jit(solution)/shard_map/pallas_call | solution.py:469
  60.5 0.5 shard_map.56
  61.0 0.0 copy-start.1
  61.0 0.5 collective-permute-start.17
  61.5 7.1 %collective-permute-start.12 = (f32[8,64,128]{2,1,0:T(8,128)S(1)}, f32[8,64,128]{2,1,0:T(8,128)S(1)}, u32[]{:S(2)}, u32[]{:S(2)}) collective-permute-start(f32[8,64,128]{2,1,0:T(8,128)S(1)} %get-tuple-element.53), channel_id=1, source_target_pairs={{0,8},{8,0},{16,24},{24,16},{32,40},{40,32},{48,56},{56,48},{1,9},... | collective-permute-start | bytes 786440 | tf_op jit(solution)/shard_map/ppermute | solution.py:413
  68.5 0.7 collective-permute-start.13
  69.2 2.9 %collective-permute-start.15 = (f32[8,32,128]{2,1,0:T(8,128)S(1)}, f32[8,32,128]{2,1,0:T(8,128)S(1)}, u32[]{:S(2)}, u32[]{:S(2)}) collective-permute-start(f32[8,32,128]{2,1,0:T(8,128)S(1)} %get-tuple-element.56), channel_id=1, source_target_pairs={{1,2},{2,1},{3,4},{4,3},{5,6},{6,5},{9,10},{10,9},{11,12},{12,11},... | collective-permute-start | bytes 393224 | tf_op jit(solution)/shard_map/ppermute | solution.py:413
  72.1 7.6 %collective-permute-done.15.rest_2_.lev_o = f32[8,32,128]{2,1,0:T(8,128)S(1)} collective-permute-done((f32[8,32,128]{2,1,0:T(8,128)S(1)}, f32[8,32,128]{2,1,0:T(8,128)S(1)}, u32[]{:S(2)}, u32[]{:S(2)}) %collective-permute-start.15) | collective-permute-done | bytes 131104 | tf_op jit(solution)/shard_map/ppermute | solution.py:413
  79.7 0.3 shard_map.57.after.rest_1_.pa
  80.0 3.9 %shard_map.58.rest_0_.u = f32[8,32,64,128]{3,2,1,0:T(8,128)S(1)} custom-call(f32[8,32,64,128]{3,2,1,0:T(8,128)S(1)} %shard_map.55.rest_0_.u, f32[16,64,128]{2,1,0:T(8,128)S(1)} %shard_map.54.after.rest_1_.pa, f32[16,64,128]{2,1,0:T(8,128)S(1)} %get-tuple-element.52.pb, f32[8,64,128]{2,1,0:T(8,128)S(1)} %collective-permute-done.12.lon_e, ...), custom_call_target="tpu_custom_call" | custom-call | flops 20000000 | tf_op jit(solution)/shard_map/pallas_call | solution.py:469
  83.9 0.5 shard_map.59
  84.5 11.3 %collective-permute-start.20 = (f32[8,64,128]{2,1,0:T(8,128)S(1)}, f32[8,64,128]{2,1,0:T(8,128)S(1)}, u32[]{:S(2)}, u32[]{:S(2)}) collective-permute-start(f32[8,64,128]{2,1,0:T(8,128)S(1)} %get-tuple-element.58), channel_id=1, source_target_pairs={{0,8},{8,0},{16,24},{24,16},{32,40},{40,32},{48,56},{56,48},{1,9},... | collective-permute-start | bytes 786440 | tf_op jit(solution)/shard_map/ppermute | solution.py:413
  95.7 0.7 collective-permute-start.21
  96.4 1.0 collective-permute-start.22
  97.4 3.1 %collective-permute-start.23 = (f32[8,32,128]{2,1,0:T(8,128)S(1)}, f32[8,32,128]{2,1,0:T(8,128)S(1)}, u32[]{:S(2)}, u32[]{:S(2)}) collective-permute-start(f32[8,32,128]{2,1,0:T(8,128)S(1)} %get-tuple-element.61), channel_id=1, source_target_pairs={{1,2},{2,1},{3,4},{4,3},{5,6},{6,5},{9,10},{10,9},{11,12},{12,11},... | collective-permute-start | bytes 393224 | tf_op jit(solution)/shard_map/ppermute | solution.py:413
  100.5 0.2 collective-permute-start.24
  100.7 0.7 collective-permute-done.22.rest_2_.lev_e
  101.5 6.8 %collective-permute-done.23.rest_3_.lev_o = f32[8,32,128]{2,1,0:T(8,128)S(1)} collective-permute-done((f32[8,32,128]{2,1,0:T(8,128)S(1)}, f32[8,32,128]{2,1,0:T(8,128)S(1)}, u32[]{:S(2)}, u32[]{:S(2)}) %collective-permute-start.23) | collective-permute-done | bytes 131104 | tf_op jit(solution)/shard_map/ppermute | solution.py:413
  108.2 5.2 %shard_map.62 = (f32[8,32,64,128]{3,2,1,0:T(8,128)}, f32[8,32,64,128]{3,2,1,0:T(8,128)S(1)}, f32[8,32,64,128]{3,2,1,0:T(8,128)S(1)}, f32[7,64,128]{2,1,0:T(8,128)S(1)}) custom-call(f32[8,32,64,128]{3,2,1,0:T(8,128)S(1)} %shard_map.58.rest_0_.u, f32[16,64,128]{2,1,0:T(8,128)S(1)} %shard_map.57.after.rest_1_.pa, ...), custom_call_target="tpu_custom_call", output_to_operand_aliasing={{1}: (7, {}), {2}: (8, {})} | custom-call | flops 20000000 | tf_op jit(solution)/shard_map/pallas_call | solution.py:488
  113.5 1.5 collective-permute-start.29
  115.0 0.3 collective-permute-start.25
  115.3 2.0 %collective-permute-start.18 = (f32[8,64,128]{2,1,0:T(8,128)S(1)}, f32[8,64,128]{2,1,0:T(8,128)S(1)}, u32[]{:S(2)}, u32[]{:S(2)}) collective-permute-start(f32[8,64,128]{2,1,0:T(8,128)S(1)} %get-tuple-element.73), channel_id=1, source_target_pairs={{0,64},{64,0},{1,65},{65,1},{2,66},{66,2},{3,67},{67,3},{4,68},{68... | collective-permute-start | bytes 786440 | tf_op jit(solution)/shard_map/ppermute | solution.py:478
  117.3 0.1 collective-permute-start.19
  117.4 4.8 %collective-permute-start.30 = (f32[7,32,128]{2,1,0:T(8,128)S(1)}, f32[7,32,128]{2,1,0:T(8,128)S(1)}, u32[]{:S(2)}, u32[]{:S(2)}) collective-permute-start(f32[7,32,128]{2,1,0:T(8,128)S(1)} %shard_map.63), channel_id=1, source_target_pairs={{0,16},{8,24},{16,0},{24,8},{32,48},{40,56},{48,32},{56,40},{1,17}... | collective-permute-start | bytes 344072 | tf_op jit(solution)/shard_map/ppermute | solution.py:425
  122.1 18.1 %collective-permute-done.30.refs_0_ = f32[7,32,128]{2,1,0:T(8,128)S(1)} collective-permute-done((f32[7,32,128]{2,1,0:T(8,128)S(1)}, f32[7,32,128]{2,1,0:T(8,128)S(1)}, u32[]{:S(2)}, u32[]{:S(2)}) %collective-permute-start.30) | collective-permute-done | bytes 114720 | tf_op jit(solution)/shard_map/ppermute | solution.py:425
  140.3 2.7 %collective-permute-start.31 = (f32[7,32,128]{2,1,0:T(8,128)S(1)}, f32[7,32,128]{2,1,0:T(8,128)S(1)}, u32[]{:S(2)}, u32[]{:S(2)}) collective-permute-start(f32[7,32,128]{2,1,0:T(8,128)S(1)} %add.12), channel_id=1, source_target_pairs={{0,32},{8,40},{16,48},{24,56},{1,33},{9,41},{17,49},{25,57},{2,34}... | collective-permute-start | bytes 344072 | tf_op jit(solution)/shard_map/ppermute | solution.py:425
  143.0 2.3 %collective-permute-done.31.refs_1_ = f32[7,32,128]{2,1,0:T(8,128)S(1)} collective-permute-done((f32[7,32,128]{2,1,0:T(8,128)S(1)}, f32[7,32,128]{2,1,0:T(8,128)S(1)}, u32[]{:S(2)}, u32[]{:S(2)}) %collective-permute-start.31) | collective-permute-done | bytes 114720 | tf_op jit(solution)/shard_map/ppermute | solution.py:425
  145.4 0.1 collective-permute-start.32
  145.5 0.3 shard_map.60.npa
  145.8 0.4 shard_map.61
  146.1 0.6 collective-permute-start.26
  146.7 0.9 collective-permute-done.26.rest_0_
  147.5 1.0 collective-permute-start.27
  148.5 4.4 %collective-permute-done.27.rest_1_ = f32[64,128]{1,0:T(8,128)S(1)} collective-permute-done((f32[64,128]{1,0:T(8,128)S(1)}, f32[64,128]{1,0:T(8,128)S(1)}, u32[]{:S(2)}, u32[]{:S(2)}) %collective-permute-start.27) | collective-permute-done | bytes 32800 | tf_op jit(solution)/shard_map/ppermute | solution.py:425
  153.0 4.3 %collective-permute-start.28 = (f32[64,128]{1,0:T(8,128)S(1)}, f32[64,128]{1,0:T(8,128)S(1)}, u32[]{:S(2)}, u32[]{:S(2)}) collective-permute-start(f32[64,128]{1,0:T(8,128)S(1)} %add.11), channel_id=1, source_target_pairs={{0,32},{8,40},{16,48},{24,56},{1,33},{9,41},{17,49},{25,57},{2,34}... | collective-permute-start | bytes 98312 | tf_op jit(solution)/shard_map/ppermute | solution.py:425
  157.3 4.4 %shard_map.65.rest_4_ = f32[8,32,64,128]{3,2,1,0:T(8,128)} custom-call(f32[8,32,64,128]{3,2,1,0:T(8,128)S(1)} %get-tuple-element.66.sums, f32[7,64,128]{2,1,0:T(8,128)S(1)} %collective-permute-done.29.other, f32[7,32,128]{2,1,0:T(8,128)S(1)} %shard_map.64.mine, f32[7,32,128]{2,1,0:T(8,128)S(1)} %collective-permute-done.32.partners), custom_call_target="tpu_custom_call" | custom-call | flops 1000000 | tf_op jit(solution)/shard_map/pallas_call | solution.py:505
  161.7 1.4 shard_map.66
  (29 shorter events, 0.2 us)
Async XLA Ops:
  1.7 22.8 %collective-permute-start.4 = (f32[16,64,128]{2,1,0:T(8,128)S(1)}, f32[16,64,128]{2,1,0:T(8,128)S(1)}, u32[]{:S(2)}, u32[]{:S(2)}) collective-permute-start(f32[16,64,128]{2,1,0:T(8,128)S(1)} %dynamic-slice_bitcast_fusion.pa), channel_id=1, source_target_pairs={{0,64},{64,0},{1,65},{65,1},{2,66},{66,2},{3,67},{67,3},{4,68},{68... | collective-permute-start | bytes 1572872 | tf_op jit(solution)/shard_map/ppermute | solution.py:431
  7.7 25.0 %collective-permute-start.5 = (f32[16,64,128]{2,1,0:T(8,128)S(1)}, f32[16,64,128]{2,1,0:T(8,128)S(1)}, u32[]{:S(2)}, u32[]{:S(2)}) collective-permute-start(f32[16,64,128]{2,1,0:T(8,128)S(1)} %get-tuple-element.37.pb), channel_id=1, source_target_pairs={{0,64},{64,0},{1,65},{65,1},{2,66},{66,2},{3,67},{67,3},{4,68},{68... | collective-permute-start | bytes 1572872 | tf_op jit(solution)/shard_map/ppermute | solution.py:442
  8.4 5.0 %collective-permute-start.2 = (f32[8,32,128]{2,1,0:T(8,128)S(1)}, f32[8,32,128]{2,1,0:T(8,128)S(1)}, u32[]{:S(2)}, u32[]{:S(2)}) collective-permute-start(f32[8,32,128]{2,1,0:T(8,128)S(1)} %get-tuple-element.40), channel_id=1, source_target_pairs={{0,1},{1,0},{2,3},{3,2},{4,5},{5,4},{6,7},{7,6},{8,9},{9,8},{10,11... | collective-permute-start | bytes 393224 | tf_op jit(solution)/shard_map/ppermute | solution.py:413
  9.9 16.9 %collective-permute-start = (f32[8,64,128]{2,1,0:T(8,128)S(1)}, f32[8,64,128]{2,1,0:T(8,128)S(1)}, u32[]{:S(2)}, u32[]{:S(2)}) collective-permute-start(f32[8,64,128]{2,1,0:T(8,128)S(1)} %get-tuple-element.38), channel_id=1, source_target_pairs={{0,8},{8,0},{16,24},{24,16},{32,40},{40,32},{48,56},{56,48},{1,9},... | collective-permute-start | bytes 786440 | tf_op jit(solution)/shard_map/ppermute | solution.py:413
  9.9 16.9 %collective-permute-start.1 = (f32[8,64,128]{2,1,0:T(8,128)S(1)}, f32[8,64,128]{2,1,0:T(8,128)S(1)}, u32[]{:S(2)}, u32[]{:S(2)}) collective-permute-start(f32[8,64,128]{2,1,0:T(8,128)S(1)} %get-tuple-element.39), channel_id=1, source_target_pairs={{8,16},{16,8},{24,32},{32,24},{40,48},{48,40},{9,17},{17,9},{25,33... | collective-permute-start | bytes 786440 | tf_op jit(solution)/shard_map/ppermute | solution.py:413
  13.3 11.2 %collective-permute-start.3 = (f32[8,32,128]{2,1,0:T(8,128)S(1)}, f32[8,32,128]{2,1,0:T(8,128)S(1)}, u32[]{:S(2)}, u32[]{:S(2)}) collective-permute-start(f32[8,32,128]{2,1,0:T(8,128)S(1)} %get-tuple-element.41), channel_id=1, source_target_pairs={{1,2},{2,1},{3,4},{4,3},{5,6},{6,5},{9,10},{10,9},{11,12},{12,11},... | collective-permute-start | bytes 393224 | tf_op jit(solution)/shard_map/ppermute | solution.py:413
  24.8 29.8 %collective-permute-start.10 = (f32[16,64,128]{2,1,0:T(8,128)S(1)}, f32[16,64,128]{2,1,0:T(8,128)S(1)}, u32[]{:S(2)}, u32[]{:S(2)}) collective-permute-start(f32[16,64,128]{2,1,0:T(8,128)S(1)} %shard_map.51.after.rest_1_.pa), channel_id=1, source_target_pairs={{0,64},{64,0},{1,65},{65,1},{2,66},{66,2},{3,67},{67,3},{4,68},{68... | collective-permute-start | bytes 1572872 | tf_op jit(solution)/shard_map/ppermute | solution.py:458
  32.7 23.8 %copy-start = (f32[8,32,64,128]{3,2,1,0:T(8,128)}, f32[8,32,64,128]{3,2,1,0:T(8,128)S(1)}, u32[]{:S(2)}) copy-start(f32[8,32,64,128]{3,2,1,0:T(8,128)S(1)} %get-tuple-element.51.f.f_in) | copy-start | bytes 25165828
  33.3 27.2 %collective-permute-start.11 = (f32[16,64,128]{2,1,0:T(8,128)S(1)}, f32[16,64,128]{2,1,0:T(8,128)S(1)}, u32[]{:S(2)}, u32[]{:S(2)}) collective-permute-start(f32[16,64,128]{2,1,0:T(8,128)S(1)} %get-tuple-element.45.pb), channel_id=1, source_target_pairs={{0,64},{64,0},{1,65},{65,1},{2,66},{66,2},{3,67},{67,3},{4,68},{68... | collective-permute-start | bytes 1572872 | tf_op jit(solution)/shard_map/ppermute | solution.py:481
  33.4 10.6 %collective-permute-start.8 = (f32[8,32,128]{2,1,0:T(8,128)S(1)}, f32[8,32,128]{2,1,0:T(8,128)S(1)}, u32[]{:S(2)}, u32[]{:S(2)}) collective-permute-start(f32[8,32,128]{2,1,0:T(8,128)S(1)} %get-tuple-element.48), channel_id=1, source_target_pairs={{0,1},{1,0},{2,3},{3,2},{4,5},{5,4},{6,7},{7,6},{8,9},{9,8},{10,11... | collective-permute-start | bytes 393224 | tf_op jit(solution)/shard_map/ppermute | solution.py:413
  33.5 23.1 %collective-permute-start.6 = (f32[8,64,128]{2,1,0:T(8,128)S(1)}, f32[8,64,128]{2,1,0:T(8,128)S(1)}, u32[]{:S(2)}, u32[]{:S(2)}) collective-permute-start(f32[8,64,128]{2,1,0:T(8,128)S(1)} %get-tuple-element.46), channel_id=1, source_target_pairs={{0,8},{8,0},{16,24},{24,16},{32,40},{40,32},{48,56},{56,48},{1,9},... | collective-permute-start | bytes 786440 | tf_op jit(solution)/shard_map/ppermute | solution.py:413
  43.4 13.2 %collective-permute-start.7 = (f32[8,64,128]{2,1,0:T(8,128)S(1)}, f32[8,64,128]{2,1,0:T(8,128)S(1)}, u32[]{:S(2)}, u32[]{:S(2)}) collective-permute-start(f32[8,64,128]{2,1,0:T(8,128)S(1)} %get-tuple-element.47), channel_id=1, source_target_pairs={{8,16},{16,8},{24,32},{32,24},{40,48},{48,40},{9,17},{17,9},{25,33... | collective-permute-start | bytes 786440 | tf_op jit(solution)/shard_map/ppermute | solution.py:413
  44.1 10.5 %collective-permute-start.9 = (f32[8,32,128]{2,1,0:T(8,128)S(1)}, f32[8,32,128]{2,1,0:T(8,128)S(1)}, u32[]{:S(2)}, u32[]{:S(2)}) collective-permute-start(f32[8,32,128]{2,1,0:T(8,128)S(1)} %get-tuple-element.49), channel_id=1, source_target_pairs={{1,2},{2,1},{3,4},{4,3},{5,6},{6,5},{9,10},{10,9},{11,12},{12,11},... | collective-permute-start | bytes 393224 | tf_op jit(solution)/shard_map/ppermute | solution.py:413
  54.8 24.9 %collective-permute-start.16 = (f32[16,64,128]{2,1,0:T(8,128)S(1)}, f32[16,64,128]{2,1,0:T(8,128)S(1)}, u32[]{:S(2)}, u32[]{:S(2)}) collective-permute-start(f32[16,64,128]{2,1,0:T(8,128)S(1)} %shard_map.54.after.rest_1_.pa), channel_id=1, source_target_pairs={{0,64},{64,0},{1,65},{65,1},{2,66},{66,2},{3,67},{67,3},{4,68},{68... | collective-permute-start | bytes 1572872 | tf_op jit(solution)/shard_map/ppermute | solution.py:458
  61.0 19.0 %copy-start.1 = (f32[8,32,64,128]{3,2,1,0:T(8,128)S(1)}, f32[8,32,64,128]{3,2,1,0:T(8,128)}, u32[]{:S(2)}) copy-start(f32[8,32,64,128]{3,2,1,0:T(8,128)} %copy-done) | copy-start | bytes 25165828
  61.0 22.9 %collective-permute-start.17 = (f32[16,64,128]{2,1,0:T(8,128)S(1)}, f32[16,64,128]{2,1,0:T(8,128)S(1)}, u32[]{:S(2)}, u32[]{:S(2)}) collective-permute-start(f32[16,64,128]{2,1,0:T(8,128)S(1)} %get-tuple-element.52.pb), channel_id=1, source_target_pairs={{0,64},{64,0},{1,65},{65,1},{2,66},{66,2},{3,67},{67,3},{4,68},{68... | collective-permute-start | bytes 1572872 | tf_op jit(solution)/shard_map/ppermute | solution.py:481
  61.5 7.7 %collective-permute-start.14 = (f32[8,32,128]{2,1,0:T(8,128)S(1)}, f32[8,32,128]{2,1,0:T(8,128)S(1)}, u32[]{:S(2)}, u32[]{:S(2)}) collective-permute-start(f32[8,32,128]{2,1,0:T(8,128)S(1)} %get-tuple-element.55), channel_id=1, source_target_pairs={{0,1},{1,0},{2,3},{3,2},{4,5},{5,4},{6,7},{7,6},{8,9},{9,8},{10,11... | collective-permute-start | bytes 393224 | tf_op jit(solution)/shard_map/ppermute | solution.py:413
  61.5 18.5 %collective-permute-start.12 = (f32[8,64,128]{2,1,0:T(8,128)S(1)}, f32[8,64,128]{2,1,0:T(8,128)S(1)}, u32[]{:S(2)}, u32[]{:S(2)}) collective-permute-start(f32[8,64,128]{2,1,0:T(8,128)S(1)} %get-tuple-element.53), channel_id=1, source_target_pairs={{0,8},{8,0},{16,24},{24,16},{32,40},{40,32},{48,56},{56,48},{1,9},... | collective-permute-start | bytes 786440 | tf_op jit(solution)/shard_map/ppermute | solution.py:413
  68.5 11.4 %collective-permute-start.13 = (f32[8,64,128]{2,1,0:T(8,128)S(1)}, f32[8,64,128]{2,1,0:T(8,128)S(1)}, u32[]{:S(2)}, u32[]{:S(2)}) collective-permute-start(f32[8,64,128]{2,1,0:T(8,128)S(1)} %get-tuple-element.54), channel_id=1, source_target_pairs={{8,16},{16,8},{24,32},{32,24},{40,48},{48,40},{9,17},{17,9},{25,33... | collective-permute-start | bytes 786440 | tf_op jit(solution)/shard_map/ppermute | solution.py:413
  69.2 10.5 %collective-permute-start.15 = (f32[8,32,128]{2,1,0:T(8,128)S(1)}, f32[8,32,128]{2,1,0:T(8,128)S(1)}, u32[]{:S(2)}, u32[]{:S(2)}) collective-permute-start(f32[8,32,128]{2,1,0:T(8,128)S(1)} %get-tuple-element.56), channel_id=1, source_target_pairs={{1,2},{2,1},{3,4},{4,3},{5,6},{6,5},{9,10},{10,9},{11,12},{12,11},... | collective-permute-start | bytes 393224 | tf_op jit(solution)/shard_map/ppermute | solution.py:413
  84.5 23.8 %collective-permute-start.20 = (f32[8,64,128]{2,1,0:T(8,128)S(1)}, f32[8,64,128]{2,1,0:T(8,128)S(1)}, u32[]{:S(2)}, u32[]{:S(2)}) collective-permute-start(f32[8,64,128]{2,1,0:T(8,128)S(1)} %get-tuple-element.58), channel_id=1, source_target_pairs={{0,8},{8,0},{16,24},{24,16},{32,40},{40,32},{48,56},{56,48},{1,9},... | collective-permute-start | bytes 786440 | tf_op jit(solution)/shard_map/ppermute | solution.py:413
  95.7 12.5 %collective-permute-start.21 = (f32[8,64,128]{2,1,0:T(8,128)S(1)}, f32[8,64,128]{2,1,0:T(8,128)S(1)}, u32[]{:S(2)}, u32[]{:S(2)}) collective-permute-start(f32[8,64,128]{2,1,0:T(8,128)S(1)} %get-tuple-element.59), channel_id=1, source_target_pairs={{8,16},{16,8},{24,32},{32,24},{40,48},{48,40},{9,17},{17,9},{25,33... | collective-permute-start | bytes 786440 | tf_op jit(solution)/shard_map/ppermute | solution.py:413
  96.4 5.0 %collective-permute-start.22 = (f32[8,32,128]{2,1,0:T(8,128)S(1)}, f32[8,32,128]{2,1,0:T(8,128)S(1)}, u32[]{:S(2)}, u32[]{:S(2)}) collective-permute-start(f32[8,32,128]{2,1,0:T(8,128)S(1)} %get-tuple-element.60), channel_id=1, source_target_pairs={{0,1},{1,0},{2,3},{3,2},{4,5},{5,4},{6,7},{7,6},{8,9},{9,8},{10,11... | collective-permute-start | bytes 393224 | tf_op jit(solution)/shard_map/ppermute | solution.py:413
  97.4 10.9 %collective-permute-start.23 = (f32[8,32,128]{2,1,0:T(8,128)S(1)}, f32[8,32,128]{2,1,0:T(8,128)S(1)}, u32[]{:S(2)}, u32[]{:S(2)}) collective-permute-start(f32[8,32,128]{2,1,0:T(8,128)S(1)} %get-tuple-element.61), channel_id=1, source_target_pairs={{1,2},{2,1},{3,4},{4,3},{5,6},{6,5},{9,10},{10,9},{11,12},{12,11},... | collective-permute-start | bytes 393224 | tf_op jit(solution)/shard_map/ppermute | solution.py:413
  100.5 45.0 %collective-permute-start.24 = (f32[8,64,128]{2,1,0:T(8,128)S(1)}, f32[8,64,128]{2,1,0:T(8,128)S(1)}, u32[]{:S(2)}, u32[]{:S(2)}) collective-permute-start(f32[8,64,128]{2,1,0:T(8,128)S(1)} %get-tuple-element.71), channel_id=1, source_target_pairs={{0,64},{64,0},{1,65},{65,1},{2,66},{66,2},{3,67},{67,3},{4,68},{68... | collective-permute-start | bytes 786440 | tf_op jit(solution)/shard_map/ppermute | solution.py:458
  113.5 3.9 %collective-permute-start.29 = (f32[7,64,128]{2,1,0:T(8,128)S(1)}, f32[7,64,128]{2,1,0:T(8,128)S(1)}, u32[]{:S(2)}, u32[]{:S(2)}) collective-permute-start(f32[7,64,128]{2,1,0:T(8,128)S(1)} %get-tuple-element.67.total), channel_id=1, source_target_pairs={{0,8},{8,0},{16,24},{24,16},{32,40},{40,32},{48,56},{56,48},{1,9},... | collective-permute-start | bytes 688136 | tf_op jit(solution)/shard_map/ppermute | solution.py:425
  115.0 30.5 %collective-permute-start.25 = (f32[8,64,128]{2,1,0:T(8,128)S(1)}, f32[8,64,128]{2,1,0:T(8,128)S(1)}, u32[]{:S(2)}, u32[]{:S(2)}) collective-permute-start(f32[8,64,128]{2,1,0:T(8,128)S(1)} %get-tuple-element.70), channel_id=1, source_target_pairs={{0,64},{64,0},{1,65},{65,1},{2,66},{66,2},{3,67},{67,3},{4,68},{68... | collective-permute-start | bytes 786440 | tf_op jit(solution)/shard_map/ppermute | solution.py:477
  115.3 30.4 %collective-permute-start.18 = (f32[8,64,128]{2,1,0:T(8,128)S(1)}, f32[8,64,128]{2,1,0:T(8,128)S(1)}, u32[]{:S(2)}, u32[]{:S(2)}) collective-permute-start(f32[8,64,128]{2,1,0:T(8,128)S(1)} %get-tuple-element.73), channel_id=1, source_target_pairs={{0,64},{64,0},{1,65},{65,1},{2,66},{66,2},{3,67},{67,3},{4,68},{68... | collective-permute-start | bytes 786440 | tf_op jit(solution)/shard_map/ppermute | solution.py:478
  117.3 28.5 %collective-permute-start.19 = (f32[8,64,128]{2,1,0:T(8,128)S(1)}, f32[8,64,128]{2,1,0:T(8,128)S(1)}, u32[]{:S(2)}, u32[]{:S(2)}) collective-permute-start(f32[8,64,128]{2,1,0:T(8,128)S(1)} %get-tuple-element.72), channel_id=1, source_target_pairs={{0,64},{64,0},{1,65},{65,1},{2,66},{66,2},{3,67},{67,3},{4,68},{68... | collective-permute-start | bytes 786440 | tf_op jit(solution)/shard_map/ppermute | solution.py:487
  117.4 22.9 %collective-permute-start.30 = (f32[7,32,128]{2,1,0:T(8,128)S(1)}, f32[7,32,128]{2,1,0:T(8,128)S(1)}, u32[]{:S(2)}, u32[]{:S(2)}) collective-permute-start(f32[7,32,128]{2,1,0:T(8,128)S(1)} %shard_map.63), channel_id=1, source_target_pairs={{0,16},{8,24},{16,0},{24,8},{32,48},{40,56},{48,32},{56,40},{1,17}... | collective-permute-start | bytes 344072 | tf_op jit(solution)/shard_map/ppermute | solution.py:425
  140.3 5.0 %collective-permute-start.31 = (f32[7,32,128]{2,1,0:T(8,128)S(1)}, f32[7,32,128]{2,1,0:T(8,128)S(1)}, u32[]{:S(2)}, u32[]{:S(2)}) collective-permute-start(f32[7,32,128]{2,1,0:T(8,128)S(1)} %add.12), channel_id=1, source_target_pairs={{0,32},{8,40},{16,48},{24,56},{1,33},{9,41},{17,49},{25,57},{2,34}... | collective-permute-start | bytes 344072 | tf_op jit(solution)/shard_map/ppermute | solution.py:425
  145.4 11.9 %collective-permute-start.32 = (f32[7,32,128]{2,1,0:T(8,128)S(1)}, f32[7,32,128]{2,1,0:T(8,128)S(1)}, u32[]{:S(2)}, u32[]{:S(2)}) collective-permute-start(f32[7,32,128]{2,1,0:T(8,128)S(1)} %shard_map.64.mine), channel_id=1, source_target_pairs={{0,8},{8,0},{16,24},{24,16},{32,40},{40,32},{48,56},{56,48},{1,9},... | collective-permute-start | bytes 344072 | tf_op jit(solution)/shard_map/ppermute | solution.py:504
  146.1 1.4 collective-permute-start.26
  147.5 5.4 %collective-permute-start.27 = (f32[64,128]{1,0:T(8,128)S(1)}, f32[64,128]{1,0:T(8,128)S(1)}, u32[]{:S(2)}, u32[]{:S(2)}) collective-permute-start(f32[64,128]{1,0:T(8,128)S(1)} %add.10), channel_id=1, source_target_pairs={{0,16},{8,24},{16,0},{24,8},{32,48},{40,56},{48,32},{56,40},{1,17}... | collective-permute-start | bytes 98312 | tf_op jit(solution)/shard_map/ppermute | solution.py:425
  153.0 8.7 %collective-permute-start.28 = (f32[64,128]{1,0:T(8,128)S(1)}, f32[64,128]{1,0:T(8,128)S(1)}, u32[]{:S(2)}, u32[]{:S(2)}) collective-permute-start(f32[64,128]{1,0:T(8,128)S(1)} %add.11), channel_id=1, source_target_pairs={{0,32},{8,40},{16,48},{24,56},{1,33},{9,41},{17,49},{25,57},{2,34}... | collective-permute-start | bytes 98312 | tf_op jit(solution)/shard_map/ppermute | solution.py:425

commit v5 on v3

--- a/solution.py
+++ b/solution.py
@@ -279,11 +279,11 @@
     total[...] = carry
 
 
-def earlier(others, first=0):
+def earlier(others):
     lon = lax.axis_index("lon")
     before = 0.0
     for bit, other in enumerate(others):
-        before += jnp.where(lon & (1 << (first + bit)) != 0, other, 0.0)
+        before += jnp.where(lon & (1 << bit) != 0, other, 0.0)
     return before
 
 
@@ -294,71 +294,65 @@
         out[p] = total[p, at] + other[p, at]
 
 
-def before_kernel(*refs):
-    *others, out = refs
-    for p in range(out.shape[0]):
-        out[p] = earlier([other[p] for other in others], 1)
-
-
-def totals_kernel(scale, sums, other, mine, partners, out, stage, sem):
+def total_rows(scale, ni, sums, before, put):
+    def row(r, _):
+        for q in range(BLOCK):
+            i = r * BLOCK + q
+            put(i, (sums(i) + before) * scale)
+        return 0
+
+    lax.fori_loop(0, ni // BLOCK, row, 0)
+
+
+def half_totals(scale, upper_half, sums, other, before, out, stage, sem):
+    nj, ni, nk = sums.shape[:3]
+    n = nk // 2
+    at = pl.ds(pl.multiple_of(jnp.where(upper_half, n, 0), n), n)
+
+    def copy_out(depth):
+        return pltpu.make_async_copy(stage.at[depth - 1], out.at[plane_at(depth, nj), :, at, :], sem.at[depth - 1])
+
+    def body(depth, _):
+        j = plane_at(depth, nj)
+        b = before[depth - 1] + earlier([other[depth - 1, at]])
+
+        def put(i, value):
+            stage[depth - 1, i] = value
+
+        total_rows(scale, ni, lambda i: sums[j, i, at], b, put)
+        copy_out(depth).start()
+        return 0
+
+    lax.fori_loop(1, nj, body, 0)
+    return [copy_out(depth) for depth in range(1, nj)]
+
+
+def totals_kernel(scale, sums, other, before, after, out, stage, sem):
+    del after
+    for copy in half_totals(scale, odd("lon"), sums, other, before, out, stage, sem):
+        copy.wait()
+
+
+def last_totals_kernel(scale, sums, other, before, npa, npb, edge_sums, *rest):
+    *others, _, _, end, out, stage, edge_stage, sem, edge_sem = rest
     nj, ni = sums.shape[:2]
-
-    def copy_out(j, depth):
-        slot = depth % 2
-        return pltpu.make_async_copy(stage.at[slot], out.at[j], sem.at[slot])
-
-    def body(depth, _):
-        j, slot = plane_at(depth, nj), depth % 2
-
-        @pl.when(depth > 2)
-        def _():
-            copy_out(j, depth).wait()
-
-        a, b = mine[depth - 1], partners[depth - 1]
-        b = jnp.concatenate([jnp.where(odd("lon"), b, a), jnp.where(odd("lon"), a, b)], axis=0)
-        b += earlier([other[depth - 1]])
-
-        def row(r, _):
-            for q in range(BLOCK):
-                i = r * BLOCK + q
-                stage[slot, i] = (sums[j, i] + b) * scale
-            return 0
-
-        lax.fori_loop(0, ni // BLOCK, row, 0)
-        copy_out(j, depth).start()
-        return 0
-
-    lax.fori_loop(1, nj, body, 0)
-    copy_out(0, 0).wait()
-    copy_out(0, 1).wait()
-
-
-def last_totals_kernel(scale, sums, npa, npb, *rest):
-    *others, _, _, end, out, stage, sem = rest
-    ni = sums.shape[0]
-    nj = out.shape[0]
     q = ni // 4
     pj = plane_at(0, nj)
     copies = [
-        pltpu.make_async_copy(npb.at[pl.ds(0, q)], end.at[pj, pl.ds(0, q)], sem.at[0]),
-        pltpu.make_async_copy(npa, end.at[pj, pl.ds(q, 2 * q)], sem.at[1]),
-        pltpu.make_async_copy(npb.at[pl.ds(q, q)], end.at[pj, pl.ds(3 * q, q)], sem.at[2]),
+        pltpu.make_async_copy(npb.at[pl.ds(0, q)], end.at[pj, pl.ds(0, q)], edge_sem.at[0]),
+        pltpu.make_async_copy(npa, end.at[pj, pl.ds(q, 2 * q)], edge_sem.at[1]),
+        pltpu.make_async_copy(npb.at[pl.ds(q, q)], end.at[pj, pl.ds(3 * q, q)], edge_sem.at[2]),
+        pltpu.make_async_copy(edge_stage, out.at[pj], edge_sem.at[3]),
     ]
-    for copy in copies:
+    for copy in copies[:3]:
         copy.start()
-    b = earlier([other[...] for other in others])
-
-    def row(r, _):
-        for p in range(BLOCK):
-            i = r * BLOCK + p
-            stage[i] = (sums[i] + b) * scale
-        return 0
-
-    for half in range(2):
-        lax.fori_loop(half * ni // 2 // BLOCK, (half + 1) * ni // 2 // BLOCK, row, 0)
-        rows = pl.ds(half * ni // 2, ni // 2)
-        copies.append(pltpu.make_async_copy(stage.at[rows], out.at[pj, rows], sem.at[3 + half]))
-        copies[-1].start()
+    copies += half_totals(scale, jnp.logical_not(odd("lon")), sums, other, before, out, stage, sem)
+
+    def put(i, value):
+        edge_stage[i] = value
+
+    total_rows(scale, ni, lambda i: edge_sums[i], earlier([other[...] for other in others]), put)
+    copies[3].start()
     for copy in copies:
         copy.wait()
 
@@ -455,7 +449,6 @@
         u, pa, pb = n_u, n_pa, n_pb
 
     scale = 1.0 / (ni * lon_size)
-    n = bits + 1
     end, sums, _, total = call(
         last_bulk_kernel,
         (H(nj, ni, nk, nm), V(nj, ni, nk, nm), V(nj, ni, nk, nm), V(nj - 1, nk, nm)),
@@ -466,41 +459,52 @@
         flops=2 * 10**7,
     )(u, pa, pb, *lon, *lev, in_vmem(d), in_vmem(f), n_pa)
     other = partner(0, total)
-    mine = call(half_kernel, V(nj - 1, nk // 2, nm), VMEM, (VMEM,) * 2, flops=10**5)(in_vmem(total), in_vmem(other))
-    others = []
-    for bit in range(1, bits):
-        others.append(partner(bit, mine))
-        mine = mine + others[-1]
-    mine = call(before_kernel, V(nj - 1, nk // 2, nm), VMEM, (VMEM,) * (bits - 1), flops=10**5)(*map(in_vmem, others))
+    half_total = call(half_kernel, V(nj - 1, nk // 2, nm), VMEM, (VMEM,) * 2, flops=10**5)(
+        in_vmem(total), in_vmem(other)
+    )
+    pairs = lon_size // 2
+    mine = []
+    for steps in sorted(range(1, pairs), key=lambda steps: (steps % 2 == 0, steps)):
+        to = [(2 * a + c, 2 * (a ^ steps) + c) for a in range(pairs) if a < a ^ steps for c in (0, 1)]
+        mine.append(lax.ppermute(half_total, "lon", to))
+    mine = functools.reduce(jnp.add, mine)
     back = lax.ppermute(mine, "lon", [(i, i ^ 1) for i in range(lon_size)])
-    out = call(
-        functools.partial(totals_kernel, scale),
-        H(nj, ni, nk, nm),
-        HBM,
-        (VMEM,) * 4,
-        limit=4,
-        scratch=(V(2, ni, nk, nm), pltpu.SemaphoreType.DMA((2,))),
-        flops=10**6,
-    )(*map(in_vmem, (sums, other, mine, back)))
     n_pa = in_vmem(n_pa)
     n_pb, edge_sums, edge_total = call(
         last_edge_kernel, (V(half, nk, nm), V(ni, nk, nm), V(nk, nm)), (VMEM,) * 3, (VMEM,) * 11, flops=2 * 10**6
     )(u, pa, pb, lat_b, *lon, *lev, d_edge, f_edge, n_pa)
     others = []
+    edge_total_1 = edge_total
     for bit in range(bits):
         others.append(partner(bit, edge_total))
         edge_total = edge_total + others[-1]
     others = tuple(map(in_vmem, others))
+    sums, other = in_vmem(sums), in_vmem(other)
+    out = call(
+        functools.partial(totals_kernel, scale),
+        H(nj, ni, nk, nm),
+        HBM,
+        (VMEM,) * 3 + (ANY,),
+        limit=5,
+        scratch=(V(nj - 1, ni, nk // 2, nm), pltpu.SemaphoreType.DMA((nj - 1,))),
+        flops=10**6,
+    )(sums, other, in_vmem(mine), edge_total_1)
+    n = 6 + bits
     end, out = call(
         functools.partial(last_totals_kernel, scale),
         (H(nj, ni, nk, nm),) * 2,
         (HBM, HBM),
-        (VMEM,) * (n + 2) + (HBM, HBM),
-        scratch=(V(ni, nk, nm), pltpu.SemaphoreType.DMA((5,))),
-        limit=4,
-        aliases={n + 2: 0, n + 3: 1},
+        (VMEM,) * n + (HBM, HBM),
+        scratch=(
+            V(nj - 1, ni, nk // 2, nm),
+            V(ni, nk, nm),
+            pltpu.SemaphoreType.DMA((nj - 1,)),
+            pltpu.SemaphoreType.DMA((4,)),
+        ),
+        limit=6,
+        aliases={n: 0, n + 1: 1},
         flops=10**6,
-    )(in_vmem(edge_sums), n_pa, in_vmem(n_pb), *others, in_hbm(end), in_hbm(out))
+    )(sums, other, in_vmem(back), n_pa, in_vmem(n_pb), in_vmem(edge_sums), *others, in_hbm(end), in_hbm(out))
     return out, end
 
 

time: 148 us -> 151 us (1.020)
  the two profiles are of different devices: /device:TPU:64 before, /device:TPU:98 now
where the time goes in v5:
time: 151 us; the launch traced here: 150 us
  waiting for transfers between devices  63.6 us (42%)
  starting transfers between devices  52.8 us (35%)
  Pallas kernels  31.7 us (21%)
    ppermute x16, waiting for transfers between devices, exchange(): return (lax.ppermute(e, axis, swaps(0)), lax.ppermute(o, axis, swaps(1)))  44.9 us
    ppermute x16, starting transfers between devices, exchange(): return (lax.ppermute(e, axis, swaps(0)), lax.ppermute(o, axis, swaps(1)))  34.4 us
    ppermute x3, waiting for transfers between devices, per_device(): mine.append(lax.ppermute(half_total, 'lon', to))  11 us
    pallas_call x2, Pallas kernels, per_device(): call(bulk_kernel, V(nj, ni, nk, nm), VMEM, (VMEM,) * 9 + (ANY,), flops=2...  8.05 us
    ppermute x4, waiting for transfers between devices, partner(): return lax.ppermute(total, 'lon', pairs)  7.75 us
    ppermute x3, starting transfers between devices, per_device(): mine.append(lax.ppermute(half_total, 'lon', to))  6.15 us
    pallas_call x1, Pallas kernels, per_device(): call(first_bulk_kernel, (V(nj, ni, nk, nm),) * 3, (VMEM,) * 3, (VMEM,) *...  5.89 us
    pallas_call x1, Pallas kernels, per_device(): call(last_bulk_kernel, (H(nj, ni, nk, nm), V(nj, ni, nk, nm), V(nj, ni, n...  5.39 us
  transfers between devices with their start and end apart: 32, of which 12 were waited for; matrix products, arithmetic and copies ran while one was open for 0% of the time, Pallas kernels for 16%

profile of v5, /device:TPU:98, one launch (start us, length us, event | category | flops | bytes accessed | tf_op | source)
XLA Modules:
  0.0 150.1 jit_solution(12126819977461321674)
XLA Ops:
  0.6 1.1 dynamic-slice_bitcast_fusion.pa
  1.7 0.6 collective-permute-start.4
  2.3 4.4 %shard_map.50 = (f32[8,32,64,128]{3,2,1,0:T(8,128)S(1)}, f32[16,64,128]{2,1,0:T(8,128)S(1)}, f32[32,64,128]{2,1,0:T(8,128)S(1)}, f32[32,64,128]{2,1,0:T(8,128)S(...) custom-call(f32[8,32,64,128]{3,2,1,0:T(8,128)} %u_in.1, ...), custom_call_target="tpu_custom_call" | custom-call | flops 1000000 | tf_op jit(solution)/shard_map/pallas_call | solution.py:406
  6.8 1.6 %collective-permute-start.5 = (f32[16,64,128]{2,1,0:T(8,128)S(1)}, f32[16,64,128]{2,1,0:T(8,128)S(1)}, u32[]{:S(2)}, u32[]{:S(2)}) collective-permute-start(f32[16,64,128]{2,1,0:T(8,128)S(1)} %get-tuple-element.37.pb), channel_id=1, source_target_pairs={{0,64},{64,0},{1,65},{65,1},{2,66},{66,2},{3,67},{67,3},{4,68},{68... | collective-permute-start | bytes 1572872 | tf_op jit(solution)/shard_map/ppermute | solution.py:416
  8.4 1.6 %collective-permute-start.2 = (f32[8,32,128]{2,1,0:T(8,128)S(1)}, f32[8,32,128]{2,1,0:T(8,128)S(1)}, u32[]{:S(2)}, u32[]{:S(2)}) collective-permute-start(f32[8,32,128]{2,1,0:T(8,128)S(1)} %get-tuple-element.40), channel_id=1, source_target_pairs={{0,1},{1,0},{2,3},{3,2},{4,5},{5,4},{6,7},{7,6},{8,9},{9,8},{10,11... | collective-permute-start | bytes 393224 | tf_op jit(solution)/shard_map/ppermute | solution.py:387
  9.9 4.1 %collective-permute-start.3 = (f32[8,32,128]{2,1,0:T(8,128)S(1)}, f32[8,32,128]{2,1,0:T(8,128)S(1)}, u32[]{:S(2)}, u32[]{:S(2)}) collective-permute-start(f32[8,32,128]{2,1,0:T(8,128)S(1)} %get-tuple-element.41), channel_id=1, source_target_pairs={{1,2},{2,1},{3,4},{4,3},{5,6},{6,5},{9,10},{10,9},{11,12},{12,11},... | collective-permute-start | bytes 393224 | tf_op jit(solution)/shard_map/ppermute | solution.py:387
  14.0 0.1 collective-permute-start
  14.1 0.0 collective-permute-done.2.lev_e
  14.1 3.1 %collective-permute-start.1 = (f32[8,64,128]{2,1,0:T(8,128)S(1)}, f32[8,64,128]{2,1,0:T(8,128)S(1)}, u32[]{:S(2)}, u32[]{:S(2)}) collective-permute-start(f32[8,64,128]{2,1,0:T(8,128)S(1)} %get-tuple-element.39), channel_id=1, source_target_pairs={{8,16},{16,8},{24,32},{32,24},{40,48},{48,40},{9,17},{17,9},{25,33... | collective-permute-start | bytes 786440 | tf_op jit(solution)/shard_map/ppermute | solution.py:387
  17.2 3.2 %collective-permute-done.3.lev_o = f32[8,32,128]{2,1,0:T(8,128)S(1)} collective-permute-done((f32[8,32,128]{2,1,0:T(8,128)S(1)}, f32[8,32,128]{2,1,0:T(8,128)S(1)}, u32[]{:S(2)}, u32[]{:S(2)}) %collective-permute-start.3) | collective-permute-done | bytes 131104 | tf_op jit(solution)/shard_map/ppermute | solution.py:387
  20.4 0.0 collective-permute-done.4.lat
  20.4 0.3 shard_map.51.after.rest_1_.pa
  20.7 0.6 collective-permute-start.10
  21.3 0.0 collective-permute-done.lon_e
  21.3 10.6 %collective-permute-done.1.lon_o = f32[8,64,128]{2,1,0:T(8,128)S(1)} collective-permute-done((f32[8,64,128]{2,1,0:T(8,128)S(1)}, f32[8,64,128]{2,1,0:T(8,128)S(1)}, u32[]{:S(2)}, u32[]{:S(2)}) %collective-permute-start.1) | collective-permute-done | bytes 262176 | tf_op jit(solution)/shard_map/ppermute | solution.py:387
  32.0 5.9 %shard_map.52 = (f32[8,32,64,128]{3,2,1,0:T(8,128)S(1)}, f32[8,32,64,128]{3,2,1,0:T(8,128)S(1)}, f32[8,32,64,128]{3,2,1,0:T(8,128)S(1)}) custom-call(f32[8,32,64,128]{3,2,1,0:T(8,128)S(1)} %get-tuple-element.36.u, f32[16,64,128]{2,1,0:T(8,128)S(1)} %dynamic-slice_bitcast_fusion.pa, f32[16,64,128]{2,1,0:T(8,128)S(1)} %get-tuple-element.37.pb, ...), custom_call_target="tpu_custom_call" | custom-call | flops 20000000 | tf_op jit(solution)/shard_map/pallas_call | solution.py:431
  37.9 0.0 collective-permute-done.5.lat
  37.9 0.6 shard_map.53
  38.4 1.9 %collective-permute-start.11 = (f32[16,64,128]{2,1,0:T(8,128)S(1)}, f32[16,64,128]{2,1,0:T(8,128)S(1)}, u32[]{:S(2)}, u32[]{:S(2)}) collective-permute-start(f32[16,64,128]{2,1,0:T(8,128)S(1)} %get-tuple-element.45.pb), channel_id=1, source_target_pairs={{0,64},{64,0},{1,65},{65,1},{2,66},{66,2},{3,67},{67,3},{4,68},{68... | collective-permute-start | bytes 1572872 | tf_op jit(solution)/shard_map/ppermute | solution.py:447
  40.3 1.6 %collective-permute-start.8 = (f32[8,32,128]{2,1,0:T(8,128)S(1)}, f32[8,32,128]{2,1,0:T(8,128)S(1)}, u32[]{:S(2)}, u32[]{:S(2)}) collective-permute-start(f32[8,32,128]{2,1,0:T(8,128)S(1)} %get-tuple-element.48), channel_id=1, source_target_pairs={{0,1},{1,0},{2,3},{3,2},{4,5},{5,4},{6,7},{7,6},{8,9},{9,8},{10,11... | collective-permute-start | bytes 393224 | tf_op jit(solution)/shard_map/ppermute | solution.py:387
  41.9 3.8 %collective-permute-start.9 = (f32[8,32,128]{2,1,0:T(8,128)S(1)}, f32[8,32,128]{2,1,0:T(8,128)S(1)}, u32[]{:S(2)}, u32[]{:S(2)}) collective-permute-start(f32[8,32,128]{2,1,0:T(8,128)S(1)} %get-tuple-element.49), channel_id=1, source_target_pairs={{1,2},{2,1},{3,4},{4,3},{5,6},{6,5},{9,10},{10,9},{11,12},{12,11},... | collective-permute-start | bytes 393224 | tf_op jit(solution)/shard_map/ppermute | solution.py:387
  45.7 1.8 %collective-permute-start.6 = (f32[8,64,128]{2,1,0:T(8,128)S(1)}, f32[8,64,128]{2,1,0:T(8,128)S(1)}, u32[]{:S(2)}, u32[]{:S(2)}) collective-permute-start(f32[8,64,128]{2,1,0:T(8,128)S(1)} %get-tuple-element.46), channel_id=1, source_target_pairs={{0,8},{8,0},{16,24},{24,16},{32,40},{40,32},{48,56},{56,48},{1,9},... | collective-permute-start | bytes 786440 | tf_op jit(solution)/shard_map/ppermute | solution.py:387
  47.4 2.1 %collective-permute-start.7 = (f32[8,64,128]{2,1,0:T(8,128)S(1)}, f32[8,64,128]{2,1,0:T(8,128)S(1)}, u32[]{:S(2)}, u32[]{:S(2)}) collective-permute-start(f32[8,64,128]{2,1,0:T(8,128)S(1)} %get-tuple-element.47), channel_id=1, source_target_pairs={{8,16},{16,8},{24,32},{32,24},{40,48},{48,40},{9,17},{17,9},{25,33... | collective-permute-start | bytes 786440 | tf_op jit(solution)/shard_map/ppermute | solution.py:387
  49.5 3.5 %collective-permute-done.9.lev_o = f32[8,32,128]{2,1,0:T(8,128)S(1)} collective-permute-done((f32[8,32,128]{2,1,0:T(8,128)S(1)}, f32[8,32,128]{2,1,0:T(8,128)S(1)}, u32[]{:S(2)}, u32[]{:S(2)}) %collective-permute-start.9) | collective-permute-done | bytes 131104 | tf_op jit(solution)/shard_map/ppermute | solution.py:387
  53.0 0.3 shard_map.54.after.rest_1_.pa
  53.3 0.1 collective-permute-start.16
  53.5 7.6 %collective-permute-done.7.lon_o = f32[8,64,128]{2,1,0:T(8,128)S(1)} collective-permute-done((f32[8,64,128]{2,1,0:T(8,128)S(1)}, f32[8,64,128]{2,1,0:T(8,128)S(1)}, u32[]{:S(2)}, u32[]{:S(2)}) %collective-permute-start.7) | collective-permute-done | bytes 262176 | tf_op jit(solution)/shard_map/ppermute | solution.py:387
  61.1 4.0 %shard_map.55.rest_0_.u = f32[8,32,64,128]{3,2,1,0:T(8,128)S(1)} custom-call(f32[8,32,64,128]{3,2,1,0:T(8,128)S(1)} %get-tuple-element.44.rest_0_.u, f32[16,64,128]{2,1,0:T(8,128)S(1)} %shard_map.51.after.rest_1_.pa, f32[16,64,128]{2,1,0:T(8,128)S(1)} %get-tuple-element.45.pb, f32[8,64,128]{2,1,0:T(8,128)S(1)} %collective-permute-done.6.lon_e, ...), custom_call_target="tpu_custom_call" | custom-call | flops 20000000 | tf_op jit(solution)/shard_map/pallas_call | solution.py:440
  65.1 0.6 shard_map.56
  65.7 1.8 %collective-permute-start.17 = (f32[16,64,128]{2,1,0:T(8,128)S(1)}, f32[16,64,128]{2,1,0:T(8,128)S(1)}, u32[]{:S(2)}, u32[]{:S(2)}) collective-permute-start(f32[16,64,128]{2,1,0:T(8,128)S(1)} %get-tuple-element.52.pb), channel_id=1, source_target_pairs={{0,64},{64,0},{1,65},{65,1},{2,66},{66,2},{3,67},{67,3},{4,68},{68... | collective-permute-start | bytes 1572872 | tf_op jit(solution)/shard_map/ppermute | solution.py:447
  67.5 1.6 %collective-permute-start.14 = (f32[8,32,128]{2,1,0:T(8,128)S(1)}, f32[8,32,128]{2,1,0:T(8,128)S(1)}, u32[]{:S(2)}, u32[]{:S(2)}) collective-permute-start(f32[8,32,128]{2,1,0:T(8,128)S(1)} %get-tuple-element.55), channel_id=1, source_target_pairs={{0,1},{1,0},{2,3},{3,2},{4,5},{5,4},{6,7},{7,6},{8,9},{9,8},{10,11... | collective-permute-start | bytes 393224 | tf_op jit(solution)/shard_map/ppermute | solution.py:387
  69.1 4.1 %collective-permute-start.15 = (f32[8,32,128]{2,1,0:T(8,128)S(1)}, f32[8,32,128]{2,1,0:T(8,128)S(1)}, u32[]{:S(2)}, u32[]{:S(2)}) collective-permute-start(f32[8,32,128]{2,1,0:T(8,128)S(1)} %get-tuple-element.56), channel_id=1, source_target_pairs={{1,2},{2,1},{3,4},{4,3},{5,6},{6,5},{9,10},{10,9},{11,12},{12,11},... | collective-permute-start | bytes 393224 | tf_op jit(solution)/shard_map/ppermute | solution.py:387
  73.1 0.5 collective-permute-start.12
  73.7 1.9 %collective-permute-start.13 = (f32[8,64,128]{2,1,0:T(8,128)S(1)}, f32[8,64,128]{2,1,0:T(8,128)S(1)}, u32[]{:S(2)}, u32[]{:S(2)}) collective-permute-start(f32[8,64,128]{2,1,0:T(8,128)S(1)} %get-tuple-element.54), channel_id=1, source_target_pairs={{8,16},{16,8},{24,32},{32,24},{40,48},{48,40},{9,17},{17,9},{25,33... | collective-permute-start | bytes 786440 | tf_op jit(solution)/shard_map/ppermute | solution.py:387
  75.6 4.6 %collective-permute-done.15.lev_o = f32[8,32,128]{2,1,0:T(8,128)S(1)} collective-permute-done((f32[8,32,128]{2,1,0:T(8,128)S(1)}, f32[8,32,128]{2,1,0:T(8,128)S(1)}, u32[]{:S(2)}, u32[]{:S(2)}) %collective-permute-start.15) | collective-permute-done | bytes 131104 | tf_op jit(solution)/shard_map/ppermute | solution.py:387
  80.2 0.3 shard_map.57.after.rest_1_.pa
  80.5 0.5 collective-permute-start.22
  80.9 8.2 %collective-permute-done.13.lon_o = f32[8,64,128]{2,1,0:T(8,128)S(1)} collective-permute-done((f32[8,64,128]{2,1,0:T(8,128)S(1)}, f32[8,64,128]{2,1,0:T(8,128)S(1)}, u32[]{:S(2)}, u32[]{:S(2)}) %collective-permute-start.13) | collective-permute-done | bytes 262176 | tf_op jit(solution)/shard_map/ppermute | solution.py:387
  89.2 4.0 %shard_map.58.rest_0_.u = f32[8,32,64,128]{3,2,1,0:T(8,128)S(1)} custom-call(f32[8,32,64,128]{3,2,1,0:T(8,128)S(1)} %shard_map.55.rest_0_.u, f32[16,64,128]{2,1,0:T(8,128)S(1)} %shard_map.54.after.rest_1_.pa, f32[16,64,128]{2,1,0:T(8,128)S(1)} %get-tuple-element.52.pb, f32[8,64,128]{2,1,0:T(8,128)S(1)} %collective-permute-done.12.lon_e, ...), custom_call_target="tpu_custom_call" | custom-call | flops 20000000 | tf_op jit(solution)/shard_map/pallas_call | solution.py:440
  93.2 0.6 shard_map.59
  93.8 0.1 collective-permute-start.18
  93.8 2.6 %collective-permute-start.19 = (f32[8,64,128]{2,1,0:T(8,128)S(1)}, f32[8,64,128]{2,1,0:T(8,128)S(1)}, u32[]{:S(2)}, u32[]{:S(2)}) collective-permute-start(f32[8,64,128]{2,1,0:T(8,128)S(1)} %get-tuple-element.59), channel_id=1, source_target_pairs={{8,16},{16,8},{24,32},{32,24},{40,48},{48,40},{9,17},{17,9},{25,33... | collective-permute-start | bytes 786440 | tf_op jit(solution)/shard_map/ppermute | solution.py:387
  96.4 1.7 %collective-permute-start.20 = (f32[8,32,128]{2,1,0:T(8,128)S(1)}, f32[8,32,128]{2,1,0:T(8,128)S(1)}, u32[]{:S(2)}, u32[]{:S(2)}) collective-permute-start(f32[8,32,128]{2,1,0:T(8,128)S(1)} %get-tuple-element.60), channel_id=1, source_target_pairs={{0,1},{1,0},{2,3},{3,2},{4,5},{5,4},{6,7},{7,6},{8,9},{9,8},{10,11... | collective-permute-start | bytes 393224 | tf_op jit(solution)/shard_map/ppermute | solution.py:387
  98.1 4.1 %collective-permute-start.21 = (f32[8,32,128]{2,1,0:T(8,128)S(1)}, f32[8,32,128]{2,1,0:T(8,128)S(1)}, u32[]{:S(2)}, u32[]{:S(2)}) collective-permute-start(f32[8,32,128]{2,1,0:T(8,128)S(1)} %get-tuple-element.61), channel_id=1, source_target_pairs={{1,2},{2,1},{3,4},{4,3},{5,6},{6,5},{9,10},{10,9},{11,12},{12,11},... | collective-permute-start | bytes 393224 | tf_op jit(solution)/shard_map/ppermute | solution.py:387
  102.2 7.1 %collective-permute-done.21.lev_o = f32[8,32,128]{2,1,0:T(8,128)S(1)} collective-permute-done((f32[8,32,128]{2,1,0:T(8,128)S(1)}, f32[8,32,128]{2,1,0:T(8,128)S(1)}, u32[]{:S(2)}, u32[]{:S(2)}) %collective-permute-start.21) | collective-permute-done | bytes 131104 | tf_op jit(solution)/shard_map/ppermute | solution.py:387
  109.3 0.3 shard_map.60.after.npa
  109.6 5.4 %shard_map.61 = (f32[8,32,64,128]{3,2,1,0:T(8,128)}, f32[8,32,64,128]{3,2,1,0:T(8,128)S(1)}, f32[8,32,64,128]{3,2,1,0:T(8,128)S(1)}, f32[7,64,128]{2,1,0:T(8,128)S(1)}) custom-call(f32[8,32,64,128]{3,2,1,0:T(8,128)S(1)} %shard_map.58.rest_0_.u, f32[16,64,128]{2,1,0:T(8,128)S(1)} %shard_map.57.after.rest_1_.pa, ...), custom_call_target="tpu_custom_call", output_to_operand_aliasing={{1}: (7, {}), {2}: (8, {})} | custom-call | flops 20000000 | tf_op jit(solution)/shard_map/pallas_call | solution.py:452
  115.0 0.5 collective-permute-start.23
  115.6 1.6 %collective-permute-start.28 = (f32[16,64,128]{2,1,0:T(8,128)S(1)}, f32[16,64,128]{2,1,0:T(8,128)S(1)}, u32[]{:S(2)}, u32[]{:S(2)}) collective-permute-start(f32[16,64,128]{2,1,0:T(8,128)S(1)} %get-tuple-element.57.pb), channel_id=1, source_target_pairs={{0,64},{64,0},{1,65},{65,1},{2,66},{66,2},{3,67},{67,3},{4,68},{68... | collective-permute-start | bytes 1572872 | tf_op jit(solution)/shard_map/ppermute | solution.py:447
  117.2 1.3 collective-permute-start.26
  118.5 1.3 collective-permute-start.25
  119.8 3.6 %collective-permute-start.24 = (f32[7,32,128]{2,1,0:T(8,128)S(1)}, f32[7,32,128]{2,1,0:T(8,128)S(1)}, u32[]{:S(2)}, u32[]{:S(2)}) collective-permute-start(f32[7,32,128]{2,1,0:T(8,128)S(1)} %shard_map.62), channel_id=1, source_target_pairs={{0,16},{8,24},{32,48},{40,56},{1,17},{9,25},{33,49},{41,57},{2,18}... | collective-permute-start | bytes 344072 | tf_op jit(solution)/shard_map/ppermute | solution.py:469
  123.3 0.9 collective-permute-done.26
  124.2 10.1 %collective-permute-done.25 = f32[7,32,128]{2,1,0:T(8,128)S(1)} collective-permute-done((f32[7,32,128]{2,1,0:T(8,128)S(1)}, f32[7,32,128]{2,1,0:T(8,128)S(1)}, u32[]{:S(2)}, u32[]{:S(2)}) %collective-permute-start.25) | collective-permute-done | bytes 114720 | tf_op jit(solution)/shard_map/ppermute | solution.py:469
  134.3 0.1 collective-permute-start.27
  134.4 0.4 shard_map.63
  134.8 0.6 collective-permute-start.29
  135.4 0.9 collective-permute-done.29.rest_0_
  136.3 1.0 collective-permute-start.30
  137.3 4.4 %collective-permute-done.30.rest_1_ = f32[64,128]{1,0:T(8,128)S(1)} collective-permute-done((f32[64,128]{1,0:T(8,128)S(1)}, f32[64,128]{1,0:T(8,128)S(1)}, u32[]{:S(2)}, u32[]{:S(2)}) %collective-permute-start.30) | collective-permute-done | bytes 32800 | tf_op jit(solution)/shard_map/ppermute | solution.py:399
  141.7 1.3 collective-permute-start.31
  143.0 2.0 %shard_map.64.rest_4_ = f32[8,32,64,128]{3,2,1,0:T(8,128)} custom-call(f32[8,32,64,128]{3,2,1,0:T(8,128)S(1)} %get-tuple-element.62.sums, f32[7,64,128]{2,1,0:T(8,128)S(1)} %collective-permute-done.23.other, f32[7,32,128]{2,1,0:T(8,128)S(1)} %add_add_fusion.before, f32[64,128]{1,0:T(8,128)S(1)} %get-tuple-element.66.after), custom_call_target="tpu_custom_call" | custom-call | flops 1000000 | tf_op jit(solution)/shard_map/pallas_call | solution.py:483
  145.0 2.5 %collective-permute-done.31.rest_2_ = f32[64,128]{1,0:T(8,128)S(1)} collective-permute-done((f32[64,128]{1,0:T(8,128)S(1)}, f32[64,128]{1,0:T(8,128)S(1)}, u32[]{:S(2)}, u32[]{:S(2)}) %collective-permute-start.31) | collective-permute-done | bytes 32800 | tf_op jit(solution)/shard_map/ppermute | solution.py:399
  147.5 2.6 %shard_map.65 = (f32[8,32,64,128]{3,2,1,0:T(8,128)}, f32[8,32,64,128]{3,2,1,0:T(8,128)}) custom-call(f32[8,32,64,128]{3,2,1,0:T(8,128)S(1)} %get-tuple-element.62.sums, f32[7,64,128]{2,1,0:T(8,128)S(1)} %collective-permute-done.23.other, f32[7,32,128]{2,1,0:T(8,128)S(1)} %collective-permute-done.27.before, ...), custom_call_target="tpu_custom_call", output_to_operand_aliasing={{0}: (9, {}), {1}: (10, {})} | custom-call | flops 1000000 | tf_op jit(solution)/shard_map/pallas_call | solution.py:493
  (20 shorter events, 0.1 us)
Async XLA Ops:
  1.7 18.7 %collective-permute-start.4 = (f32[16,64,128]{2,1,0:T(8,128)S(1)}, f32[16,64,128]{2,1,0:T(8,128)S(1)}, u32[]{:S(2)}, u32[]{:S(2)}) collective-permute-start(f32[16,64,128]{2,1,0:T(8,128)S(1)} %dynamic-slice_bitcast_fusion.pa), channel_id=1, source_target_pairs={{0,64},{64,0},{1,65},{65,1},{2,66},{66,2},{3,67},{67,3},{4,68},{68... | collective-permute-start | bytes 1572872 | tf_op jit(solution)/shard_map/ppermute | solution.py:405
  6.8 31.1 %collective-permute-start.5 = (f32[16,64,128]{2,1,0:T(8,128)S(1)}, f32[16,64,128]{2,1,0:T(8,128)S(1)}, u32[]{:S(2)}, u32[]{:S(2)}) collective-permute-start(f32[16,64,128]{2,1,0:T(8,128)S(1)} %get-tuple-element.37.pb), channel_id=1, source_target_pairs={{0,64},{64,0},{1,65},{65,1},{2,66},{66,2},{3,67},{67,3},{4,68},{68... | collective-permute-start | bytes 1572872 | tf_op jit(solution)/shard_map/ppermute | solution.py:416
  8.4 5.7 %collective-permute-start.2 = (f32[8,32,128]{2,1,0:T(8,128)S(1)}, f32[8,32,128]{2,1,0:T(8,128)S(1)}, u32[]{:S(2)}, u32[]{:S(2)}) collective-permute-start(f32[8,32,128]{2,1,0:T(8,128)S(1)} %get-tuple-element.40), channel_id=1, source_target_pairs={{0,1},{1,0},{2,3},{3,2},{4,5},{5,4},{6,7},{7,6},{8,9},{9,8},{10,11... | collective-permute-start | bytes 393224 | tf_op jit(solution)/shard_map/ppermute | solution.py:387
  9.9 10.5 %collective-permute-start.3 = (f32[8,32,128]{2,1,0:T(8,128)S(1)}, f32[8,32,128]{2,1,0:T(8,128)S(1)}, u32[]{:S(2)}, u32[]{:S(2)}) collective-permute-start(f32[8,32,128]{2,1,0:T(8,128)S(1)} %get-tuple-element.41), channel_id=1, source_target_pairs={{1,2},{2,1},{3,4},{4,3},{5,6},{6,5},{9,10},{10,9},{11,12},{12,11},... | collective-permute-start | bytes 393224 | tf_op jit(solution)/shard_map/ppermute | solution.py:387
  14.0 7.3 %collective-permute-start = (f32[8,64,128]{2,1,0:T(8,128)S(1)}, f32[8,64,128]{2,1,0:T(8,128)S(1)}, u32[]{:S(2)}, u32[]{:S(2)}) collective-permute-start(f32[8,64,128]{2,1,0:T(8,128)S(1)} %get-tuple-element.38), channel_id=1, source_target_pairs={{0,8},{8,0},{16,24},{24,16},{32,40},{40,32},{48,56},{56,48},{1,9},... | collective-permute-start | bytes 786440 | tf_op jit(solution)/shard_map/ppermute | solution.py:387
  14.1 17.8 %collective-permute-start.1 = (f32[8,64,128]{2,1,0:T(8,128)S(1)}, f32[8,64,128]{2,1,0:T(8,128)S(1)}, u32[]{:S(2)}, u32[]{:S(2)}) collective-permute-start(f32[8,64,128]{2,1,0:T(8,128)S(1)} %get-tuple-element.39), channel_id=1, source_target_pairs={{8,16},{16,8},{24,32},{32,24},{40,48},{48,40},{9,17},{17,9},{25,33... | collective-permute-start | bytes 786440 | tf_op jit(solution)/shard_map/ppermute | solution.py:387
  20.7 32.3 %collective-permute-start.10 = (f32[16,64,128]{2,1,0:T(8,128)S(1)}, f32[16,64,128]{2,1,0:T(8,128)S(1)}, u32[]{:S(2)}, u32[]{:S(2)}) collective-permute-start(f32[16,64,128]{2,1,0:T(8,128)S(1)} %shard_map.51.after.rest_1_.pa), channel_id=1, source_target_pairs={{0,64},{64,0},{1,65},{65,1},{2,66},{66,2},{3,67},{67,3},{4,68},{68... | collective-permute-start | bytes 1572872 | tf_op jit(solution)/shard_map/ppermute | solution.py:429
  38.4 26.7 %collective-permute-start.11 = (f32[16,64,128]{2,1,0:T(8,128)S(1)}, f32[16,64,128]{2,1,0:T(8,128)S(1)}, u32[]{:S(2)}, u32[]{:S(2)}) collective-permute-start(f32[16,64,128]{2,1,0:T(8,128)S(1)} %get-tuple-element.45.pb), channel_id=1, source_target_pairs={{0,64},{64,0},{1,65},{65,1},{2,66},{66,2},{3,67},{67,3},{4,68},{68... | collective-permute-start | bytes 1572872 | tf_op jit(solution)/shard_map/ppermute | solution.py:447
  40.3 7.1 %collective-permute-start.8 = (f32[8,32,128]{2,1,0:T(8,128)S(1)}, f32[8,32,128]{2,1,0:T(8,128)S(1)}, u32[]{:S(2)}, u32[]{:S(2)}) collective-permute-start(f32[8,32,128]{2,1,0:T(8,128)S(1)} %get-tuple-element.48), channel_id=1, source_target_pairs={{0,1},{1,0},{2,3},{3,2},{4,5},{5,4},{6,7},{7,6},{8,9},{9,8},{10,11... | collective-permute-start | bytes 393224 | tf_op jit(solution)/shard_map/ppermute | solution.py:387
  41.9 11.1 %collective-permute-start.9 = (f32[8,32,128]{2,1,0:T(8,128)S(1)}, f32[8,32,128]{2,1,0:T(8,128)S(1)}, u32[]{:S(2)}, u32[]{:S(2)}) collective-permute-start(f32[8,32,128]{2,1,0:T(8,128)S(1)} %get-tuple-element.49), channel_id=1, source_target_pairs={{1,2},{2,1},{3,4},{4,3},{5,6},{6,5},{9,10},{10,9},{11,12},{12,11},... | collective-permute-start | bytes 393224 | tf_op jit(solution)/shard_map/ppermute | solution.py:387
  45.7 7.8 %collective-permute-start.6 = (f32[8,64,128]{2,1,0:T(8,128)S(1)}, f32[8,64,128]{2,1,0:T(8,128)S(1)}, u32[]{:S(2)}, u32[]{:S(2)}) collective-permute-start(f32[8,64,128]{2,1,0:T(8,128)S(1)} %get-tuple-element.46), channel_id=1, source_target_pairs={{0,8},{8,0},{16,24},{24,16},{32,40},{40,32},{48,56},{56,48},{1,9},... | collective-permute-start | bytes 786440 | tf_op jit(solution)/shard_map/ppermute | solution.py:387
  47.4 13.6 %collective-permute-start.7 = (f32[8,64,128]{2,1,0:T(8,128)S(1)}, f32[8,64,128]{2,1,0:T(8,128)S(1)}, u32[]{:S(2)}, u32[]{:S(2)}) collective-permute-start(f32[8,64,128]{2,1,0:T(8,128)S(1)} %get-tuple-element.47), channel_id=1, source_target_pairs={{8,16},{16,8},{24,32},{32,24},{40,48},{48,40},{9,17},{17,9},{25,33... | collective-permute-start | bytes 786440 | tf_op jit(solution)/shard_map/ppermute | solution.py:387
  53.3 26.8 %collective-permute-start.16 = (f32[16,64,128]{2,1,0:T(8,128)S(1)}, f32[16,64,128]{2,1,0:T(8,128)S(1)}, u32[]{:S(2)}, u32[]{:S(2)}) collective-permute-start(f32[16,64,128]{2,1,0:T(8,128)S(1)} %shard_map.54.after.rest_1_.pa), channel_id=1, source_target_pairs={{0,64},{64,0},{1,65},{65,1},{2,66},{66,2},{3,67},{67,3},{4,68},{68... | collective-permute-start | bytes 1572872 | tf_op jit(solution)/shard_map/ppermute | solution.py:429
  65.7 27.5 %collective-permute-start.17 = (f32[16,64,128]{2,1,0:T(8,128)S(1)}, f32[16,64,128]{2,1,0:T(8,128)S(1)}, u32[]{:S(2)}, u32[]{:S(2)}) collective-permute-start(f32[16,64,128]{2,1,0:T(8,128)S(1)} %get-tuple-element.52.pb), channel_id=1, source_target_pairs={{0,64},{64,0},{1,65},{65,1},{2,66},{66,2},{3,67},{67,3},{4,68},{68... | collective-permute-start | bytes 1572872 | tf_op jit(solution)/shard_map/ppermute | solution.py:447
  67.5 6.2 %collective-permute-start.14 = (f32[8,32,128]{2,1,0:T(8,128)S(1)}, f32[8,32,128]{2,1,0:T(8,128)S(1)}, u32[]{:S(2)}, u32[]{:S(2)}) collective-permute-start(f32[8,32,128]{2,1,0:T(8,128)S(1)} %get-tuple-element.55), channel_id=1, source_target_pairs={{0,1},{1,0},{2,3},{3,2},{4,5},{5,4},{6,7},{7,6},{8,9},{9,8},{10,11... | collective-permute-start | bytes 393224 | tf_op jit(solution)/shard_map/ppermute | solution.py:387
  69.1 11.1 %collective-permute-start.15 = (f32[8,32,128]{2,1,0:T(8,128)S(1)}, f32[8,32,128]{2,1,0:T(8,128)S(1)}, u32[]{:S(2)}, u32[]{:S(2)}) collective-permute-start(f32[8,32,128]{2,1,0:T(8,128)S(1)} %get-tuple-element.56), channel_id=1, source_target_pairs={{1,2},{2,1},{3,4},{4,3},{5,6},{6,5},{9,10},{10,9},{11,12},{12,11},... | collective-permute-start | bytes 393224 | tf_op jit(solution)/shard_map/ppermute | solution.py:387
  73.1 7.8 %collective-permute-start.12 = (f32[8,64,128]{2,1,0:T(8,128)S(1)}, f32[8,64,128]{2,1,0:T(8,128)S(1)}, u32[]{:S(2)}, u32[]{:S(2)}) collective-permute-start(f32[8,64,128]{2,1,0:T(8,128)S(1)} %get-tuple-element.53), channel_id=1, source_target_pairs={{0,8},{8,0},{16,24},{24,16},{32,40},{40,32},{48,56},{56,48},{1,9},... | collective-permute-start | bytes 786440 | tf_op jit(solution)/shard_map/ppermute | solution.py:387
  73.7 15.5 %collective-permute-start.13 = (f32[8,64,128]{2,1,0:T(8,128)S(1)}, f32[8,64,128]{2,1,0:T(8,128)S(1)}, u32[]{:S(2)}, u32[]{:S(2)}) collective-permute-start(f32[8,64,128]{2,1,0:T(8,128)S(1)} %get-tuple-element.54), channel_id=1, source_target_pairs={{8,16},{16,8},{24,32},{32,24},{40,48},{48,40},{9,17},{17,9},{25,33... | collective-permute-start | bytes 786440 | tf_op jit(solution)/shard_map/ppermute | solution.py:387
  80.5 28.8 %collective-permute-start.22 = (f32[16,64,128]{2,1,0:T(8,128)S(1)}, f32[16,64,128]{2,1,0:T(8,128)S(1)}, u32[]{:S(2)}, u32[]{:S(2)}) collective-permute-start(f32[16,64,128]{2,1,0:T(8,128)S(1)} %shard_map.57.after.rest_1_.pa), channel_id=1, source_target_pairs={{0,64},{64,0},{1,65},{65,1},{2,66},{66,2},{3,67},{67,3},{4,68},{68... | collective-permute-start | bytes 1572872 | tf_op jit(solution)/shard_map/ppermute | solution.py:429
  93.8 15.9 %collective-permute-start.18 = (f32[8,64,128]{2,1,0:T(8,128)S(1)}, f32[8,64,128]{2,1,0:T(8,128)S(1)}, u32[]{:S(2)}, u32[]{:S(2)}) collective-permute-start(f32[8,64,128]{2,1,0:T(8,128)S(1)} %get-tuple-element.58), channel_id=1, source_target_pairs={{0,8},{8,0},{16,24},{24,16},{32,40},{40,32},{48,56},{56,48},{1,9},... | collective-permute-start | bytes 786440 | tf_op jit(solution)/shard_map/ppermute | solution.py:387
  93.8 15.8 %collective-permute-start.19 = (f32[8,64,128]{2,1,0:T(8,128)S(1)}, f32[8,64,128]{2,1,0:T(8,128)S(1)}, u32[]{:S(2)}, u32[]{:S(2)}) collective-permute-start(f32[8,64,128]{2,1,0:T(8,128)S(1)} %get-tuple-element.59), channel_id=1, source_target_pairs={{8,16},{16,8},{24,32},{32,24},{40,48},{48,40},{9,17},{17,9},{25,33... | collective-permute-start | bytes 786440 | tf_op jit(solution)/shard_map/ppermute | solution.py:387
  96.4 5.7 %collective-permute-start.20 = (f32[8,32,128]{2,1,0:T(8,128)S(1)}, f32[8,32,128]{2,1,0:T(8,128)S(1)}, u32[]{:S(2)}, u32[]{:S(2)}) collective-permute-start(f32[8,32,128]{2,1,0:T(8,128)S(1)} %get-tuple-element.60), channel_id=1, source_target_pairs={{0,1},{1,0},{2,3},{3,2},{4,5},{5,4},{6,7},{7,6},{8,9},{9,8},{10,11... | collective-permute-start | bytes 393224 | tf_op jit(solution)/shard_map/ppermute | solution.py:387
  98.1 11.2 %collective-permute-start.21 = (f32[8,32,128]{2,1,0:T(8,128)S(1)}, f32[8,32,128]{2,1,0:T(8,128)S(1)}, u32[]{:S(2)}, u32[]{:S(2)}) collective-permute-start(f32[8,32,128]{2,1,0:T(8,128)S(1)} %get-tuple-element.61), channel_id=1, source_target_pairs={{1,2},{2,1},{3,4},{4,3},{5,6},{6,5},{9,10},{10,9},{11,12},{12,11},... | collective-permute-start | bytes 393224 | tf_op jit(solution)/shard_map/ppermute | solution.py:387
  115.0 2.1 %collective-permute-start.23 = (f32[7,64,128]{2,1,0:T(8,128)S(1)}, f32[7,64,128]{2,1,0:T(8,128)S(1)}, u32[]{:S(2)}, u32[]{:S(2)}) collective-permute-start(f32[7,64,128]{2,1,0:T(8,128)S(1)} %get-tuple-element.63.total), channel_id=1, source_target_pairs={{0,8},{8,0},{16,24},{24,16},{32,40},{40,32},{48,56},{56,48},{1,9},... | collective-permute-start | bytes 688136 | tf_op jit(solution)/shard_map/ppermute | solution.py:399
  115.6 18.8 %collective-permute-start.28 = (f32[16,64,128]{2,1,0:T(8,128)S(1)}, f32[16,64,128]{2,1,0:T(8,128)S(1)}, u32[]{:S(2)}, u32[]{:S(2)}) collective-permute-start(f32[16,64,128]{2,1,0:T(8,128)S(1)} %get-tuple-element.57.pb), channel_id=1, source_target_pairs={{0,64},{64,0},{1,65},{65,1},{2,66},{66,2},{3,67},{67,3},{4,68},{68... | collective-permute-start | bytes 1572872 | tf_op jit(solution)/shard_map/ppermute | solution.py:447
  117.2 7.1 %collective-permute-start.26 = (f32[7,32,128]{2,1,0:T(8,128)S(1)}, f32[7,32,128]{2,1,0:T(8,128)S(1)}, u32[]{:S(2)}, u32[]{:S(2)}) collective-permute-start(f32[7,32,128]{2,1,0:T(8,128)S(1)} %shard_map.62), channel_id=1, source_target_pairs={{0,32},{8,40},{16,48},{24,56},{1,33},{9,41},{17,49},{25,57},{2,34}... | collective-permute-start | bytes 344072 | tf_op jit(solution)/shard_map/ppermute | solution.py:469
  118.5 15.8 %collective-permute-start.25 = (f32[7,32,128]{2,1,0:T(8,128)S(1)}, f32[7,32,128]{2,1,0:T(8,128)S(1)}, u32[]{:S(2)}, u32[]{:S(2)}) collective-permute-start(f32[7,32,128]{2,1,0:T(8,128)S(1)} %shard_map.62), channel_id=1, source_target_pairs={{0,48},{8,56},{16,32},{24,40},{1,49},{9,57},{17,33},{25,41},{2,50}... | collective-permute-start | bytes 344072 | tf_op jit(solution)/shard_map/ppermute | solution.py:469
  119.8 14.5 %collective-permute-start.24 = (f32[7,32,128]{2,1,0:T(8,128)S(1)}, f32[7,32,128]{2,1,0:T(8,128)S(1)}, u32[]{:S(2)}, u32[]{:S(2)}) collective-permute-start(f32[7,32,128]{2,1,0:T(8,128)S(1)} %shard_map.62), channel_id=1, source_target_pairs={{0,16},{8,24},{32,48},{40,56},{1,17},{9,25},{33,49},{41,57},{2,18}... | collective-permute-start | bytes 344072 | tf_op jit(solution)/shard_map/ppermute | solution.py:469
  134.3 13.2 %collective-permute-start.27 = (f32[7,32,128]{2,1,0:T(8,128)S(1)}, f32[7,32,128]{2,1,0:T(8,128)S(1)}, u32[]{:S(2)}, u32[]{:S(2)}) collective-permute-start(f32[7,32,128]{2,1,0:T(8,128)S(1)} %add_add_fusion.before), channel_id=1, source_target_pairs={{0,8},{8,0},{16,24},{24,16},{32,40},{40,32},{48,56},{56,48},{1,9},... | collective-permute-start | bytes 344072 | tf_op jit(solution)/shard_map/ppermute | solution.py:471
  134.8 1.4 collective-permute-start.29
  136.3 5.4 %collective-permute-start.30 = (f32[64,128]{1,0:T(8,128)S(1)}, f32[64,128]{1,0:T(8,128)S(1)}, u32[]{:S(2)}, u32[]{:S(2)}) collective-permute-start(f32[64,128]{1,0:T(8,128)S(1)} %add.15), channel_id=1, source_target_pairs={{0,16},{8,24},{16,0},{24,8},{32,48},{40,56},{48,32},{56,40},{1,17}... | collective-permute-start | bytes 98312 | tf_op jit(solution)/shard_map/ppermute | solution.py:399
  141.7 5.8 %collective-permute-start.31 = (f32[64,128]{1,0:T(8,128)S(1)}, f32[64,128]{1,0:T(8,128)S(1)}, u32[]{:S(2)}, u32[]{:S(2)}) collective-permute-start(f32[64,128]{1,0:T(8,128)S(1)} %add.16), channel_id=1, source_target_pairs={{0,32},{8,40},{16,48},{24,56},{1,33},{9,41},{17,49},{25,57},{2,34}... | collective-permute-start | bytes 98312 | tf_op jit(solution)/shard_map/ppermute | solution.py:399

commit v6 on v5

--- a/solution.py
+++ b/solution.py
@@ -279,11 +279,11 @@
     total[...] = carry
 
 
-def earlier(others):
+def earlier(others, first=0):
     lon = lax.axis_index("lon")
     before = 0.0
     for bit, other in enumerate(others):
-        before += jnp.where(lon & (1 << bit) != 0, other, 0.0)
+        before += jnp.where(lon & (1 << (first + bit)) != 0, other, 0.0)
     return before
 
 
@@ -292,6 +292,12 @@
     at = pl.ds(pl.multiple_of(jnp.where(odd("lon"), n, 0), n), n)
     for p in range(out.shape[0]):
         out[p] = total[p, at] + other[p, at]
+
+
+def before_kernel(*refs):
+    *others, out = refs
+    for p in range(out.shape[0]):
+        out[p] = earlier([other[p] for other in others], 1)
 
 
 def total_rows(scale, ni, sums, before, put):
@@ -462,12 +468,11 @@
     half_total = call(half_kernel, V(nj - 1, nk // 2, nm), VMEM, (VMEM,) * 2, flops=10**5)(
         in_vmem(total), in_vmem(other)
     )
-    pairs = lon_size // 2
-    mine = []
-    for steps in sorted(range(1, pairs), key=lambda steps: (steps % 2 == 0, steps)):
-        to = [(2 * a + c, 2 * (a ^ steps) + c) for a in range(pairs) if a < a ^ steps for c in (0, 1)]
-        mine.append(lax.ppermute(half_total, "lon", to))
-    mine = functools.reduce(jnp.add, mine)
+    later = []
+    for bit in range(1, bits):
+        later.append(partner(bit, half_total))
+        half_total = half_total + later[-1]
+    mine = call(before_kernel, V(nj - 1, nk // 2, nm), VMEM, (VMEM,) * (bits - 1), flops=10**5)(*map(in_vmem, later))
     back = lax.ppermute(mine, "lon", [(i, i ^ 1) for i in range(lon_size)])
     n_pa = in_vmem(n_pa)
     n_pb, edge_sums, edge_total = call(

time: 151 us -> 147 us (0.974)
  waiting for transfers between devices: 63.6 us -> 60.9 us
    ppermute x3 -> x0, waiting for transfers between devices: 11 us -> none  [per_device(): mine.append(lax.ppermute(half_total, 'lon', to))]
    ppermute x4 -> x6, waiting for transfers between devices: 7.75 us -> 18.4 us  [partner(): return lax.ppermute(total, 'lon', pairs)]
    ppermute x3 -> x0, starting transfers between devices: 6.15 us -> none  [per_device(): mine.append(lax.ppermute(half_total, 'lon', to))]
    ppermute x4 -> x6, starting transfers between devices: 3.44 us -> 7.47 us  [partner(): return lax.ppermute(total, 'lon', pairs)]
    ppermute x16, waiting for transfers between devices: 44.9 us -> 42.5 us  [exchange(): return (lax.ppermute(e, axis, swaps(0)), lax.ppermute(o, axis, swaps(1)))]
  transfers between devices with their start and end apart: 32 -> 31, of which waited for: 12 -> 13; matrix products, arithmetic and copies ran while one was open for 0% -> 0% of each run, Pallas kernels for 16% -> 19%
where the time goes in v6:
time: 147 us; the launch traced here: 146 us
  waiting for transfers between devices  60.9 us (41%)
  starting transfers between devices  52 us (35%)
  Pallas kernels  30.9 us (21%)
    ppermute x16, waiting for transfers between devices, exchange(): return (lax.ppermute(e, axis, swaps(0)), lax.ppermute(o, axis, swaps(1)))  42.5 us
    ppermute x16, starting transfers between devices, exchange(): return (lax.ppermute(e, axis, swaps(0)), lax.ppermute(o, axis, swaps(1)))  34.5 us
    ppermute x6, waiting for transfers between devices, partner(): return lax.ppermute(total, 'lon', pairs)  18.4 us
    pallas_call x2, Pallas kernels, per_device(): call(bulk_kernel, V(nj, ni, nk, nm), VMEM, (VMEM,) * 9 + (ANY,), flops=2...  7.72 us
    ppermute x6, starting transfers between devices, partner(): return lax.ppermute(total, 'lon', pairs)  7.47 us
    ppermute x3, starting transfers between devices, per_device(): lat_b = lax.ppermute(n_pb, 'lat', swap)  6.48 us
    pallas_call x1, Pallas kernels, per_device(): call(first_bulk_kernel, (V(nj, ni, nk, nm),) * 3, (VMEM,) * 3, (VMEM,) *...  5.85 us
    pallas_call x1, Pallas kernels, per_device(): call(last_bulk_kernel, (H(nj, ni, nk, nm), V(nj, ni, nk, nm), V(nj, ni, n...  5.24 us
  transfers between devices with their start and end apart: 31, of which 13 were waited for; matrix products, arithmetic and copies ran while one was open for 0% of the time, Pallas kernels for 19%

profile of v6, /device:TPU:98, one launch (start us, length us, event | category | flops | bytes accessed | tf_op | source)
XLA Modules:
  0.0 145.9 jit_solution(11599882554631303126)
XLA Ops:
  0.6 1.1 dynamic-slice_bitcast_fusion.pa
  1.7 0.6 collective-permute-start.4
  2.3 4.4 %shard_map.50 = (f32[8,32,64,128]{3,2,1,0:T(8,128)S(1)}, f32[16,64,128]{2,1,0:T(8,128)S(1)}, f32[32,64,128]{2,1,0:T(8,128)S(1)}, f32[32,64,128]{2,1,0:T(8,128)S(...) custom-call(f32[8,32,64,128]{3,2,1,0:T(8,128)} %u_in.1, ...), custom_call_target="tpu_custom_call" | custom-call | flops 1000000 | tf_op jit(solution)/shard_map/pallas_call | solution.py:412
  6.8 1.6 %collective-permute-start.5 = (f32[16,64,128]{2,1,0:T(8,128)S(1)}, f32[16,64,128]{2,1,0:T(8,128)S(1)}, u32[]{:S(2)}, u32[]{:S(2)}) collective-permute-start(f32[16,64,128]{2,1,0:T(8,128)S(1)} %get-tuple-element.37.pb), channel_id=1, source_target_pairs={{0,64},{64,0},{1,65},{65,1},{2,66},{66,2},{3,67},{67,3},{4,68},{68... | collective-permute-start | bytes 1572872 | tf_op jit(solution)/shard_map/ppermute | solution.py:422
  8.4 1.6 %collective-permute-start.2 = (f32[8,32,128]{2,1,0:T(8,128)S(1)}, f32[8,32,128]{2,1,0:T(8,128)S(1)}, u32[]{:S(2)}, u32[]{:S(2)}) collective-permute-start(f32[8,32,128]{2,1,0:T(8,128)S(1)} %get-tuple-element.40), channel_id=1, source_target_pairs={{0,1},{1,0},{2,3},{3,2},{4,5},{5,4},{6,7},{7,6},{8,9},{9,8},{10,11... | collective-permute-start | bytes 393224 | tf_op jit(solution)/shard_map/ppermute | solution.py:393
  9.9 4.1 %collective-permute-start.3 = (f32[8,32,128]{2,1,0:T(8,128)S(1)}, f32[8,32,128]{2,1,0:T(8,128)S(1)}, u32[]{:S(2)}, u32[]{:S(2)}) collective-permute-start(f32[8,32,128]{2,1,0:T(8,128)S(1)} %get-tuple-element.41), channel_id=1, source_target_pairs={{1,2},{2,1},{3,4},{4,3},{5,6},{6,5},{9,10},{10,9},{11,12},{12,11},... | collective-permute-start | bytes 393224 | tf_op jit(solution)/shard_map/ppermute | solution.py:393
  14.0 0.1 collective-permute-start
  14.1 3.1 %collective-permute-start.1 = (f32[8,64,128]{2,1,0:T(8,128)S(1)}, f32[8,64,128]{2,1,0:T(8,128)S(1)}, u32[]{:S(2)}, u32[]{:S(2)}) collective-permute-start(f32[8,64,128]{2,1,0:T(8,128)S(1)} %get-tuple-element.39), channel_id=1, source_target_pairs={{8,16},{16,8},{24,32},{32,24},{40,48},{48,40},{9,17},{17,9},{25,33... | collective-permute-start | bytes 786440 | tf_op jit(solution)/shard_map/ppermute | solution.py:393
  17.2 3.2 %collective-permute-done.3.lev_o = f32[8,32,128]{2,1,0:T(8,128)S(1)} collective-permute-done((f32[8,32,128]{2,1,0:T(8,128)S(1)}, f32[8,32,128]{2,1,0:T(8,128)S(1)}, u32[]{:S(2)}, u32[]{:S(2)}) %collective-permute-start.3) | collective-permute-done | bytes 131104 | tf_op jit(solution)/shard_map/ppermute | solution.py:393
  20.4 0.0 collective-permute-done.4.lat
  20.4 0.3 shard_map.51.after.rest_1_.pa
  20.7 0.6 collective-permute-start.10
  21.3 10.7 %collective-permute-done.1.lon_o = f32[8,64,128]{2,1,0:T(8,128)S(1)} collective-permute-done((f32[8,64,128]{2,1,0:T(8,128)S(1)}, f32[8,64,128]{2,1,0:T(8,128)S(1)}, u32[]{:S(2)}, u32[]{:S(2)}) %collective-permute-start.1) | collective-permute-done | bytes 262176 | tf_op jit(solution)/shard_map/ppermute | solution.py:393
  32.0 5.9 %shard_map.52 = (f32[8,32,64,128]{3,2,1,0:T(8,128)S(1)}, f32[8,32,64,128]{3,2,1,0:T(8,128)S(1)}, f32[8,32,64,128]{3,2,1,0:T(8,128)S(1)}) custom-call(f32[8,32,64,128]{3,2,1,0:T(8,128)S(1)} %get-tuple-element.36.u, f32[16,64,128]{2,1,0:T(8,128)S(1)} %dynamic-slice_bitcast_fusion.pa, f32[16,64,128]{2,1,0:T(8,128)S(1)} %get-tuple-element.37.pb, ...), custom_call_target="tpu_custom_call" | custom-call | flops 20000000 | tf_op jit(solution)/shard_map/pallas_call | solution.py:437
  37.8 0.0 collective-permute-done.5.lat
  37.8 0.5 shard_map.53
  38.4 1.9 %collective-permute-start.11 = (f32[16,64,128]{2,1,0:T(8,128)S(1)}, f32[16,64,128]{2,1,0:T(8,128)S(1)}, u32[]{:S(2)}, u32[]{:S(2)}) collective-permute-start(f32[16,64,128]{2,1,0:T(8,128)S(1)} %get-tuple-element.45.pb), channel_id=1, source_target_pairs={{0,64},{64,0},{1,65},{65,1},{2,66},{66,2},{3,67},{67,3},{4,68},{68... | collective-permute-start | bytes 1572872 | tf_op jit(solution)/shard_map/ppermute | solution.py:453
  40.3 1.6 %collective-permute-start.8 = (f32[8,32,128]{2,1,0:T(8,128)S(1)}, f32[8,32,128]{2,1,0:T(8,128)S(1)}, u32[]{:S(2)}, u32[]{:S(2)}) collective-permute-start(f32[8,32,128]{2,1,0:T(8,128)S(1)} %get-tuple-element.48), channel_id=1, source_target_pairs={{0,1},{1,0},{2,3},{3,2},{4,5},{5,4},{6,7},{7,6},{8,9},{9,8},{10,11... | collective-permute-start | bytes 393224 | tf_op jit(solution)/shard_map/ppermute | solution.py:393
  41.8 3.8 %collective-permute-start.9 = (f32[8,32,128]{2,1,0:T(8,128)S(1)}, f32[8,32,128]{2,1,0:T(8,128)S(1)}, u32[]{:S(2)}, u32[]{:S(2)}) collective-permute-start(f32[8,32,128]{2,1,0:T(8,128)S(1)} %get-tuple-element.49), channel_id=1, source_target_pairs={{1,2},{2,1},{3,4},{4,3},{5,6},{6,5},{9,10},{10,9},{11,12},{12,11},... | collective-permute-start | bytes 393224 | tf_op jit(solution)/shard_map/ppermute | solution.py:393
  45.6 1.8 %collective-permute-start.6 = (f32[8,64,128]{2,1,0:T(8,128)S(1)}, f32[8,64,128]{2,1,0:T(8,128)S(1)}, u32[]{:S(2)}, u32[]{:S(2)}) collective-permute-start(f32[8,64,128]{2,1,0:T(8,128)S(1)} %get-tuple-element.46), channel_id=1, source_target_pairs={{0,8},{8,0},{16,24},{24,16},{32,40},{40,32},{48,56},{56,48},{1,9},... | collective-permute-start | bytes 786440 | tf_op jit(solution)/shard_map/ppermute | solution.py:393
  47.4 0.0 collective-permute-done.8.lev_e
  47.4 2.1 %collective-permute-start.7 = (f32[8,64,128]{2,1,0:T(8,128)S(1)}, f32[8,64,128]{2,1,0:T(8,128)S(1)}, u32[]{:S(2)}, u32[]{:S(2)}) collective-permute-start(f32[8,64,128]{2,1,0:T(8,128)S(1)} %get-tuple-element.47), channel_id=1, source_target_pairs={{8,16},{16,8},{24,32},{32,24},{40,48},{48,40},{9,17},{17,9},{25,33... | collective-permute-start | bytes 786440 | tf_op jit(solution)/shard_map/ppermute | solution.py:393
  49.5 3.5 %collective-permute-done.9.lev_o = f32[8,32,128]{2,1,0:T(8,128)S(1)} collective-permute-done((f32[8,32,128]{2,1,0:T(8,128)S(1)}, f32[8,32,128]{2,1,0:T(8,128)S(1)}, u32[]{:S(2)}, u32[]{:S(2)}) %collective-permute-start.9) | collective-permute-done | bytes 131104 | tf_op jit(solution)/shard_map/ppermute | solution.py:393
  53.0 0.0 collective-permute-done.10.lat
  53.0 0.3 shard_map.54.after.rest_1_.pa
  53.3 0.1 collective-permute-start.16
  53.4 7.6 %collective-permute-done.7.lon_o = f32[8,64,128]{2,1,0:T(8,128)S(1)} collective-permute-done((f32[8,64,128]{2,1,0:T(8,128)S(1)}, f32[8,64,128]{2,1,0:T(8,128)S(1)}, u32[]{:S(2)}, u32[]{:S(2)}) %collective-permute-start.7) | collective-permute-done | bytes 262176 | tf_op jit(solution)/shard_map/ppermute | solution.py:393
  61.0 3.9 %shard_map.55.rest_0_.u = f32[8,32,64,128]{3,2,1,0:T(8,128)S(1)} custom-call(f32[8,32,64,128]{3,2,1,0:T(8,128)S(1)} %get-tuple-element.44.rest_0_.u, f32[16,64,128]{2,1,0:T(8,128)S(1)} %shard_map.51.after.rest_1_.pa, f32[16,64,128]{2,1,0:T(8,128)S(1)} %get-tuple-element.45.pb, f32[8,64,128]{2,1,0:T(8,128)S(1)} %collective-permute-done.6.lon_e, ...), custom_call_target="tpu_custom_call" | custom-call | flops 20000000 | tf_op jit(solution)/shard_map/pallas_call | solution.py:446
  64.9 0.5 shard_map.56
  65.5 1.8 %collective-permute-start.17 = (f32[16,64,128]{2,1,0:T(8,128)S(1)}, f32[16,64,128]{2,1,0:T(8,128)S(1)}, u32[]{:S(2)}, u32[]{:S(2)}) collective-permute-start(f32[16,64,128]{2,1,0:T(8,128)S(1)} %get-tuple-element.52.pb), channel_id=1, source_target_pairs={{0,64},{64,0},{1,65},{65,1},{2,66},{66,2},{3,67},{67,3},{4,68},{68... | collective-permute-start | bytes 1572872 | tf_op jit(solution)/shard_map/ppermute | solution.py:453
  67.3 1.6 %collective-permute-start.14 = (f32[8,32,128]{2,1,0:T(8,128)S(1)}, f32[8,32,128]{2,1,0:T(8,128)S(1)}, u32[]{:S(2)}, u32[]{:S(2)}) collective-permute-start(f32[8,32,128]{2,1,0:T(8,128)S(1)} %get-tuple-element.55), channel_id=1, source_target_pairs={{0,1},{1,0},{2,3},{3,2},{4,5},{5,4},{6,7},{7,6},{8,9},{9,8},{10,11... | collective-permute-start | bytes 393224 | tf_op jit(solution)/shard_map/ppermute | solution.py:393
  68.9 4.1 %collective-permute-start.15 = (f32[8,32,128]{2,1,0:T(8,128)S(1)}, f32[8,32,128]{2,1,0:T(8,128)S(1)}, u32[]{:S(2)}, u32[]{:S(2)}) collective-permute-start(f32[8,32,128]{2,1,0:T(8,128)S(1)} %get-tuple-element.56), channel_id=1, source_target_pairs={{1,2},{2,1},{3,4},{4,3},{5,6},{6,5},{9,10},{10,9},{11,12},{12,11},... | collective-permute-start | bytes 393224 | tf_op jit(solution)/shard_map/ppermute | solution.py:393
  72.9 0.6 collective-permute-start.12
  73.5 1.9 %collective-permute-start.13 = (f32[8,64,128]{2,1,0:T(8,128)S(1)}, f32[8,64,128]{2,1,0:T(8,128)S(1)}, u32[]{:S(2)}, u32[]{:S(2)}) collective-permute-start(f32[8,64,128]{2,1,0:T(8,128)S(1)} %get-tuple-element.54), channel_id=1, source_target_pairs={{8,16},{16,8},{24,32},{32,24},{40,48},{48,40},{9,17},{17,9},{25,33... | collective-permute-start | bytes 786440 | tf_op jit(solution)/shard_map/ppermute | solution.py:393
  75.4 4.6 %collective-permute-done.15.lev_o = f32[8,32,128]{2,1,0:T(8,128)S(1)} collective-permute-done((f32[8,32,128]{2,1,0:T(8,128)S(1)}, f32[8,32,128]{2,1,0:T(8,128)S(1)}, u32[]{:S(2)}, u32[]{:S(2)}) %collective-permute-start.15) | collective-permute-done | bytes 131104 | tf_op jit(solution)/shard_map/ppermute | solution.py:393
  80.1 0.3 shard_map.57.after.rest_1_.pa
  80.3 0.5 collective-permute-start.22
  80.8 8.3 %collective-permute-done.13.lon_o = f32[8,64,128]{2,1,0:T(8,128)S(1)} collective-permute-done((f32[8,64,128]{2,1,0:T(8,128)S(1)}, f32[8,64,128]{2,1,0:T(8,128)S(1)}, u32[]{:S(2)}, u32[]{:S(2)}) %collective-permute-start.13) | collective-permute-done | bytes 262176 | tf_op jit(solution)/shard_map/ppermute | solution.py:393
  89.1 3.9 %shard_map.58.rest_0_.u = f32[8,32,64,128]{3,2,1,0:T(8,128)S(1)} custom-call(f32[8,32,64,128]{3,2,1,0:T(8,128)S(1)} %shard_map.55.rest_0_.u, f32[16,64,128]{2,1,0:T(8,128)S(1)} %shard_map.54.after.rest_1_.pa, f32[16,64,128]{2,1,0:T(8,128)S(1)} %get-tuple-element.52.pb, f32[8,64,128]{2,1,0:T(8,128)S(1)} %collective-permute-done.12.lon_e, ...), custom_call_target="tpu_custom_call" | custom-call | flops 20000000 | tf_op jit(solution)/shard_map/pallas_call | solution.py:446
  93.0 0.5 shard_map.59
  93.5 0.1 collective-permute-start.18
  93.6 2.7 %collective-permute-start.19 = (f32[8,64,128]{2,1,0:T(8,128)S(1)}, f32[8,64,128]{2,1,0:T(8,128)S(1)}, u32[]{:S(2)}, u32[]{:S(2)}) collective-permute-start(f32[8,64,128]{2,1,0:T(8,128)S(1)} %get-tuple-element.59), channel_id=1, source_target_pairs={{8,16},{16,8},{24,32},{32,24},{40,48},{48,40},{9,17},{17,9},{25,33... | collective-permute-start | bytes 786440 | tf_op jit(solution)/shard_map/ppermute | solution.py:393
  96.3 1.7 %collective-permute-start.20 = (f32[8,32,128]{2,1,0:T(8,128)S(1)}, f32[8,32,128]{2,1,0:T(8,128)S(1)}, u32[]{:S(2)}, u32[]{:S(2)}) collective-permute-start(f32[8,32,128]{2,1,0:T(8,128)S(1)} %get-tuple-element.60), channel_id=1, source_target_pairs={{0,1},{1,0},{2,3},{3,2},{4,5},{5,4},{6,7},{7,6},{8,9},{9,8},{10,11... | collective-permute-start | bytes 393224 | tf_op jit(solution)/shard_map/ppermute | solution.py:393
  98.0 4.1 %collective-permute-start.21 = (f32[8,32,128]{2,1,0:T(8,128)S(1)}, f32[8,32,128]{2,1,0:T(8,128)S(1)}, u32[]{:S(2)}, u32[]{:S(2)}) collective-permute-start(f32[8,32,128]{2,1,0:T(8,128)S(1)} %get-tuple-element.61), channel_id=1, source_target_pairs={{1,2},{2,1},{3,4},{4,3},{5,6},{6,5},{9,10},{10,9},{11,12},{12,11},... | collective-permute-start | bytes 393224 | tf_op jit(solution)/shard_map/ppermute | solution.py:393
  102.0 2.8 %collective-permute-start.27 = (f32[16,64,128]{2,1,0:T(8,128)S(1)}, f32[16,64,128]{2,1,0:T(8,128)S(1)}, u32[]{:S(2)}, u32[]{:S(2)}) collective-permute-start(f32[16,64,128]{2,1,0:T(8,128)S(1)} %get-tuple-element.57.pb), channel_id=1, source_target_pairs={{0,64},{64,0},{1,65},{65,1},{2,66},{66,2},{3,67},{67,3},{4,68},{68... | collective-permute-start | bytes 1572872 | tf_op jit(solution)/shard_map/ppermute | solution.py:453
  104.8 4.5 %collective-permute-done.21.lev_o = f32[8,32,128]{2,1,0:T(8,128)S(1)} collective-permute-done((f32[8,32,128]{2,1,0:T(8,128)S(1)}, f32[8,32,128]{2,1,0:T(8,128)S(1)}, u32[]{:S(2)}, u32[]{:S(2)}) %collective-permute-start.21) | collective-permute-done | bytes 131104 | tf_op jit(solution)/shard_map/ppermute | solution.py:393
  109.3 0.3 shard_map.60.after.npa
  109.6 5.2 %shard_map.61 = (f32[8,32,64,128]{3,2,1,0:T(8,128)}, f32[8,32,64,128]{3,2,1,0:T(8,128)S(1)}, f32[8,32,64,128]{3,2,1,0:T(8,128)S(1)}, f32[7,64,128]{2,1,0:T(8,128)S(1)}) custom-call(f32[8,32,64,128]{3,2,1,0:T(8,128)S(1)} %shard_map.58.rest_0_.u, f32[16,64,128]{2,1,0:T(8,128)S(1)} %shard_map.57.after.rest_1_.pa, ...), custom_call_target="tpu_custom_call", output_to_operand_aliasing={{1}: (7, {}), {2}: (8, {})} | custom-call | flops 20000000 | tf_op jit(solution)/shard_map/pallas_call | solution.py:458
  114.8 0.5 collective-permute-start.23
  115.3 1.1 collective-permute-done.23.other
  116.4 2.1 %collective-permute-start.24 = (f32[7,32,128]{2,1,0:T(8,128)S(1)}, f32[7,32,128]{2,1,0:T(8,128)S(1)}, u32[]{:S(2)}, u32[]{:S(2)}) collective-permute-start(f32[7,32,128]{2,1,0:T(8,128)S(1)} %shard_map.62), channel_id=1, source_target_pairs={{0,16},{8,24},{16,0},{24,8},{32,48},{40,56},{48,32},{56,40},{1,17}... | collective-permute-start | bytes 344072 | tf_op jit(solution)/shard_map/ppermute | solution.py:405
  118.5 4.9 %collective-permute-done.24.refs_0_ = f32[7,32,128]{2,1,0:T(8,128)S(1)} collective-permute-done((f32[7,32,128]{2,1,0:T(8,128)S(1)}, f32[7,32,128]{2,1,0:T(8,128)S(1)}, u32[]{:S(2)}, u32[]{:S(2)}) %collective-permute-start.24) | collective-permute-done | bytes 114720 | tf_op jit(solution)/shard_map/ppermute | solution.py:405
  123.4 1.3 collective-permute-start.25
  124.7 5.4 %collective-permute-done.25.refs_1_ = f32[7,32,128]{2,1,0:T(8,128)S(1)} collective-permute-done((f32[7,32,128]{2,1,0:T(8,128)S(1)}, f32[7,32,128]{2,1,0:T(8,128)S(1)}, u32[]{:S(2)}, u32[]{:S(2)}) %collective-permute-start.25) | collective-permute-done | bytes 114720 | tf_op jit(solution)/shard_map/ppermute | solution.py:405
  130.1 0.1 collective-permute-start.26
  130.2 0.4 shard_map.64
  130.6 0.6 collective-permute-start.28
  131.2 0.9 collective-permute-done.28.rest_0_
  132.0 1.8 %collective-permute-start.29 = (f32[64,128]{1,0:T(8,128)S(1)}, f32[64,128]{1,0:T(8,128)S(1)}, u32[]{:S(2)}, u32[]{:S(2)}) collective-permute-start(f32[64,128]{1,0:T(8,128)S(1)} %add.11), channel_id=1, source_target_pairs={{0,16},{8,24},{16,0},{24,8},{32,48},{40,56},{48,32},{56,40},{1,17}... | collective-permute-start | bytes 98312 | tf_op jit(solution)/shard_map/ppermute | solution.py:405
  133.8 3.6 %collective-permute-done.29.rest_1_ = f32[64,128]{1,0:T(8,128)S(1)} collective-permute-done((f32[64,128]{1,0:T(8,128)S(1)}, f32[64,128]{1,0:T(8,128)S(1)}, u32[]{:S(2)}, u32[]{:S(2)}) %collective-permute-start.29) | collective-permute-done | bytes 32800 | tf_op jit(solution)/shard_map/ppermute | solution.py:405
  137.5 1.3 collective-permute-start.30
  138.7 2.0 %shard_map.65.rest_4_ = f32[8,32,64,128]{3,2,1,0:T(8,128)} custom-call(f32[8,32,64,128]{3,2,1,0:T(8,128)S(1)} %get-tuple-element.62.sums, f32[7,64,128]{2,1,0:T(8,128)S(1)} %collective-permute-done.23.other, f32[7,32,128]{2,1,0:T(8,128)S(1)} %shard_map.63.before, f32[64,128]{1,0:T(8,128)S(1)} %get-tuple-element.66.after), custom_call_target="tpu_custom_call" | custom-call | flops 1000000 | tf_op jit(solution)/shard_map/pallas_call | solution.py:488
  140.7 2.5 %collective-permute-done.30.rest_2_ = f32[64,128]{1,0:T(8,128)S(1)} collective-permute-done((f32[64,128]{1,0:T(8,128)S(1)}, f32[64,128]{1,0:T(8,128)S(1)}, u32[]{:S(2)}, u32[]{:S(2)}) %collective-permute-start.30) | collective-permute-done | bytes 32800 | tf_op jit(solution)/shard_map/ppermute | solution.py:405
  143.3 2.6 %shard_map.66 = (f32[8,32,64,128]{3,2,1,0:T(8,128)}, f32[8,32,64,128]{3,2,1,0:T(8,128)}) custom-call(f32[8,32,64,128]{3,2,1,0:T(8,128)S(1)} %get-tuple-element.62.sums, f32[7,64,128]{2,1,0:T(8,128)S(1)} %collective-permute-done.23.other, f32[7,32,128]{2,1,0:T(8,128)S(1)} %collective-permute-done.26.before, ...), custom_call_target="tpu_custom_call", output_to_operand_aliasing={{0}: (9, {}), {1}: (10, {})} | custom-call | flops 1000000 | tf_op jit(solution)/shard_map/pallas_call | solution.py:498
  (19 shorter events, 0.1 us)
Async XLA Ops:
  1.7 18.7 %collective-permute-start.4 = (f32[16,64,128]{2,1,0:T(8,128)S(1)}, f32[16,64,128]{2,1,0:T(8,128)S(1)}, u32[]{:S(2)}, u32[]{:S(2)}) collective-permute-start(f32[16,64,128]{2,1,0:T(8,128)S(1)} %dynamic-slice_bitcast_fusion.pa), channel_id=1, source_target_pairs={{0,64},{64,0},{1,65},{65,1},{2,66},{66,2},{3,67},{67,3},{4,68},{68... | collective-permute-start | bytes 1572872 | tf_op jit(solution)/shard_map/ppermute | solution.py:411
  6.8 31.0 %collective-permute-start.5 = (f32[16,64,128]{2,1,0:T(8,128)S(1)}, f32[16,64,128]{2,1,0:T(8,128)S(1)}, u32[]{:S(2)}, u32[]{:S(2)}) collective-permute-start(f32[16,64,128]{2,1,0:T(8,128)S(1)} %get-tuple-element.37.pb), channel_id=1, source_target_pairs={{0,64},{64,0},{1,65},{65,1},{2,66},{66,2},{3,67},{67,3},{4,68},{68... | collective-permute-start | bytes 1572872 | tf_op jit(solution)/shard_map/ppermute | solution.py:422
  8.4 5.7 %collective-permute-start.2 = (f32[8,32,128]{2,1,0:T(8,128)S(1)}, f32[8,32,128]{2,1,0:T(8,128)S(1)}, u32[]{:S(2)}, u32[]{:S(2)}) collective-permute-start(f32[8,32,128]{2,1,0:T(8,128)S(1)} %get-tuple-element.40), channel_id=1, source_target_pairs={{0,1},{1,0},{2,3},{3,2},{4,5},{5,4},{6,7},{7,6},{8,9},{9,8},{10,11... | collective-permute-start | bytes 393224 | tf_op jit(solution)/shard_map/ppermute | solution.py:393
  9.9 10.5 %collective-permute-start.3 = (f32[8,32,128]{2,1,0:T(8,128)S(1)}, f32[8,32,128]{2,1,0:T(8,128)S(1)}, u32[]{:S(2)}, u32[]{:S(2)}) collective-permute-start(f32[8,32,128]{2,1,0:T(8,128)S(1)} %get-tuple-element.41), channel_id=1, source_target_pairs={{1,2},{2,1},{3,4},{4,3},{5,6},{6,5},{9,10},{10,9},{11,12},{12,11},... | collective-permute-start | bytes 393224 | tf_op jit(solution)/shard_map/ppermute | solution.py:393
  14.0 7.3 %collective-permute-start = (f32[8,64,128]{2,1,0:T(8,128)S(1)}, f32[8,64,128]{2,1,0:T(8,128)S(1)}, u32[]{:S(2)}, u32[]{:S(2)}) collective-permute-start(f32[8,64,128]{2,1,0:T(8,128)S(1)} %get-tuple-element.38), channel_id=1, source_target_pairs={{0,8},{8,0},{16,24},{24,16},{32,40},{40,32},{48,56},{56,48},{1,9},... | collective-permute-start | bytes 786440 | tf_op jit(solution)/shard_map/ppermute | solution.py:393
  14.1 17.8 %collective-permute-start.1 = (f32[8,64,128]{2,1,0:T(8,128)S(1)}, f32[8,64,128]{2,1,0:T(8,128)S(1)}, u32[]{:S(2)}, u32[]{:S(2)}) collective-permute-start(f32[8,64,128]{2,1,0:T(8,128)S(1)} %get-tuple-element.39), channel_id=1, source_target_pairs={{8,16},{16,8},{24,32},{32,24},{40,48},{48,40},{9,17},{17,9},{25,33... | collective-permute-start | bytes 786440 | tf_op jit(solution)/shard_map/ppermute | solution.py:393
  20.7 32.3 %collective-permute-start.10 = (f32[16,64,128]{2,1,0:T(8,128)S(1)}, f32[16,64,128]{2,1,0:T(8,128)S(1)}, u32[]{:S(2)}, u32[]{:S(2)}) collective-permute-start(f32[16,64,128]{2,1,0:T(8,128)S(1)} %shard_map.51.after.rest_1_.pa), channel_id=1, source_target_pairs={{0,64},{64,0},{1,65},{65,1},{2,66},{66,2},{3,67},{67,3},{4,68},{68... | collective-permute-start | bytes 1572872 | tf_op jit(solution)/shard_map/ppermute | solution.py:435
  38.4 26.5 %collective-permute-start.11 = (f32[16,64,128]{2,1,0:T(8,128)S(1)}, f32[16,64,128]{2,1,0:T(8,128)S(1)}, u32[]{:S(2)}, u32[]{:S(2)}) collective-permute-start(f32[16,64,128]{2,1,0:T(8,128)S(1)} %get-tuple-element.45.pb), channel_id=1, source_target_pairs={{0,64},{64,0},{1,65},{65,1},{2,66},{66,2},{3,67},{67,3},{4,68},{68... | collective-permute-start | bytes 1572872 | tf_op jit(solution)/shard_map/ppermute | solution.py:453
  40.3 7.1 %collective-permute-start.8 = (f32[8,32,128]{2,1,0:T(8,128)S(1)}, f32[8,32,128]{2,1,0:T(8,128)S(1)}, u32[]{:S(2)}, u32[]{:S(2)}) collective-permute-start(f32[8,32,128]{2,1,0:T(8,128)S(1)} %get-tuple-element.48), channel_id=1, source_target_pairs={{0,1},{1,0},{2,3},{3,2},{4,5},{5,4},{6,7},{7,6},{8,9},{9,8},{10,11... | collective-permute-start | bytes 393224 | tf_op jit(solution)/shard_map/ppermute | solution.py:393
  41.8 11.1 %collective-permute-start.9 = (f32[8,32,128]{2,1,0:T(8,128)S(1)}, f32[8,32,128]{2,1,0:T(8,128)S(1)}, u32[]{:S(2)}, u32[]{:S(2)}) collective-permute-start(f32[8,32,128]{2,1,0:T(8,128)S(1)} %get-tuple-element.49), channel_id=1, source_target_pairs={{1,2},{2,1},{3,4},{4,3},{5,6},{6,5},{9,10},{10,9},{11,12},{12,11},... | collective-permute-start | bytes 393224 | tf_op jit(solution)/shard_map/ppermute | solution.py:393
  45.6 7.8 %collective-permute-start.6 = (f32[8,64,128]{2,1,0:T(8,128)S(1)}, f32[8,64,128]{2,1,0:T(8,128)S(1)}, u32[]{:S(2)}, u32[]{:S(2)}) collective-permute-start(f32[8,64,128]{2,1,0:T(8,128)S(1)} %get-tuple-element.46), channel_id=1, source_target_pairs={{0,8},{8,0},{16,24},{24,16},{32,40},{40,32},{48,56},{56,48},{1,9},... | collective-permute-start | bytes 786440 | tf_op jit(solution)/shard_map/ppermute | solution.py:393
  47.4 13.6 %collective-permute-start.7 = (f32[8,64,128]{2,1,0:T(8,128)S(1)}, f32[8,64,128]{2,1,0:T(8,128)S(1)}, u32[]{:S(2)}, u32[]{:S(2)}) collective-permute-start(f32[8,64,128]{2,1,0:T(8,128)S(1)} %get-tuple-element.47), channel_id=1, source_target_pairs={{8,16},{16,8},{24,32},{32,24},{40,48},{48,40},{9,17},{17,9},{25,33... | collective-permute-start | bytes 786440 | tf_op jit(solution)/shard_map/ppermute | solution.py:393
  53.3 26.8 %collective-permute-start.16 = (f32[16,64,128]{2,1,0:T(8,128)S(1)}, f32[16,64,128]{2,1,0:T(8,128)S(1)}, u32[]{:S(2)}, u32[]{:S(2)}) collective-permute-start(f32[16,64,128]{2,1,0:T(8,128)S(1)} %shard_map.54.after.rest_1_.pa), channel_id=1, source_target_pairs={{0,64},{64,0},{1,65},{65,1},{2,66},{66,2},{3,67},{67,3},{4,68},{68... | collective-permute-start | bytes 1572872 | tf_op jit(solution)/shard_map/ppermute | solution.py:435
  65.5 27.5 %collective-permute-start.17 = (f32[16,64,128]{2,1,0:T(8,128)S(1)}, f32[16,64,128]{2,1,0:T(8,128)S(1)}, u32[]{:S(2)}, u32[]{:S(2)}) collective-permute-start(f32[16,64,128]{2,1,0:T(8,128)S(1)} %get-tuple-element.52.pb), channel_id=1, source_target_pairs={{0,64},{64,0},{1,65},{65,1},{2,66},{66,2},{3,67},{67,3},{4,68},{68... | collective-permute-start | bytes 1572872 | tf_op jit(solution)/shard_map/ppermute | solution.py:453
  67.3 6.2 %collective-permute-start.14 = (f32[8,32,128]{2,1,0:T(8,128)S(1)}, f32[8,32,128]{2,1,0:T(8,128)S(1)}, u32[]{:S(2)}, u32[]{:S(2)}) collective-permute-start(f32[8,32,128]{2,1,0:T(8,128)S(1)} %get-tuple-element.55), channel_id=1, source_target_pairs={{0,1},{1,0},{2,3},{3,2},{4,5},{5,4},{6,7},{7,6},{8,9},{9,8},{10,11... | collective-permute-start | bytes 393224 | tf_op jit(solution)/shard_map/ppermute | solution.py:393
  68.9 11.2 %collective-permute-start.15 = (f32[8,32,128]{2,1,0:T(8,128)S(1)}, f32[8,32,128]{2,1,0:T(8,128)S(1)}, u32[]{:S(2)}, u32[]{:S(2)}) collective-permute-start(f32[8,32,128]{2,1,0:T(8,128)S(1)} %get-tuple-element.56), channel_id=1, source_target_pairs={{1,2},{2,1},{3,4},{4,3},{5,6},{6,5},{9,10},{10,9},{11,12},{12,11},... | collective-permute-start | bytes 393224 | tf_op jit(solution)/shard_map/ppermute | solution.py:393
  72.9 7.9 %collective-permute-start.12 = (f32[8,64,128]{2,1,0:T(8,128)S(1)}, f32[8,64,128]{2,1,0:T(8,128)S(1)}, u32[]{:S(2)}, u32[]{:S(2)}) collective-permute-start(f32[8,64,128]{2,1,0:T(8,128)S(1)} %get-tuple-element.53), channel_id=1, source_target_pairs={{0,8},{8,0},{16,24},{24,16},{32,40},{40,32},{48,56},{56,48},{1,9},... | collective-permute-start | bytes 786440 | tf_op jit(solution)/shard_map/ppermute | solution.py:393
  73.5 15.6 %collective-permute-start.13 = (f32[8,64,128]{2,1,0:T(8,128)S(1)}, f32[8,64,128]{2,1,0:T(8,128)S(1)}, u32[]{:S(2)}, u32[]{:S(2)}) collective-permute-start(f32[8,64,128]{2,1,0:T(8,128)S(1)} %get-tuple-element.54), channel_id=1, source_target_pairs={{8,16},{16,8},{24,32},{32,24},{40,48},{48,40},{9,17},{17,9},{25,33... | collective-permute-start | bytes 786440 | tf_op jit(solution)/shard_map/ppermute | solution.py:393
  80.3 28.9 %collective-permute-start.22 = (f32[16,64,128]{2,1,0:T(8,128)S(1)}, f32[16,64,128]{2,1,0:T(8,128)S(1)}, u32[]{:S(2)}, u32[]{:S(2)}) collective-permute-start(f32[16,64,128]{2,1,0:T(8,128)S(1)} %shard_map.57.after.rest_1_.pa), channel_id=1, source_target_pairs={{0,64},{64,0},{1,65},{65,1},{2,66},{66,2},{3,67},{67,3},{4,68},{68... | collective-permute-start | bytes 1572872 | tf_op jit(solution)/shard_map/ppermute | solution.py:435
  93.5 16.0 %collective-permute-start.18 = (f32[8,64,128]{2,1,0:T(8,128)S(1)}, f32[8,64,128]{2,1,0:T(8,128)S(1)}, u32[]{:S(2)}, u32[]{:S(2)}) collective-permute-start(f32[8,64,128]{2,1,0:T(8,128)S(1)} %get-tuple-element.58), channel_id=1, source_target_pairs={{0,8},{8,0},{16,24},{24,16},{32,40},{40,32},{48,56},{56,48},{1,9},... | collective-permute-start | bytes 786440 | tf_op jit(solution)/shard_map/ppermute | solution.py:393
  93.6 15.9 %collective-permute-start.19 = (f32[8,64,128]{2,1,0:T(8,128)S(1)}, f32[8,64,128]{2,1,0:T(8,128)S(1)}, u32[]{:S(2)}, u32[]{:S(2)}) collective-permute-start(f32[8,64,128]{2,1,0:T(8,128)S(1)} %get-tuple-element.59), channel_id=1, source_target_pairs={{8,16},{16,8},{24,32},{32,24},{40,48},{48,40},{9,17},{17,9},{25,33... | collective-permute-start | bytes 786440 | tf_op jit(solution)/shard_map/ppermute | solution.py:393
  96.3 5.7 %collective-permute-start.20 = (f32[8,32,128]{2,1,0:T(8,128)S(1)}, f32[8,32,128]{2,1,0:T(8,128)S(1)}, u32[]{:S(2)}, u32[]{:S(2)}) collective-permute-start(f32[8,32,128]{2,1,0:T(8,128)S(1)} %get-tuple-element.60), channel_id=1, source_target_pairs={{0,1},{1,0},{2,3},{3,2},{4,5},{5,4},{6,7},{7,6},{8,9},{9,8},{10,11... | collective-permute-start | bytes 393224 | tf_op jit(solution)/shard_map/ppermute | solution.py:393
  98.0 11.3 %collective-permute-start.21 = (f32[8,32,128]{2,1,0:T(8,128)S(1)}, f32[8,32,128]{2,1,0:T(8,128)S(1)}, u32[]{:S(2)}, u32[]{:S(2)}) collective-permute-start(f32[8,32,128]{2,1,0:T(8,128)S(1)} %get-tuple-element.61), channel_id=1, source_target_pairs={{1,2},{2,1},{3,4},{4,3},{5,6},{6,5},{9,10},{10,9},{11,12},{12,11},... | collective-permute-start | bytes 393224 | tf_op jit(solution)/shard_map/ppermute | solution.py:393
  102.0 28.2 %collective-permute-start.27 = (f32[16,64,128]{2,1,0:T(8,128)S(1)}, f32[16,64,128]{2,1,0:T(8,128)S(1)}, u32[]{:S(2)}, u32[]{:S(2)}) collective-permute-start(f32[16,64,128]{2,1,0:T(8,128)S(1)} %get-tuple-element.57.pb), channel_id=1, source_target_pairs={{0,64},{64,0},{1,65},{65,1},{2,66},{66,2},{3,67},{67,3},{4,68},{68... | collective-permute-start | bytes 1572872 | tf_op jit(solution)/shard_map/ppermute | solution.py:453
  114.8 1.6 %collective-permute-start.23 = (f32[7,64,128]{2,1,0:T(8,128)S(1)}, f32[7,64,128]{2,1,0:T(8,128)S(1)}, u32[]{:S(2)}, u32[]{:S(2)}) collective-permute-start(f32[7,64,128]{2,1,0:T(8,128)S(1)} %get-tuple-element.63.total), channel_id=1, source_target_pairs={{0,8},{8,0},{16,24},{24,16},{32,40},{40,32},{48,56},{56,48},{1,9},... | collective-permute-start | bytes 688136 | tf_op jit(solution)/shard_map/ppermute | solution.py:405
  116.4 7.0 %collective-permute-start.24 = (f32[7,32,128]{2,1,0:T(8,128)S(1)}, f32[7,32,128]{2,1,0:T(8,128)S(1)}, u32[]{:S(2)}, u32[]{:S(2)}) collective-permute-start(f32[7,32,128]{2,1,0:T(8,128)S(1)} %shard_map.62), channel_id=1, source_target_pairs={{0,16},{8,24},{16,0},{24,8},{32,48},{40,56},{48,32},{56,40},{1,17}... | collective-permute-start | bytes 344072 | tf_op jit(solution)/shard_map/ppermute | solution.py:405
  123.4 6.7 %collective-permute-start.25 = (f32[7,32,128]{2,1,0:T(8,128)S(1)}, f32[7,32,128]{2,1,0:T(8,128)S(1)}, u32[]{:S(2)}, u32[]{:S(2)}) collective-permute-start(f32[7,32,128]{2,1,0:T(8,128)S(1)} %add.10), channel_id=1, source_target_pairs={{0,32},{8,40},{16,48},{24,56},{1,33},{9,41},{17,49},{25,57},{2,34}... | collective-permute-start | bytes 344072 | tf_op jit(solution)/shard_map/ppermute | solution.py:405
  130.1 13.1 %collective-permute-start.26 = (f32[7,32,128]{2,1,0:T(8,128)S(1)}, f32[7,32,128]{2,1,0:T(8,128)S(1)}, u32[]{:S(2)}, u32[]{:S(2)}) collective-permute-start(f32[7,32,128]{2,1,0:T(8,128)S(1)} %shard_map.63.before), channel_id=1, source_target_pairs={{0,8},{8,0},{16,24},{24,16},{32,40},{40,32},{48,56},{56,48},{1,9},... | collective-permute-start | bytes 344072 | tf_op jit(solution)/shard_map/ppermute | solution.py:476
  130.6 1.4 collective-permute-start.28
  132.0 5.4 %collective-permute-start.29 = (f32[64,128]{1,0:T(8,128)S(1)}, f32[64,128]{1,0:T(8,128)S(1)}, u32[]{:S(2)}, u32[]{:S(2)}) collective-permute-start(f32[64,128]{1,0:T(8,128)S(1)} %add.11), channel_id=1, source_target_pairs={{0,16},{8,24},{16,0},{24,8},{32,48},{40,56},{48,32},{56,40},{1,17}... | collective-permute-start | bytes 98312 | tf_op jit(solution)/shard_map/ppermute | solution.py:405
  137.5 5.8 %collective-permute-start.30 = (f32[64,128]{1,0:T(8,128)S(1)}, f32[64,128]{1,0:T(8,128)S(1)}, u32[]{:S(2)}, u32[]{:S(2)}) collective-permute-start(f32[64,128]{1,0:T(8,128)S(1)} %add.12), channel_id=1, source_target_pairs={{0,32},{8,40},{16,48},{24,56},{1,33},{9,41},{17,49},{25,57},{2,34}... | collective-permute-start | bytes 98312 | tf_op jit(solution)/shard_map/ppermute | solution.py:405

commit v7 on v5

--- a/solution.py
+++ b/solution.py
@@ -279,19 +279,21 @@
     total[...] = carry
 
 
-def earlier(others):
-    lon = lax.axis_index("lon")
-    before = 0.0
-    for bit, other in enumerate(others):
-        before += jnp.where(lon & (1 << bit) != 0, other, 0.0)
-    return before
-
-
-def half_kernel(total, other, out):
+def low_pair():
+    return lax.axis_index("lon") & 2 == 0
+
+
+def half_kernel(total, other, out, low):
     n = out.shape[1]
     at = pl.ds(pl.multiple_of(jnp.where(odd("lon"), n, 0), n), n)
     for p in range(out.shape[0]):
         out[p] = total[p, at] + other[p, at]
+        low[p] = jnp.where(low_pair(), out[p], 0.0)
+
+
+def pair_kernel(total, other, out, low):
+    out[...] = total[...] + other[...]
+    low[...] = jnp.where(low_pair(), out[...], 0.0)
 
 
 def total_rows(scale, ni, sums, before, put):
@@ -314,7 +316,7 @@
 
     def body(depth, _):
         j = plane_at(depth, nj)
-        b = before[depth - 1] + earlier([other[depth - 1, at]])
+        b = before[depth - 1] + jnp.where(odd("lon"), other[depth - 1, at], 0.0)
 
         def put(i, value):
             stage[depth - 1, i] = value
@@ -327,14 +329,8 @@
     return [copy_out(depth) for depth in range(1, nj)]
 
 
-def totals_kernel(scale, sums, other, before, after, out, stage, sem):
-    del after
-    for copy in half_totals(scale, odd("lon"), sums, other, before, out, stage, sem):
-        copy.wait()
-
-
-def last_totals_kernel(scale, sums, other, before, npa, npb, edge_sums, *rest):
-    *others, _, _, end, out, stage, edge_stage, sem, edge_sem = rest
+def totals_kernel(scale, sums, other, before, npa, npb, end_in, end, out, stage, sem, edge_sem):
+    del end_in
     nj, ni = sums.shape[:2]
     q = ni // 4
     pj = plane_at(0, nj)
@@ -342,17 +338,27 @@
         pltpu.make_async_copy(npb.at[pl.ds(0, q)], end.at[pj, pl.ds(0, q)], edge_sem.at[0]),
         pltpu.make_async_copy(npa, end.at[pj, pl.ds(q, 2 * q)], edge_sem.at[1]),
         pltpu.make_async_copy(npb.at[pl.ds(q, q)], end.at[pj, pl.ds(3 * q, q)], edge_sem.at[2]),
-        pltpu.make_async_copy(edge_stage, out.at[pj], edge_sem.at[3]),
     ]
-    for copy in copies[:3]:
+    for copy in copies:
         copy.start()
-    copies += half_totals(scale, jnp.logical_not(odd("lon")), sums, other, before, out, stage, sem)
+    copies += half_totals(scale, odd("lon"), sums, other, before, out, stage, sem)
+    for copy in copies:
+        copy.wait()
+
+
+def last_totals_kernel(scale, sums, other, before, edge_sums, edge_other, edge_before, out_in, out, stage, edge_stage, sem, edge_sem):
+    del out_in
+    nj, ni = sums.shape[:2]
+    pj = plane_at(0, nj)
 
     def put(i, value):
         edge_stage[i] = value
 
-    total_rows(scale, ni, lambda i: edge_sums[i], earlier([other[...] for other in others]), put)
-    copies[3].start()
+    b = edge_before[...] + jnp.where(odd("lon"), edge_other[...], 0.0)
+    total_rows(scale, ni, lambda i: edge_sums[i], b, put)
+    copies = [pltpu.make_async_copy(edge_stage, out.at[pj], edge_sem)]
+    copies[0].start()
+    copies += half_totals(scale, jnp.logical_not(odd("lon")), sums, other, before, out, stage, sem)
     for copy in copies:
         copy.wait()
 
@@ -392,13 +398,15 @@
     def lev_exchange(e, o):
         return exchange("lev", lev_size, e, o)
 
-    def partner(bit, total):
-        pairs = [(i, i ^ (1 << bit)) for i in range(lon_size)]
-        if 2 << bit == lon_size:
-            pairs = [(a, b) for a, b in pairs if a < b]
-        return lax.ppermute(total, "lon", pairs)
-
-    bits = lon_size.bit_length() - 1
+    core_swap = [(i, i ^ 1) for i in range(lon_size)]
+
+    def earlier(kernel, total, other, shape):
+        total, low = call(kernel, (V(*shape),) * 2, (VMEM,) * 2, (VMEM,) * 2, flops=10**5)(
+            in_vmem(total), in_vmem(other)
+        )
+        far = lax.ppermute(total, "lon", [(i, i + 4) for i in range(4)])
+        near = lax.ppermute(low + far, "lon", [(i, i ^ 2) for i in range(lon_size) if i & 2 == 0 or i & 4])
+        return far + near
 
     pj = jnp.where(lax.axis_index("lat") == 0, nj - 1, 0)
     pa = lax.dynamic_slice(initial_state, (pj, ni // 4, 0, 0), (1, half, nk, nm))[0]
@@ -458,53 +466,45 @@
         aliases={7: 1, 8: 2},
         flops=2 * 10**7,
     )(u, pa, pb, *lon, *lev, in_vmem(d), in_vmem(f), n_pa)
-    other = partner(0, total)
-    half_total = call(half_kernel, V(nj - 1, nk // 2, nm), VMEM, (VMEM,) * 2, flops=10**5)(
-        in_vmem(total), in_vmem(other)
-    )
-    pairs = lon_size // 2
-    mine = []
-    for steps in sorted(range(1, pairs), key=lambda steps: (steps % 2 == 0, steps)):
-        to = [(2 * a + c, 2 * (a ^ steps) + c) for a in range(pairs) if a < a ^ steps for c in (0, 1)]
-        mine.append(lax.ppermute(half_total, "lon", to))
-    mine = functools.reduce(jnp.add, mine)
-    back = lax.ppermute(mine, "lon", [(i, i ^ 1) for i in range(lon_size)])
+    other = lax.ppermute(total, "lon", core_swap)
+    mine = earlier(half_kernel, total, other, (nj - 1, nk // 2, nm))
+    back = lax.ppermute(mine, "lon", core_swap)
     n_pa = in_vmem(n_pa)
     n_pb, edge_sums, edge_total = call(
         last_edge_kernel, (V(half, nk, nm), V(ni, nk, nm), V(nk, nm)), (VMEM,) * 3, (VMEM,) * 11, flops=2 * 10**6
     )(u, pa, pb, lat_b, *lon, *lev, d_edge, f_edge, n_pa)
-    others = []
-    edge_total_1 = edge_total
-    for bit in range(bits):
-        others.append(partner(bit, edge_total))
-        edge_total = edge_total + others[-1]
-    others = tuple(map(in_vmem, others))
+    edge_other = lax.ppermute(edge_total, "lon", core_swap)
+    edge_before = earlier(pair_kernel, edge_total, edge_other, (nk, nm))
     sums, other = in_vmem(sums), in_vmem(other)
+    end, out = call(
+        functools.partial(totals_kernel, scale),
+        (H(nj, ni, nk, nm),) * 2,
+        (HBM, HBM),
+        (VMEM,) * 5 + (HBM,),
+        limit=5,
+        scratch=(
+            V(nj - 1, ni, nk // 2, nm),
+            pltpu.SemaphoreType.DMA((nj - 1,)),
+            pltpu.SemaphoreType.DMA((3,)),
+        ),
+        aliases={5: 0},
+        flops=10**6,
+    )(sums, other, in_vmem(mine), n_pa, in_vmem(n_pb), in_hbm(end))
     out = call(
-        functools.partial(totals_kernel, scale),
+        functools.partial(last_totals_kernel, scale),
         H(nj, ni, nk, nm),
         HBM,
-        (VMEM,) * 3 + (ANY,),
-        limit=5,
-        scratch=(V(nj - 1, ni, nk // 2, nm), pltpu.SemaphoreType.DMA((nj - 1,))),
-        flops=10**6,
-    )(sums, other, in_vmem(mine), edge_total_1)
-    n = 6 + bits
-    end, out = call(
-        functools.partial(last_totals_kernel, scale),
-        (H(nj, ni, nk, nm),) * 2,
-        (HBM, HBM),
-        (VMEM,) * n + (HBM, HBM),
+        (VMEM,) * 6 + (HBM,),
         scratch=(
             V(nj - 1, ni, nk // 2, nm),
             V(ni, nk, nm),
             pltpu.SemaphoreType.DMA((nj - 1,)),
-            pltpu.SemaphoreType.DMA((4,)),
+            pltpu.SemaphoreType.DMA,
         ),
         limit=6,
-        aliases={n: 0, n + 1: 1},
+        aliases={6: 0},
         flops=10**6,
-    )(sums, other, in_vmem(back), n_pa, in_vmem(n_pb), in_vmem(edge_sums), *others, in_hbm(end), in_hbm(out))
+    )(sums, other, *map(in_vmem, (back, edge_sums, edge_other, edge_before)), in_hbm(out))
     return out, end
 
 

time: 151 us -> 153 us (1.013)
  starting transfers between devices: 52.8 us -> 55.6 us
    ppermute x16, waiting for transfers between devices: 44.9 us -> 42.2 us  [exchange(): return (lax.ppermute(e, axis, swaps(0)), lax.ppermute(o, axis, swaps(1)))]
    ppermute x8 -> x7, waiting for transfers between devices: 18.7 us -> 20.4 us  [the longest x2 10.5 us: earlier(): far = lax.ppermute(total, 'lon', [(i, i + 4) for i in range(4)])]
    ppermute x8 -> x7, starting transfers between devices: 9.68 us -> 11.3 us  [the longest x2 7.55 us: earlier(): lax.ppermute(low + far, 'lon', [(i, i ^ 2) for i in range(lon_size) if i...]
    pallas_call x3 -> x4, Pallas kernels: 4.62 us -> 4.66 us  [the longest x1 2.37 us: per_device(): call(functools.partial(last_totals_kernel, scale), H(nj, ni, nk, nm), HBM...]
  transfers between devices with their start and end apart: 32 -> 31, of which waited for: 12 -> 13; matrix products, arithmetic and copies ran while one was open for 0% -> 0% of each run, Pallas kernels for 16% -> 19%
where the time goes in v7:
time: 153 us; the launch traced here: 152 us
  waiting for transfers between devices  62.7 us (41%)
  starting transfers between devices  55.6 us (36%)
  Pallas kernels  31.5 us (21%)
    ppermute x16, waiting for transfers between devices, exchange(): return (lax.ppermute(e, axis, swaps(0)), lax.ppermute(o, axis, swaps(1)))  42.2 us
    ppermute x16, starting transfers between devices, exchange(): return (lax.ppermute(e, axis, swaps(0)), lax.ppermute(o, axis, swaps(1)))  34.4 us
    ppermute x2, waiting for transfers between devices, earlier(): far = lax.ppermute(total, 'lon', [(i, i + 4) for i in range(4)])  10.5 us
    pallas_call x2, Pallas kernels, per_device(): call(bulk_kernel, V(nj, ni, nk, nm), VMEM, (VMEM,) * 9 + (ANY,), flops=2...  8.05 us
    ppermute x2, waiting for transfers between devices, earlier(): lax.ppermute(low + far, 'lon', [(i, i ^ 2) for i in range(lon_size) if i...  7.93 us
    ppermute x2, starting transfers between devices, earlier(): lax.ppermute(low + far, 'lon', [(i, i ^ 2) for i in range(lon_size) if i...  7.55 us
    ppermute x3, starting transfers between devices, per_device(): lat_b = lax.ppermute(n_pb, 'lat', swap)  6.48 us
    pallas_call x1, Pallas kernels, per_device(): call(first_bulk_kernel, (V(nj, ni, nk, nm),) * 3, (VMEM,) * 3, (VMEM,) *...  5.89 us
  transfers between devices with their start and end apart: 31, of which 13 were waited for; matrix products, arithmetic and copies ran while one was open for 0% of the time, Pallas kernels for 19%

profile of v7, /device:TPU:98, one launch (start us, length us, event | category | flops | bytes accessed | tf_op | source)
XLA Modules:
  0.0 151.9 jit_solution(12892146688311826014)
XLA Ops:
  0.6 1.1 dynamic-slice_bitcast_fusion.pa
  1.7 0.6 collective-permute-start.4
  2.3 4.4 %shard_map.50 = (f32[8,32,64,128]{3,2,1,0:T(8,128)S(1)}, f32[16,64,128]{2,1,0:T(8,128)S(1)}, f32[32,64,128]{2,1,0:T(8,128)S(1)}, f32[32,64,128]{2,1,0:T(8,128)S(...) custom-call(f32[8,32,64,128]{3,2,1,0:T(8,128)} %u_in.1, ...), custom_call_target="tpu_custom_call" | custom-call | flops 1000000 | tf_op jit(solution)/shard_map/pallas_call | solution.py:414
  6.8 1.6 %collective-permute-start.5 = (f32[16,64,128]{2,1,0:T(8,128)S(1)}, f32[16,64,128]{2,1,0:T(8,128)S(1)}, u32[]{:S(2)}, u32[]{:S(2)}) collective-permute-start(f32[16,64,128]{2,1,0:T(8,128)S(1)} %get-tuple-element.41.pb), channel_id=1, source_target_pairs={{0,64},{64,0},{1,65},{65,1},{2,66},{66,2},{3,67},{67,3},{4,68},{68... | collective-permute-start | bytes 1572872 | tf_op jit(solution)/shard_map/ppermute | solution.py:424
  8.4 1.6 %collective-permute-start.2 = (f32[8,32,128]{2,1,0:T(8,128)S(1)}, f32[8,32,128]{2,1,0:T(8,128)S(1)}, u32[]{:S(2)}, u32[]{:S(2)}) collective-permute-start(f32[8,32,128]{2,1,0:T(8,128)S(1)} %get-tuple-element.44), channel_id=1, source_target_pairs={{0,1},{1,0},{2,3},{3,2},{4,5},{5,4},{6,7},{7,6},{8,9},{9,8},{10,11... | collective-permute-start | bytes 393224 | tf_op jit(solution)/shard_map/ppermute | solution.py:393
  9.9 4.1 %collective-permute-start.3 = (f32[8,32,128]{2,1,0:T(8,128)S(1)}, f32[8,32,128]{2,1,0:T(8,128)S(1)}, u32[]{:S(2)}, u32[]{:S(2)}) collective-permute-start(f32[8,32,128]{2,1,0:T(8,128)S(1)} %get-tuple-element.45), channel_id=1, source_target_pairs={{1,2},{2,1},{3,4},{4,3},{5,6},{6,5},{9,10},{10,9},{11,12},{12,11},... | collective-permute-start | bytes 393224 | tf_op jit(solution)/shard_map/ppermute | solution.py:393
  14.0 0.1 collective-permute-start
  14.1 0.0 collective-permute-done.2.lev_e
  14.1 3.1 %collective-permute-start.1 = (f32[8,64,128]{2,1,0:T(8,128)S(1)}, f32[8,64,128]{2,1,0:T(8,128)S(1)}, u32[]{:S(2)}, u32[]{:S(2)}) collective-permute-start(f32[8,64,128]{2,1,0:T(8,128)S(1)} %get-tuple-element.43), channel_id=1, source_target_pairs={{8,16},{16,8},{24,32},{32,24},{40,48},{48,40},{9,17},{17,9},{25,33... | collective-permute-start | bytes 786440 | tf_op jit(solution)/shard_map/ppermute | solution.py:393
  17.2 3.2 %collective-permute-done.3.lev_o = f32[8,32,128]{2,1,0:T(8,128)S(1)} collective-permute-done((f32[8,32,128]{2,1,0:T(8,128)S(1)}, f32[8,32,128]{2,1,0:T(8,128)S(1)}, u32[]{:S(2)}, u32[]{:S(2)}) %collective-permute-start.3) | collective-permute-done | bytes 131104 | tf_op jit(solution)/shard_map/ppermute | solution.py:393
  20.4 0.0 collective-permute-done.4.lat
  20.4 0.3 shard_map.51.after.rest_1_.pa
  20.7 0.6 collective-permute-start.10
  21.3 10.7 %collective-permute-done.1.lon_o = f32[8,64,128]{2,1,0:T(8,128)S(1)} collective-permute-done((f32[8,64,128]{2,1,0:T(8,128)S(1)}, f32[8,64,128]{2,1,0:T(8,128)S(1)}, u32[]{:S(2)}, u32[]{:S(2)}) %collective-permute-start.1) | collective-permute-done | bytes 262176 | tf_op jit(solution)/shard_map/ppermute | solution.py:393
  32.0 5.9 %shard_map.52 = (f32[8,32,64,128]{3,2,1,0:T(8,128)S(1)}, f32[8,32,64,128]{3,2,1,0:T(8,128)S(1)}, f32[8,32,64,128]{3,2,1,0:T(8,128)S(1)}) custom-call(f32[8,32,64,128]{3,2,1,0:T(8,128)S(1)} %get-tuple-element.40.u, f32[16,64,128]{2,1,0:T(8,128)S(1)} %dynamic-slice_bitcast_fusion.pa, f32[16,64,128]{2,1,0:T(8,128)S(1)} %get-tuple-element.41.pb, ...), custom_call_target="tpu_custom_call" | custom-call | flops 20000000 | tf_op jit(solution)/shard_map/pallas_call | solution.py:439
  37.9 0.0 collective-permute-done.5.lat
  37.9 0.6 shard_map.53
  38.4 1.9 %collective-permute-start.11 = (f32[16,64,128]{2,1,0:T(8,128)S(1)}, f32[16,64,128]{2,1,0:T(8,128)S(1)}, u32[]{:S(2)}, u32[]{:S(2)}) collective-permute-start(f32[16,64,128]{2,1,0:T(8,128)S(1)} %get-tuple-element.49.pb), channel_id=1, source_target_pairs={{0,64},{64,0},{1,65},{65,1},{2,66},{66,2},{3,67},{67,3},{4,68},{68... | collective-permute-start | bytes 1572872 | tf_op jit(solution)/shard_map/ppermute | solution.py:455
  40.3 1.6 %collective-permute-start.8 = (f32[8,32,128]{2,1,0:T(8,128)S(1)}, f32[8,32,128]{2,1,0:T(8,128)S(1)}, u32[]{:S(2)}, u32[]{:S(2)}) collective-permute-start(f32[8,32,128]{2,1,0:T(8,128)S(1)} %get-tuple-element.52), channel_id=1, source_target_pairs={{0,1},{1,0},{2,3},{3,2},{4,5},{5,4},{6,7},{7,6},{8,9},{9,8},{10,11... | collective-permute-start | bytes 393224 | tf_op jit(solution)/shard_map/ppermute | solution.py:393
  41.9 3.8 %collective-permute-start.9 = (f32[8,32,128]{2,1,0:T(8,128)S(1)}, f32[8,32,128]{2,1,0:T(8,128)S(1)}, u32[]{:S(2)}, u32[]{:S(2)}) collective-permute-start(f32[8,32,128]{2,1,0:T(8,128)S(1)} %get-tuple-element.53), channel_id=1, source_target_pairs={{1,2},{2,1},{3,4},{4,3},{5,6},{6,5},{9,10},{10,9},{11,12},{12,11},... | collective-permute-start | bytes 393224 | tf_op jit(solution)/shard_map/ppermute | solution.py:393
  45.7 1.8 %collective-permute-start.6 = (f32[8,64,128]{2,1,0:T(8,128)S(1)}, f32[8,64,128]{2,1,0:T(8,128)S(1)}, u32[]{:S(2)}, u32[]{:S(2)}) collective-permute-start(f32[8,64,128]{2,1,0:T(8,128)S(1)} %get-tuple-element.50), channel_id=1, source_target_pairs={{0,8},{8,0},{16,24},{24,16},{32,40},{40,32},{48,56},{56,48},{1,9},... | collective-permute-start | bytes 786440 | tf_op jit(solution)/shard_map/ppermute | solution.py:393
  47.4 0.0 collective-permute-done.8.lev_e
  47.4 2.1 %collective-permute-start.7 = (f32[8,64,128]{2,1,0:T(8,128)S(1)}, f32[8,64,128]{2,1,0:T(8,128)S(1)}, u32[]{:S(2)}, u32[]{:S(2)}) collective-permute-start(f32[8,64,128]{2,1,0:T(8,128)S(1)} %get-tuple-element.51), channel_id=1, source_target_pairs={{8,16},{16,8},{24,32},{32,24},{40,48},{48,40},{9,17},{17,9},{25,33... | collective-permute-start | bytes 786440 | tf_op jit(solution)/shard_map/ppermute | solution.py:393
  49.5 3.5 %collective-permute-done.9.lev_o = f32[8,32,128]{2,1,0:T(8,128)S(1)} collective-permute-done((f32[8,32,128]{2,1,0:T(8,128)S(1)}, f32[8,32,128]{2,1,0:T(8,128)S(1)}, u32[]{:S(2)}, u32[]{:S(2)}) %collective-permute-start.9) | collective-permute-done | bytes 131104 | tf_op jit(solution)/shard_map/ppermute | solution.py:393
  53.0 0.3 shard_map.54.after.rest_1_.pa
  53.3 0.1 collective-permute-start.16
  53.5 7.6 %collective-permute-done.7.lon_o = f32[8,64,128]{2,1,0:T(8,128)S(1)} collective-permute-done((f32[8,64,128]{2,1,0:T(8,128)S(1)}, f32[8,64,128]{2,1,0:T(8,128)S(1)}, u32[]{:S(2)}, u32[]{:S(2)}) %collective-permute-start.7) | collective-permute-done | bytes 262176 | tf_op jit(solution)/shard_map/ppermute | solution.py:393
  61.1 4.0 %shard_map.55.rest_0_.u = f32[8,32,64,128]{3,2,1,0:T(8,128)S(1)} custom-call(f32[8,32,64,128]{3,2,1,0:T(8,128)S(1)} %get-tuple-element.48.rest_0_.u, f32[16,64,128]{2,1,0:T(8,128)S(1)} %shard_map.51.after.rest_1_.pa, f32[16,64,128]{2,1,0:T(8,128)S(1)} %get-tuple-element.49.pb, f32[8,64,128]{2,1,0:T(8,128)S(1)} %collective-permute-done.6.lon_e, ...), custom_call_target="tpu_custom_call" | custom-call | flops 20000000 | tf_op jit(solution)/shard_map/pallas_call | solution.py:448
  65.1 0.6 shard_map.56
  65.7 1.8 %collective-permute-start.17 = (f32[16,64,128]{2,1,0:T(8,128)S(1)}, f32[16,64,128]{2,1,0:T(8,128)S(1)}, u32[]{:S(2)}, u32[]{:S(2)}) collective-permute-start(f32[16,64,128]{2,1,0:T(8,128)S(1)} %get-tuple-element.56.pb), channel_id=1, source_target_pairs={{0,64},{64,0},{1,65},{65,1},{2,66},{66,2},{3,67},{67,3},{4,68},{68... | collective-permute-start | bytes 1572872 | tf_op jit(solution)/shard_map/ppermute | solution.py:455
  67.5 1.6 %collective-permute-start.14 = (f32[8,32,128]{2,1,0:T(8,128)S(1)}, f32[8,32,128]{2,1,0:T(8,128)S(1)}, u32[]{:S(2)}, u32[]{:S(2)}) collective-permute-start(f32[8,32,128]{2,1,0:T(8,128)S(1)} %get-tuple-element.59), channel_id=1, source_target_pairs={{0,1},{1,0},{2,3},{3,2},{4,5},{5,4},{6,7},{7,6},{8,9},{9,8},{10,11... | collective-permute-start | bytes 393224 | tf_op jit(solution)/shard_map/ppermute | solution.py:393
  69.1 4.1 %collective-permute-start.15 = (f32[8,32,128]{2,1,0:T(8,128)S(1)}, f32[8,32,128]{2,1,0:T(8,128)S(1)}, u32[]{:S(2)}, u32[]{:S(2)}) collective-permute-start(f32[8,32,128]{2,1,0:T(8,128)S(1)} %get-tuple-element.60), channel_id=1, source_target_pairs={{1,2},{2,1},{3,4},{4,3},{5,6},{6,5},{9,10},{10,9},{11,12},{12,11},... | collective-permute-start | bytes 393224 | tf_op jit(solution)/shard_map/ppermute | solution.py:393
  73.1 0.5 collective-permute-start.12
  73.7 1.9 %collective-permute-start.13 = (f32[8,64,128]{2,1,0:T(8,128)S(1)}, f32[8,64,128]{2,1,0:T(8,128)S(1)}, u32[]{:S(2)}, u32[]{:S(2)}) collective-permute-start(f32[8,64,128]{2,1,0:T(8,128)S(1)} %get-tuple-element.58), channel_id=1, source_target_pairs={{8,16},{16,8},{24,32},{32,24},{40,48},{48,40},{9,17},{17,9},{25,33... | collective-permute-start | bytes 786440 | tf_op jit(solution)/shard_map/ppermute | solution.py:393
  75.6 4.6 %collective-permute-done.15.lev_o = f32[8,32,128]{2,1,0:T(8,128)S(1)} collective-permute-done((f32[8,32,128]{2,1,0:T(8,128)S(1)}, f32[8,32,128]{2,1,0:T(8,128)S(1)}, u32[]{:S(2)}, u32[]{:S(2)}) %collective-permute-start.15) | collective-permute-done | bytes 131104 | tf_op jit(solution)/shard_map/ppermute | solution.py:393
  80.2 0.3 shard_map.57.after.rest_1_.pa
  80.5 0.5 collective-permute-start.22
  80.9 8.2 %collective-permute-done.13.lon_o = f32[8,64,128]{2,1,0:T(8,128)S(1)} collective-permute-done((f32[8,64,128]{2,1,0:T(8,128)S(1)}, f32[8,64,128]{2,1,0:T(8,128)S(1)}, u32[]{:S(2)}, u32[]{:S(2)}) %collective-permute-start.13) | collective-permute-done | bytes 262176 | tf_op jit(solution)/shard_map/ppermute | solution.py:393
  89.2 4.0 %shard_map.58.rest_0_.u = f32[8,32,64,128]{3,2,1,0:T(8,128)S(1)} custom-call(f32[8,32,64,128]{3,2,1,0:T(8,128)S(1)} %shard_map.55.rest_0_.u, f32[16,64,128]{2,1,0:T(8,128)S(1)} %shard_map.54.after.rest_1_.pa, f32[16,64,128]{2,1,0:T(8,128)S(1)} %get-tuple-element.56.pb, f32[8,64,128]{2,1,0:T(8,128)S(1)} %collective-permute-done.12.lon_e, ...), custom_call_target="tpu_custom_call" | custom-call | flops 20000000 | tf_op jit(solution)/shard_map/pallas_call | solution.py:448
  93.2 0.6 shard_map.59
  93.8 0.1 collective-permute-start.18
  93.9 2.6 %collective-permute-start.19 = (f32[8,64,128]{2,1,0:T(8,128)S(1)}, f32[8,64,128]{2,1,0:T(8,128)S(1)}, u32[]{:S(2)}, u32[]{:S(2)}) collective-permute-start(f32[8,64,128]{2,1,0:T(8,128)S(1)} %get-tuple-element.63), channel_id=1, source_target_pairs={{8,16},{16,8},{24,32},{32,24},{40,48},{48,40},{9,17},{17,9},{25,33... | collective-permute-start | bytes 786440 | tf_op jit(solution)/shard_map/ppermute | solution.py:393
  96.4 1.7 %collective-permute-start.20 = (f32[8,32,128]{2,1,0:T(8,128)S(1)}, f32[8,32,128]{2,1,0:T(8,128)S(1)}, u32[]{:S(2)}, u32[]{:S(2)}) collective-permute-start(f32[8,32,128]{2,1,0:T(8,128)S(1)} %get-tuple-element.64), channel_id=1, source_target_pairs={{0,1},{1,0},{2,3},{3,2},{4,5},{5,4},{6,7},{7,6},{8,9},{9,8},{10,11... | collective-permute-start | bytes 393224 | tf_op jit(solution)/shard_map/ppermute | solution.py:393
  98.1 4.1 %collective-permute-start.21 = (f32[8,32,128]{2,1,0:T(8,128)S(1)}, f32[8,32,128]{2,1,0:T(8,128)S(1)}, u32[]{:S(2)}, u32[]{:S(2)}) collective-permute-start(f32[8,32,128]{2,1,0:T(8,128)S(1)} %get-tuple-element.65), channel_id=1, source_target_pairs={{1,2},{2,1},{3,4},{4,3},{5,6},{6,5},{9,10},{10,9},{11,12},{12,11},... | collective-permute-start | bytes 393224 | tf_op jit(solution)/shard_map/ppermute | solution.py:393
  102.2 2.8 %collective-permute-start.27 = (f32[16,64,128]{2,1,0:T(8,128)S(1)}, f32[16,64,128]{2,1,0:T(8,128)S(1)}, u32[]{:S(2)}, u32[]{:S(2)}) collective-permute-start(f32[16,64,128]{2,1,0:T(8,128)S(1)} %get-tuple-element.61.pb), channel_id=1, source_target_pairs={{0,64},{64,0},{1,65},{65,1},{2,66},{66,2},{3,67},{67,3},{4,68},{68... | collective-permute-start | bytes 1572872 | tf_op jit(solution)/shard_map/ppermute | solution.py:455
  104.9 4.4 %collective-permute-done.21.lev_o = f32[8,32,128]{2,1,0:T(8,128)S(1)} collective-permute-done((f32[8,32,128]{2,1,0:T(8,128)S(1)}, f32[8,32,128]{2,1,0:T(8,128)S(1)}, u32[]{:S(2)}, u32[]{:S(2)}) %collective-permute-start.21) | collective-permute-done | bytes 131104 | tf_op jit(solution)/shard_map/ppermute | solution.py:393
  109.3 0.3 shard_map.60.after.npa
  109.6 5.4 %shard_map.61 = (f32[8,32,64,128]{3,2,1,0:T(8,128)}, f32[8,32,64,128]{3,2,1,0:T(8,128)S(1)}, f32[8,32,64,128]{3,2,1,0:T(8,128)S(1)}, f32[7,64,128]{2,1,0:T(8,128)S(1)}) custom-call(f32[8,32,64,128]{3,2,1,0:T(8,128)S(1)} %shard_map.58.rest_0_.u, f32[16,64,128]{2,1,0:T(8,128)S(1)} %shard_map.57.after.rest_1_.pa, ...), custom_call_target="tpu_custom_call", output_to_operand_aliasing={{1}: (7, {}), {2}: (8, {})} | custom-call | flops 20000000 | tf_op jit(solution)/shard_map/pallas_call | solution.py:460
  115.0 0.5 collective-permute-start.23
  115.5 1.1 collective-permute-done.23.other
  116.7 1.3 collective-permute-start.24
  118.0 6.0 %collective-permute-done.24 = f32[7,32,128]{2,1,0:T(8,128)S(1)} collective-permute-done((f32[7,32,128]{2,1,0:T(8,128)S(1)}, f32[7,32,128]{2,1,0:T(8,128)S(1)}, u32[]{:S(2)}, u32[]{:S(2)}) %collective-permute-start.24) | collective-permute-done | bytes 114720 | tf_op jit(solution)/shard_map/ppermute | solution.py:407
  124.0 3.8 %collective-permute-start.25 = (f32[7,32,128]{2,1,0:T(8,128)S(1)}, f32[7,32,128]{2,1,0:T(8,128)S(1)}, u32[]{:S(2)}, u32[]{:S(2)}) collective-permute-start(f32[7,32,128]{2,1,0:T(8,128)S(1)} %add.13), channel_id=1, source_target_pairs={{0,16},{8,24},{32,48},{40,56},{48,32},{56,40},{1,17},{9,25},{33,49... | collective-permute-start | bytes 344072 | tf_op jit(solution)/shard_map/ppermute | solution.py:408
  127.8 4.4 %collective-permute-done.25 = f32[7,32,128]{2,1,0:T(8,128)S(1)} collective-permute-done((f32[7,32,128]{2,1,0:T(8,128)S(1)}, f32[7,32,128]{2,1,0:T(8,128)S(1)}, u32[]{:S(2)}, u32[]{:S(2)}) %collective-permute-start.25) | collective-permute-done | bytes 114720 | tf_op jit(solution)/shard_map/ppermute | solution.py:408
  132.2 0.1 collective-permute-start.26
  132.3 0.4 shard_map.63
  132.7 0.6 collective-permute-start.28
  133.3 0.9 collective-permute-done.28.other.edge_other
  134.1 1.3 collective-permute-start.29
  135.4 4.5 %collective-permute-done.29 = f32[64,128]{1,0:T(8,128)S(1)} collective-permute-done((f32[64,128]{1,0:T(8,128)S(1)}, f32[64,128]{1,0:T(8,128)S(1)}, u32[]{:S(2)}, u32[]{:S(2)}) %collective-permute-start.29) | collective-permute-done | bytes 32800 | tf_op jit(solution)/shard_map/ppermute | solution.py:407
  139.9 3.8 %collective-permute-start.30 = (f32[64,128]{1,0:T(8,128)S(1)}, f32[64,128]{1,0:T(8,128)S(1)}, u32[]{:S(2)}, u32[]{:S(2)}) collective-permute-start(f32[64,128]{1,0:T(8,128)S(1)} %add.15), channel_id=1, source_target_pairs={{0,16},{8,24},{32,48},{40,56},{48,32},{56,40},{1,17},{9,25},{33,49... | collective-permute-start | bytes 98312 | tf_op jit(solution)/shard_map/ppermute | solution.py:408
  143.7 3.5 %collective-permute-done.30 = f32[64,128]{1,0:T(8,128)S(1)} collective-permute-done((f32[64,128]{1,0:T(8,128)S(1)}, f32[64,128]{1,0:T(8,128)S(1)}, u32[]{:S(2)}, u32[]{:S(2)}) %collective-permute-start.30) | collective-permute-done | bytes 32800 | tf_op jit(solution)/shard_map/ppermute | solution.py:408
  147.3 2.3 %shard_map.65 = (f32[8,32,64,128]{3,2,1,0:T(8,128)}, f32[8,32,64,128]{3,2,1,0:T(8,128)}) custom-call(f32[8,32,64,128]{3,2,1,0:T(8,128)S(1)} %get-tuple-element.66.sums, f32[7,64,128]{2,1,0:T(8,128)S(1)} %collective-permute-done.23.other, f32[7,32,128]{2,1,0:T(8,128)S(1)} %add.14.before, ...), custom_call_target="tpu_custom_call", output_to_operand_aliasing={{0}: (5, {})} | custom-call | flops 1000000 | tf_op jit(solution)/shard_map/pallas_call | solution.py:479
  149.5 2.4 %shard_map.66 = f32[8,32,64,128]{3,2,1,0:T(8,128)} custom-call(f32[8,32,64,128]{3,2,1,0:T(8,128)S(1)} %get-tuple-element.66.sums, f32[7,64,128]{2,1,0:T(8,128)S(1)} %collective-permute-done.23.other, f32[7,32,128]{2,1,0:T(8,128)S(1)} %collective-permute-done.26.before, ...), custom_call_target="tpu_custom_call", output_to_operand_aliasing={{}: (6, {})} | custom-call | flops 1000000 | tf_op jit(solution)/shard_map/pallas_call | solution.py:493
  (20 shorter events, 0.1 us)
Async XLA Ops:
  1.7 18.7 %collective-permute-start.4 = (f32[16,64,128]{2,1,0:T(8,128)S(1)}, f32[16,64,128]{2,1,0:T(8,128)S(1)}, u32[]{:S(2)}, u32[]{:S(2)}) collective-permute-start(f32[16,64,128]{2,1,0:T(8,128)S(1)} %dynamic-slice_bitcast_fusion.pa), channel_id=1, source_target_pairs={{0,64},{64,0},{1,65},{65,1},{2,66},{66,2},{3,67},{67,3},{4,68},{68... | collective-permute-start | bytes 1572872 | tf_op jit(solution)/shard_map/ppermute | solution.py:413
  6.8 31.1 %collective-permute-start.5 = (f32[16,64,128]{2,1,0:T(8,128)S(1)}, f32[16,64,128]{2,1,0:T(8,128)S(1)}, u32[]{:S(2)}, u32[]{:S(2)}) collective-permute-start(f32[16,64,128]{2,1,0:T(8,128)S(1)} %get-tuple-element.41.pb), channel_id=1, source_target_pairs={{0,64},{64,0},{1,65},{65,1},{2,66},{66,2},{3,67},{67,3},{4,68},{68... | collective-permute-start | bytes 1572872 | tf_op jit(solution)/shard_map/ppermute | solution.py:424
  8.4 5.7 %collective-permute-start.2 = (f32[8,32,128]{2,1,0:T(8,128)S(1)}, f32[8,32,128]{2,1,0:T(8,128)S(1)}, u32[]{:S(2)}, u32[]{:S(2)}) collective-permute-start(f32[8,32,128]{2,1,0:T(8,128)S(1)} %get-tuple-element.44), channel_id=1, source_target_pairs={{0,1},{1,0},{2,3},{3,2},{4,5},{5,4},{6,7},{7,6},{8,9},{9,8},{10,11... | collective-permute-start | bytes 393224 | tf_op jit(solution)/shard_map/ppermute | solution.py:393
  9.9 10.5 %collective-permute-start.3 = (f32[8,32,128]{2,1,0:T(8,128)S(1)}, f32[8,32,128]{2,1,0:T(8,128)S(1)}, u32[]{:S(2)}, u32[]{:S(2)}) collective-permute-start(f32[8,32,128]{2,1,0:T(8,128)S(1)} %get-tuple-element.45), channel_id=1, source_target_pairs={{1,2},{2,1},{3,4},{4,3},{5,6},{6,5},{9,10},{10,9},{11,12},{12,11},... | collective-permute-start | bytes 393224 | tf_op jit(solution)/shard_map/ppermute | solution.py:393
  14.0 7.3 %collective-permute-start = (f32[8,64,128]{2,1,0:T(8,128)S(1)}, f32[8,64,128]{2,1,0:T(8,128)S(1)}, u32[]{:S(2)}, u32[]{:S(2)}) collective-permute-start(f32[8,64,128]{2,1,0:T(8,128)S(1)} %get-tuple-element.42), channel_id=1, source_target_pairs={{0,8},{8,0},{16,24},{24,16},{32,40},{40,32},{48,56},{56,48},{1,9},... | collective-permute-start | bytes 786440 | tf_op jit(solution)/shard_map/ppermute | solution.py:393
  14.1 17.8 %collective-permute-start.1 = (f32[8,64,128]{2,1,0:T(8,128)S(1)}, f32[8,64,128]{2,1,0:T(8,128)S(1)}, u32[]{:S(2)}, u32[]{:S(2)}) collective-permute-start(f32[8,64,128]{2,1,0:T(8,128)S(1)} %get-tuple-element.43), channel_id=1, source_target_pairs={{8,16},{16,8},{24,32},{32,24},{40,48},{48,40},{9,17},{17,9},{25,33... | collective-permute-start | bytes 786440 | tf_op jit(solution)/shard_map/ppermute | solution.py:393
  20.7 32.3 %collective-permute-start.10 = (f32[16,64,128]{2,1,0:T(8,128)S(1)}, f32[16,64,128]{2,1,0:T(8,128)S(1)}, u32[]{:S(2)}, u32[]{:S(2)}) collective-permute-start(f32[16,64,128]{2,1,0:T(8,128)S(1)} %shard_map.51.after.rest_1_.pa), channel_id=1, source_target_pairs={{0,64},{64,0},{1,65},{65,1},{2,66},{66,2},{3,67},{67,3},{4,68},{68... | collective-permute-start | bytes 1572872 | tf_op jit(solution)/shard_map/ppermute | solution.py:437
  38.4 26.7 %collective-permute-start.11 = (f32[16,64,128]{2,1,0:T(8,128)S(1)}, f32[16,64,128]{2,1,0:T(8,128)S(1)}, u32[]{:S(2)}, u32[]{:S(2)}) collective-permute-start(f32[16,64,128]{2,1,0:T(8,128)S(1)} %get-tuple-element.49.pb), channel_id=1, source_target_pairs={{0,64},{64,0},{1,65},{65,1},{2,66},{66,2},{3,67},{67,3},{4,68},{68... | collective-permute-start | bytes 1572872 | tf_op jit(solution)/shard_map/ppermute | solution.py:455
  40.3 7.1 %collective-permute-start.8 = (f32[8,32,128]{2,1,0:T(8,128)S(1)}, f32[8,32,128]{2,1,0:T(8,128)S(1)}, u32[]{:S(2)}, u32[]{:S(2)}) collective-permute-start(f32[8,32,128]{2,1,0:T(8,128)S(1)} %get-tuple-element.52), channel_id=1, source_target_pairs={{0,1},{1,0},{2,3},{3,2},{4,5},{5,4},{6,7},{7,6},{8,9},{9,8},{10,11... | collective-permute-start | bytes 393224 | tf_op jit(solution)/shard_map/ppermute | solution.py:393
  41.9 11.1 %collective-permute-start.9 = (f32[8,32,128]{2,1,0:T(8,128)S(1)}, f32[8,32,128]{2,1,0:T(8,128)S(1)}, u32[]{:S(2)}, u32[]{:S(2)}) collective-permute-start(f32[8,32,128]{2,1,0:T(8,128)S(1)} %get-tuple-element.53), channel_id=1, source_target_pairs={{1,2},{2,1},{3,4},{4,3},{5,6},{6,5},{9,10},{10,9},{11,12},{12,11},... | collective-permute-start | bytes 393224 | tf_op jit(solution)/shard_map/ppermute | solution.py:393
  45.7 7.8 %collective-permute-start.6 = (f32[8,64,128]{2,1,0:T(8,128)S(1)}, f32[8,64,128]{2,1,0:T(8,128)S(1)}, u32[]{:S(2)}, u32[]{:S(2)}) collective-permute-start(f32[8,64,128]{2,1,0:T(8,128)S(1)} %get-tuple-element.50), channel_id=1, source_target_pairs={{0,8},{8,0},{16,24},{24,16},{32,40},{40,32},{48,56},{56,48},{1,9},... | collective-permute-start | bytes 786440 | tf_op jit(solution)/shard_map/ppermute | solution.py:393
  47.4 13.6 %collective-permute-start.7 = (f32[8,64,128]{2,1,0:T(8,128)S(1)}, f32[8,64,128]{2,1,0:T(8,128)S(1)}, u32[]{:S(2)}, u32[]{:S(2)}) collective-permute-start(f32[8,64,128]{2,1,0:T(8,128)S(1)} %get-tuple-element.51), channel_id=1, source_target_pairs={{8,16},{16,8},{24,32},{32,24},{40,48},{48,40},{9,17},{17,9},{25,33... | collective-permute-start | bytes 786440 | tf_op jit(solution)/shard_map/ppermute | solution.py:393
  53.3 26.9 %collective-permute-start.16 = (f32[16,64,128]{2,1,0:T(8,128)S(1)}, f32[16,64,128]{2,1,0:T(8,128)S(1)}, u32[]{:S(2)}, u32[]{:S(2)}) collective-permute-start(f32[16,64,128]{2,1,0:T(8,128)S(1)} %shard_map.54.after.rest_1_.pa), channel_id=1, source_target_pairs={{0,64},{64,0},{1,65},{65,1},{2,66},{66,2},{3,67},{67,3},{4,68},{68... | collective-permute-start | bytes 1572872 | tf_op jit(solution)/shard_map/ppermute | solution.py:437
  65.7 27.5 %collective-permute-start.17 = (f32[16,64,128]{2,1,0:T(8,128)S(1)}, f32[16,64,128]{2,1,0:T(8,128)S(1)}, u32[]{:S(2)}, u32[]{:S(2)}) collective-permute-start(f32[16,64,128]{2,1,0:T(8,128)S(1)} %get-tuple-element.56.pb), channel_id=1, source_target_pairs={{0,64},{64,0},{1,65},{65,1},{2,66},{66,2},{3,67},{67,3},{4,68},{68... | collective-permute-start | bytes 1572872 | tf_op jit(solution)/shard_map/ppermute | solution.py:455
  67.5 6.2 %collective-permute-start.14 = (f32[8,32,128]{2,1,0:T(8,128)S(1)}, f32[8,32,128]{2,1,0:T(8,128)S(1)}, u32[]{:S(2)}, u32[]{:S(2)}) collective-permute-start(f32[8,32,128]{2,1,0:T(8,128)S(1)} %get-tuple-element.59), channel_id=1, source_target_pairs={{0,1},{1,0},{2,3},{3,2},{4,5},{5,4},{6,7},{7,6},{8,9},{9,8},{10,11... | collective-permute-start | bytes 393224 | tf_op jit(solution)/shard_map/ppermute | solution.py:393
  69.1 11.1 %collective-permute-start.15 = (f32[8,32,128]{2,1,0:T(8,128)S(1)}, f32[8,32,128]{2,1,0:T(8,128)S(1)}, u32[]{:S(2)}, u32[]{:S(2)}) collective-permute-start(f32[8,32,128]{2,1,0:T(8,128)S(1)} %get-tuple-element.60), channel_id=1, source_target_pairs={{1,2},{2,1},{3,4},{4,3},{5,6},{6,5},{9,10},{10,9},{11,12},{12,11},... | collective-permute-start | bytes 393224 | tf_op jit(solution)/shard_map/ppermute | solution.py:393
  73.1 7.8 %collective-permute-start.12 = (f32[8,64,128]{2,1,0:T(8,128)S(1)}, f32[8,64,128]{2,1,0:T(8,128)S(1)}, u32[]{:S(2)}, u32[]{:S(2)}) collective-permute-start(f32[8,64,128]{2,1,0:T(8,128)S(1)} %get-tuple-element.57), channel_id=1, source_target_pairs={{0,8},{8,0},{16,24},{24,16},{32,40},{40,32},{48,56},{56,48},{1,9},... | collective-permute-start | bytes 786440 | tf_op jit(solution)/shard_map/ppermute | solution.py:393
  73.7 15.5 %collective-permute-start.13 = (f32[8,64,128]{2,1,0:T(8,128)S(1)}, f32[8,64,128]{2,1,0:T(8,128)S(1)}, u32[]{:S(2)}, u32[]{:S(2)}) collective-permute-start(f32[8,64,128]{2,1,0:T(8,128)S(1)} %get-tuple-element.58), channel_id=1, source_target_pairs={{8,16},{16,8},{24,32},{32,24},{40,48},{48,40},{9,17},{17,9},{25,33... | collective-permute-start | bytes 786440 | tf_op jit(solution)/shard_map/ppermute | solution.py:393
  80.5 28.9 %collective-permute-start.22 = (f32[16,64,128]{2,1,0:T(8,128)S(1)}, f32[16,64,128]{2,1,0:T(8,128)S(1)}, u32[]{:S(2)}, u32[]{:S(2)}) collective-permute-start(f32[16,64,128]{2,1,0:T(8,128)S(1)} %shard_map.57.after.rest_1_.pa), channel_id=1, source_target_pairs={{0,64},{64,0},{1,65},{65,1},{2,66},{66,2},{3,67},{67,3},{4,68},{68... | collective-permute-start | bytes 1572872 | tf_op jit(solution)/shard_map/ppermute | solution.py:437
  93.8 15.8 %collective-permute-start.18 = (f32[8,64,128]{2,1,0:T(8,128)S(1)}, f32[8,64,128]{2,1,0:T(8,128)S(1)}, u32[]{:S(2)}, u32[]{:S(2)}) collective-permute-start(f32[8,64,128]{2,1,0:T(8,128)S(1)} %get-tuple-element.62), channel_id=1, source_target_pairs={{0,8},{8,0},{16,24},{24,16},{32,40},{40,32},{48,56},{56,48},{1,9},... | collective-permute-start | bytes 786440 | tf_op jit(solution)/shard_map/ppermute | solution.py:393
  93.9 15.7 %collective-permute-start.19 = (f32[8,64,128]{2,1,0:T(8,128)S(1)}, f32[8,64,128]{2,1,0:T(8,128)S(1)}, u32[]{:S(2)}, u32[]{:S(2)}) collective-permute-start(f32[8,64,128]{2,1,0:T(8,128)S(1)} %get-tuple-element.63), channel_id=1, source_target_pairs={{8,16},{16,8},{24,32},{32,24},{40,48},{48,40},{9,17},{17,9},{25,33... | collective-permute-start | bytes 786440 | tf_op jit(solution)/shard_map/ppermute | solution.py:393
  96.4 5.7 %collective-permute-start.20 = (f32[8,32,128]{2,1,0:T(8,128)S(1)}, f32[8,32,128]{2,1,0:T(8,128)S(1)}, u32[]{:S(2)}, u32[]{:S(2)}) collective-permute-start(f32[8,32,128]{2,1,0:T(8,128)S(1)} %get-tuple-element.64), channel_id=1, source_target_pairs={{0,1},{1,0},{2,3},{3,2},{4,5},{5,4},{6,7},{7,6},{8,9},{9,8},{10,11... | collective-permute-start | bytes 393224 | tf_op jit(solution)/shard_map/ppermute | solution.py:393
  98.1 11.2 %collective-permute-start.21 = (f32[8,32,128]{2,1,0:T(8,128)S(1)}, f32[8,32,128]{2,1,0:T(8,128)S(1)}, u32[]{:S(2)}, u32[]{:S(2)}) collective-permute-start(f32[8,32,128]{2,1,0:T(8,128)S(1)} %get-tuple-element.65), channel_id=1, source_target_pairs={{1,2},{2,1},{3,4},{4,3},{5,6},{6,5},{9,10},{10,9},{11,12},{12,11},... | collective-permute-start | bytes 393224 | tf_op jit(solution)/shard_map/ppermute | solution.py:393
  102.2 30.2 %collective-permute-start.27 = (f32[16,64,128]{2,1,0:T(8,128)S(1)}, f32[16,64,128]{2,1,0:T(8,128)S(1)}, u32[]{:S(2)}, u32[]{:S(2)}) collective-permute-start(f32[16,64,128]{2,1,0:T(8,128)S(1)} %get-tuple-element.61.pb), channel_id=1, source_target_pairs={{0,64},{64,0},{1,65},{65,1},{2,66},{66,2},{3,67},{67,3},{4,68},{68... | collective-permute-start | bytes 1572872 | tf_op jit(solution)/shard_map/ppermute | solution.py:455
  115.0 1.7 %collective-permute-start.23 = (f32[7,64,128]{2,1,0:T(8,128)S(1)}, f32[7,64,128]{2,1,0:T(8,128)S(1)}, u32[]{:S(2)}, u32[]{:S(2)}) collective-permute-start(f32[7,64,128]{2,1,0:T(8,128)S(1)} %get-tuple-element.67.total), channel_id=1, source_target_pairs={{0,8},{8,0},{16,24},{24,16},{32,40},{40,32},{48,56},{56,48},{1,9},... | collective-permute-start | bytes 688136 | tf_op jit(solution)/shard_map/ppermute | solution.py:469
  116.7 7.3 %collective-permute-start.24 = (f32[7,32,128]{2,1,0:T(8,128)S(1)}, f32[7,32,128]{2,1,0:T(8,128)S(1)}, u32[]{:S(2)}, u32[]{:S(2)}) collective-permute-start(f32[7,32,128]{2,1,0:T(8,128)S(1)} %get-tuple-element.68), channel_id=1, source_target_pairs={{0,32},{8,40},{16,48},{24,56},{1,33},{9,41},{17,49},{25,57},{2,34}... | collective-permute-start | bytes 344072 | tf_op jit(solution)/shard_map/ppermute | solution.py:407
  124.0 8.2 %collective-permute-start.25 = (f32[7,32,128]{2,1,0:T(8,128)S(1)}, f32[7,32,128]{2,1,0:T(8,128)S(1)}, u32[]{:S(2)}, u32[]{:S(2)}) collective-permute-start(f32[7,32,128]{2,1,0:T(8,128)S(1)} %add.13), channel_id=1, source_target_pairs={{0,16},{8,24},{32,48},{40,56},{48,32},{56,40},{1,17},{9,25},{33,49... | collective-permute-start | bytes 344072 | tf_op jit(solution)/shard_map/ppermute | solution.py:408
  132.2 17.3 %collective-permute-start.26 = (f32[7,32,128]{2,1,0:T(8,128)S(1)}, f32[7,32,128]{2,1,0:T(8,128)S(1)}, u32[]{:S(2)}, u32[]{:S(2)}) collective-permute-start(f32[7,32,128]{2,1,0:T(8,128)S(1)} %add.14.before), channel_id=1, source_target_pairs={{0,8},{8,0},{16,24},{24,16},{32,40},{40,32},{48,56},{56,48},{1,9},... | collective-permute-start | bytes 344072 | tf_op jit(solution)/shard_map/ppermute | solution.py:471
  132.7 1.4 collective-permute-start.28
  134.1 5.8 %collective-permute-start.29 = (f32[64,128]{1,0:T(8,128)S(1)}, f32[64,128]{1,0:T(8,128)S(1)}, u32[]{:S(2)}, u32[]{:S(2)}) collective-permute-start(f32[64,128]{1,0:T(8,128)S(1)} %get-tuple-element.72), channel_id=1, source_target_pairs={{0,32},{8,40},{16,48},{24,56},{1,33},{9,41},{17,49},{25,57},{2,34}... | collective-permute-start | bytes 98312 | tf_op jit(solution)/shard_map/ppermute | solution.py:407
  139.9 7.3 %collective-permute-start.30 = (f32[64,128]{1,0:T(8,128)S(1)}, f32[64,128]{1,0:T(8,128)S(1)}, u32[]{:S(2)}, u32[]{:S(2)}) collective-permute-start(f32[64,128]{1,0:T(8,128)S(1)} %add.15), channel_id=1, source_target_pairs={{0,16},{8,24},{32,48},{40,56},{48,32},{56,40},{1,17},{9,25},{33,49... | collective-permute-start | bytes 98312 | tf_op jit(solution)/shard_map/ppermute | solution.py:408

commit v8 on v6

--- a/solution.py
+++ b/solution.py
@@ -68,18 +68,24 @@
     return jnp.where(odd(axis), o, e)
 
 
-def faces_kernel(u, lon_e, lon_o, lev_e, lev_o):
+def across(j, whole, half, relayed):
+    return whole[j] + jnp.concatenate([half[j], relayed[j]], axis=0)
+
+
+def faces_kernel(u, lon_e, lon_o, lon_h, lon_r, lev_e, lev_o):
     nj, ni, nk, _ = u.shape
     at_e = jnp.where(odd("lon"), 0, ni - 1)
     for j in range(nj):
         lon_e[j] = u[j, at_e]
         lon_o[j] = u[j, ni - 1 - at_e]
+        lon_h[j] = u[j, ni - 1 - at_e, : nk // 2]
+        lon_r[j] = u[j, ni - 1 - at_e, nk // 2 :]
         lo, hi = u[j, :, 0, :], u[j, :, nk - 1, :]
         lev_e[j] = lower("lev", lo, hi)
         lev_o[j] = upper("lev", lo, hi)
 
 
-def load_kernel(u_in, d_in, f_in, u, pb, d_edge, f_edge, lon_e, lon_o, lev_e, lev_o, sem):
+def load_kernel(u_in, d_in, f_in, u, pb, d_edge, f_edge, lon_e, lon_o, lon_h, lon_r, lev_e, lev_o, sem):
     nj, ni = u.shape[:2]
     q = ni // 4
     pj = plane_at(0, nj)
@@ -94,7 +100,7 @@
         copy.start()
     for copy in copies:
         copy.wait()
-    faces_kernel(u, lon_e, lon_o, lev_e, lev_o)
+    faces_kernel(u, lon_e, lon_o, lon_h, lon_r, lev_e, lev_o)
 
 
 def lev_rows(lev_e, lev_o, j, base):
@@ -135,7 +141,7 @@
     edge_rows(0, n, n // 2, pa, lambda: pb[n // 2 - 1], lambda: pb[n // 2], u, lat, lev_e, lev_o, d, f, put)
 
 
-def edge_b_kernel(u, pa, pb, lat, lon_e, lon_o, lev_e, lev_o, d, f, *rest):
+def edge_b_kernel(u, pa, pb, lat, lon_e, lon_o, lon_h, lon_r, lev_e, lev_o, d, f, *rest):
     nj, ni, nk, _ = u.shape
     q = ni // 4
     pj = plane_at(0, nj)
@@ -146,20 +152,22 @@
         return carry
 
     args = (u, lat, lev_e, lev_o, d, f, put)
-    edge_rows(0, q, 0, pb, lambda: lower("lon", lon_e[pj], lon_o[pj]), lambda: pa[0], *args)
-    edge_rows(q, 2 * q, 2 * q, pb, lambda: pa[2 * q - 1], lambda: upper("lon", lon_e[pj], lon_o[pj]), *args)
+    edge_rows(0, q, 0, pb, lambda: lower("lon", lon_e[pj], across(pj, lon_o, lon_h, lon_r)), lambda: pa[0], *args)
+    edge_rows(q, 2 * q, 2 * q, pb, lambda: pa[2 * q - 1], lambda: upper("lon", lon_e[pj], across(pj, lon_o, lon_h, lon_r)), *args)
     if len(rest) > 1:
-        nu, npa, _, s_lon_e, s_lon_o, s_lev_e, s_lev_o = rest
-        faces_kernel(nu, s_lon_e, s_lon_o, s_lev_e, s_lev_o)
+        nu, npa, _, s_lon_e, s_lon_o, s_lon_h, s_lon_r, s_lev_e, s_lev_o = rest
+        faces_kernel(nu, s_lon_e, s_lon_o, s_lon_h, s_lon_r, s_lev_e, s_lev_o)
         s_lon_e[pj] = lower("lon", out[0], out[2 * q - 1])
         s_lon_o[pj] = upper("lon", out[0], out[2 * q - 1])
+        s_lon_h[pj] = upper("lon", out[0, : nk // 2], out[2 * q - 1, : nk // 2])
+        s_lon_r[pj] = upper("lon", out[0, nk // 2 :], out[2 * q - 1, nk // 2 :])
         for s_lev, side in ((s_lev_e, lower), (s_lev_o, upper)):
             s_lev[pj, :q] = side("lev", out[:q, 0, :], out[:q, nk - 1, :])
             s_lev[pj, q : 3 * q] = side("lev", npa[:, 0, :], npa[:, nk - 1, :])
             s_lev[pj, 3 * q :] = side("lev", out[q:, 0, :], out[q:, nk - 1, :])
 
 
-def bulk_planes(u, pa, pb, lon_e, lon_o, lev_e, lev_o, d, f, put, start, finish):
+def bulk_planes(u, pa, pb, lon_e, lon_o, lon_h, lon_r, lev_e, lev_o, d, f, put, start, finish):
     nj, ni, _, _ = u.shape
     q = ni // 4
 
@@ -168,8 +176,8 @@
             lo,
             hi,
             lambda i: u[j, i],
-            (lambda: lower("lon", lon_e[j], lon_o[j])) if lo == 0 else None,
-            (lambda: upper("lon", lon_e[j], lon_o[j])) if hi == ni else None,
+            (lambda: lower("lon", lon_e[j], across(j, lon_o, lon_h, lon_r))) if lo == 0 else None,
+            (lambda: upper("lon", lon_e[j], across(j, lon_o, lon_h, lon_r))) if hi == ni else None,
             nb,
             *lev_rows(lev_e, lev_o, j, 0),
             lambda i: d[j, i],
@@ -215,7 +223,7 @@
     return put
 
 
-def first_bulk_kernel(u, pa, pb, lon_e, lon_o, lev_e, lev_o, d_in, f_in, after, out, d, f, sem):
+def first_bulk_kernel(u, pa, pb, lon_e, lon_o, lon_h, lon_r, lev_e, lev_o, d_in, f_in, after, out, d, f, sem):
     del after
     nj = u.shape[0]
 
@@ -233,15 +241,15 @@
         for copy in copies(j, depth):
             copy.wait()
 
-    bulk_planes(u, pa, pb, lon_e, lon_o, lev_e, lev_o, d, f, plain_put(out), start, nothing)
-
-
-def bulk_kernel(u, pa, pb, lon_e, lon_o, lev_e, lev_o, d, f, after, out):
+    bulk_planes(u, pa, pb, lon_e, lon_o, lon_h, lon_r, lev_e, lev_o, d, f, plain_put(out), start, nothing)
+
+
+def bulk_kernel(u, pa, pb, lon_e, lon_o, lon_h, lon_r, lev_e, lev_o, d, f, after, out):
     del after
-    bulk_planes(u, pa, pb, lon_e, lon_o, lev_e, lev_o, d, f, plain_put(out), nothing, nothing)
-
-
-def last_bulk_kernel(u, pa, pb, lon_e, lon_o, lev_e, lev_o, d_in, f_in, after, end, d, f, total, sem):
+    bulk_planes(u, pa, pb, lon_e, lon_o, lon_h, lon_r, lev_e, lev_o, d, f, plain_put(out), nothing, nothing)
+
+
+def last_bulk_kernel(u, pa, pb, lon_e, lon_o, lon_h, lon_r, lev_e, lev_o, d_in, f_in, after, end, d, f, total, sem):
     del d_in, f_in, after
     nj = u.shape[0]
 
@@ -258,13 +266,13 @@
         total[depth - 1] = carry
         copy_out(j, depth).start()
 
-    bulk_planes(u, pa, pb, lon_e, lon_o, lev_e, lev_o, d, f, put, nothing, finish)
+    bulk_planes(u, pa, pb, lon_e, lon_o, lon_h, lon_r, lev_e, lev_o, d, f, put, nothing, finish)
     for depth in range(1, nj):
         copy_out(plane_at(depth, nj), depth).wait()
 
 
-def last_edge_kernel(u, pa, pb, lat, lon_e, lon_o, lev_e, lev_o, d, f, npa, npb, sums, total):
-    edge_b_kernel(u, pa, pb, lat, lon_e, lon_o, lev_e, lev_o, d, f, npb)
+def last_edge_kernel(u, pa, pb, lat, lon_e, lon_o, lon_h, lon_r, lev_e, lev_o, d, f, npa, npb, sums, total):
+    edge_b_kernel(u, pa, pb, lat, lon_e, lon_o, lon_h, lon_r, lev_e, lev_o, d, f, npb)
     ni = sums.shape[0]
     q = ni // 4
     carry = zero_carry(u)
@@ -384,19 +392,22 @@
     H = lambda *shape: pltpu.HBM(shape, dtype)
 
     swap = [(0, 1), (1, 0)]
-    faces_out = (V(nj, nk, nm), V(nj, nk, nm), V(nj, ni, nm), V(nj, ni, nm))
-
-    def exchange(axis, size, e, o):
-        def swaps(first):
-            return [(a, b) for i in range(first, size - 1, 2) for a, b in ((i, i + 1), (i + 1, i))]
-
-        return lax.ppermute(e, axis, swaps(0)), lax.ppermute(o, axis, swaps(1))
-
-    def lon_exchange(e, o):
-        return exchange("lon", lon_size, e, o)
+    faces_out = (V(nj, nk, nm),) * 2 + (V(nj, nk // 2, nm),) * 2 + (V(nj, ni, nm),) * 2
+
+    def swaps(*pairs):
+        return [(a, b) for p in pairs for a, b in (p, p[::-1])]
+
+    def lon_exchange(e, o, o_half, o_rest):
+        e = lax.ppermute(e, "lon", swaps((0, 1), (2, 3), (4, 5), (6, 7)))
+        o_rest = lax.ppermute(o_rest, "lon", [(3, 7), (4, 0)])
+        o = lax.ppermute(o, "lon", swaps((1, 2), (5, 6)))
+        o_half = lax.ppermute(o_half, "lon", swaps((3, 4)))
+        o_rest = lax.ppermute(o_rest, "lon", [(7, 4), (0, 3)])
+        return e, o, o_half, o_rest
 
     def lev_exchange(e, o):
-        return exchange("lev", lev_size, e, o)
+        e_pairs, o_pairs = ([(i, i + 1) for i in range(first, lev_size - 1, 2)] for first in (0, 1))
+        return lax.ppermute(e, "lev", swaps(*e_pairs)), lax.ppermute(o, "lev", swaps(*o_pairs))
 
     def partner(bit, total):
         pairs = [(i, i ^ (1 << bit)) for i in range(lon_size)]
@@ -412,14 +423,14 @@
     u, pb, d_edge, f_edge, *faces = call(
         load_kernel,
         (V(nj, ni, nk, nm), V(half, nk, nm), V(ni, nk, nm), V(ni, nk, nm)) + faces_out,
-        (VMEM,) * 8,
+        (VMEM,) * 10,
         (HBM,) * 3,
         scratch=(pltpu.SemaphoreType.DMA((nj + 4,)),),
         flops=10**6,
     )(*map(in_hbm, (initial_state, scaled_diffusivity, scaled_forcing)))
-    lev = lev_exchange(*faces[2:])
-    lon = lon_exchange(*faces[:2])
+    lon = lon_exchange(*faces[:4])
     lat_b = lax.ppermute(pb, "lat", swap)
+    lev = lev_exchange(*faces[4:])
     d_edge, f_edge = in_vmem(d_edge), in_vmem(f_edge)
     d, f = in_hbm(scaled_diffusivity), in_hbm(scaled_forcing)
 
@@ -438,20 +449,20 @@
                 first_bulk_kernel,
                 (V(nj, ni, nk, nm),) * 3,
                 (VMEM,) * 3,
-                (VMEM,) * 7 + (HBM,) * 2 + (ANY,),
+                (VMEM,) * 9 + (HBM,) * 2 + (ANY,),
                 scratch=(pltpu.SemaphoreType.DMA((2, nj)),),
                 flops=2 * 10**7,
             )(u, pa, pb, *lon, *lev, d, f, n_pa)
         else:
             n_u = call(
-                bulk_kernel, V(nj, ni, nk, nm), VMEM, (VMEM,) * 9 + (ANY,), flops=2 * 10**7
+                bulk_kernel, V(nj, ni, nk, nm), VMEM, (VMEM,) * 11 + (ANY,), flops=2 * 10**7
             )(u, pa, pb, *lon, *lev, in_vmem(d), in_vmem(f), n_pa)
         n_pb, *faces = call(
-            edge_b_kernel, (V(half, nk, nm),) + faces_out, (VMEM,) * 5, (VMEM,) * 12, flops=10**6
+            edge_b_kernel, (V(half, nk, nm),) + faces_out, (VMEM,) * 7, (VMEM,) * 14, flops=10**6
         )(u, pa, pb, lat_b, *lon, *lev, d_edge, f_edge, in_vmem(n_u), in_vmem(n_pa))
-        lon = lon_exchange(*faces[:2])
+        lon = lon_exchange(*faces[:4])
         lat_b = lax.ppermute(n_pb, "lat", swap)
-        lev = lev_exchange(*faces[2:])
+        lev = lev_exchange(*faces[4:])
         u, pa, pb = n_u, n_pa, n_pb
 
     scale = 1.0 / (ni * lon_size)
@@ -459,9 +470,9 @@
         last_bulk_kernel,
         (H(nj, ni, nk, nm), V(nj, ni, nk, nm), V(nj, ni, nk, nm), V(nj - 1, nk, nm)),
         (HBM, VMEM, VMEM, VMEM),
-        (VMEM,) * 9 + (ANY,),
+        (VMEM,) * 11 + (ANY,),
         scratch=(pltpu.SemaphoreType.DMA((nj,)),),
-        aliases={7: 1, 8: 2},
+        aliases={9: 1, 10: 2},
         flops=2 * 10**7,
     )(u, pa, pb, *lon, *lev, in_vmem(d), in_vmem(f), n_pa)
     other = partner(0, total)
@@ -476,7 +487,7 @@
     back = lax.ppermute(mine, "lon", [(i, i ^ 1) for i in range(lon_size)])
     n_pa = in_vmem(n_pa)
     n_pb, edge_sums, edge_total = call(
-        last_edge_kernel, (V(half, nk, nm), V(ni, nk, nm), V(nk, nm)), (VMEM,) * 3, (VMEM,) * 11, flops=2 * 10**6
+        last_edge_kernel, (V(half, nk, nm), V(ni, nk, nm), V(nk, nm)), (VMEM,) * 3, (VMEM,) * 13, flops=2 * 10**6
     )(u, pa, pb, lat_b, *lon, *lev, d_edge, f_edge, n_pa)
     others = []
     edge_total_1 = edge_total

time: 147 us -> 172 us (1.17)
  waiting for transfers between devices: 60.9 us -> 81.2 us
  starting transfers between devices: 52 us -> 56.1 us
    ppermute x16 -> x28, waiting for transfers between devices: 42.5 us -> 59.1 us  [the longest x4 34.1 us: lon_exchange(): o_rest = lax.ppermute(o_rest, 'lon', [(7, 4), (0, 3)])]
    ppermute x16 -> x28, starting transfers between devices: 34.5 us -> 43.5 us  [the longest x4 17.3 us: lev_exchange(): lax.ppermute(o, 'lev', swaps(*o_pairs))]
    ppermute x6, starting transfers between devices: 7.47 us -> 3.59 us  [partner(): return lax.ppermute(total, 'lon', pairs)]
    ppermute x6, waiting for transfers between devices: 18.4 us -> 22 us  [partner(): return lax.ppermute(total, 'lon', pairs)]
    ppermute x3, starting transfers between devices: 6.48 us -> 4.15 us  [per_device(): lat_b = lax.ppermute(n_pb, 'lat', swap)]
  transfers between devices with their start and end apart: 31 -> 43, of which waited for: 13 -> 18; matrix products, arithmetic and copies ran while one was open for 0% -> 0% of each run, Pallas kernels for 19% -> 17%
where the time goes in v8:
time: 172 us; the launch traced here: 171 us
  waiting for transfers between devices  81.2 us (47%)
  starting transfers between devices  56.1 us (33%)
  Pallas kernels  31 us (18%)
    ppermute x4, waiting for transfers between devices, lon_exchange(): o_rest = lax.ppermute(o_rest, 'lon', [(7, 4), (0, 3)])  34.1 us
    ppermute x6, waiting for transfers between devices, partner(): return lax.ppermute(total, 'lon', pairs)  22 us
    ppermute x4, starting transfers between devices, lev_exchange(): lax.ppermute(o, 'lev', swaps(*o_pairs))  17.3 us
    ppermute x4, waiting for transfers between devices, lon_exchange(): o_half = lax.ppermute(o_half, 'lon', swaps((3, 4)))  12.7 us
    ppermute x4, waiting for transfers between devices, lev_exchange(): lax.ppermute(o, 'lev', swaps(*o_pairs))  12.3 us
    ppermute x4, starting transfers between devices, lon_exchange(): o_half = lax.ppermute(o_half, 'lon', swaps((3, 4)))  8.11 us
    pallas_call x2, Pallas kernels, per_device(): call(bulk_kernel, V(nj, ni, nk, nm), VMEM, (VMEM,) * 11 + (ANY,), flops=2...  7.77 us
    pallas_call x1, Pallas kernels, per_device(): call(first_bulk_kernel, (V(nj, ni, nk, nm),) * 3, (VMEM,) * 3, (VMEM,) *...  5.86 us
  transfers between devices with their start and end apart: 43, of which 18 were waited for; matrix products, arithmetic and copies ran while one was open for 0% of the time, Pallas kernels for 17%

profile of v8, /device:TPU:98, one launch (start us, length us, event | category | flops | bytes accessed | tf_op | source)
XLA Modules:
  0.0 170.6 jit_solution(3259308241053912886)
XLA Ops:
  0.6 1.1 dynamic-slice_bitcast_fusion.pa
  1.7 0.6 collective-permute-start.7
  2.3 4.4 %shard_map.50 = (f32[8,32,64,128]{3,2,1,0:T(8,128)S(1)}, f32[16,64,128]{2,1,0:T(8,128)S(1)}, f32[32,64,128]{2,1,0:T(8,128)S(1)}, f32[32,64,128]{2,1,0:T(8,128)S(...) custom-call(f32[8,32,64,128]{3,2,1,0:T(8,128)} %u_in.1, ...), custom_call_target="tpu_custom_call" | custom-call | flops 1000000 | tf_op jit(solution)/shard_map/pallas_call | solution.py:423
  6.8 1.6 collective-permute-start.8
  8.4 1.6 collective-permute-start.5
  9.9 4.1 %collective-permute-start.6 = (f32[8,32,128]{2,1,0:T(8,128)S(1)}, f32[8,32,128]{2,1,0:T(8,128)S(1)}, u32[]{:S(2)}, u32[]{:S(2)}) collective-permute-start(f32[8,32,128]{2,1,0:T(8,128)S(1)} %get-tuple-element.51), channel_id=1, source_target_pairs={{1,2},{2,1},{3,4},{4,3},{5,6},{6,5},{9,10},{10,9},{11,12},{12,11},... | collective-permute-start | bytes 393224 | tf_op jit(solution)/shard_map/ppermute | solution.py:410
  14.0 1.9 %collective-permute-start.2 = (f32[8,32,128]{2,1,0:T(8,128)S(1)}, f32[8,32,128]{2,1,0:T(8,128)S(1)}, u32[]{:S(2)}, u32[]{:S(2)}) collective-permute-start(f32[8,32,128]{2,1,0:T(8,128)S(1)} %get-tuple-element.48), channel_id=1, source_target_pairs={{24,32},{32,24},{25,33},{33,25},{26,34},{34,26},{27,35},{35,27},{2... | collective-permute-start | bytes 393224 | tf_op jit(solution)/shard_map/ppermute | solution.py:404
  16.0 1.3 collective-permute-start.3
  17.3 3.2 %collective-permute-done.6.lev_o = f32[8,32,128]{2,1,0:T(8,128)S(1)} collective-permute-done((f32[8,32,128]{2,1,0:T(8,128)S(1)}, f32[8,32,128]{2,1,0:T(8,128)S(1)}, u32[]{:S(2)}, u32[]{:S(2)}) %collective-permute-start.6) | collective-permute-done | bytes 131104 | tf_op jit(solution)/shard_map/ppermute | solution.py:410
  20.8 0.6 collective-permute-start.16
  21.4 7.8 %collective-permute-done.2.lon_h = f32[8,32,128]{2,1,0:T(8,128)S(1)} collective-permute-done((f32[8,32,128]{2,1,0:T(8,128)S(1)}, f32[8,32,128]{2,1,0:T(8,128)S(1)}, u32[]{:S(2)}, u32[]{:S(2)}) %collective-permute-start.2) | collective-permute-done | bytes 131104 | tf_op jit(solution)/shard_map/ppermute | solution.py:404
  29.1 0.7 collective-permute-start.1
  29.8 1.3 collective-permute-start.4
  31.1 9.4 %collective-permute-done.4.lon_r = f32[8,32,128]{2,1,0:T(8,128)S(1)} collective-permute-done((f32[8,32,128]{2,1,0:T(8,128)S(1)}, f32[8,32,128]{2,1,0:T(8,128)S(1)}, u32[]{:S(2)}, u32[]{:S(2)}) %collective-permute-start.4) | collective-permute-done | bytes 131104 | tf_op jit(solution)/shard_map/ppermute | solution.py:405
  40.6 5.9 %shard_map.52 = (f32[8,32,64,128]{3,2,1,0:T(8,128)S(1)}, f32[8,32,64,128]{3,2,1,0:T(8,128)S(1)}, f32[8,32,64,128]{3,2,1,0:T(8,128)S(1)}) custom-call(f32[8,32,64,128]{3,2,1,0:T(8,128)S(1)} %get-tuple-element.44.u, f32[16,64,128]{2,1,0:T(8,128)S(1)} %dynamic-slice_bitcast_fusion.pa, f32[16,64,128]{2,1,0:T(8,128)S(1)} %get-tuple-element.45.pb, ...), custom_call_target="tpu_custom_call" | custom-call | flops 20000000 | tf_op jit(solution)/shard_map/pallas_call | solution.py:448
  46.4 0.6 shard_map.53
  47.0 1.9 %collective-permute-start.17 = (f32[16,64,128]{2,1,0:T(8,128)S(1)}, f32[16,64,128]{2,1,0:T(8,128)S(1)}, u32[]{:S(2)}, u32[]{:S(2)}) collective-permute-start(f32[16,64,128]{2,1,0:T(8,128)S(1)} %get-tuple-element.55.pb), channel_id=1, source_target_pairs={{0,64},{64,0},{1,65},{65,1},{2,66},{66,2},{3,67},{67,3},{4,68},{68... | collective-permute-start | bytes 1572872 | tf_op jit(solution)/shard_map/ppermute | solution.py:464
  48.9 1.6 collective-permute-start.14
  50.5 4.1 %collective-permute-start.15 = (f32[8,32,128]{2,1,0:T(8,128)S(1)}, f32[8,32,128]{2,1,0:T(8,128)S(1)}, u32[]{:S(2)}, u32[]{:S(2)}) collective-permute-start(f32[8,32,128]{2,1,0:T(8,128)S(1)} %get-tuple-element.61), channel_id=1, source_target_pairs={{1,2},{2,1},{3,4},{4,3},{5,6},{6,5},{9,10},{10,9},{11,12},{12,11},... | collective-permute-start | bytes 393224 | tf_op jit(solution)/shard_map/ppermute | solution.py:410
  54.5 2.2 %collective-permute-start.11 = (f32[8,32,128]{2,1,0:T(8,128)S(1)}, f32[8,32,128]{2,1,0:T(8,128)S(1)}, u32[]{:S(2)}, u32[]{:S(2)}) collective-permute-start(f32[8,32,128]{2,1,0:T(8,128)S(1)} %get-tuple-element.58), channel_id=1, source_target_pairs={{24,32},{32,24},{25,33},{33,25},{26,34},{34,26},{27,35},{35,27},{2... | collective-permute-start | bytes 393224 | tf_op jit(solution)/shard_map/ppermute | solution.py:404
  56.7 1.3 collective-permute-start.12
  58.0 3.5 %collective-permute-done.15.lev_o = f32[8,32,128]{2,1,0:T(8,128)S(1)} collective-permute-done((f32[8,32,128]{2,1,0:T(8,128)S(1)}, f32[8,32,128]{2,1,0:T(8,128)S(1)}, u32[]{:S(2)}, u32[]{:S(2)}) %collective-permute-start.15) | collective-permute-done | bytes 131104 | tf_op jit(solution)/shard_map/ppermute | solution.py:410
  61.5 0.6 collective-permute-start.9
  62.1 0.7 collective-permute-start.10
  63.1 1.4 collective-permute-done.11.lon_h
  64.5 1.7 %collective-permute-start.25 = (f32[16,64,128]{2,1,0:T(8,128)S(1)}, f32[16,64,128]{2,1,0:T(8,128)S(1)}, u32[]{:S(2)}, u32[]{:S(2)}) collective-permute-start(f32[16,64,128]{2,1,0:T(8,128)S(1)} %shard_map.54.after.rest_1_.pa), channel_id=1, source_target_pairs={{0,64},{64,0},{1,65},{65,1},{2,66},{66,2},{3,67},{67,3},{4,68},{68... | collective-permute-start | bytes 1572872 | tf_op jit(solution)/shard_map/ppermute | solution.py:446
  66.2 1.3 collective-permute-start.13
  67.6 13.0 %collective-permute-done.13.lon_r = f32[8,32,128]{2,1,0:T(8,128)S(1)} collective-permute-done((f32[8,32,128]{2,1,0:T(8,128)S(1)}, f32[8,32,128]{2,1,0:T(8,128)S(1)}, u32[]{:S(2)}, u32[]{:S(2)}) %collective-permute-start.13) | collective-permute-done | bytes 131104 | tf_op jit(solution)/shard_map/ppermute | solution.py:405
  80.5 3.9 %shard_map.55.rest_0_.u = f32[8,32,64,128]{3,2,1,0:T(8,128)S(1)} custom-call(f32[8,32,64,128]{3,2,1,0:T(8,128)S(1)} %get-tuple-element.54.rest_0_.u, f32[16,64,128]{2,1,0:T(8,128)S(1)} %shard_map.51.after.rest_1_.pa, f32[16,64,128]{2,1,0:T(8,128)S(1)} %get-tuple-element.55.pb, f32[8,64,128]{2,1,0:T(8,128)S(1)} %collective-permute-done.9.lon_e, ...), custom_call_target="tpu_custom_call" | custom-call | flops 20000000 | tf_op jit(solution)/shard_map/pallas_call | solution.py:457
  84.4 0.6 shard_map.56
  85.0 1.0 collective-permute-start.26
  86.0 3.6 %collective-permute-start.24 = (f32[8,32,128]{2,1,0:T(8,128)S(1)}, f32[8,32,128]{2,1,0:T(8,128)S(1)}, u32[]{:S(2)}, u32[]{:S(2)}) collective-permute-start(f32[8,32,128]{2,1,0:T(8,128)S(1)} %get-tuple-element.70), channel_id=1, source_target_pairs={{1,2},{2,1},{3,4},{4,3},{5,6},{6,5},{9,10},{10,9},{11,12},{12,11},... | collective-permute-start | bytes 393224 | tf_op jit(solution)/shard_map/ppermute | solution.py:410
  89.7 1.9 %collective-permute-start.20 = (f32[8,32,128]{2,1,0:T(8,128)S(1)}, f32[8,32,128]{2,1,0:T(8,128)S(1)}, u32[]{:S(2)}, u32[]{:S(2)}) collective-permute-start(f32[8,32,128]{2,1,0:T(8,128)S(1)} %get-tuple-element.67), channel_id=1, source_target_pairs={{24,32},{32,24},{25,33},{33,25},{26,34},{34,26},{27,35},{35,27},{2... | collective-permute-start | bytes 393224 | tf_op jit(solution)/shard_map/ppermute | solution.py:404
  91.6 1.3 collective-permute-start.21
  92.9 3.6 %collective-permute-done.24.lev_o = f32[8,32,128]{2,1,0:T(8,128)S(1)} collective-permute-done((f32[8,32,128]{2,1,0:T(8,128)S(1)}, f32[8,32,128]{2,1,0:T(8,128)S(1)}, u32[]{:S(2)}, u32[]{:S(2)}) %collective-permute-start.24) | collective-permute-done | bytes 131104 | tf_op jit(solution)/shard_map/ppermute | solution.py:410
  96.5 0.7 collective-permute-start.19
  97.5 0.9 collective-permute-done.20.lon_h
  98.6 1.3 collective-permute-start.22
  99.9 7.9 %collective-permute-done.22.lon_r = f32[8,32,128]{2,1,0:T(8,128)S(1)} collective-permute-done((f32[8,32,128]{2,1,0:T(8,128)S(1)}, f32[8,32,128]{2,1,0:T(8,128)S(1)}, u32[]{:S(2)}, u32[]{:S(2)}) %collective-permute-start.22) | collective-permute-done | bytes 131104 | tf_op jit(solution)/shard_map/ppermute | solution.py:405
  107.8 3.9 %shard_map.58.rest_0_.u = f32[8,32,64,128]{3,2,1,0:T(8,128)S(1)} custom-call(f32[8,32,64,128]{3,2,1,0:T(8,128)S(1)} %shard_map.55.rest_0_.u, f32[16,64,128]{2,1,0:T(8,128)S(1)} %shard_map.54.after.rest_1_.pa, f32[16,64,128]{2,1,0:T(8,128)S(1)} %get-tuple-element.64.pb, f32[8,64,128]{2,1,0:T(8,128)S(1)} %collective-permute-done.18.lon_e, ...), custom_call_target="tpu_custom_call" | custom-call | flops 20000000 | tf_op jit(solution)/shard_map/pallas_call | solution.py:457
  111.7 0.6 shard_map.59
  112.3 1.3 collective-permute-start.30
  113.6 1.2 collective-permute-start.32
  114.8 5.5 %collective-permute-start.33 = (f32[8,32,128]{2,1,0:T(8,128)S(1)}, f32[8,32,128]{2,1,0:T(8,128)S(1)}, u32[]{:S(2)}, u32[]{:S(2)}) collective-permute-start(f32[8,32,128]{2,1,0:T(8,128)S(1)} %get-tuple-element.77), channel_id=1, source_target_pairs={{1,2},{2,1},{3,4},{4,3},{5,6},{6,5},{9,10},{10,9},{11,12},{12,11},... | collective-permute-start | bytes 393224 | tf_op jit(solution)/shard_map/ppermute | solution.py:410
  120.4 0.7 collective-permute-start.28
  121.1 2.1 %collective-permute-start.29 = (f32[8,32,128]{2,1,0:T(8,128)S(1)}, f32[8,32,128]{2,1,0:T(8,128)S(1)}, u32[]{:S(2)}, u32[]{:S(2)}) collective-permute-start(f32[8,32,128]{2,1,0:T(8,128)S(1)} %get-tuple-element.74), channel_id=1, source_target_pairs={{24,32},{32,24},{25,33},{33,25},{26,34},{34,26},{27,35},{35,27},{2... | collective-permute-start | bytes 393224 | tf_op jit(solution)/shard_map/ppermute | solution.py:404
  123.2 2.0 %collective-permute-done.33.lev_o = f32[8,32,128]{2,1,0:T(8,128)S(1)} collective-permute-done((f32[8,32,128]{2,1,0:T(8,128)S(1)}, f32[8,32,128]{2,1,0:T(8,128)S(1)}, u32[]{:S(2)}, u32[]{:S(2)}) %collective-permute-start.33) | collective-permute-done | bytes 131104 | tf_op jit(solution)/shard_map/ppermute | solution.py:410
  125.2 1.3 collective-permute-start.31
  126.5 1.2 collective-permute-start.39
  128.0 2.6 %collective-permute-done.29.lon_h = f32[8,32,128]{2,1,0:T(8,128)S(1)} collective-permute-done((f32[8,32,128]{2,1,0:T(8,128)S(1)}, f32[8,32,128]{2,1,0:T(8,128)S(1)}, u32[]{:S(2)}, u32[]{:S(2)}) %collective-permute-start.29) | collective-permute-done | bytes 131104 | tf_op jit(solution)/shard_map/ppermute | solution.py:404
  130.6 3.8 %collective-permute-done.31.lon_r = f32[8,32,128]{2,1,0:T(8,128)S(1)} collective-permute-done((f32[8,32,128]{2,1,0:T(8,128)S(1)}, f32[8,32,128]{2,1,0:T(8,128)S(1)}, u32[]{:S(2)}, u32[]{:S(2)}) %collective-permute-start.31) | collective-permute-done | bytes 131104 | tf_op jit(solution)/shard_map/ppermute | solution.py:405
  134.4 5.2 %shard_map.61 = (f32[8,32,64,128]{3,2,1,0:T(8,128)}, f32[8,32,64,128]{3,2,1,0:T(8,128)S(1)}, f32[8,32,64,128]{3,2,1,0:T(8,128)S(1)}, f32[7,64,128]{2,1,0:T(8,128)S(1)}) custom-call(f32[8,32,64,128]{3,2,1,0:T(8,128)S(1)} %shard_map.58.rest_0_.u, f32[16,64,128]{2,1,0:T(8,128)S(1)} %shard_map.57.after.rest_1_.pa, ...), custom_call_target="tpu_custom_call", output_to_operand_aliasing={{1}: (9, {}), {2}: (10, {})} | custom-call | flops 20000000 | tf_op jit(solution)/shard_map/pallas_call | solution.py:469
  139.7 1.5 collective-permute-done.35.other
  141.3 6.7 %collective-permute-done.36.refs_0_ = f32[7,32,128]{2,1,0:T(8,128)S(1)} collective-permute-done((f32[7,32,128]{2,1,0:T(8,128)S(1)}, f32[7,32,128]{2,1,0:T(8,128)S(1)}, u32[]{:S(2)}, u32[]{:S(2)}) %collective-permute-start.36) | collective-permute-done | bytes 114720 | tf_op jit(solution)/shard_map/ppermute | solution.py:416
  148.0 1.3 collective-permute-start.37
  149.3 5.4 %collective-permute-done.37.refs_1_ = f32[7,32,128]{2,1,0:T(8,128)S(1)} collective-permute-done((f32[7,32,128]{2,1,0:T(8,128)S(1)}, f32[7,32,128]{2,1,0:T(8,128)S(1)}, u32[]{:S(2)}, u32[]{:S(2)}) %collective-permute-start.37) | collective-permute-done | bytes 114720 | tf_op jit(solution)/shard_map/ppermute | solution.py:416
  154.8 0.4 shard_map.64
  155.2 0.6 collective-permute-start.40
  155.8 0.9 collective-permute-done.40.rest_0_
  156.9 5.1 %collective-permute-done.41.rest_1_ = f32[64,128]{1,0:T(8,128)S(1)} collective-permute-done((f32[64,128]{1,0:T(8,128)S(1)}, f32[64,128]{1,0:T(8,128)S(1)}, u32[]{:S(2)}, u32[]{:S(2)}) %collective-permute-start.41) | collective-permute-done | bytes 32800 | tf_op jit(solution)/shard_map/ppermute | solution.py:416
  162.1 1.3 collective-permute-start.42
  163.3 2.0 %shard_map.65.rest_4_ = f32[8,32,64,128]{3,2,1,0:T(8,128)} custom-call(f32[8,32,64,128]{3,2,1,0:T(8,128)S(1)} %get-tuple-element.78.sums, f32[7,64,128]{2,1,0:T(8,128)S(1)} %collective-permute-done.35.other, f32[7,32,128]{2,1,0:T(8,128)S(1)} %shard_map.63.before, f32[64,128]{1,0:T(8,128)S(1)} %get-tuple-element.82.after), custom_call_target="tpu_custom_call" | custom-call | flops 1000000 | tf_op jit(solution)/shard_map/pallas_call | solution.py:499
  165.3 2.5 %collective-permute-done.42.rest_2_ = f32[64,128]{1,0:T(8,128)S(1)} collective-permute-done((f32[64,128]{1,0:T(8,128)S(1)}, f32[64,128]{1,0:T(8,128)S(1)}, u32[]{:S(2)}, u32[]{:S(2)}) %collective-permute-start.42) | collective-permute-done | bytes 32800 | tf_op jit(solution)/shard_map/ppermute | solution.py:416
  167.9 2.6 %shard_map.66 = (f32[8,32,64,128]{3,2,1,0:T(8,128)}, f32[8,32,64,128]{3,2,1,0:T(8,128)}) custom-call(f32[8,32,64,128]{3,2,1,0:T(8,128)S(1)} %get-tuple-element.78.sums, f32[7,64,128]{2,1,0:T(8,128)S(1)} %collective-permute-done.35.other, f32[7,32,128]{2,1,0:T(8,128)S(1)} %collective-permute-done.38.before, ...), custom_call_target="tpu_custom_call", output_to_operand_aliasing={{0}: (9, {}), {1}: (10, {})} | custom-call | flops 1000000 | tf_op jit(solution)/shard_map/pallas_call | solution.py:509
  (43 shorter events, 2.1 us)
Async XLA Ops:
  1.7 18.8 %collective-permute-start.7 = (f32[16,64,128]{2,1,0:T(8,128)S(1)}, f32[16,64,128]{2,1,0:T(8,128)S(1)}, u32[]{:S(2)}, u32[]{:S(2)}) collective-permute-start(f32[16,64,128]{2,1,0:T(8,128)S(1)} %dynamic-slice_bitcast_fusion.pa), channel_id=1, source_target_pairs={{0,64},{64,0},{1,65},{65,1},{2,66},{66,2},{3,67},{67,3},{4,68},{68... | collective-permute-start | bytes 1572872 | tf_op jit(solution)/shard_map/ppermute | solution.py:422
  6.8 39.6 %collective-permute-start.8 = (f32[16,64,128]{2,1,0:T(8,128)S(1)}, f32[16,64,128]{2,1,0:T(8,128)S(1)}, u32[]{:S(2)}, u32[]{:S(2)}) collective-permute-start(f32[16,64,128]{2,1,0:T(8,128)S(1)} %get-tuple-element.45.pb), channel_id=1, source_target_pairs={{0,64},{64,0},{1,65},{65,1},{2,66},{66,2},{3,67},{67,3},{4,68},{68... | collective-permute-start | bytes 1572872 | tf_op jit(solution)/shard_map/ppermute | solution.py:432
  8.4 7.6 %collective-permute-start.5 = (f32[8,32,128]{2,1,0:T(8,128)S(1)}, f32[8,32,128]{2,1,0:T(8,128)S(1)}, u32[]{:S(2)}, u32[]{:S(2)}) collective-permute-start(f32[8,32,128]{2,1,0:T(8,128)S(1)} %get-tuple-element.50), channel_id=1, source_target_pairs={{0,1},{1,0},{2,3},{3,2},{4,5},{5,4},{6,7},{7,6},{8,9},{9,8},{10,11... | collective-permute-start | bytes 393224 | tf_op jit(solution)/shard_map/ppermute | solution.py:410
  9.9 10.6 %collective-permute-start.6 = (f32[8,32,128]{2,1,0:T(8,128)S(1)}, f32[8,32,128]{2,1,0:T(8,128)S(1)}, u32[]{:S(2)}, u32[]{:S(2)}) collective-permute-start(f32[8,32,128]{2,1,0:T(8,128)S(1)} %get-tuple-element.51), channel_id=1, source_target_pairs={{1,2},{2,1},{3,4},{4,3},{5,6},{6,5},{9,10},{10,9},{11,12},{12,11},... | collective-permute-start | bytes 393224 | tf_op jit(solution)/shard_map/ppermute | solution.py:410
  14.0 15.1 %collective-permute-start.2 = (f32[8,32,128]{2,1,0:T(8,128)S(1)}, f32[8,32,128]{2,1,0:T(8,128)S(1)}, u32[]{:S(2)}, u32[]{:S(2)}) collective-permute-start(f32[8,32,128]{2,1,0:T(8,128)S(1)} %get-tuple-element.48), channel_id=1, source_target_pairs={{24,32},{32,24},{25,33},{33,25},{26,34},{34,26},{27,35},{35,27},{2... | collective-permute-start | bytes 393224 | tf_op jit(solution)/shard_map/ppermute | solution.py:404
  16.0 13.9 %collective-permute-start.3 = (f32[8,32,128]{2,1,0:T(8,128)S(1)}, f32[8,32,128]{2,1,0:T(8,128)S(1)}, u32[]{:S(2)}, u32[]{:S(2)}) collective-permute-start(f32[8,32,128]{2,1,0:T(8,128)S(1)} %get-tuple-element.49), channel_id=1, source_target_pairs={{24,56},{32,0},{25,57},{33,1},{26,58},{34,2},{27,59},{35,3},{28,60... | collective-permute-start | bytes 393224 | tf_op jit(solution)/shard_map/ppermute | solution.py:402
  20.5 20.0 %collective-permute-start = (f32[8,64,128]{2,1,0:T(8,128)S(1)}, f32[8,64,128]{2,1,0:T(8,128)S(1)}, u32[]{:S(2)}, u32[]{:S(2)}) collective-permute-start(f32[8,64,128]{2,1,0:T(8,128)S(1)} %get-tuple-element.46), channel_id=1, source_target_pairs={{0,8},{8,0},{16,24},{24,16},{32,40},{40,32},{48,56},{56,48},{1,9},... | collective-permute-start | bytes 786440 | tf_op jit(solution)/shard_map/ppermute | solution.py:401
  20.8 41.4 %collective-permute-start.16 = (f32[16,64,128]{2,1,0:T(8,128)S(1)}, f32[16,64,128]{2,1,0:T(8,128)S(1)}, u32[]{:S(2)}, u32[]{:S(2)}) collective-permute-start(f32[16,64,128]{2,1,0:T(8,128)S(1)} %shard_map.51.after.rest_1_.pa), channel_id=1, source_target_pairs={{0,64},{64,0},{1,65},{65,1},{2,66},{66,2},{3,67},{67,3},{4,68},{68... | collective-permute-start | bytes 1572872 | tf_op jit(solution)/shard_map/ppermute | solution.py:446
  29.1 11.4 %collective-permute-start.1 = (f32[8,64,128]{2,1,0:T(8,128)S(1)}, f32[8,64,128]{2,1,0:T(8,128)S(1)}, u32[]{:S(2)}, u32[]{:S(2)}) collective-permute-start(f32[8,64,128]{2,1,0:T(8,128)S(1)} %get-tuple-element.47), channel_id=1, source_target_pairs={{8,16},{16,8},{40,48},{48,40},{9,17},{17,9},{41,49},{49,41},{10,18... | collective-permute-start | bytes 786440 | tf_op jit(solution)/shard_map/ppermute | solution.py:403
  29.8 10.7 %collective-permute-start.4 = (f32[8,32,128]{2,1,0:T(8,128)S(1)}, f32[8,32,128]{2,1,0:T(8,128)S(1)}, u32[]{:S(2)}, u32[]{:S(2)}) collective-permute-start(f32[8,32,128]{2,1,0:T(8,128)S(1)} %collective-permute-done.3), channel_id=1, source_target_pairs={{56,32},{0,24},{57,33},{1,25},{58,34},{2,26},{59,35},{3,27},{60,36... | collective-permute-start | bytes 393224 | tf_op jit(solution)/shard_map/ppermute | solution.py:405
  47.0 37.4 %collective-permute-start.17 = (f32[16,64,128]{2,1,0:T(8,128)S(1)}, f32[16,64,128]{2,1,0:T(8,128)S(1)}, u32[]{:S(2)}, u32[]{:S(2)}) collective-permute-start(f32[16,64,128]{2,1,0:T(8,128)S(1)} %get-tuple-element.55.pb), channel_id=1, source_target_pairs={{0,64},{64,0},{1,65},{65,1},{2,66},{66,2},{3,67},{67,3},{4,68},{68... | collective-permute-start | bytes 1572872 | tf_op jit(solution)/shard_map/ppermute | solution.py:464
  48.9 7.8 %collective-permute-start.14 = (f32[8,32,128]{2,1,0:T(8,128)S(1)}, f32[8,32,128]{2,1,0:T(8,128)S(1)}, u32[]{:S(2)}, u32[]{:S(2)}) collective-permute-start(f32[8,32,128]{2,1,0:T(8,128)S(1)} %get-tuple-element.60), channel_id=1, source_target_pairs={{0,1},{1,0},{2,3},{3,2},{4,5},{5,4},{6,7},{7,6},{8,9},{9,8},{10,11... | collective-permute-start | bytes 393224 | tf_op jit(solution)/shard_map/ppermute | solution.py:410
  50.5 11.0 %collective-permute-start.15 = (f32[8,32,128]{2,1,0:T(8,128)S(1)}, f32[8,32,128]{2,1,0:T(8,128)S(1)}, u32[]{:S(2)}, u32[]{:S(2)}) collective-permute-start(f32[8,32,128]{2,1,0:T(8,128)S(1)} %get-tuple-element.61), channel_id=1, source_target_pairs={{1,2},{2,1},{3,4},{4,3},{5,6},{6,5},{9,10},{10,9},{11,12},{12,11},... | collective-permute-start | bytes 393224 | tf_op jit(solution)/shard_map/ppermute | solution.py:410
  54.5 10.0 %collective-permute-start.11 = (f32[8,32,128]{2,1,0:T(8,128)S(1)}, f32[8,32,128]{2,1,0:T(8,128)S(1)}, u32[]{:S(2)}, u32[]{:S(2)}) collective-permute-start(f32[8,32,128]{2,1,0:T(8,128)S(1)} %get-tuple-element.58), channel_id=1, source_target_pairs={{24,32},{32,24},{25,33},{33,25},{26,34},{34,26},{27,35},{35,27},{2... | collective-permute-start | bytes 393224 | tf_op jit(solution)/shard_map/ppermute | solution.py:404
  56.7 9.5 %collective-permute-start.12 = (f32[8,32,128]{2,1,0:T(8,128)S(1)}, f32[8,32,128]{2,1,0:T(8,128)S(1)}, u32[]{:S(2)}, u32[]{:S(2)}) collective-permute-start(f32[8,32,128]{2,1,0:T(8,128)S(1)} %get-tuple-element.59), channel_id=1, source_target_pairs={{24,56},{32,0},{25,57},{33,1},{26,58},{34,2},{27,59},{35,3},{28,60... | collective-permute-start | bytes 393224 | tf_op jit(solution)/shard_map/ppermute | solution.py:402
  61.5 6.0 %collective-permute-start.9 = (f32[8,64,128]{2,1,0:T(8,128)S(1)}, f32[8,64,128]{2,1,0:T(8,128)S(1)}, u32[]{:S(2)}, u32[]{:S(2)}) collective-permute-start(f32[8,64,128]{2,1,0:T(8,128)S(1)} %get-tuple-element.56), channel_id=1, source_target_pairs={{0,8},{8,0},{16,24},{24,16},{32,40},{40,32},{48,56},{56,48},{1,9},... | collective-permute-start | bytes 786440 | tf_op jit(solution)/shard_map/ppermute | solution.py:401
  62.1 5.4 %collective-permute-start.10 = (f32[8,64,128]{2,1,0:T(8,128)S(1)}, f32[8,64,128]{2,1,0:T(8,128)S(1)}, u32[]{:S(2)}, u32[]{:S(2)}) collective-permute-start(f32[8,64,128]{2,1,0:T(8,128)S(1)} %get-tuple-element.57), channel_id=1, source_target_pairs={{8,16},{16,8},{40,48},{48,40},{9,17},{17,9},{41,49},{49,41},{10,18... | collective-permute-start | bytes 786440 | tf_op jit(solution)/shard_map/ppermute | solution.py:403
  64.5 32.0 %collective-permute-start.25 = (f32[16,64,128]{2,1,0:T(8,128)S(1)}, f32[16,64,128]{2,1,0:T(8,128)S(1)}, u32[]{:S(2)}, u32[]{:S(2)}) collective-permute-start(f32[16,64,128]{2,1,0:T(8,128)S(1)} %shard_map.54.after.rest_1_.pa), channel_id=1, source_target_pairs={{0,64},{64,0},{1,65},{65,1},{2,66},{66,2},{3,67},{67,3},{4,68},{68... | collective-permute-start | bytes 1572872 | tf_op jit(solution)/shard_map/ppermute | solution.py:446
  66.2 14.3 %collective-permute-start.13 = (f32[8,32,128]{2,1,0:T(8,128)S(1)}, f32[8,32,128]{2,1,0:T(8,128)S(1)}, u32[]{:S(2)}, u32[]{:S(2)}) collective-permute-start(f32[8,32,128]{2,1,0:T(8,128)S(1)} %collective-permute-done.12), channel_id=1, source_target_pairs={{56,32},{0,24},{57,33},{1,25},{58,34},{2,26},{59,35},{3,27},{60,36... | collective-permute-start | bytes 393224 | tf_op jit(solution)/shard_map/ppermute | solution.py:405
  85.0 26.7 %collective-permute-start.26 = (f32[16,64,128]{2,1,0:T(8,128)S(1)}, f32[16,64,128]{2,1,0:T(8,128)S(1)}, u32[]{:S(2)}, u32[]{:S(2)}) collective-permute-start(f32[16,64,128]{2,1,0:T(8,128)S(1)} %get-tuple-element.64.pb), channel_id=1, source_target_pairs={{0,64},{64,0},{1,65},{65,1},{2,66},{66,2},{3,67},{67,3},{4,68},{68... | collective-permute-start | bytes 1572872 | tf_op jit(solution)/shard_map/ppermute | solution.py:464
  86.0 5.6 %collective-permute-start.23 = (f32[8,32,128]{2,1,0:T(8,128)S(1)}, f32[8,32,128]{2,1,0:T(8,128)S(1)}, u32[]{:S(2)}, u32[]{:S(2)}) collective-permute-start(f32[8,32,128]{2,1,0:T(8,128)S(1)} %get-tuple-element.69), channel_id=1, source_target_pairs={{0,1},{1,0},{2,3},{3,2},{4,5},{5,4},{6,7},{7,6},{8,9},{9,8},{10,11... | collective-permute-start | bytes 393224 | tf_op jit(solution)/shard_map/ppermute | solution.py:410
  86.0 10.5 %collective-permute-start.24 = (f32[8,32,128]{2,1,0:T(8,128)S(1)}, f32[8,32,128]{2,1,0:T(8,128)S(1)}, u32[]{:S(2)}, u32[]{:S(2)}) collective-permute-start(f32[8,32,128]{2,1,0:T(8,128)S(1)} %get-tuple-element.70), channel_id=1, source_target_pairs={{1,2},{2,1},{3,4},{4,3},{5,6},{6,5},{9,10},{10,9},{11,12},{12,11},... | collective-permute-start | bytes 393224 | tf_op jit(solution)/shard_map/ppermute | solution.py:410
  89.7 8.7 %collective-permute-start.20 = (f32[8,32,128]{2,1,0:T(8,128)S(1)}, f32[8,32,128]{2,1,0:T(8,128)S(1)}, u32[]{:S(2)}, u32[]{:S(2)}) collective-permute-start(f32[8,32,128]{2,1,0:T(8,128)S(1)} %get-tuple-element.67), channel_id=1, source_target_pairs={{24,32},{32,24},{25,33},{33,25},{26,34},{34,26},{27,35},{35,27},{2... | collective-permute-start | bytes 393224 | tf_op jit(solution)/shard_map/ppermute | solution.py:404
  91.6 7.0 %collective-permute-start.21 = (f32[8,32,128]{2,1,0:T(8,128)S(1)}, f32[8,32,128]{2,1,0:T(8,128)S(1)}, u32[]{:S(2)}, u32[]{:S(2)}) collective-permute-start(f32[8,32,128]{2,1,0:T(8,128)S(1)} %get-tuple-element.68), channel_id=1, source_target_pairs={{24,56},{32,0},{25,57},{33,1},{26,58},{34,2},{27,59},{35,3},{28,60... | collective-permute-start | bytes 393224 | tf_op jit(solution)/shard_map/ppermute | solution.py:402
  96.5 11.3 %collective-permute-start.18 = (f32[8,64,128]{2,1,0:T(8,128)S(1)}, f32[8,64,128]{2,1,0:T(8,128)S(1)}, u32[]{:S(2)}, u32[]{:S(2)}) collective-permute-start(f32[8,64,128]{2,1,0:T(8,128)S(1)} %get-tuple-element.65), channel_id=1, source_target_pairs={{0,8},{8,0},{16,24},{24,16},{32,40},{40,32},{48,56},{56,48},{1,9},... | collective-permute-start | bytes 786440 | tf_op jit(solution)/shard_map/ppermute | solution.py:401
  96.5 11.3 %collective-permute-start.19 = (f32[8,64,128]{2,1,0:T(8,128)S(1)}, f32[8,64,128]{2,1,0:T(8,128)S(1)}, u32[]{:S(2)}, u32[]{:S(2)}) collective-permute-start(f32[8,64,128]{2,1,0:T(8,128)S(1)} %get-tuple-element.66), channel_id=1, source_target_pairs={{8,16},{16,8},{40,48},{48,40},{9,17},{17,9},{41,49},{49,41},{10,18... | collective-permute-start | bytes 786440 | tf_op jit(solution)/shard_map/ppermute | solution.py:403
  98.4 28.1 %collective-permute-start.34 = (f32[16,64,128]{2,1,0:T(8,128)S(1)}, f32[16,64,128]{2,1,0:T(8,128)S(1)}, u32[]{:S(2)}, u32[]{:S(2)}) collective-permute-start(f32[16,64,128]{2,1,0:T(8,128)S(1)} %shard_map.57.after.rest_1_.pa), channel_id=1, source_target_pairs={{0,64},{64,0},{1,65},{65,1},{2,66},{66,2},{3,67},{67,3},{4,68},{68... | collective-permute-start | bytes 1572872 | tf_op jit(solution)/shard_map/ppermute | solution.py:446
  98.6 9.2 %collective-permute-start.22 = (f32[8,32,128]{2,1,0:T(8,128)S(1)}, f32[8,32,128]{2,1,0:T(8,128)S(1)}, u32[]{:S(2)}, u32[]{:S(2)}) collective-permute-start(f32[8,32,128]{2,1,0:T(8,128)S(1)} %collective-permute-done.21), channel_id=1, source_target_pairs={{56,32},{0,24},{57,33},{1,25},{58,34},{2,26},{59,35},{3,27},{60,36... | collective-permute-start | bytes 393224 | tf_op jit(solution)/shard_map/ppermute | solution.py:405
  112.3 8.1 %collective-permute-start.30 = (f32[8,32,128]{2,1,0:T(8,128)S(1)}, f32[8,32,128]{2,1,0:T(8,128)S(1)}, u32[]{:S(2)}, u32[]{:S(2)}) collective-permute-start(f32[8,32,128]{2,1,0:T(8,128)S(1)} %get-tuple-element.75), channel_id=1, source_target_pairs={{24,56},{32,0},{25,57},{33,1},{26,58},{34,2},{27,59},{35,3},{28,60... | collective-permute-start | bytes 393224 | tf_op jit(solution)/shard_map/ppermute | solution.py:402
  113.6 7.5 %collective-permute-start.32 = (f32[8,32,128]{2,1,0:T(8,128)S(1)}, f32[8,32,128]{2,1,0:T(8,128)S(1)}, u32[]{:S(2)}, u32[]{:S(2)}) collective-permute-start(f32[8,32,128]{2,1,0:T(8,128)S(1)} %get-tuple-element.76), channel_id=1, source_target_pairs={{0,1},{1,0},{2,3},{3,2},{4,5},{5,4},{6,7},{7,6},{8,9},{9,8},{10,11... | collective-permute-start | bytes 393224 | tf_op jit(solution)/shard_map/ppermute | solution.py:410
  114.8 10.5 %collective-permute-start.33 = (f32[8,32,128]{2,1,0:T(8,128)S(1)}, f32[8,32,128]{2,1,0:T(8,128)S(1)}, u32[]{:S(2)}, u32[]{:S(2)}) collective-permute-start(f32[8,32,128]{2,1,0:T(8,128)S(1)} %get-tuple-element.77), channel_id=1, source_target_pairs={{1,2},{2,1},{3,4},{4,3},{5,6},{6,5},{9,10},{10,9},{11,12},{12,11},... | collective-permute-start | bytes 393224 | tf_op jit(solution)/shard_map/ppermute | solution.py:410
  120.3 10.3 %collective-permute-start.27 = (f32[8,64,128]{2,1,0:T(8,128)S(1)}, f32[8,64,128]{2,1,0:T(8,128)S(1)}, u32[]{:S(2)}, u32[]{:S(2)}) collective-permute-start(f32[8,64,128]{2,1,0:T(8,128)S(1)} %get-tuple-element.72), channel_id=1, source_target_pairs={{0,8},{8,0},{16,24},{24,16},{32,40},{40,32},{48,56},{56,48},{1,9},... | collective-permute-start | bytes 786440 | tf_op jit(solution)/shard_map/ppermute | solution.py:401
  120.4 10.2 %collective-permute-start.28 = (f32[8,64,128]{2,1,0:T(8,128)S(1)}, f32[8,64,128]{2,1,0:T(8,128)S(1)}, u32[]{:S(2)}, u32[]{:S(2)}) collective-permute-start(f32[8,64,128]{2,1,0:T(8,128)S(1)} %get-tuple-element.73), channel_id=1, source_target_pairs={{8,16},{16,8},{40,48},{48,40},{9,17},{17,9},{41,49},{49,41},{10,18... | collective-permute-start | bytes 786440 | tf_op jit(solution)/shard_map/ppermute | solution.py:403
  121.1 9.5 %collective-permute-start.29 = (f32[8,32,128]{2,1,0:T(8,128)S(1)}, f32[8,32,128]{2,1,0:T(8,128)S(1)}, u32[]{:S(2)}, u32[]{:S(2)}) collective-permute-start(f32[8,32,128]{2,1,0:T(8,128)S(1)} %get-tuple-element.74), channel_id=1, source_target_pairs={{24,32},{32,24},{25,33},{33,25},{26,34},{34,26},{27,35},{35,27},{2... | collective-permute-start | bytes 393224 | tf_op jit(solution)/shard_map/ppermute | solution.py:404
  125.2 9.2 %collective-permute-start.31 = (f32[8,32,128]{2,1,0:T(8,128)S(1)}, f32[8,32,128]{2,1,0:T(8,128)S(1)}, u32[]{:S(2)}, u32[]{:S(2)}) collective-permute-start(f32[8,32,128]{2,1,0:T(8,128)S(1)} %collective-permute-done.30), channel_id=1, source_target_pairs={{56,32},{0,24},{57,33},{1,25},{58,34},{2,26},{59,35},{3,27},{60,36... | collective-permute-start | bytes 393224 | tf_op jit(solution)/shard_map/ppermute | solution.py:405
  126.5 28.3 %collective-permute-start.39 = (f32[16,64,128]{2,1,0:T(8,128)S(1)}, f32[16,64,128]{2,1,0:T(8,128)S(1)}, u32[]{:S(2)}, u32[]{:S(2)}) collective-permute-start(f32[16,64,128]{2,1,0:T(8,128)S(1)} %get-tuple-element.71.pb), channel_id=1, source_target_pairs={{0,64},{64,0},{1,65},{65,1},{2,66},{66,2},{3,67},{67,3},{4,68},{68... | collective-permute-start | bytes 1572872 | tf_op jit(solution)/shard_map/ppermute | solution.py:464
  139.6 1.6 collective-permute-start.35
  141.2 6.8 %collective-permute-start.36 = (f32[7,32,128]{2,1,0:T(8,128)S(1)}, f32[7,32,128]{2,1,0:T(8,128)S(1)}, u32[]{:S(2)}, u32[]{:S(2)}) collective-permute-start(f32[7,32,128]{2,1,0:T(8,128)S(1)} %shard_map.62), channel_id=1, source_target_pairs={{0,16},{8,24},{16,0},{24,8},{32,48},{40,56},{48,32},{56,40},{1,17}... | collective-permute-start | bytes 344072 | tf_op jit(solution)/shard_map/ppermute | solution.py:416
  148.0 6.7 %collective-permute-start.37 = (f32[7,32,128]{2,1,0:T(8,128)S(1)}, f32[7,32,128]{2,1,0:T(8,128)S(1)}, u32[]{:S(2)}, u32[]{:S(2)}) collective-permute-start(f32[7,32,128]{2,1,0:T(8,128)S(1)} %add.10), channel_id=1, source_target_pairs={{0,32},{8,40},{16,48},{24,56},{1,33},{9,41},{17,49},{25,57},{2,34}... | collective-permute-start | bytes 344072 | tf_op jit(solution)/shard_map/ppermute | solution.py:416
  154.7 13.1 %collective-permute-start.38 = (f32[7,32,128]{2,1,0:T(8,128)S(1)}, f32[7,32,128]{2,1,0:T(8,128)S(1)}, u32[]{:S(2)}, u32[]{:S(2)}) collective-permute-start(f32[7,32,128]{2,1,0:T(8,128)S(1)} %shard_map.63.before), channel_id=1, source_target_pairs={{0,8},{8,0},{16,24},{24,16},{32,40},{40,32},{48,56},{56,48},{1,9},... | collective-permute-start | bytes 344072 | tf_op jit(solution)/shard_map/ppermute | solution.py:487
  155.2 1.4 collective-permute-start.40
  156.6 5.4 %collective-permute-start.41 = (f32[64,128]{1,0:T(8,128)S(1)}, f32[64,128]{1,0:T(8,128)S(1)}, u32[]{:S(2)}, u32[]{:S(2)}) collective-permute-start(f32[64,128]{1,0:T(8,128)S(1)} %add.11), channel_id=1, source_target_pairs={{0,16},{8,24},{16,0},{24,8},{32,48},{40,56},{48,32},{56,40},{1,17}... | collective-permute-start | bytes 98312 | tf_op jit(solution)/shard_map/ppermute | solution.py:416
  162.1 5.8 %collective-permute-start.42 = (f32[64,128]{1,0:T(8,128)S(1)}, f32[64,128]{1,0:T(8,128)S(1)}, u32[]{:S(2)}, u32[]{:S(2)}) collective-permute-start(f32[64,128]{1,0:T(8,128)S(1)} %add.12), channel_id=1, source_target_pairs={{0,32},{8,40},{16,48},{24,56},{1,33},{9,41},{17,49},{25,57},{2,34}... | collective-permute-start | bytes 98312 | tf_op jit(solution)/shard_map/ppermute | solution.py:416

commit v9 on v6

--- a/solution.py
+++ b/solution.py
@@ -9,6 +9,7 @@
 
 
 STEPS = 4
+LATE = 2
 BLOCK = 4
 VMEM = pl.BlockSpec(memory_space=pltpu.VMEM)
 HBM = pl.BlockSpec(memory_space=pltpu.HBM)
@@ -77,6 +78,13 @@
         lo, hi = u[j, :, 0, :], u[j, :, nk - 1, :]
         lev_e[j] = lower("lev", lo, hi)
         lev_o[j] = upper("lev", lo, hi)
+
+
+def load_a_kernel(u_in, pa, sem):
+    n = pa.shape[0]
+    copy = pltpu.make_async_copy(u_in.at[plane_at(0, u_in.shape[0]), pl.ds(n // 2, n)], pa, sem)
+    copy.start()
+    copy.wait()
 
 
 def load_kernel(u_in, d_in, f_in, u, pb, d_edge, f_edge, lon_e, lon_o, lev_e, lev_o, sem):
@@ -256,14 +264,30 @@
 
     def finish(j, depth, carry):
         total[depth - 1] = carry
-        copy_out(j, depth).start()
+
+        @pl.when(depth < nj - LATE)
+        def _():
+            copy_out(j, depth).start()
 
     bulk_planes(u, pa, pb, lon_e, lon_o, lev_e, lev_o, d, f, put, nothing, finish)
-    for depth in range(1, nj):
+    for depth in range(1, nj - LATE):
         copy_out(plane_at(depth, nj), depth).wait()
 
 
-def last_edge_kernel(u, pa, pb, lat, lon_e, lon_o, lev_e, lev_o, d, f, npa, npb, sums, total):
+def late_kernel(f, end_in, end, sem):
+    del end_in
+    nj = f.shape[0]
+    copies = []
+    for p in range(LATE):
+        j = plane_at(nj - LATE + p, nj)
+        copies.append(pltpu.make_async_copy(f.at[j], end.at[j], sem.at[p]))
+        copies[-1].start()
+    for copy in copies:
+        copy.wait()
+
+
+def last_edge_kernel(u, pa, pb, lat, lon_e, lon_o, lev_e, lev_o, d, f, npa, after, npb, sums, total):
+    del after
     edge_b_kernel(u, pa, pb, lat, lon_e, lon_o, lev_e, lev_o, d, f, npb)
     ni = sums.shape[0]
     q = ni // 4
@@ -406,8 +430,9 @@
 
     bits = lon_size.bit_length() - 1
 
-    pj = jnp.where(lax.axis_index("lat") == 0, nj - 1, 0)
-    pa = lax.dynamic_slice(initial_state, (pj, ni // 4, 0, 0), (1, half, nk, nm))[0]
+    pa = call(
+        load_a_kernel, V(half, nk, nm), VMEM, (HBM,), scratch=(pltpu.SemaphoreType.DMA,), flops=10**5
+    )(in_hbm(initial_state))
     lat_a = lax.ppermute(pa, "lat", swap)
     u, pb, d_edge, f_edge, *faces = call(
         load_kernel,
@@ -417,9 +442,9 @@
         scratch=(pltpu.SemaphoreType.DMA((nj + 4,)),),
         flops=10**6,
     )(*map(in_hbm, (initial_state, scaled_diffusivity, scaled_forcing)))
-    lev = lev_exchange(*faces[2:])
     lon = lon_exchange(*faces[:2])
     lat_b = lax.ppermute(pb, "lat", swap)
+    lev = lev_exchange(*faces[2:])
     d_edge, f_edge = in_vmem(d_edge), in_vmem(f_edge)
     d, f = in_hbm(scaled_diffusivity), in_hbm(scaled_forcing)
 
@@ -455,7 +480,7 @@
         u, pa, pb = n_u, n_pa, n_pb
 
     scale = 1.0 / (ni * lon_size)
-    end, sums, _, total = call(
+    end, sums, values, total = call(
         last_bulk_kernel,
         (H(nj, ni, nk, nm), V(nj, ni, nk, nm), V(nj, ni, nk, nm), V(nj - 1, nk, nm)),
         (HBM, VMEM, VMEM, VMEM),
@@ -465,6 +490,15 @@
         flops=2 * 10**7,
     )(u, pa, pb, *lon, *lev, in_vmem(d), in_vmem(f), n_pa)
     other = partner(0, total)
+    end = call(
+        late_kernel,
+        H(nj, ni, nk, nm),
+        HBM,
+        (VMEM, HBM),
+        scratch=(pltpu.SemaphoreType.DMA((LATE,)),),
+        aliases={1: 0},
+        flops=10**5,
+    )(in_vmem(values), in_hbm(end))
     half_total = call(half_kernel, V(nj - 1, nk // 2, nm), VMEM, (VMEM,) * 2, flops=10**5)(
         in_vmem(total), in_vmem(other)
     )
@@ -476,8 +510,12 @@
     back = lax.ppermute(mine, "lon", [(i, i ^ 1) for i in range(lon_size)])
     n_pa = in_vmem(n_pa)
     n_pb, edge_sums, edge_total = call(
-        last_edge_kernel, (V(half, nk, nm), V(ni, nk, nm), V(nk, nm)), (VMEM,) * 3, (VMEM,) * 11, flops=2 * 10**6
-    )(u, pa, pb, lat_b, *lon, *lev, d_edge, f_edge, n_pa)
+        last_edge_kernel,
+        (V(half, nk, nm), V(ni, nk, nm), V(nk, nm)),
+        (VMEM,) * 3,
+        (VMEM,) * 11 + (ANY,),
+        flops=2 * 10**6,
+    )(u, pa, pb, lat_b, *lon, *lev, d_edge, f_edge, n_pa, in_hbm(end))
     others = []
     edge_total_1 = edge_total
     for bit in range(bits):

time: 147 us -> 148 us (level)
  Pallas kernels: 30.9 us -> 32.4 us
    pallas_call x0 -> x2, Pallas kernels: none -> 2.41 us  [the longest x1 1.35 us: per_device(): call(late_kernel, H(nj, ni, nk, nm), HBM, (VMEM, HBM), scratch=(pltpu.Sem...]
  transfers between devices with their start and end apart: 31 -> 31, of which waited for: 13 -> 13; matrix products, arithmetic and copies ran while one was open for 0% -> 0% of each run, Pallas kernels for 19% -> 20%
where the time goes in v9:
time: 148 us; the launch traced here: 147 us
  waiting for transfers between devices  61.7 us (42%)
  starting transfers between devices  51.5 us (35%)
  Pallas kernels  32.4 us (22%)
    ppermute x16, waiting for transfers between devices, exchange(): return (lax.ppermute(e, axis, swaps(0)), lax.ppermute(o, axis, swaps(1)))  42.7 us
    ppermute x16, starting transfers between devices, exchange(): return (lax.ppermute(e, axis, swaps(0)), lax.ppermute(o, axis, swaps(1)))  34.9 us
    ppermute x6, waiting for transfers between devices, partner(): return lax.ppermute(total, 'lon', pairs)  19 us
    pallas_call x2, Pallas kernels, per_device(): call(bulk_kernel, V(nj, ni, nk, nm), VMEM, (VMEM,) * 9 + (ANY,), flops=2...  7.72 us
    ppermute x6, starting transfers between devices, partner(): return lax.ppermute(total, 'lon', pairs)  6.81 us
    ppermute x3, starting transfers between devices, per_device(): lat_b = lax.ppermute(n_pb, 'lat', swap)  6.35 us
    pallas_call x1, Pallas kernels, per_device(): call(first_bulk_kernel, (V(nj, ni, nk, nm),) * 3, (VMEM,) * 3, (VMEM,) *...  5.85 us
    pallas_call x1, Pallas kernels, per_device(): call(load_kernel, (V(nj, ni, nk, nm), V(half, nk, nm), V(ni, nk, nm), V(n...  4.43 us
  transfers between devices with their start and end apart: 31, of which 13 were waited for; matrix products, arithmetic and copies ran while one was open for 0% of the time, Pallas kernels for 20%

profile of v9, /device:TPU:98, one launch (start us, length us, event | category | flops | bytes accessed | tf_op | source)
XLA Modules:
  0.0 146.6 jit_solution(17200116203731472881)
XLA Ops:
  0.6 1.1 shard_map.51.pa
  1.7 0.6 collective-permute-start.4
  2.3 4.4 %shard_map.50 = (f32[8,32,64,128]{3,2,1,0:T(8,128)S(1)}, f32[16,64,128]{2,1,0:T(8,128)S(1)}, f32[32,64,128]{2,1,0:T(8,128)S(1)}, f32[32,64,128]{2,1,0:T(8,128)S(...) custom-call(f32[8,32,64,128]{3,2,1,0:T(8,128)} %u_in.3, ...), custom_call_target="tpu_custom_call" | custom-call | flops 1000000 | tf_op jit(solution)/shard_map/pallas_call | solution.py:437
  6.8 1.6 %collective-permute-start.5 = (f32[16,64,128]{2,1,0:T(8,128)S(1)}, f32[16,64,128]{2,1,0:T(8,128)S(1)}, u32[]{:S(2)}, u32[]{:S(2)}) collective-permute-start(f32[16,64,128]{2,1,0:T(8,128)S(1)} %get-tuple-element.38.pb), channel_id=1, source_target_pairs={{0,64},{64,0},{1,65},{65,1},{2,66},{66,2},{3,67},{67,3},{4,68},{68... | collective-permute-start | bytes 1572872 | tf_op jit(solution)/shard_map/ppermute | solution.py:446
  8.3 1.6 %collective-permute-start.2 = (f32[8,32,128]{2,1,0:T(8,128)S(1)}, f32[8,32,128]{2,1,0:T(8,128)S(1)}, u32[]{:S(2)}, u32[]{:S(2)}) collective-permute-start(f32[8,32,128]{2,1,0:T(8,128)S(1)} %get-tuple-element.41), channel_id=1, source_target_pairs={{0,1},{1,0},{2,3},{3,2},{4,5},{5,4},{6,7},{7,6},{8,9},{9,8},{10,11... | collective-permute-start | bytes 393224 | tf_op jit(solution)/shard_map/ppermute | solution.py:417
  9.9 4.1 %collective-permute-start.3 = (f32[8,32,128]{2,1,0:T(8,128)S(1)}, f32[8,32,128]{2,1,0:T(8,128)S(1)}, u32[]{:S(2)}, u32[]{:S(2)}) collective-permute-start(f32[8,32,128]{2,1,0:T(8,128)S(1)} %get-tuple-element.42), channel_id=1, source_target_pairs={{1,2},{2,1},{3,4},{4,3},{5,6},{6,5},{9,10},{10,9},{11,12},{12,11},... | collective-permute-start | bytes 393224 | tf_op jit(solution)/shard_map/ppermute | solution.py:417
  14.0 0.1 collective-permute-start
  14.1 0.0 collective-permute-done.2.lev_e
  14.1 3.1 %collective-permute-start.1 = (f32[8,64,128]{2,1,0:T(8,128)S(1)}, f32[8,64,128]{2,1,0:T(8,128)S(1)}, u32[]{:S(2)}, u32[]{:S(2)}) collective-permute-start(f32[8,64,128]{2,1,0:T(8,128)S(1)} %get-tuple-element.40), channel_id=1, source_target_pairs={{8,16},{16,8},{24,32},{32,24},{40,48},{48,40},{9,17},{17,9},{25,33... | collective-permute-start | bytes 786440 | tf_op jit(solution)/shard_map/ppermute | solution.py:417
  17.1 3.2 %collective-permute-done.3.lev_o = f32[8,32,128]{2,1,0:T(8,128)S(1)} collective-permute-done((f32[8,32,128]{2,1,0:T(8,128)S(1)}, f32[8,32,128]{2,1,0:T(8,128)S(1)}, u32[]{:S(2)}, u32[]{:S(2)}) %collective-permute-start.3) | collective-permute-done | bytes 131104 | tf_op jit(solution)/shard_map/ppermute | solution.py:417
  20.4 0.3 shard_map.52.after.rest_1_.pa
  20.6 0.6 collective-permute-start.10
  21.3 10.7 %collective-permute-done.1.lon_o = f32[8,64,128]{2,1,0:T(8,128)S(1)} collective-permute-done((f32[8,64,128]{2,1,0:T(8,128)S(1)}, f32[8,64,128]{2,1,0:T(8,128)S(1)}, u32[]{:S(2)}, u32[]{:S(2)}) %collective-permute-start.1) | collective-permute-done | bytes 262176 | tf_op jit(solution)/shard_map/ppermute | solution.py:417
  31.9 5.9 %shard_map.53 = (f32[8,32,64,128]{3,2,1,0:T(8,128)S(1)}, f32[8,32,64,128]{3,2,1,0:T(8,128)S(1)}, f32[8,32,64,128]{3,2,1,0:T(8,128)S(1)}) custom-call(f32[8,32,64,128]{3,2,1,0:T(8,128)S(1)} %get-tuple-element.37.u, f32[16,64,128]{2,1,0:T(8,128)S(1)} %shard_map.51.pa, f32[16,64,128]{2,1,0:T(8,128)S(1)} %get-tuple-element.38.pb, ...), custom_call_target="tpu_custom_call" | custom-call | flops 20000000 | tf_op jit(solution)/shard_map/pallas_call | solution.py:462
  37.8 0.0 copy-start
  37.8 0.5 shard_map.54
  38.4 1.9 %collective-permute-start.11 = (f32[16,64,128]{2,1,0:T(8,128)S(1)}, f32[16,64,128]{2,1,0:T(8,128)S(1)}, u32[]{:S(2)}, u32[]{:S(2)}) collective-permute-start(f32[16,64,128]{2,1,0:T(8,128)S(1)} %get-tuple-element.46.pb), channel_id=1, source_target_pairs={{0,64},{64,0},{1,65},{65,1},{2,66},{66,2},{3,67},{67,3},{4,68},{68... | collective-permute-start | bytes 1572872 | tf_op jit(solution)/shard_map/ppermute | solution.py:478
  40.2 1.6 %collective-permute-start.8 = (f32[8,32,128]{2,1,0:T(8,128)S(1)}, f32[8,32,128]{2,1,0:T(8,128)S(1)}, u32[]{:S(2)}, u32[]{:S(2)}) collective-permute-start(f32[8,32,128]{2,1,0:T(8,128)S(1)} %get-tuple-element.49), channel_id=1, source_target_pairs={{0,1},{1,0},{2,3},{3,2},{4,5},{5,4},{6,7},{7,6},{8,9},{9,8},{10,11... | collective-permute-start | bytes 393224 | tf_op jit(solution)/shard_map/ppermute | solution.py:417
  41.8 3.8 %collective-permute-start.9 = (f32[8,32,128]{2,1,0:T(8,128)S(1)}, f32[8,32,128]{2,1,0:T(8,128)S(1)}, u32[]{:S(2)}, u32[]{:S(2)}) collective-permute-start(f32[8,32,128]{2,1,0:T(8,128)S(1)} %get-tuple-element.50), channel_id=1, source_target_pairs={{1,2},{2,1},{3,4},{4,3},{5,6},{6,5},{9,10},{10,9},{11,12},{12,11},... | collective-permute-start | bytes 393224 | tf_op jit(solution)/shard_map/ppermute | solution.py:417
  45.6 1.8 %collective-permute-start.6 = (f32[8,64,128]{2,1,0:T(8,128)S(1)}, f32[8,64,128]{2,1,0:T(8,128)S(1)}, u32[]{:S(2)}, u32[]{:S(2)}) collective-permute-start(f32[8,64,128]{2,1,0:T(8,128)S(1)} %get-tuple-element.47), channel_id=1, source_target_pairs={{0,8},{8,0},{16,24},{24,16},{32,40},{40,32},{48,56},{56,48},{1,9},... | collective-permute-start | bytes 786440 | tf_op jit(solution)/shard_map/ppermute | solution.py:417
  47.4 2.1 %collective-permute-start.7 = (f32[8,64,128]{2,1,0:T(8,128)S(1)}, f32[8,64,128]{2,1,0:T(8,128)S(1)}, u32[]{:S(2)}, u32[]{:S(2)}) collective-permute-start(f32[8,64,128]{2,1,0:T(8,128)S(1)} %get-tuple-element.48), channel_id=1, source_target_pairs={{8,16},{16,8},{24,32},{32,24},{40,48},{48,40},{9,17},{17,9},{25,33... | collective-permute-start | bytes 786440 | tf_op jit(solution)/shard_map/ppermute | solution.py:417
  49.4 3.5 %collective-permute-done.9.lev_o = f32[8,32,128]{2,1,0:T(8,128)S(1)} collective-permute-done((f32[8,32,128]{2,1,0:T(8,128)S(1)}, f32[8,32,128]{2,1,0:T(8,128)S(1)}, u32[]{:S(2)}, u32[]{:S(2)}) %collective-permute-start.9) | collective-permute-done | bytes 131104 | tf_op jit(solution)/shard_map/ppermute | solution.py:417
  53.0 0.3 shard_map.55.after.rest_1_.pa
  53.2 0.1 collective-permute-start.16
  53.4 7.6 %collective-permute-done.7.lon_o = f32[8,64,128]{2,1,0:T(8,128)S(1)} collective-permute-done((f32[8,64,128]{2,1,0:T(8,128)S(1)}, f32[8,64,128]{2,1,0:T(8,128)S(1)}, u32[]{:S(2)}, u32[]{:S(2)}) %collective-permute-start.7) | collective-permute-done | bytes 262176 | tf_op jit(solution)/shard_map/ppermute | solution.py:417
  61.0 3.9 %shard_map.56.rest_0_.u = f32[8,32,64,128]{3,2,1,0:T(8,128)S(1)} custom-call(f32[8,32,64,128]{3,2,1,0:T(8,128)S(1)} %get-tuple-element.45.rest_0_.u, f32[16,64,128]{2,1,0:T(8,128)S(1)} %shard_map.52.after.rest_1_.pa, f32[16,64,128]{2,1,0:T(8,128)S(1)} %get-tuple-element.46.pb, f32[8,64,128]{2,1,0:T(8,128)S(1)} %collective-permute-done.6.lon_e, ...), custom_call_target="tpu_custom_call" | custom-call | flops 20000000 | tf_op jit(solution)/shard_map/pallas_call | solution.py:471
  64.9 0.5 shard_map.57
  65.4 1.8 %collective-permute-start.17 = (f32[16,64,128]{2,1,0:T(8,128)S(1)}, f32[16,64,128]{2,1,0:T(8,128)S(1)}, u32[]{:S(2)}, u32[]{:S(2)}) collective-permute-start(f32[16,64,128]{2,1,0:T(8,128)S(1)} %get-tuple-element.53.pb), channel_id=1, source_target_pairs={{0,64},{64,0},{1,65},{65,1},{2,66},{66,2},{3,67},{67,3},{4,68},{68... | collective-permute-start | bytes 1572872 | tf_op jit(solution)/shard_map/ppermute | solution.py:478
  67.3 1.6 %collective-permute-start.14 = (f32[8,32,128]{2,1,0:T(8,128)S(1)}, f32[8,32,128]{2,1,0:T(8,128)S(1)}, u32[]{:S(2)}, u32[]{:S(2)}) collective-permute-start(f32[8,32,128]{2,1,0:T(8,128)S(1)} %get-tuple-element.56), channel_id=1, source_target_pairs={{0,1},{1,0},{2,3},{3,2},{4,5},{5,4},{6,7},{7,6},{8,9},{9,8},{10,11... | collective-permute-start | bytes 393224 | tf_op jit(solution)/shard_map/ppermute | solution.py:417
  68.8 4.1 %collective-permute-start.15 = (f32[8,32,128]{2,1,0:T(8,128)S(1)}, f32[8,32,128]{2,1,0:T(8,128)S(1)}, u32[]{:S(2)}, u32[]{:S(2)}) collective-permute-start(f32[8,32,128]{2,1,0:T(8,128)S(1)} %get-tuple-element.57), channel_id=1, source_target_pairs={{1,2},{2,1},{3,4},{4,3},{5,6},{6,5},{9,10},{10,9},{11,12},{12,11},... | collective-permute-start | bytes 393224 | tf_op jit(solution)/shard_map/ppermute | solution.py:417
  72.9 0.6 collective-permute-start.12
  73.5 1.9 %collective-permute-start.13 = (f32[8,64,128]{2,1,0:T(8,128)S(1)}, f32[8,64,128]{2,1,0:T(8,128)S(1)}, u32[]{:S(2)}, u32[]{:S(2)}) collective-permute-start(f32[8,64,128]{2,1,0:T(8,128)S(1)} %get-tuple-element.55), channel_id=1, source_target_pairs={{8,16},{16,8},{24,32},{32,24},{40,48},{48,40},{9,17},{17,9},{25,33... | collective-permute-start | bytes 786440 | tf_op jit(solution)/shard_map/ppermute | solution.py:417
  75.4 4.6 %collective-permute-done.15.lev_o = f32[8,32,128]{2,1,0:T(8,128)S(1)} collective-permute-done((f32[8,32,128]{2,1,0:T(8,128)S(1)}, f32[8,32,128]{2,1,0:T(8,128)S(1)}, u32[]{:S(2)}, u32[]{:S(2)}) %collective-permute-start.15) | collective-permute-done | bytes 131104 | tf_op jit(solution)/shard_map/ppermute | solution.py:417
  80.0 0.3 shard_map.58.after.rest_1_.pa
  80.3 0.5 collective-permute-start.22
  80.7 8.4 %collective-permute-done.13.lon_o = f32[8,64,128]{2,1,0:T(8,128)S(1)} collective-permute-done((f32[8,64,128]{2,1,0:T(8,128)S(1)}, f32[8,64,128]{2,1,0:T(8,128)S(1)}, u32[]{:S(2)}, u32[]{:S(2)}) %collective-permute-start.13) | collective-permute-done | bytes 262176 | tf_op jit(solution)/shard_map/ppermute | solution.py:417
  89.1 3.9 %shard_map.59.rest_0_.u = f32[8,32,64,128]{3,2,1,0:T(8,128)S(1)} custom-call(f32[8,32,64,128]{3,2,1,0:T(8,128)S(1)} %shard_map.56.rest_0_.u, f32[16,64,128]{2,1,0:T(8,128)S(1)} %shard_map.55.after.rest_1_.pa, f32[16,64,128]{2,1,0:T(8,128)S(1)} %get-tuple-element.53.pb, f32[8,64,128]{2,1,0:T(8,128)S(1)} %collective-permute-done.12.lon_e, ...), custom_call_target="tpu_custom_call" | custom-call | flops 20000000 | tf_op jit(solution)/shard_map/pallas_call | solution.py:471
  93.0 0.5 shard_map.60
  93.5 0.0 copy-start.1
  93.5 0.1 collective-permute-start.18
  93.6 3.0 %collective-permute-start.19 = (f32[8,64,128]{2,1,0:T(8,128)S(1)}, f32[8,64,128]{2,1,0:T(8,128)S(1)}, u32[]{:S(2)}, u32[]{:S(2)}) collective-permute-start(f32[8,64,128]{2,1,0:T(8,128)S(1)} %get-tuple-element.60), channel_id=1, source_target_pairs={{8,16},{16,8},{24,32},{32,24},{40,48},{48,40},{9,17},{17,9},{25,33... | collective-permute-start | bytes 786440 | tf_op jit(solution)/shard_map/ppermute | solution.py:417
  96.7 1.7 %collective-permute-start.20 = (f32[8,32,128]{2,1,0:T(8,128)S(1)}, f32[8,32,128]{2,1,0:T(8,128)S(1)}, u32[]{:S(2)}, u32[]{:S(2)}) collective-permute-start(f32[8,32,128]{2,1,0:T(8,128)S(1)} %get-tuple-element.61), channel_id=1, source_target_pairs={{0,1},{1,0},{2,3},{3,2},{4,5},{5,4},{6,7},{7,6},{8,9},{9,8},{10,11... | collective-permute-start | bytes 393224 | tf_op jit(solution)/shard_map/ppermute | solution.py:417
  98.3 4.1 %collective-permute-start.21 = (f32[8,32,128]{2,1,0:T(8,128)S(1)}, f32[8,32,128]{2,1,0:T(8,128)S(1)}, u32[]{:S(2)}, u32[]{:S(2)}) collective-permute-start(f32[8,32,128]{2,1,0:T(8,128)S(1)} %get-tuple-element.62), channel_id=1, source_target_pairs={{1,2},{2,1},{3,4},{4,3},{5,6},{6,5},{9,10},{10,9},{11,12},{12,11},... | collective-permute-start | bytes 393224 | tf_op jit(solution)/shard_map/ppermute | solution.py:417
  102.4 2.6 %collective-permute-start.27 = (f32[16,64,128]{2,1,0:T(8,128)S(1)}, f32[16,64,128]{2,1,0:T(8,128)S(1)}, u32[]{:S(2)}, u32[]{:S(2)}) collective-permute-start(f32[16,64,128]{2,1,0:T(8,128)S(1)} %get-tuple-element.58.pb), channel_id=1, source_target_pairs={{0,64},{64,0},{1,65},{65,1},{2,66},{66,2},{3,67},{67,3},{4,68},{68... | collective-permute-start | bytes 1572872 | tf_op jit(solution)/shard_map/ppermute | solution.py:478
  105.0 4.7 %collective-permute-done.21.lev_o = f32[8,32,128]{2,1,0:T(8,128)S(1)} collective-permute-done((f32[8,32,128]{2,1,0:T(8,128)S(1)}, f32[8,32,128]{2,1,0:T(8,128)S(1)}, u32[]{:S(2)}, u32[]{:S(2)}) %collective-permute-start.21) | collective-permute-done | bytes 131104 | tf_op jit(solution)/shard_map/ppermute | solution.py:417
  109.7 0.3 shard_map.61.after.npa
  110.0 4.3 %shard_map.62 = (f32[8,32,64,128]{3,2,1,0:T(8,128)}, f32[8,32,64,128]{3,2,1,0:T(8,128)S(1)}, f32[8,32,64,128]{3,2,1,0:T(8,128)S(1)}, f32[7,64,128]{2,1,0:T(8,128)S(1)}) custom-call(f32[8,32,64,128]{3,2,1,0:T(8,128)S(1)} %shard_map.59.rest_0_.u, f32[16,64,128]{2,1,0:T(8,128)S(1)} %shard_map.58.after.rest_1_.pa, ...), custom_call_target="tpu_custom_call", output_to_operand_aliasing={{1}: (7, {}), {2}: (8, {})} | custom-call | flops 20000000 | tf_op jit(solution)/shard_map/pallas_call | solution.py:483
  114.3 0.4 collective-permute-start.23
  114.7 1.2 collective-permute-done.23.other
  115.9 1.8 %collective-permute-start.24 = (f32[7,32,128]{2,1,0:T(8,128)S(1)}, f32[7,32,128]{2,1,0:T(8,128)S(1)}, u32[]{:S(2)}, u32[]{:S(2)}) collective-permute-start(f32[7,32,128]{2,1,0:T(8,128)S(1)} %shard_map.63), channel_id=1, source_target_pairs={{0,16},{8,24},{16,0},{24,8},{32,48},{40,56},{48,32},{56,40},{1,17}... | collective-permute-start | bytes 344072 | tf_op jit(solution)/shard_map/ppermute | solution.py:429
  117.7 5.1 %collective-permute-done.24.refs_0_ = f32[7,32,128]{2,1,0:T(8,128)S(1)} collective-permute-done((f32[7,32,128]{2,1,0:T(8,128)S(1)}, f32[7,32,128]{2,1,0:T(8,128)S(1)}, u32[]{:S(2)}, u32[]{:S(2)}) %collective-permute-start.24) | collective-permute-done | bytes 114720 | tf_op jit(solution)/shard_map/ppermute | solution.py:429
  122.8 1.3 collective-permute-start.25
  124.1 5.4 %collective-permute-done.25.refs_1_ = f32[7,32,128]{2,1,0:T(8,128)S(1)} collective-permute-done((f32[7,32,128]{2,1,0:T(8,128)S(1)}, f32[7,32,128]{2,1,0:T(8,128)S(1)}, u32[]{:S(2)}, u32[]{:S(2)}) %collective-permute-start.25) | collective-permute-done | bytes 114720 | tf_op jit(solution)/shard_map/ppermute | solution.py:429
  129.5 0.1 collective-permute-start.26
  129.6 1.3 shard_map.65.after.rest_3_
  131.0 0.4 shard_map.66
  131.4 0.6 collective-permute-start.28
  131.9 0.9 collective-permute-done.28.rest_0_
  132.8 1.6 %collective-permute-start.29 = (f32[64,128]{1,0:T(8,128)S(1)}, f32[64,128]{1,0:T(8,128)S(1)}, u32[]{:S(2)}, u32[]{:S(2)}) collective-permute-start(f32[64,128]{1,0:T(8,128)S(1)} %add.10), channel_id=1, source_target_pairs={{0,16},{8,24},{16,0},{24,8},{32,48},{40,56},{48,32},{56,40},{1,17}... | collective-permute-start | bytes 98312 | tf_op jit(solution)/shard_map/ppermute | solution.py:429
  134.3 3.9 %collective-permute-done.29.rest_1_ = f32[64,128]{1,0:T(8,128)S(1)} collective-permute-done((f32[64,128]{1,0:T(8,128)S(1)}, f32[64,128]{1,0:T(8,128)S(1)}, u32[]{:S(2)}, u32[]{:S(2)}) %collective-permute-start.29) | collective-permute-done | bytes 32800 | tf_op jit(solution)/shard_map/ppermute | solution.py:429
  138.2 1.3 collective-permute-start.30
  139.5 2.0 %shard_map.67.rest_4_ = f32[8,32,64,128]{3,2,1,0:T(8,128)} custom-call(f32[8,32,64,128]{3,2,1,0:T(8,128)S(1)} %get-tuple-element.63.sums, f32[7,64,128]{2,1,0:T(8,128)S(1)} %collective-permute-done.23.other, f32[7,32,128]{2,1,0:T(8,128)S(1)} %shard_map.64.before, f32[64,128]{1,0:T(8,128)S(1)} %get-tuple-element.69.after), custom_call_target="tpu_custom_call" | custom-call | flops 1000000 | tf_op jit(solution)/shard_map/pallas_call | solution.py:526
  141.5 2.5 %collective-permute-done.30.rest_2_ = f32[64,128]{1,0:T(8,128)S(1)} collective-permute-done((f32[64,128]{1,0:T(8,128)S(1)}, f32[64,128]{1,0:T(8,128)S(1)}, u32[]{:S(2)}, u32[]{:S(2)}) %collective-permute-start.30) | collective-permute-done | bytes 32800 | tf_op jit(solution)/shard_map/ppermute | solution.py:429
  144.0 2.6 %shard_map.68 = (f32[8,32,64,128]{3,2,1,0:T(8,128)}, f32[8,32,64,128]{3,2,1,0:T(8,128)}) custom-call(f32[8,32,64,128]{3,2,1,0:T(8,128)S(1)} %get-tuple-element.63.sums, f32[7,64,128]{2,1,0:T(8,128)S(1)} %collective-permute-done.23.other, f32[7,32,128]{2,1,0:T(8,128)S(1)} %collective-permute-done.26.before, ...), custom_call_target="tpu_custom_call", output_to_operand_aliasing={{0}: (9, {}), {1}: (10, {})} | custom-call | flops 1000000 | tf_op jit(solution)/shard_map/pallas_call | solution.py:536
  (24 shorter events, 0.1 us)
Async XLA Ops:
  1.7 18.7 %collective-permute-start.4 = (f32[16,64,128]{2,1,0:T(8,128)S(1)}, f32[16,64,128]{2,1,0:T(8,128)S(1)}, u32[]{:S(2)}, u32[]{:S(2)}) collective-permute-start(f32[16,64,128]{2,1,0:T(8,128)S(1)} %shard_map.51.pa), channel_id=1, source_target_pairs={{0,64},{64,0},{1,65},{65,1},{2,66},{66,2},{3,67},{67,3},{4,68},{68... | collective-permute-start | bytes 1572872 | tf_op jit(solution)/shard_map/ppermute | solution.py:436
  6.8 31.0 %collective-permute-start.5 = (f32[16,64,128]{2,1,0:T(8,128)S(1)}, f32[16,64,128]{2,1,0:T(8,128)S(1)}, u32[]{:S(2)}, u32[]{:S(2)}) collective-permute-start(f32[16,64,128]{2,1,0:T(8,128)S(1)} %get-tuple-element.38.pb), channel_id=1, source_target_pairs={{0,64},{64,0},{1,65},{65,1},{2,66},{66,2},{3,67},{67,3},{4,68},{68... | collective-permute-start | bytes 1572872 | tf_op jit(solution)/shard_map/ppermute | solution.py:446
  8.3 5.7 %collective-permute-start.2 = (f32[8,32,128]{2,1,0:T(8,128)S(1)}, f32[8,32,128]{2,1,0:T(8,128)S(1)}, u32[]{:S(2)}, u32[]{:S(2)}) collective-permute-start(f32[8,32,128]{2,1,0:T(8,128)S(1)} %get-tuple-element.41), channel_id=1, source_target_pairs={{0,1},{1,0},{2,3},{3,2},{4,5},{5,4},{6,7},{7,6},{8,9},{9,8},{10,11... | collective-permute-start | bytes 393224 | tf_op jit(solution)/shard_map/ppermute | solution.py:417
  9.9 10.5 %collective-permute-start.3 = (f32[8,32,128]{2,1,0:T(8,128)S(1)}, f32[8,32,128]{2,1,0:T(8,128)S(1)}, u32[]{:S(2)}, u32[]{:S(2)}) collective-permute-start(f32[8,32,128]{2,1,0:T(8,128)S(1)} %get-tuple-element.42), channel_id=1, source_target_pairs={{1,2},{2,1},{3,4},{4,3},{5,6},{6,5},{9,10},{10,9},{11,12},{12,11},... | collective-permute-start | bytes 393224 | tf_op jit(solution)/shard_map/ppermute | solution.py:417
  14.0 7.3 %collective-permute-start = (f32[8,64,128]{2,1,0:T(8,128)S(1)}, f32[8,64,128]{2,1,0:T(8,128)S(1)}, u32[]{:S(2)}, u32[]{:S(2)}) collective-permute-start(f32[8,64,128]{2,1,0:T(8,128)S(1)} %get-tuple-element.39), channel_id=1, source_target_pairs={{0,8},{8,0},{16,24},{24,16},{32,40},{40,32},{48,56},{56,48},{1,9},... | collective-permute-start | bytes 786440 | tf_op jit(solution)/shard_map/ppermute | solution.py:417
  14.1 17.8 %collective-permute-start.1 = (f32[8,64,128]{2,1,0:T(8,128)S(1)}, f32[8,64,128]{2,1,0:T(8,128)S(1)}, u32[]{:S(2)}, u32[]{:S(2)}) collective-permute-start(f32[8,64,128]{2,1,0:T(8,128)S(1)} %get-tuple-element.40), channel_id=1, source_target_pairs={{8,16},{16,8},{24,32},{32,24},{40,48},{48,40},{9,17},{17,9},{25,33... | collective-permute-start | bytes 786440 | tf_op jit(solution)/shard_map/ppermute | solution.py:417
  20.6 32.3 %collective-permute-start.10 = (f32[16,64,128]{2,1,0:T(8,128)S(1)}, f32[16,64,128]{2,1,0:T(8,128)S(1)}, u32[]{:S(2)}, u32[]{:S(2)}) collective-permute-start(f32[16,64,128]{2,1,0:T(8,128)S(1)} %shard_map.52.after.rest_1_.pa), channel_id=1, source_target_pairs={{0,64},{64,0},{1,65},{65,1},{2,66},{66,2},{3,67},{67,3},{4,68},{68... | collective-permute-start | bytes 1572872 | tf_op jit(solution)/shard_map/ppermute | solution.py:460
  37.8 51.3 %copy-start = (f32[8,32,64,128]{3,2,1,0:T(8,128)}, f32[8,32,64,128]{3,2,1,0:T(8,128)S(1)}, u32[]{:S(2)}) copy-start(f32[8,32,64,128]{3,2,1,0:T(8,128)S(1)} %get-tuple-element.52.f.f_in) | copy-start | bytes 25165828
  38.4 26.5 %collective-permute-start.11 = (f32[16,64,128]{2,1,0:T(8,128)S(1)}, f32[16,64,128]{2,1,0:T(8,128)S(1)}, u32[]{:S(2)}, u32[]{:S(2)}) collective-permute-start(f32[16,64,128]{2,1,0:T(8,128)S(1)} %get-tuple-element.46.pb), channel_id=1, source_target_pairs={{0,64},{64,0},{1,65},{65,1},{2,66},{66,2},{3,67},{67,3},{4,68},{68... | collective-permute-start | bytes 1572872 | tf_op jit(solution)/shard_map/ppermute | solution.py:478
  40.2 7.1 %collective-permute-start.8 = (f32[8,32,128]{2,1,0:T(8,128)S(1)}, f32[8,32,128]{2,1,0:T(8,128)S(1)}, u32[]{:S(2)}, u32[]{:S(2)}) collective-permute-start(f32[8,32,128]{2,1,0:T(8,128)S(1)} %get-tuple-element.49), channel_id=1, source_target_pairs={{0,1},{1,0},{2,3},{3,2},{4,5},{5,4},{6,7},{7,6},{8,9},{9,8},{10,11... | collective-permute-start | bytes 393224 | tf_op jit(solution)/shard_map/ppermute | solution.py:417
  41.8 11.1 %collective-permute-start.9 = (f32[8,32,128]{2,1,0:T(8,128)S(1)}, f32[8,32,128]{2,1,0:T(8,128)S(1)}, u32[]{:S(2)}, u32[]{:S(2)}) collective-permute-start(f32[8,32,128]{2,1,0:T(8,128)S(1)} %get-tuple-element.50), channel_id=1, source_target_pairs={{1,2},{2,1},{3,4},{4,3},{5,6},{6,5},{9,10},{10,9},{11,12},{12,11},... | collective-permute-start | bytes 393224 | tf_op jit(solution)/shard_map/ppermute | solution.py:417
  45.6 7.8 %collective-permute-start.6 = (f32[8,64,128]{2,1,0:T(8,128)S(1)}, f32[8,64,128]{2,1,0:T(8,128)S(1)}, u32[]{:S(2)}, u32[]{:S(2)}) collective-permute-start(f32[8,64,128]{2,1,0:T(8,128)S(1)} %get-tuple-element.47), channel_id=1, source_target_pairs={{0,8},{8,0},{16,24},{24,16},{32,40},{40,32},{48,56},{56,48},{1,9},... | collective-permute-start | bytes 786440 | tf_op jit(solution)/shard_map/ppermute | solution.py:417
  47.4 13.6 %collective-permute-start.7 = (f32[8,64,128]{2,1,0:T(8,128)S(1)}, f32[8,64,128]{2,1,0:T(8,128)S(1)}, u32[]{:S(2)}, u32[]{:S(2)}) collective-permute-start(f32[8,64,128]{2,1,0:T(8,128)S(1)} %get-tuple-element.48), channel_id=1, source_target_pairs={{8,16},{16,8},{24,32},{32,24},{40,48},{48,40},{9,17},{17,9},{25,33... | collective-permute-start | bytes 786440 | tf_op jit(solution)/shard_map/ppermute | solution.py:417
  53.2 26.8 %collective-permute-start.16 = (f32[16,64,128]{2,1,0:T(8,128)S(1)}, f32[16,64,128]{2,1,0:T(8,128)S(1)}, u32[]{:S(2)}, u32[]{:S(2)}) collective-permute-start(f32[16,64,128]{2,1,0:T(8,128)S(1)} %shard_map.55.after.rest_1_.pa), channel_id=1, source_target_pairs={{0,64},{64,0},{1,65},{65,1},{2,66},{66,2},{3,67},{67,3},{4,68},{68... | collective-permute-start | bytes 1572872 | tf_op jit(solution)/shard_map/ppermute | solution.py:460
  65.4 27.5 %collective-permute-start.17 = (f32[16,64,128]{2,1,0:T(8,128)S(1)}, f32[16,64,128]{2,1,0:T(8,128)S(1)}, u32[]{:S(2)}, u32[]{:S(2)}) collective-permute-start(f32[16,64,128]{2,1,0:T(8,128)S(1)} %get-tuple-element.53.pb), channel_id=1, source_target_pairs={{0,64},{64,0},{1,65},{65,1},{2,66},{66,2},{3,67},{67,3},{4,68},{68... | collective-permute-start | bytes 1572872 | tf_op jit(solution)/shard_map/ppermute | solution.py:478
  67.3 6.2 %collective-permute-start.14 = (f32[8,32,128]{2,1,0:T(8,128)S(1)}, f32[8,32,128]{2,1,0:T(8,128)S(1)}, u32[]{:S(2)}, u32[]{:S(2)}) collective-permute-start(f32[8,32,128]{2,1,0:T(8,128)S(1)} %get-tuple-element.56), channel_id=1, source_target_pairs={{0,1},{1,0},{2,3},{3,2},{4,5},{5,4},{6,7},{7,6},{8,9},{9,8},{10,11... | collective-permute-start | bytes 393224 | tf_op jit(solution)/shard_map/ppermute | solution.py:417
  68.8 11.2 %collective-permute-start.15 = (f32[8,32,128]{2,1,0:T(8,128)S(1)}, f32[8,32,128]{2,1,0:T(8,128)S(1)}, u32[]{:S(2)}, u32[]{:S(2)}) collective-permute-start(f32[8,32,128]{2,1,0:T(8,128)S(1)} %get-tuple-element.57), channel_id=1, source_target_pairs={{1,2},{2,1},{3,4},{4,3},{5,6},{6,5},{9,10},{10,9},{11,12},{12,11},... | collective-permute-start | bytes 393224 | tf_op jit(solution)/shard_map/ppermute | solution.py:417
  72.9 7.8 %collective-permute-start.12 = (f32[8,64,128]{2,1,0:T(8,128)S(1)}, f32[8,64,128]{2,1,0:T(8,128)S(1)}, u32[]{:S(2)}, u32[]{:S(2)}) collective-permute-start(f32[8,64,128]{2,1,0:T(8,128)S(1)} %get-tuple-element.54), channel_id=1, source_target_pairs={{0,8},{8,0},{16,24},{24,16},{32,40},{40,32},{48,56},{56,48},{1,9},... | collective-permute-start | bytes 786440 | tf_op jit(solution)/shard_map/ppermute | solution.py:417
  73.5 15.6 %collective-permute-start.13 = (f32[8,64,128]{2,1,0:T(8,128)S(1)}, f32[8,64,128]{2,1,0:T(8,128)S(1)}, u32[]{:S(2)}, u32[]{:S(2)}) collective-permute-start(f32[8,64,128]{2,1,0:T(8,128)S(1)} %get-tuple-element.55), channel_id=1, source_target_pairs={{8,16},{16,8},{24,32},{32,24},{40,48},{48,40},{9,17},{17,9},{25,33... | collective-permute-start | bytes 786440 | tf_op jit(solution)/shard_map/ppermute | solution.py:417
  80.3 29.4 %collective-permute-start.22 = (f32[16,64,128]{2,1,0:T(8,128)S(1)}, f32[16,64,128]{2,1,0:T(8,128)S(1)}, u32[]{:S(2)}, u32[]{:S(2)}) collective-permute-start(f32[16,64,128]{2,1,0:T(8,128)S(1)} %shard_map.58.after.rest_1_.pa), channel_id=1, source_target_pairs={{0,64},{64,0},{1,65},{65,1},{2,66},{66,2},{3,67},{67,3},{4,68},{68... | collective-permute-start | bytes 1572872 | tf_op jit(solution)/shard_map/ppermute | solution.py:460
  93.5 16.5 %copy-start.1 = (f32[8,32,64,128]{3,2,1,0:T(8,128)S(1)}, f32[8,32,64,128]{3,2,1,0:T(8,128)}, u32[]{:S(2)}) copy-start(f32[8,32,64,128]{3,2,1,0:T(8,128)} %copy-done) | copy-start | bytes 25165828
  93.5 16.5 %collective-permute-start.18 = (f32[8,64,128]{2,1,0:T(8,128)S(1)}, f32[8,64,128]{2,1,0:T(8,128)S(1)}, u32[]{:S(2)}, u32[]{:S(2)}) collective-permute-start(f32[8,64,128]{2,1,0:T(8,128)S(1)} %get-tuple-element.59), channel_id=1, source_target_pairs={{0,8},{8,0},{16,24},{24,16},{32,40},{40,32},{48,56},{56,48},{1,9},... | collective-permute-start | bytes 786440 | tf_op jit(solution)/shard_map/ppermute | solution.py:417
  93.6 16.4 %collective-permute-start.19 = (f32[8,64,128]{2,1,0:T(8,128)S(1)}, f32[8,64,128]{2,1,0:T(8,128)S(1)}, u32[]{:S(2)}, u32[]{:S(2)}) collective-permute-start(f32[8,64,128]{2,1,0:T(8,128)S(1)} %get-tuple-element.60), channel_id=1, source_target_pairs={{8,16},{16,8},{24,32},{32,24},{40,48},{48,40},{9,17},{17,9},{25,33... | collective-permute-start | bytes 786440 | tf_op jit(solution)/shard_map/ppermute | solution.py:417
  96.7 5.7 %collective-permute-start.20 = (f32[8,32,128]{2,1,0:T(8,128)S(1)}, f32[8,32,128]{2,1,0:T(8,128)S(1)}, u32[]{:S(2)}, u32[]{:S(2)}) collective-permute-start(f32[8,32,128]{2,1,0:T(8,128)S(1)} %get-tuple-element.61), channel_id=1, source_target_pairs={{0,1},{1,0},{2,3},{3,2},{4,5},{5,4},{6,7},{7,6},{8,9},{9,8},{10,11... | collective-permute-start | bytes 393224 | tf_op jit(solution)/shard_map/ppermute | solution.py:417
  98.3 11.4 %collective-permute-start.21 = (f32[8,32,128]{2,1,0:T(8,128)S(1)}, f32[8,32,128]{2,1,0:T(8,128)S(1)}, u32[]{:S(2)}, u32[]{:S(2)}) collective-permute-start(f32[8,32,128]{2,1,0:T(8,128)S(1)} %get-tuple-element.62), channel_id=1, source_target_pairs={{1,2},{2,1},{3,4},{4,3},{5,6},{6,5},{9,10},{10,9},{11,12},{12,11},... | collective-permute-start | bytes 393224 | tf_op jit(solution)/shard_map/ppermute | solution.py:417
  102.4 28.6 %collective-permute-start.27 = (f32[16,64,128]{2,1,0:T(8,128)S(1)}, f32[16,64,128]{2,1,0:T(8,128)S(1)}, u32[]{:S(2)}, u32[]{:S(2)}) collective-permute-start(f32[16,64,128]{2,1,0:T(8,128)S(1)} %get-tuple-element.58.pb), channel_id=1, source_target_pairs={{0,64},{64,0},{1,65},{65,1},{2,66},{66,2},{3,67},{67,3},{4,68},{68... | collective-permute-start | bytes 1572872 | tf_op jit(solution)/shard_map/ppermute | solution.py:478
  114.3 1.6 %collective-permute-start.23 = (f32[7,64,128]{2,1,0:T(8,128)S(1)}, f32[7,64,128]{2,1,0:T(8,128)S(1)}, u32[]{:S(2)}, u32[]{:S(2)}) collective-permute-start(f32[7,64,128]{2,1,0:T(8,128)S(1)} %get-tuple-element.64.total), channel_id=1, source_target_pairs={{0,8},{8,0},{16,24},{24,16},{32,40},{40,32},{48,56},{56,48},{1,9},... | collective-permute-start | bytes 688136 | tf_op jit(solution)/shard_map/ppermute | solution.py:429
  115.9 6.9 %collective-permute-start.24 = (f32[7,32,128]{2,1,0:T(8,128)S(1)}, f32[7,32,128]{2,1,0:T(8,128)S(1)}, u32[]{:S(2)}, u32[]{:S(2)}) collective-permute-start(f32[7,32,128]{2,1,0:T(8,128)S(1)} %shard_map.63), channel_id=1, source_target_pairs={{0,16},{8,24},{16,0},{24,8},{32,48},{40,56},{48,32},{56,40},{1,17}... | collective-permute-start | bytes 344072 | tf_op jit(solution)/shard_map/ppermute | solution.py:429
  122.8 6.7 %collective-permute-start.25 = (f32[7,32,128]{2,1,0:T(8,128)S(1)}, f32[7,32,128]{2,1,0:T(8,128)S(1)}, u32[]{:S(2)}, u32[]{:S(2)}) collective-permute-start(f32[7,32,128]{2,1,0:T(8,128)S(1)} %add.9), channel_id=1, source_target_pairs={{0,32},{8,40},{16,48},{24,56},{1,33},{9,41},{17,49},{25,57},{2,34}... | collective-permute-start | bytes 344072 | tf_op jit(solution)/shard_map/ppermute | solution.py:429
  129.5 14.5 %collective-permute-start.26 = (f32[7,32,128]{2,1,0:T(8,128)S(1)}, f32[7,32,128]{2,1,0:T(8,128)S(1)}, u32[]{:S(2)}, u32[]{:S(2)}) collective-permute-start(f32[7,32,128]{2,1,0:T(8,128)S(1)} %shard_map.64.before), channel_id=1, source_target_pairs={{0,8},{8,0},{16,24},{24,16},{32,40},{40,32},{48,56},{56,48},{1,9},... | collective-permute-start | bytes 344072 | tf_op jit(solution)/shard_map/ppermute | solution.py:510
  131.4 1.4 collective-permute-start.28
  132.8 5.4 %collective-permute-start.29 = (f32[64,128]{1,0:T(8,128)S(1)}, f32[64,128]{1,0:T(8,128)S(1)}, u32[]{:S(2)}, u32[]{:S(2)}) collective-permute-start(f32[64,128]{1,0:T(8,128)S(1)} %add.10), channel_id=1, source_target_pairs={{0,16},{8,24},{16,0},{24,8},{32,48},{40,56},{48,32},{56,40},{1,17}... | collective-permute-start | bytes 98312 | tf_op jit(solution)/shard_map/ppermute | solution.py:429
  138.2 5.8 %collective-permute-start.30 = (f32[64,128]{1,0:T(8,128)S(1)}, f32[64,128]{1,0:T(8,128)S(1)}, u32[]{:S(2)}, u32[]{:S(2)}) collective-permute-start(f32[64,128]{1,0:T(8,128)S(1)} %add.11), channel_id=1, source_target_pairs={{0,32},{8,40},{16,48},{24,56},{1,33},{9,41},{17,49},{25,57},{2,34}... | collective-permute-start | bytes 98312 | tf_op jit(solution)/shard_map/ppermute | solution.py:429

commit v10 on v9

--- a/solution.py
+++ b/solution.py
@@ -416,8 +416,12 @@
 
         return lax.ppermute(e, axis, swaps(0)), lax.ppermute(o, axis, swaps(1))
 
-    def lon_exchange(e, o):
-        return exchange("lon", lon_size, e, o)
+    def lon_exchange(e, o, relay):
+        if not relay:
+            return exchange("lon", lon_size, e, o)
+        relayed = lax.ppermute(o, "lon", [(3, 7), (4, 0)])
+        e, o = (lax.ppermute(x, "lon", [p for i in a for p in ((i, i + 1), (i + 1, i))]) for x, a in ((e, (0, 2, 4, 6)), (o, (1, 5))))
+        return e, o + lax.ppermute(relayed, "lon", [(7, 4), (0, 3)])
 
     def lev_exchange(e, o):
         return exchange("lev", lev_size, e, o)
@@ -442,7 +446,7 @@
         scratch=(pltpu.SemaphoreType.DMA((nj + 4,)),),
         flops=10**6,
     )(*map(in_hbm, (initial_state, scaled_diffusivity, scaled_forcing)))
-    lon = lon_exchange(*faces[:2])
+    lon = lon_exchange(*faces[:2], True)
     lat_b = lax.ppermute(pb, "lat", swap)
     lev = lev_exchange(*faces[2:])
     d_edge, f_edge = in_vmem(d_edge), in_vmem(f_edge)
@@ -474,7 +478,7 @@
         n_pb, *faces = call(
             edge_b_kernel, (V(half, nk, nm),) + faces_out, (VMEM,) * 5, (VMEM,) * 12, flops=10**6
         )(u, pa, pb, lat_b, *lon, *lev, d_edge, f_edge, in_vmem(n_u), in_vmem(n_pa))
-        lon = lon_exchange(*faces[:2])
+        lon = lon_exchange(*faces[:2], step % 2 == 1)
         lat_b = lax.ppermute(n_pb, "lat", swap)
         lev = lev_exchange(*faces[2:])
         u, pa, pb = n_u, n_pa, n_pb

time: 148 us -> 147 us (level)
  starting transfers between devices: 51.5 us -> 49.7 us
  waiting for transfers between devices: 61.7 us -> 63.4 us
    ppermute x16 -> x12, waiting for transfers between devices: 42.7 us -> 28.1 us  [exchange(): return (lax.ppermute(e, axis, swaps(0)), lax.ppermute(o, axis, swaps(1)))]
    ppermute x0 -> x8, waiting for transfers between devices: none -> 13.2 us  [the longest x2 13.1 us: lon_exchange(): return (e, o + lax.ppermute(relayed, 'lon', [(7, 4), (0, 3)]))]
    ppermute x0 -> x8, starting transfers between devices: none -> 7.67 us  [the longest x2 3.63 us: lon_exchange(): relayed = lax.ppermute(o, 'lon', [(3, 7), (4, 0)])]
    ppermute x16 -> x12, starting transfers between devices: 34.9 us -> 30.7 us  [exchange(): return (lax.ppermute(e, axis, swaps(0)), lax.ppermute(o, axis, swaps(1)))]
    ppermute x6, starting transfers between devices: 6.81 us -> 3.59 us  [partner(): return lax.ppermute(total, 'lon', pairs)]
    ppermute x6, waiting for transfers between devices: 19 us -> 22 us  [partner(): return lax.ppermute(total, 'lon', pairs)]
    ppermute x3, starting transfers between devices: 6.35 us -> 4.44 us  [per_device(): lat_b = lax.ppermute(n_pb, 'lat', swap)]
  transfers between devices with their start and end apart: 31 -> 35, of which waited for: 13 -> 15; matrix products, arithmetic and copies ran while one was open for 0% -> 0% of each run, Pallas kernels for 20% -> 20%
where the time goes in v10:
time: 147 us
  waiting for transfers between devices  63.4 us (43%)
  starting transfers between devices  49.7 us (34%)
  Pallas kernels  32.6 us (22%)
    ppermute x12, starting transfers between devices, exchange(): return (lax.ppermute(e, axis, swaps(0)), lax.ppermute(o, axis, swaps(1)))  30.7 us
    ppermute x12, waiting for transfers between devices, exchange(): return (lax.ppermute(e, axis, swaps(0)), lax.ppermute(o, axis, swaps(1)))  28.1 us
    ppermute x6, waiting for transfers between devices, partner(): return lax.ppermute(total, 'lon', pairs)  22 us
    ppermute x2, waiting for transfers between devices, lon_exchange(): return (e, o + lax.ppermute(relayed, 'lon', [(7, 4), (0, 3)]))  13.1 us
    pallas_call x2, Pallas kernels, per_device(): call(bulk_kernel, V(nj, ni, nk, nm), VMEM, (VMEM,) * 9 + (ANY,), flops=2...  7.78 us
    pallas_call x1, Pallas kernels, per_device(): call(first_bulk_kernel, (V(nj, ni, nk, nm),) * 3, (VMEM,) * 3, (VMEM,) *...  5.88 us
    ppermute x3, starting transfers between devices, per_device(): lat_b = lax.ppermute(n_pb, 'lat', swap)  4.44 us
    pallas_call x1, Pallas kernels, per_device(): call(load_kernel, (V(nj, ni, nk, nm), V(half, nk, nm), V(ni, nk, nm), V(n...  4.43 us
  transfers between devices with their start and end apart: 35, of which 15 were waited for; matrix products, arithmetic and copies ran while one was open for 0% of the time, Pallas kernels for 20%

profile of v10, /device:TPU:98, one launch (start us, length us, event | category | flops | bytes accessed | tf_op | source)
XLA Modules:
  0.0 147.0 jit_solution(13030420952642934920)
XLA Ops:
  0.6 1.1 shard_map.51.pa
  1.7 0.6 collective-permute-start.6
  2.3 4.4 %shard_map.50 = (f32[8,32,64,128]{3,2,1,0:T(8,128)S(1)}, f32[16,64,128]{2,1,0:T(8,128)S(1)}, f32[32,64,128]{2,1,0:T(8,128)S(1)}, f32[32,64,128]{2,1,0:T(8,128)S(...) custom-call(f32[8,32,64,128]{3,2,1,0:T(8,128)} %u_in.3, ...), custom_call_target="tpu_custom_call" | custom-call | flops 1000000 | tf_op jit(solution)/shard_map/pallas_call | solution.py:441
  6.8 2.3 %collective-permute-start.2 = (f32[8,64,128]{2,1,0:T(8,128)S(1)}, f32[8,64,128]{2,1,0:T(8,128)S(1)}, u32[]{:S(2)}, u32[]{:S(2)}) collective-permute-start(f32[8,64,128]{2,1,0:T(8,128)S(1)} %get-tuple-element.40), channel_id=1, source_target_pairs={{24,56},{32,0},{25,57},{33,1},{26,58},{34,2},{27,59},{35,3},{28,60... | collective-permute-start | bytes 786440 | tf_op jit(solution)/shard_map/ppermute | solution.py:422
  9.1 1.6 %collective-permute-start.7 = (f32[16,64,128]{2,1,0:T(8,128)S(1)}, f32[16,64,128]{2,1,0:T(8,128)S(1)}, u32[]{:S(2)}, u32[]{:S(2)}) collective-permute-start(f32[16,64,128]{2,1,0:T(8,128)S(1)} %get-tuple-element.38.pb), channel_id=1, source_target_pairs={{0,64},{64,0},{1,65},{65,1},{2,66},{66,2},{3,67},{67,3},{4,68},{68... | collective-permute-start | bytes 1572872 | tf_op jit(solution)/shard_map/ppermute | solution.py:450
  10.7 1.6 %collective-permute-start.4 = (f32[8,32,128]{2,1,0:T(8,128)S(1)}, f32[8,32,128]{2,1,0:T(8,128)S(1)}, u32[]{:S(2)}, u32[]{:S(2)}) collective-permute-start(f32[8,32,128]{2,1,0:T(8,128)S(1)} %get-tuple-element.41), channel_id=1, source_target_pairs={{0,1},{1,0},{2,3},{3,2},{4,5},{5,4},{6,7},{7,6},{8,9},{9,8},{10,11... | collective-permute-start | bytes 393224 | tf_op jit(solution)/shard_map/ppermute | solution.py:417
  12.2 3.8 %collective-permute-start.5 = (f32[8,32,128]{2,1,0:T(8,128)S(1)}, f32[8,32,128]{2,1,0:T(8,128)S(1)}, u32[]{:S(2)}, u32[]{:S(2)}) collective-permute-start(f32[8,32,128]{2,1,0:T(8,128)S(1)} %get-tuple-element.42), channel_id=1, source_target_pairs={{1,2},{2,1},{3,4},{4,3},{5,6},{6,5},{9,10},{10,9},{11,12},{12,11},... | collective-permute-start | bytes 393224 | tf_op jit(solution)/shard_map/ppermute | solution.py:417
  16.0 0.7 collective-permute-start.1
  16.7 1.3 collective-permute-start.3
  18.0 4.7 %collective-permute-done.5.lev_o = f32[8,32,128]{2,1,0:T(8,128)S(1)} collective-permute-done((f32[8,32,128]{2,1,0:T(8,128)S(1)}, f32[8,32,128]{2,1,0:T(8,128)S(1)}, u32[]{:S(2)}, u32[]{:S(2)}) %collective-permute-start.5) | collective-permute-done | bytes 131104 | tf_op jit(solution)/shard_map/ppermute | solution.py:417
  22.7 0.3 shard_map.52.after.rest_1_.pa
  23.0 0.6 collective-permute-start.12
  23.6 8.5 %collective-permute-done.3 = f32[8,64,128]{2,1,0:T(8,128)S(1)} collective-permute-done((f32[8,64,128]{2,1,0:T(8,128)S(1)}, f32[8,64,128]{2,1,0:T(8,128)S(1)}, u32[]{:S(2)}, u32[]{:S(2)}) %collective-permute-start.3) | collective-permute-done | bytes 262176 | tf_op jit(solution)/shard_map/ppermute | solution.py:424
  32.1 5.9 %shard_map.53 = (f32[8,32,64,128]{3,2,1,0:T(8,128)S(1)}, f32[8,32,64,128]{3,2,1,0:T(8,128)S(1)}, f32[8,32,64,128]{3,2,1,0:T(8,128)S(1)}) custom-call(f32[8,32,64,128]{3,2,1,0:T(8,128)S(1)} %get-tuple-element.37.u, f32[16,64,128]{2,1,0:T(8,128)S(1)} %shard_map.51.pa, f32[16,64,128]{2,1,0:T(8,128)S(1)} %get-tuple-element.38.pb, ...), custom_call_target="tpu_custom_call" | custom-call | flops 20000000 | tf_op jit(solution)/shard_map/pallas_call | solution.py:466
  38.0 0.6 shard_map.54
  38.6 1.9 %collective-permute-start.13 = (f32[16,64,128]{2,1,0:T(8,128)S(1)}, f32[16,64,128]{2,1,0:T(8,128)S(1)}, u32[]{:S(2)}, u32[]{:S(2)}) collective-permute-start(f32[16,64,128]{2,1,0:T(8,128)S(1)} %get-tuple-element.46.pb), channel_id=1, source_target_pairs={{0,64},{64,0},{1,65},{65,1},{2,66},{66,2},{3,67},{67,3},{4,68},{68... | collective-permute-start | bytes 1572872 | tf_op jit(solution)/shard_map/ppermute | solution.py:482
  40.5 1.6 %collective-permute-start.10 = (f32[8,32,128]{2,1,0:T(8,128)S(1)}, f32[8,32,128]{2,1,0:T(8,128)S(1)}, u32[]{:S(2)}, u32[]{:S(2)}) collective-permute-start(f32[8,32,128]{2,1,0:T(8,128)S(1)} %get-tuple-element.49), channel_id=1, source_target_pairs={{0,1},{1,0},{2,3},{3,2},{4,5},{5,4},{6,7},{7,6},{8,9},{9,8},{10,11... | collective-permute-start | bytes 393224 | tf_op jit(solution)/shard_map/ppermute | solution.py:417
  42.1 4.1 %collective-permute-start.11 = (f32[8,32,128]{2,1,0:T(8,128)S(1)}, f32[8,32,128]{2,1,0:T(8,128)S(1)}, u32[]{:S(2)}, u32[]{:S(2)}) collective-permute-start(f32[8,32,128]{2,1,0:T(8,128)S(1)} %get-tuple-element.50), channel_id=1, source_target_pairs={{1,2},{2,1},{3,4},{4,3},{5,6},{6,5},{9,10},{10,9},{11,12},{12,11},... | collective-permute-start | bytes 393224 | tf_op jit(solution)/shard_map/ppermute | solution.py:417
  46.1 1.3 collective-permute-start.8
  47.5 1.9 %collective-permute-start.9 = (f32[8,64,128]{2,1,0:T(8,128)S(1)}, f32[8,64,128]{2,1,0:T(8,128)S(1)}, u32[]{:S(2)}, u32[]{:S(2)}) collective-permute-start(f32[8,64,128]{2,1,0:T(8,128)S(1)} %get-tuple-element.48), channel_id=1, source_target_pairs={{8,16},{16,8},{24,32},{32,24},{40,48},{48,40},{9,17},{17,9},{25,33... | collective-permute-start | bytes 786440 | tf_op jit(solution)/shard_map/ppermute | solution.py:417
  49.4 4.0 %collective-permute-done.11.lev_o = f32[8,32,128]{2,1,0:T(8,128)S(1)} collective-permute-done((f32[8,32,128]{2,1,0:T(8,128)S(1)}, f32[8,32,128]{2,1,0:T(8,128)S(1)}, u32[]{:S(2)}, u32[]{:S(2)}) %collective-permute-start.11) | collective-permute-done | bytes 131104 | tf_op jit(solution)/shard_map/ppermute | solution.py:417
  53.4 0.3 shard_map.55.after.rest_1_.pa
  53.6 0.2 collective-permute-start.20
  53.8 6.6 %collective-permute-done.9.lon_o = f32[8,64,128]{2,1,0:T(8,128)S(1)} collective-permute-done((f32[8,64,128]{2,1,0:T(8,128)S(1)}, f32[8,64,128]{2,1,0:T(8,128)S(1)}, u32[]{:S(2)}, u32[]{:S(2)}) %collective-permute-start.9) | collective-permute-done | bytes 262176 | tf_op jit(solution)/shard_map/ppermute | solution.py:417
  60.4 3.9 %shard_map.56.rest_0_.u = f32[8,32,64,128]{3,2,1,0:T(8,128)S(1)} custom-call(f32[8,32,64,128]{3,2,1,0:T(8,128)S(1)} %get-tuple-element.45.rest_0_.u, f32[16,64,128]{2,1,0:T(8,128)S(1)} %shard_map.52.after.rest_1_.pa, f32[16,64,128]{2,1,0:T(8,128)S(1)} %get-tuple-element.46.pb, f32[8,64,128]{2,1,0:T(8,128)S(1)} %collective-permute-done.8.lon_e, ...), custom_call_target="tpu_custom_call" | custom-call | flops 20000000 | tf_op jit(solution)/shard_map/pallas_call | solution.py:475
  64.2 0.6 shard_map.57
  64.8 1.3 collective-permute-start.16
  66.1 1.5 %collective-permute-start.21 = (f32[16,64,128]{2,1,0:T(8,128)S(1)}, f32[16,64,128]{2,1,0:T(8,128)S(1)}, u32[]{:S(2)}, u32[]{:S(2)}) collective-permute-start(f32[16,64,128]{2,1,0:T(8,128)S(1)} %get-tuple-element.53.pb), channel_id=1, source_target_pairs={{0,64},{64,0},{1,65},{65,1},{2,66},{66,2},{3,67},{67,3},{4,68},{68... | collective-permute-start | bytes 1572872 | tf_op jit(solution)/shard_map/ppermute | solution.py:482
  67.6 1.6 %collective-permute-start.18 = (f32[8,32,128]{2,1,0:T(8,128)S(1)}, f32[8,32,128]{2,1,0:T(8,128)S(1)}, u32[]{:S(2)}, u32[]{:S(2)}) collective-permute-start(f32[8,32,128]{2,1,0:T(8,128)S(1)} %get-tuple-element.56), channel_id=1, source_target_pairs={{0,1},{1,0},{2,3},{3,2},{4,5},{5,4},{6,7},{7,6},{8,9},{9,8},{10,11... | collective-permute-start | bytes 393224 | tf_op jit(solution)/shard_map/ppermute | solution.py:417
  69.2 3.8 %collective-permute-start.19 = (f32[8,32,128]{2,1,0:T(8,128)S(1)}, f32[8,32,128]{2,1,0:T(8,128)S(1)}, u32[]{:S(2)}, u32[]{:S(2)}) collective-permute-start(f32[8,32,128]{2,1,0:T(8,128)S(1)} %get-tuple-element.57), channel_id=1, source_target_pairs={{1,2},{2,1},{3,4},{4,3},{5,6},{6,5},{9,10},{10,9},{11,12},{12,11},... | collective-permute-start | bytes 393224 | tf_op jit(solution)/shard_map/ppermute | solution.py:417
  73.0 0.6 collective-permute-done.18.lev_e
  73.6 0.7 collective-permute-start.15
  74.2 1.3 collective-permute-start.17
  75.5 5.4 %collective-permute-done.19.lev_o = f32[8,32,128]{2,1,0:T(8,128)S(1)} collective-permute-done((f32[8,32,128]{2,1,0:T(8,128)S(1)}, f32[8,32,128]{2,1,0:T(8,128)S(1)}, u32[]{:S(2)}, u32[]{:S(2)}) %collective-permute-start.19) | collective-permute-done | bytes 131104 | tf_op jit(solution)/shard_map/ppermute | solution.py:417
  80.9 0.1 collective-permute-start.14
  81.0 0.3 shard_map.58.after.rest_1_.pa
  81.3 0.3 collective-permute-start.26
  81.6 4.6 %collective-permute-done.17 = f32[8,64,128]{2,1,0:T(8,128)S(1)} collective-permute-done((f32[8,64,128]{2,1,0:T(8,128)S(1)}, f32[8,64,128]{2,1,0:T(8,128)S(1)}, u32[]{:S(2)}, u32[]{:S(2)}) %collective-permute-start.17) | collective-permute-done | bytes 262176 | tf_op jit(solution)/shard_map/ppermute | solution.py:424
  86.3 3.9 %shard_map.59.rest_0_.u = f32[8,32,64,128]{3,2,1,0:T(8,128)S(1)} custom-call(f32[8,32,64,128]{3,2,1,0:T(8,128)S(1)} %shard_map.56.rest_0_.u, f32[16,64,128]{2,1,0:T(8,128)S(1)} %shard_map.55.after.rest_1_.pa, f32[16,64,128]{2,1,0:T(8,128)S(1)} %get-tuple-element.53.pb, f32[8,64,128]{2,1,0:T(8,128)S(1)} %collective-permute-done.14.lon_e, ...), custom_call_target="tpu_custom_call" | custom-call | flops 20000000 | tf_op jit(solution)/shard_map/pallas_call | solution.py:475
  90.2 0.6 shard_map.60
  90.8 0.6 collective-permute-start.22
  91.4 4.8 %collective-permute-start.23 = (f32[8,64,128]{2,1,0:T(8,128)S(1)}, f32[8,64,128]{2,1,0:T(8,128)S(1)}, u32[]{:S(2)}, u32[]{:S(2)}) collective-permute-start(f32[8,64,128]{2,1,0:T(8,128)S(1)} %get-tuple-element.60), channel_id=1, source_target_pairs={{8,16},{16,8},{24,32},{32,24},{40,48},{48,40},{9,17},{17,9},{25,33... | collective-permute-start | bytes 786440 | tf_op jit(solution)/shard_map/ppermute | solution.py:417
  96.2 2.2 %collective-permute-start.24 = (f32[8,32,128]{2,1,0:T(8,128)S(1)}, f32[8,32,128]{2,1,0:T(8,128)S(1)}, u32[]{:S(2)}, u32[]{:S(2)}) collective-permute-start(f32[8,32,128]{2,1,0:T(8,128)S(1)} %get-tuple-element.61), channel_id=1, source_target_pairs={{0,1},{1,0},{2,3},{3,2},{4,5},{5,4},{6,7},{7,6},{8,9},{9,8},{10,11... | collective-permute-start | bytes 393224 | tf_op jit(solution)/shard_map/ppermute | solution.py:417
  98.4 3.6 %collective-permute-start.25 = (f32[8,32,128]{2,1,0:T(8,128)S(1)}, f32[8,32,128]{2,1,0:T(8,128)S(1)}, u32[]{:S(2)}, u32[]{:S(2)}) collective-permute-start(f32[8,32,128]{2,1,0:T(8,128)S(1)} %get-tuple-element.62), channel_id=1, source_target_pairs={{1,2},{2,1},{3,4},{4,3},{5,6},{6,5},{9,10},{10,9},{11,12},{12,11},... | collective-permute-start | bytes 393224 | tf_op jit(solution)/shard_map/ppermute | solution.py:417
  102.0 0.4 collective-permute-done.24.lev_e
  102.4 1.1 collective-permute-start.31
  103.5 6.5 %collective-permute-done.25.lev_o = f32[8,32,128]{2,1,0:T(8,128)S(1)} collective-permute-done((f32[8,32,128]{2,1,0:T(8,128)S(1)}, f32[8,32,128]{2,1,0:T(8,128)S(1)}, u32[]{:S(2)}, u32[]{:S(2)}) %collective-permute-start.25) | collective-permute-done | bytes 131104 | tf_op jit(solution)/shard_map/ppermute | solution.py:417
  110.0 0.3 shard_map.61.after.npa
  110.3 4.3 %shard_map.62 = (f32[8,32,64,128]{3,2,1,0:T(8,128)}, f32[8,32,64,128]{3,2,1,0:T(8,128)S(1)}, f32[8,32,64,128]{3,2,1,0:T(8,128)S(1)}, f32[7,64,128]{2,1,0:T(8,128)S(1)}) custom-call(f32[8,32,64,128]{3,2,1,0:T(8,128)S(1)} %shard_map.59.rest_0_.u, f32[16,64,128]{2,1,0:T(8,128)S(1)} %shard_map.58.after.rest_1_.pa, ...), custom_call_target="tpu_custom_call", output_to_operand_aliasing={{1}: (7, {}), {2}: (8, {})} | custom-call | flops 20000000 | tf_op jit(solution)/shard_map/pallas_call | solution.py:487
  114.6 0.1 collective-permute-start.27
  114.7 1.5 %collective-permute-done.27.other = f32[7,64,128]{2,1,0:T(8,128)S(1)} collective-permute-done((f32[7,64,128]{2,1,0:T(8,128)S(1)}, f32[7,64,128]{2,1,0:T(8,128)S(1)}, u32[]{:S(2)}, u32[]{:S(2)}) %collective-permute-start.27) | collective-permute-done | bytes 229408 | tf_op jit(solution)/shard_map/ppermute | solution.py:433
  116.3 6.7 %collective-permute-done.28.refs_0_ = f32[7,32,128]{2,1,0:T(8,128)S(1)} collective-permute-done((f32[7,32,128]{2,1,0:T(8,128)S(1)}, f32[7,32,128]{2,1,0:T(8,128)S(1)}, u32[]{:S(2)}, u32[]{:S(2)}) %collective-permute-start.28) | collective-permute-done | bytes 114720 | tf_op jit(solution)/shard_map/ppermute | solution.py:433
  123.0 1.3 collective-permute-start.29
  124.3 5.4 %collective-permute-done.29.refs_1_ = f32[7,32,128]{2,1,0:T(8,128)S(1)} collective-permute-done((f32[7,32,128]{2,1,0:T(8,128)S(1)}, f32[7,32,128]{2,1,0:T(8,128)S(1)}, u32[]{:S(2)}, u32[]{:S(2)}) %collective-permute-start.29) | collective-permute-done | bytes 114720 | tf_op jit(solution)/shard_map/ppermute | solution.py:433
  129.8 1.3 shard_map.65.after.rest_3_
  131.2 0.4 shard_map.66
  131.5 0.6 collective-permute-start.32
  132.1 0.9 collective-permute-done.32.rest_0_
  133.0 0.3 collective-permute-start.33
  133.3 5.1 %collective-permute-done.33.rest_1_ = f32[64,128]{1,0:T(8,128)S(1)} collective-permute-done((f32[64,128]{1,0:T(8,128)S(1)}, f32[64,128]{1,0:T(8,128)S(1)}, u32[]{:S(2)}, u32[]{:S(2)}) %collective-permute-start.33) | collective-permute-done | bytes 32800 | tf_op jit(solution)/shard_map/ppermute | solution.py:433
  138.4 1.3 collective-permute-start.34
  139.7 2.0 %shard_map.67.rest_4_ = f32[8,32,64,128]{3,2,1,0:T(8,128)} custom-call(f32[8,32,64,128]{3,2,1,0:T(8,128)S(1)} %get-tuple-element.63.sums, f32[7,64,128]{2,1,0:T(8,128)S(1)} %collective-permute-done.27.other, f32[7,32,128]{2,1,0:T(8,128)S(1)} %shard_map.64.before, f32[64,128]{1,0:T(8,128)S(1)} %get-tuple-element.69.after), custom_call_target="tpu_custom_call" | custom-call | flops 1000000 | tf_op jit(solution)/shard_map/pallas_call | solution.py:530
  141.7 2.5 %collective-permute-done.34.rest_2_ = f32[64,128]{1,0:T(8,128)S(1)} collective-permute-done((f32[64,128]{1,0:T(8,128)S(1)}, f32[64,128]{1,0:T(8,128)S(1)}, u32[]{:S(2)}, u32[]{:S(2)}) %collective-permute-start.34) | collective-permute-done | bytes 32800 | tf_op jit(solution)/shard_map/ppermute | solution.py:433
  144.2 2.6 %shard_map.68 = (f32[8,32,64,128]{3,2,1,0:T(8,128)}, f32[8,32,64,128]{3,2,1,0:T(8,128)}) custom-call(f32[8,32,64,128]{3,2,1,0:T(8,128)S(1)} %get-tuple-element.63.sums, f32[7,64,128]{2,1,0:T(8,128)S(1)} %collective-permute-done.27.other, f32[7,32,128]{2,1,0:T(8,128)S(1)} %collective-permute-done.30.before, ...), custom_call_target="tpu_custom_call", output_to_operand_aliasing={{0}: (9, {}), {1}: (10, {})} | custom-call | flops 1000000 | tf_op jit(solution)/shard_map/pallas_call | solution.py:540
  (34 shorter events, 0.4 us)
Async XLA Ops:
  1.7 21.0 %collective-permute-start.6 = (f32[16,64,128]{2,1,0:T(8,128)S(1)}, f32[16,64,128]{2,1,0:T(8,128)S(1)}, u32[]{:S(2)}, u32[]{:S(2)}) collective-permute-start(f32[16,64,128]{2,1,0:T(8,128)S(1)} %shard_map.51.pa), channel_id=1, source_target_pairs={{0,64},{64,0},{1,65},{65,1},{2,66},{66,2},{3,67},{67,3},{4,68},{68... | collective-permute-start | bytes 1572872 | tf_op jit(solution)/shard_map/ppermute | solution.py:440
  6.8 10.0 %collective-permute-start.2 = (f32[8,64,128]{2,1,0:T(8,128)S(1)}, f32[8,64,128]{2,1,0:T(8,128)S(1)}, u32[]{:S(2)}, u32[]{:S(2)}) collective-permute-start(f32[8,64,128]{2,1,0:T(8,128)S(1)} %get-tuple-element.40), channel_id=1, source_target_pairs={{24,56},{32,0},{25,57},{33,1},{26,58},{34,2},{27,59},{35,3},{28,60... | collective-permute-start | bytes 786440 | tf_op jit(solution)/shard_map/ppermute | solution.py:422
  9.1 28.9 %collective-permute-start.7 = (f32[16,64,128]{2,1,0:T(8,128)S(1)}, f32[16,64,128]{2,1,0:T(8,128)S(1)}, u32[]{:S(2)}, u32[]{:S(2)}) collective-permute-start(f32[16,64,128]{2,1,0:T(8,128)S(1)} %get-tuple-element.38.pb), channel_id=1, source_target_pairs={{0,64},{64,0},{1,65},{65,1},{2,66},{66,2},{3,67},{67,3},{4,68},{68... | collective-permute-start | bytes 1572872 | tf_op jit(solution)/shard_map/ppermute | solution.py:450
  10.7 5.4 %collective-permute-start.4 = (f32[8,32,128]{2,1,0:T(8,128)S(1)}, f32[8,32,128]{2,1,0:T(8,128)S(1)}, u32[]{:S(2)}, u32[]{:S(2)}) collective-permute-start(f32[8,32,128]{2,1,0:T(8,128)S(1)} %get-tuple-element.41), channel_id=1, source_target_pairs={{0,1},{1,0},{2,3},{3,2},{4,5},{5,4},{6,7},{7,6},{8,9},{9,8},{10,11... | collective-permute-start | bytes 393224 | tf_op jit(solution)/shard_map/ppermute | solution.py:417
  12.2 10.5 %collective-permute-start.5 = (f32[8,32,128]{2,1,0:T(8,128)S(1)}, f32[8,32,128]{2,1,0:T(8,128)S(1)}, u32[]{:S(2)}, u32[]{:S(2)}) collective-permute-start(f32[8,32,128]{2,1,0:T(8,128)S(1)} %get-tuple-element.42), channel_id=1, source_target_pairs={{1,2},{2,1},{3,4},{4,3},{5,6},{6,5},{9,10},{10,9},{11,12},{12,11},... | collective-permute-start | bytes 393224 | tf_op jit(solution)/shard_map/ppermute | solution.py:417
  16.0 7.6 %collective-permute-start.1 = (f32[8,64,128]{2,1,0:T(8,128)S(1)}, f32[8,64,128]{2,1,0:T(8,128)S(1)}, u32[]{:S(2)}, u32[]{:S(2)}) collective-permute-start(f32[8,64,128]{2,1,0:T(8,128)S(1)} %get-tuple-element.40), channel_id=1, source_target_pairs={{8,16},{16,8},{40,48},{48,40},{9,17},{17,9},{41,49},{49,41},{10,18... | collective-permute-start | bytes 786440 | tf_op jit(solution)/shard_map/ppermute | solution.py:423
  16.7 15.4 %collective-permute-start.3 = (f32[8,64,128]{2,1,0:T(8,128)S(1)}, f32[8,64,128]{2,1,0:T(8,128)S(1)}, u32[]{:S(2)}, u32[]{:S(2)}) collective-permute-start(f32[8,64,128]{2,1,0:T(8,128)S(1)} %collective-permute-done.2), channel_id=1, source_target_pairs={{56,32},{0,24},{57,33},{1,25},{58,34},{2,26},{59,35},{3,27},{60,36... | collective-permute-start | bytes 786440 | tf_op jit(solution)/shard_map/ppermute | solution.py:424
  22.7 9.4 %collective-permute-start = (f32[8,64,128]{2,1,0:T(8,128)S(1)}, f32[8,64,128]{2,1,0:T(8,128)S(1)}, u32[]{:S(2)}, u32[]{:S(2)}) collective-permute-start(f32[8,64,128]{2,1,0:T(8,128)S(1)} %get-tuple-element.39), channel_id=1, source_target_pairs={{0,8},{8,0},{16,24},{24,16},{32,40},{40,32},{48,56},{56,48},{1,9},... | collective-permute-start | bytes 786440 | tf_op jit(solution)/shard_map/ppermute | solution.py:423
  23.0 30.4 %collective-permute-start.12 = (f32[16,64,128]{2,1,0:T(8,128)S(1)}, f32[16,64,128]{2,1,0:T(8,128)S(1)}, u32[]{:S(2)}, u32[]{:S(2)}) collective-permute-start(f32[16,64,128]{2,1,0:T(8,128)S(1)} %shard_map.52.after.rest_1_.pa), channel_id=1, source_target_pairs={{0,64},{64,0},{1,65},{65,1},{2,66},{66,2},{3,67},{67,3},{4,68},{68... | collective-permute-start | bytes 1572872 | tf_op jit(solution)/shard_map/ppermute | solution.py:464
  38.0 48.3 %copy-start = (f32[8,32,64,128]{3,2,1,0:T(8,128)}, f32[8,32,64,128]{3,2,1,0:T(8,128)S(1)}, u32[]{:S(2)}) copy-start(f32[8,32,64,128]{3,2,1,0:T(8,128)S(1)} %get-tuple-element.52.f.f_in) | copy-start | bytes 25165828
  38.6 25.6 %collective-permute-start.13 = (f32[16,64,128]{2,1,0:T(8,128)S(1)}, f32[16,64,128]{2,1,0:T(8,128)S(1)}, u32[]{:S(2)}, u32[]{:S(2)}) collective-permute-start(f32[16,64,128]{2,1,0:T(8,128)S(1)} %get-tuple-element.46.pb), channel_id=1, source_target_pairs={{0,64},{64,0},{1,65},{65,1},{2,66},{66,2},{3,67},{67,3},{4,68},{68... | collective-permute-start | bytes 1572872 | tf_op jit(solution)/shard_map/ppermute | solution.py:482
  40.5 7.0 %collective-permute-start.10 = (f32[8,32,128]{2,1,0:T(8,128)S(1)}, f32[8,32,128]{2,1,0:T(8,128)S(1)}, u32[]{:S(2)}, u32[]{:S(2)}) collective-permute-start(f32[8,32,128]{2,1,0:T(8,128)S(1)} %get-tuple-element.49), channel_id=1, source_target_pairs={{0,1},{1,0},{2,3},{3,2},{4,5},{5,4},{6,7},{7,6},{8,9},{9,8},{10,11... | collective-permute-start | bytes 393224 | tf_op jit(solution)/shard_map/ppermute | solution.py:417
  42.1 11.3 %collective-permute-start.11 = (f32[8,32,128]{2,1,0:T(8,128)S(1)}, f32[8,32,128]{2,1,0:T(8,128)S(1)}, u32[]{:S(2)}, u32[]{:S(2)}) collective-permute-start(f32[8,32,128]{2,1,0:T(8,128)S(1)} %get-tuple-element.50), channel_id=1, source_target_pairs={{1,2},{2,1},{3,4},{4,3},{5,6},{6,5},{9,10},{10,9},{11,12},{12,11},... | collective-permute-start | bytes 393224 | tf_op jit(solution)/shard_map/ppermute | solution.py:417
  46.1 7.7 %collective-permute-start.8 = (f32[8,64,128]{2,1,0:T(8,128)S(1)}, f32[8,64,128]{2,1,0:T(8,128)S(1)}, u32[]{:S(2)}, u32[]{:S(2)}) collective-permute-start(f32[8,64,128]{2,1,0:T(8,128)S(1)} %get-tuple-element.47), channel_id=1, source_target_pairs={{0,8},{8,0},{16,24},{24,16},{32,40},{40,32},{48,56},{56,48},{1,9},... | collective-permute-start | bytes 786440 | tf_op jit(solution)/shard_map/ppermute | solution.py:417
  47.5 12.9 %collective-permute-start.9 = (f32[8,64,128]{2,1,0:T(8,128)S(1)}, f32[8,64,128]{2,1,0:T(8,128)S(1)}, u32[]{:S(2)}, u32[]{:S(2)}) collective-permute-start(f32[8,64,128]{2,1,0:T(8,128)S(1)} %get-tuple-element.48), channel_id=1, source_target_pairs={{8,16},{16,8},{24,32},{32,24},{40,48},{48,40},{9,17},{17,9},{25,33... | collective-permute-start | bytes 786440 | tf_op jit(solution)/shard_map/ppermute | solution.py:417
  53.6 27.4 %collective-permute-start.20 = (f32[16,64,128]{2,1,0:T(8,128)S(1)}, f32[16,64,128]{2,1,0:T(8,128)S(1)}, u32[]{:S(2)}, u32[]{:S(2)}) collective-permute-start(f32[16,64,128]{2,1,0:T(8,128)S(1)} %shard_map.55.after.rest_1_.pa), channel_id=1, source_target_pairs={{0,64},{64,0},{1,65},{65,1},{2,66},{66,2},{3,67},{67,3},{4,68},{68... | collective-permute-start | bytes 1572872 | tf_op jit(solution)/shard_map/ppermute | solution.py:464
  64.8 9.4 %collective-permute-start.16 = (f32[8,64,128]{2,1,0:T(8,128)S(1)}, f32[8,64,128]{2,1,0:T(8,128)S(1)}, u32[]{:S(2)}, u32[]{:S(2)}) collective-permute-start(f32[8,64,128]{2,1,0:T(8,128)S(1)} %get-tuple-element.55), channel_id=1, source_target_pairs={{24,56},{32,0},{25,57},{33,1},{26,58},{34,2},{27,59},{35,3},{28,60... | collective-permute-start | bytes 786440 | tf_op jit(solution)/shard_map/ppermute | solution.py:422
  66.1 24.1 %collective-permute-start.21 = (f32[16,64,128]{2,1,0:T(8,128)S(1)}, f32[16,64,128]{2,1,0:T(8,128)S(1)}, u32[]{:S(2)}, u32[]{:S(2)}) collective-permute-start(f32[16,64,128]{2,1,0:T(8,128)S(1)} %get-tuple-element.53.pb), channel_id=1, source_target_pairs={{0,64},{64,0},{1,65},{65,1},{2,66},{66,2},{3,67},{67,3},{4,68},{68... | collective-permute-start | bytes 1572872 | tf_op jit(solution)/shard_map/ppermute | solution.py:482
  67.6 6.0 %collective-permute-start.18 = (f32[8,32,128]{2,1,0:T(8,128)S(1)}, f32[8,32,128]{2,1,0:T(8,128)S(1)}, u32[]{:S(2)}, u32[]{:S(2)}) collective-permute-start(f32[8,32,128]{2,1,0:T(8,128)S(1)} %get-tuple-element.56), channel_id=1, source_target_pairs={{0,1},{1,0},{2,3},{3,2},{4,5},{5,4},{6,7},{7,6},{8,9},{9,8},{10,11... | collective-permute-start | bytes 393224 | tf_op jit(solution)/shard_map/ppermute | solution.py:417
  69.2 11.7 %collective-permute-start.19 = (f32[8,32,128]{2,1,0:T(8,128)S(1)}, f32[8,32,128]{2,1,0:T(8,128)S(1)}, u32[]{:S(2)}, u32[]{:S(2)}) collective-permute-start(f32[8,32,128]{2,1,0:T(8,128)S(1)} %get-tuple-element.57), channel_id=1, source_target_pairs={{1,2},{2,1},{3,4},{4,3},{5,6},{6,5},{9,10},{10,9},{11,12},{12,11},... | collective-permute-start | bytes 393224 | tf_op jit(solution)/shard_map/ppermute | solution.py:417
  73.6 8.0 %collective-permute-start.15 = (f32[8,64,128]{2,1,0:T(8,128)S(1)}, f32[8,64,128]{2,1,0:T(8,128)S(1)}, u32[]{:S(2)}, u32[]{:S(2)}) collective-permute-start(f32[8,64,128]{2,1,0:T(8,128)S(1)} %get-tuple-element.55), channel_id=1, source_target_pairs={{8,16},{16,8},{40,48},{48,40},{9,17},{17,9},{41,49},{49,41},{10,18... | collective-permute-start | bytes 786440 | tf_op jit(solution)/shard_map/ppermute | solution.py:423
  74.2 12.0 %collective-permute-start.17 = (f32[8,64,128]{2,1,0:T(8,128)S(1)}, f32[8,64,128]{2,1,0:T(8,128)S(1)}, u32[]{:S(2)}, u32[]{:S(2)}) collective-permute-start(f32[8,64,128]{2,1,0:T(8,128)S(1)} %collective-permute-done.16), channel_id=1, source_target_pairs={{56,32},{0,24},{57,33},{1,25},{58,34},{2,26},{59,35},{3,27},{60,36... | collective-permute-start | bytes 786440 | tf_op jit(solution)/shard_map/ppermute | solution.py:424
  80.9 5.4 %collective-permute-start.14 = (f32[8,64,128]{2,1,0:T(8,128)S(1)}, f32[8,64,128]{2,1,0:T(8,128)S(1)}, u32[]{:S(2)}, u32[]{:S(2)}) collective-permute-start(f32[8,64,128]{2,1,0:T(8,128)S(1)} %get-tuple-element.54), channel_id=1, source_target_pairs={{0,8},{8,0},{16,24},{24,16},{32,40},{40,32},{48,56},{56,48},{1,9},... | collective-permute-start | bytes 786440 | tf_op jit(solution)/shard_map/ppermute | solution.py:423
  81.3 28.7 %collective-permute-start.26 = (f32[16,64,128]{2,1,0:T(8,128)S(1)}, f32[16,64,128]{2,1,0:T(8,128)S(1)}, u32[]{:S(2)}, u32[]{:S(2)}) collective-permute-start(f32[16,64,128]{2,1,0:T(8,128)S(1)} %shard_map.58.after.rest_1_.pa), channel_id=1, source_target_pairs={{0,64},{64,0},{1,65},{65,1},{2,66},{66,2},{3,67},{67,3},{4,68},{68... | collective-permute-start | bytes 1572872 | tf_op jit(solution)/shard_map/ppermute | solution.py:464
  90.8 19.5 %copy-start.1 = (f32[8,32,64,128]{3,2,1,0:T(8,128)S(1)}, f32[8,32,64,128]{3,2,1,0:T(8,128)}, u32[]{:S(2)}) copy-start(f32[8,32,64,128]{3,2,1,0:T(8,128)} %copy-done) | copy-start | bytes 25165828
  90.8 19.5 %collective-permute-start.22 = (f32[8,64,128]{2,1,0:T(8,128)S(1)}, f32[8,64,128]{2,1,0:T(8,128)S(1)}, u32[]{:S(2)}, u32[]{:S(2)}) collective-permute-start(f32[8,64,128]{2,1,0:T(8,128)S(1)} %get-tuple-element.59), channel_id=1, source_target_pairs={{0,8},{8,0},{16,24},{24,16},{32,40},{40,32},{48,56},{56,48},{1,9},... | collective-permute-start | bytes 786440 | tf_op jit(solution)/shard_map/ppermute | solution.py:417
  91.4 18.9 %collective-permute-start.23 = (f32[8,64,128]{2,1,0:T(8,128)S(1)}, f32[8,64,128]{2,1,0:T(8,128)S(1)}, u32[]{:S(2)}, u32[]{:S(2)}) collective-permute-start(f32[8,64,128]{2,1,0:T(8,128)S(1)} %get-tuple-element.60), channel_id=1, source_target_pairs={{8,16},{16,8},{24,32},{32,24},{40,48},{48,40},{9,17},{17,9},{25,33... | collective-permute-start | bytes 786440 | tf_op jit(solution)/shard_map/ppermute | solution.py:417
  96.2 6.2 %collective-permute-start.24 = (f32[8,32,128]{2,1,0:T(8,128)S(1)}, f32[8,32,128]{2,1,0:T(8,128)S(1)}, u32[]{:S(2)}, u32[]{:S(2)}) collective-permute-start(f32[8,32,128]{2,1,0:T(8,128)S(1)} %get-tuple-element.61), channel_id=1, source_target_pairs={{0,1},{1,0},{2,3},{3,2},{4,5},{5,4},{6,7},{7,6},{8,9},{9,8},{10,11... | collective-permute-start | bytes 393224 | tf_op jit(solution)/shard_map/ppermute | solution.py:417
  98.4 11.6 %collective-permute-start.25 = (f32[8,32,128]{2,1,0:T(8,128)S(1)}, f32[8,32,128]{2,1,0:T(8,128)S(1)}, u32[]{:S(2)}, u32[]{:S(2)}) collective-permute-start(f32[8,32,128]{2,1,0:T(8,128)S(1)} %get-tuple-element.62), channel_id=1, source_target_pairs={{1,2},{2,1},{3,4},{4,3},{5,6},{6,5},{9,10},{10,9},{11,12},{12,11},... | collective-permute-start | bytes 393224 | tf_op jit(solution)/shard_map/ppermute | solution.py:417
  102.4 28.8 %collective-permute-start.31 = (f32[16,64,128]{2,1,0:T(8,128)S(1)}, f32[16,64,128]{2,1,0:T(8,128)S(1)}, u32[]{:S(2)}, u32[]{:S(2)}) collective-permute-start(f32[16,64,128]{2,1,0:T(8,128)S(1)} %get-tuple-element.58.pb), channel_id=1, source_target_pairs={{0,64},{64,0},{1,65},{65,1},{2,66},{66,2},{3,67},{67,3},{4,68},{68... | collective-permute-start | bytes 1572872 | tf_op jit(solution)/shard_map/ppermute | solution.py:482
  114.6 1.6 %collective-permute-start.27 = (f32[7,64,128]{2,1,0:T(8,128)S(1)}, f32[7,64,128]{2,1,0:T(8,128)S(1)}, u32[]{:S(2)}, u32[]{:S(2)}) collective-permute-start(f32[7,64,128]{2,1,0:T(8,128)S(1)} %get-tuple-element.64.total), channel_id=1, source_target_pairs={{0,8},{8,0},{16,24},{24,16},{32,40},{40,32},{48,56},{56,48},{1,9},... | collective-permute-start | bytes 688136 | tf_op jit(solution)/shard_map/ppermute | solution.py:433
  116.2 6.8 %collective-permute-start.28 = (f32[7,32,128]{2,1,0:T(8,128)S(1)}, f32[7,32,128]{2,1,0:T(8,128)S(1)}, u32[]{:S(2)}, u32[]{:S(2)}) collective-permute-start(f32[7,32,128]{2,1,0:T(8,128)S(1)} %shard_map.63), channel_id=1, source_target_pairs={{0,16},{8,24},{16,0},{24,8},{32,48},{40,56},{48,32},{56,40},{1,17}... | collective-permute-start | bytes 344072 | tf_op jit(solution)/shard_map/ppermute | solution.py:433
  123.0 6.7 %collective-permute-start.29 = (f32[7,32,128]{2,1,0:T(8,128)S(1)}, f32[7,32,128]{2,1,0:T(8,128)S(1)}, u32[]{:S(2)}, u32[]{:S(2)}) collective-permute-start(f32[7,32,128]{2,1,0:T(8,128)S(1)} %add.17), channel_id=1, source_target_pairs={{0,32},{8,40},{16,48},{24,56},{1,33},{9,41},{17,49},{25,57},{2,34}... | collective-permute-start | bytes 344072 | tf_op jit(solution)/shard_map/ppermute | solution.py:433
  129.7 14.5 %collective-permute-start.30 = (f32[7,32,128]{2,1,0:T(8,128)S(1)}, f32[7,32,128]{2,1,0:T(8,128)S(1)}, u32[]{:S(2)}, u32[]{:S(2)}) collective-permute-start(f32[7,32,128]{2,1,0:T(8,128)S(1)} %shard_map.64.before), channel_id=1, source_target_pairs={{0,8},{8,0},{16,24},{24,16},{32,40},{40,32},{48,56},{56,48},{1,9},... | collective-permute-start | bytes 344072 | tf_op jit(solution)/shard_map/ppermute | solution.py:514
  131.5 1.4 collective-permute-start.32
  133.0 5.4 %collective-permute-start.33 = (f32[64,128]{1,0:T(8,128)S(1)}, f32[64,128]{1,0:T(8,128)S(1)}, u32[]{:S(2)}, u32[]{:S(2)}) collective-permute-start(f32[64,128]{1,0:T(8,128)S(1)} %add.18), channel_id=1, source_target_pairs={{0,16},{8,24},{16,0},{24,8},{32,48},{40,56},{48,32},{56,40},{1,17}... | collective-permute-start | bytes 98312 | tf_op jit(solution)/shard_map/ppermute | solution.py:433
  138.4 5.8 %collective-permute-start.34 = (f32[64,128]{1,0:T(8,128)S(1)}, f32[64,128]{1,0:T(8,128)S(1)}, u32[]{:S(2)}, u32[]{:S(2)}) collective-permute-start(f32[64,128]{1,0:T(8,128)S(1)} %add.19), channel_id=1, source_target_pairs={{0,32},{8,40},{16,48},{24,56},{1,33},{9,41},{17,49},{25,57},{2,34}... | collective-permute-start | bytes 98312 | tf_op jit(solution)/shard_map/ppermute | solution.py:433

commit v11 on v10

--- a/solution.py
+++ b/solution.py
@@ -286,8 +286,7 @@
         copy.wait()
 
 
-def last_edge_kernel(u, pa, pb, lat, lon_e, lon_o, lev_e, lev_o, d, f, npa, after, npb, sums, total):
-    del after
+def last_edge_kernel(u, pa, pb, lat, lon_e, lon_o, lev_e, lev_o, d, f, npa, npb, sums, total):
     edge_b_kernel(u, pa, pb, lat, lon_e, lon_o, lev_e, lev_o, d, f, npb)
     ni = sums.shape[0]
     q = ni // 4
@@ -514,12 +513,8 @@
     back = lax.ppermute(mine, "lon", [(i, i ^ 1) for i in range(lon_size)])
     n_pa = in_vmem(n_pa)
     n_pb, edge_sums, edge_total = call(
-        last_edge_kernel,
-        (V(half, nk, nm), V(ni, nk, nm), V(nk, nm)),
-        (VMEM,) * 3,
-        (VMEM,) * 11 + (ANY,),
-        flops=2 * 10**6,
-    )(u, pa, pb, lat_b, *lon, *lev, d_edge, f_edge, n_pa, in_hbm(end))
+        last_edge_kernel, (V(half, nk, nm), V(ni, nk, nm), V(nk, nm)), (VMEM,) * 3, (VMEM,) * 11, flops=2 * 10**6
+    )(u, pa, pb, lat_b, *lon, *lev, d_edge, f_edge, n_pa)
     others = []
     edge_total_1 = edge_total
     for bit in range(bits):

time: 147 us -> 147 us (level); the launches traced: 147 us -> 145 us
  no operation moved by 1% of the time
where the time goes in v11:
time: 147 us; the launch traced here: 145 us
  waiting for transfers between devices  62.3 us (42%)
  starting transfers between devices  49.3 us (34%)
  Pallas kernels  32.5 us (22%)
    ppermute x12, starting transfers between devices, exchange(): return (lax.ppermute(e, axis, swaps(0)), lax.ppermute(o, axis, swaps(1)))  30.8 us
    ppermute x12, waiting for transfers between devices, exchange(): return (lax.ppermute(e, axis, swaps(0)), lax.ppermute(o, axis, swaps(1)))  28.4 us
    ppermute x6, waiting for transfers between devices, partner(): return lax.ppermute(total, 'lon', pairs)  20.7 us
    ppermute x2, waiting for transfers between devices, lon_exchange(): return (e, o + lax.ppermute(relayed, 'lon', [(7, 4), (0, 3)]))  13.2 us
    pallas_call x2, Pallas kernels, per_device(): call(bulk_kernel, V(nj, ni, nk, nm), VMEM, (VMEM,) * 9 + (ANY,), flops=2...  7.75 us
    pallas_call x1, Pallas kernels, per_device(): call(first_bulk_kernel, (V(nj, ni, nk, nm),) * 3, (VMEM,) * 3, (VMEM,) *...  5.88 us
    pallas_call x1, Pallas kernels, per_device(): call(load_kernel, (V(nj, ni, nk, nm), V(half, nk, nm), V(ni, nk, nm), V(n...  4.43 us
    pallas_call x1, Pallas kernels, per_device(): call(last_bulk_kernel, (H(nj, ni, nk, nm), V(nj, ni, nk, nm), V(nj, ni, n...  4.28 us
  transfers between devices with their start and end apart: 35, of which 15 were waited for; matrix products, arithmetic and copies ran while one was open for 0% of the time, Pallas kernels for 20%

profile of v11, /device:TPU:98, one launch (start us, length us, event | category | flops | bytes accessed | tf_op | source)
XLA Modules:
  0.0 145.3 jit_solution(13626196776200702809)
XLA Ops:
  0.6 1.1 shard_map.51.pa
  1.7 0.6 collective-permute-start.6
  2.3 4.4 %shard_map.50 = (f32[8,32,64,128]{3,2,1,0:T(8,128)S(1)}, f32[16,64,128]{2,1,0:T(8,128)S(1)}, f32[32,64,128]{2,1,0:T(8,128)S(1)}, f32[32,64,128]{2,1,0:T(8,128)S(...) custom-call(f32[8,32,64,128]{3,2,1,0:T(8,128)} %u_in.3, ...), custom_call_target="tpu_custom_call" | custom-call | flops 1000000 | tf_op jit(solution)/shard_map/pallas_call | solution.py:440
  6.8 2.3 %collective-permute-start.2 = (f32[8,64,128]{2,1,0:T(8,128)S(1)}, f32[8,64,128]{2,1,0:T(8,128)S(1)}, u32[]{:S(2)}, u32[]{:S(2)}) collective-permute-start(f32[8,64,128]{2,1,0:T(8,128)S(1)} %get-tuple-element.40), channel_id=1, source_target_pairs={{24,56},{32,0},{25,57},{33,1},{26,58},{34,2},{27,59},{35,3},{28,60... | collective-permute-start | bytes 786440 | tf_op jit(solution)/shard_map/ppermute | solution.py:421
  9.1 1.6 %collective-permute-start.7 = (f32[16,64,128]{2,1,0:T(8,128)S(1)}, f32[16,64,128]{2,1,0:T(8,128)S(1)}, u32[]{:S(2)}, u32[]{:S(2)}) collective-permute-start(f32[16,64,128]{2,1,0:T(8,128)S(1)} %get-tuple-element.38.pb), channel_id=1, source_target_pairs={{0,64},{64,0},{1,65},{65,1},{2,66},{66,2},{3,67},{67,3},{4,68},{68... | collective-permute-start | bytes 1572872 | tf_op jit(solution)/shard_map/ppermute | solution.py:449
  10.7 1.6 %collective-permute-start.4 = (f32[8,32,128]{2,1,0:T(8,128)S(1)}, f32[8,32,128]{2,1,0:T(8,128)S(1)}, u32[]{:S(2)}, u32[]{:S(2)}) collective-permute-start(f32[8,32,128]{2,1,0:T(8,128)S(1)} %get-tuple-element.41), channel_id=1, source_target_pairs={{0,1},{1,0},{2,3},{3,2},{4,5},{5,4},{6,7},{7,6},{8,9},{9,8},{10,11... | collective-permute-start | bytes 393224 | tf_op jit(solution)/shard_map/ppermute | solution.py:416
  12.2 3.8 %collective-permute-start.5 = (f32[8,32,128]{2,1,0:T(8,128)S(1)}, f32[8,32,128]{2,1,0:T(8,128)S(1)}, u32[]{:S(2)}, u32[]{:S(2)}) collective-permute-start(f32[8,32,128]{2,1,0:T(8,128)S(1)} %get-tuple-element.42), channel_id=1, source_target_pairs={{1,2},{2,1},{3,4},{4,3},{5,6},{6,5},{9,10},{10,9},{11,12},{12,11},... | collective-permute-start | bytes 393224 | tf_op jit(solution)/shard_map/ppermute | solution.py:416
  16.0 0.7 collective-permute-start.1
  16.7 1.3 collective-permute-start.3
  18.0 4.7 %collective-permute-done.5.lev_o = f32[8,32,128]{2,1,0:T(8,128)S(1)} collective-permute-done((f32[8,32,128]{2,1,0:T(8,128)S(1)}, f32[8,32,128]{2,1,0:T(8,128)S(1)}, u32[]{:S(2)}, u32[]{:S(2)}) %collective-permute-start.5) | collective-permute-done | bytes 131104 | tf_op jit(solution)/shard_map/ppermute | solution.py:416
  22.7 0.3 shard_map.52.after.rest_1_.pa
  23.0 0.6 collective-permute-start.12
  23.6 8.5 %collective-permute-done.3 = f32[8,64,128]{2,1,0:T(8,128)S(1)} collective-permute-done((f32[8,64,128]{2,1,0:T(8,128)S(1)}, f32[8,64,128]{2,1,0:T(8,128)S(1)}, u32[]{:S(2)}, u32[]{:S(2)}) %collective-permute-start.3) | collective-permute-done | bytes 262176 | tf_op jit(solution)/shard_map/ppermute | solution.py:423
  32.1 5.9 %shard_map.53 = (f32[8,32,64,128]{3,2,1,0:T(8,128)S(1)}, f32[8,32,64,128]{3,2,1,0:T(8,128)S(1)}, f32[8,32,64,128]{3,2,1,0:T(8,128)S(1)}) custom-call(f32[8,32,64,128]{3,2,1,0:T(8,128)S(1)} %get-tuple-element.37.u, f32[16,64,128]{2,1,0:T(8,128)S(1)} %shard_map.51.pa, f32[16,64,128]{2,1,0:T(8,128)S(1)} %get-tuple-element.38.pb, ...), custom_call_target="tpu_custom_call" | custom-call | flops 20000000 | tf_op jit(solution)/shard_map/pallas_call | solution.py:465
  38.0 0.6 shard_map.54
  38.6 1.9 %collective-permute-start.13 = (f32[16,64,128]{2,1,0:T(8,128)S(1)}, f32[16,64,128]{2,1,0:T(8,128)S(1)}, u32[]{:S(2)}, u32[]{:S(2)}) collective-permute-start(f32[16,64,128]{2,1,0:T(8,128)S(1)} %get-tuple-element.46.pb), channel_id=1, source_target_pairs={{0,64},{64,0},{1,65},{65,1},{2,66},{66,2},{3,67},{67,3},{4,68},{68... | collective-permute-start | bytes 1572872 | tf_op jit(solution)/shard_map/ppermute | solution.py:481
  40.5 1.6 %collective-permute-start.10 = (f32[8,32,128]{2,1,0:T(8,128)S(1)}, f32[8,32,128]{2,1,0:T(8,128)S(1)}, u32[]{:S(2)}, u32[]{:S(2)}) collective-permute-start(f32[8,32,128]{2,1,0:T(8,128)S(1)} %get-tuple-element.49), channel_id=1, source_target_pairs={{0,1},{1,0},{2,3},{3,2},{4,5},{5,4},{6,7},{7,6},{8,9},{9,8},{10,11... | collective-permute-start | bytes 393224 | tf_op jit(solution)/shard_map/ppermute | solution.py:416
  42.1 4.1 %collective-permute-start.11 = (f32[8,32,128]{2,1,0:T(8,128)S(1)}, f32[8,32,128]{2,1,0:T(8,128)S(1)}, u32[]{:S(2)}, u32[]{:S(2)}) collective-permute-start(f32[8,32,128]{2,1,0:T(8,128)S(1)} %get-tuple-element.50), channel_id=1, source_target_pairs={{1,2},{2,1},{3,4},{4,3},{5,6},{6,5},{9,10},{10,9},{11,12},{12,11},... | collective-permute-start | bytes 393224 | tf_op jit(solution)/shard_map/ppermute | solution.py:416
  46.1 1.3 collective-permute-start.8
  47.5 1.9 %collective-permute-start.9 = (f32[8,64,128]{2,1,0:T(8,128)S(1)}, f32[8,64,128]{2,1,0:T(8,128)S(1)}, u32[]{:S(2)}, u32[]{:S(2)}) collective-permute-start(f32[8,64,128]{2,1,0:T(8,128)S(1)} %get-tuple-element.48), channel_id=1, source_target_pairs={{8,16},{16,8},{24,32},{32,24},{40,48},{48,40},{9,17},{17,9},{25,33... | collective-permute-start | bytes 786440 | tf_op jit(solution)/shard_map/ppermute | solution.py:416
  49.4 4.0 %collective-permute-done.11.lev_o = f32[8,32,128]{2,1,0:T(8,128)S(1)} collective-permute-done((f32[8,32,128]{2,1,0:T(8,128)S(1)}, f32[8,32,128]{2,1,0:T(8,128)S(1)}, u32[]{:S(2)}, u32[]{:S(2)}) %collective-permute-start.11) | collective-permute-done | bytes 131104 | tf_op jit(solution)/shard_map/ppermute | solution.py:416
  53.4 0.3 shard_map.55.after.rest_1_.pa
  53.6 0.2 collective-permute-start.20
  53.8 6.6 %collective-permute-done.9.lon_o = f32[8,64,128]{2,1,0:T(8,128)S(1)} collective-permute-done((f32[8,64,128]{2,1,0:T(8,128)S(1)}, f32[8,64,128]{2,1,0:T(8,128)S(1)}, u32[]{:S(2)}, u32[]{:S(2)}) %collective-permute-start.9) | collective-permute-done | bytes 262176 | tf_op jit(solution)/shard_map/ppermute | solution.py:416
  60.3 3.9 %shard_map.56.rest_0_.u = f32[8,32,64,128]{3,2,1,0:T(8,128)S(1)} custom-call(f32[8,32,64,128]{3,2,1,0:T(8,128)S(1)} %get-tuple-element.45.rest_0_.u, f32[16,64,128]{2,1,0:T(8,128)S(1)} %shard_map.52.after.rest_1_.pa, f32[16,64,128]{2,1,0:T(8,128)S(1)} %get-tuple-element.46.pb, f32[8,64,128]{2,1,0:T(8,128)S(1)} %collective-permute-done.8.lon_e, ...), custom_call_target="tpu_custom_call" | custom-call | flops 20000000 | tf_op jit(solution)/shard_map/pallas_call | solution.py:474
  64.2 0.6 shard_map.57
  64.8 1.3 collective-permute-start.16
  66.1 1.5 %collective-permute-start.21 = (f32[16,64,128]{2,1,0:T(8,128)S(1)}, f32[16,64,128]{2,1,0:T(8,128)S(1)}, u32[]{:S(2)}, u32[]{:S(2)}) collective-permute-start(f32[16,64,128]{2,1,0:T(8,128)S(1)} %get-tuple-element.53.pb), channel_id=1, source_target_pairs={{0,64},{64,0},{1,65},{65,1},{2,66},{66,2},{3,67},{67,3},{4,68},{68... | collective-permute-start | bytes 1572872 | tf_op jit(solution)/shard_map/ppermute | solution.py:481
  67.6 1.6 %collective-permute-start.18 = (f32[8,32,128]{2,1,0:T(8,128)S(1)}, f32[8,32,128]{2,1,0:T(8,128)S(1)}, u32[]{:S(2)}, u32[]{:S(2)}) collective-permute-start(f32[8,32,128]{2,1,0:T(8,128)S(1)} %get-tuple-element.56), channel_id=1, source_target_pairs={{0,1},{1,0},{2,3},{3,2},{4,5},{5,4},{6,7},{7,6},{8,9},{9,8},{10,11... | collective-permute-start | bytes 393224 | tf_op jit(solution)/shard_map/ppermute | solution.py:416
  69.2 3.8 %collective-permute-start.19 = (f32[8,32,128]{2,1,0:T(8,128)S(1)}, f32[8,32,128]{2,1,0:T(8,128)S(1)}, u32[]{:S(2)}, u32[]{:S(2)}) collective-permute-start(f32[8,32,128]{2,1,0:T(8,128)S(1)} %get-tuple-element.57), channel_id=1, source_target_pairs={{1,2},{2,1},{3,4},{4,3},{5,6},{6,5},{9,10},{10,9},{11,12},{12,11},... | collective-permute-start | bytes 393224 | tf_op jit(solution)/shard_map/ppermute | solution.py:416
  73.0 0.6 collective-permute-done.18.lev_e
  73.5 0.7 collective-permute-start.15
  74.2 1.3 collective-permute-start.17
  75.5 5.4 %collective-permute-done.19.lev_o = f32[8,32,128]{2,1,0:T(8,128)S(1)} collective-permute-done((f32[8,32,128]{2,1,0:T(8,128)S(1)}, f32[8,32,128]{2,1,0:T(8,128)S(1)}, u32[]{:S(2)}, u32[]{:S(2)}) %collective-permute-start.19) | collective-permute-done | bytes 131104 | tf_op jit(solution)/shard_map/ppermute | solution.py:416
  80.9 0.1 collective-permute-start.14
  81.0 0.3 shard_map.58.after.rest_1_.pa
  81.3 0.3 collective-permute-start.26
  81.5 4.7 %collective-permute-done.17 = f32[8,64,128]{2,1,0:T(8,128)S(1)} collective-permute-done((f32[8,64,128]{2,1,0:T(8,128)S(1)}, f32[8,64,128]{2,1,0:T(8,128)S(1)}, u32[]{:S(2)}, u32[]{:S(2)}) %collective-permute-start.17) | collective-permute-done | bytes 262176 | tf_op jit(solution)/shard_map/ppermute | solution.py:423
  86.3 3.9 %shard_map.59.rest_0_.u = f32[8,32,64,128]{3,2,1,0:T(8,128)S(1)} custom-call(f32[8,32,64,128]{3,2,1,0:T(8,128)S(1)} %shard_map.56.rest_0_.u, f32[16,64,128]{2,1,0:T(8,128)S(1)} %shard_map.55.after.rest_1_.pa, f32[16,64,128]{2,1,0:T(8,128)S(1)} %get-tuple-element.53.pb, f32[8,64,128]{2,1,0:T(8,128)S(1)} %collective-permute-done.14.lon_e, ...), custom_call_target="tpu_custom_call" | custom-call | flops 20000000 | tf_op jit(solution)/shard_map/pallas_call | solution.py:474
  90.2 0.6 shard_map.60
  90.7 0.6 collective-permute-start.22
  91.4 4.7 %collective-permute-start.23 = (f32[8,64,128]{2,1,0:T(8,128)S(1)}, f32[8,64,128]{2,1,0:T(8,128)S(1)}, u32[]{:S(2)}, u32[]{:S(2)}) collective-permute-start(f32[8,64,128]{2,1,0:T(8,128)S(1)} %get-tuple-element.60), channel_id=1, source_target_pairs={{8,16},{16,8},{24,32},{32,24},{40,48},{48,40},{9,17},{17,9},{25,33... | collective-permute-start | bytes 786440 | tf_op jit(solution)/shard_map/ppermute | solution.py:416
  96.1 2.2 %collective-permute-start.24 = (f32[8,32,128]{2,1,0:T(8,128)S(1)}, f32[8,32,128]{2,1,0:T(8,128)S(1)}, u32[]{:S(2)}, u32[]{:S(2)}) collective-permute-start(f32[8,32,128]{2,1,0:T(8,128)S(1)} %get-tuple-element.61), channel_id=1, source_target_pairs={{0,1},{1,0},{2,3},{3,2},{4,5},{5,4},{6,7},{7,6},{8,9},{9,8},{10,11... | collective-permute-start | bytes 393224 | tf_op jit(solution)/shard_map/ppermute | solution.py:416
  98.3 3.6 %collective-permute-start.25 = (f32[8,32,128]{2,1,0:T(8,128)S(1)}, f32[8,32,128]{2,1,0:T(8,128)S(1)}, u32[]{:S(2)}, u32[]{:S(2)}) collective-permute-start(f32[8,32,128]{2,1,0:T(8,128)S(1)} %get-tuple-element.62), channel_id=1, source_target_pairs={{1,2},{2,1},{3,4},{4,3},{5,6},{6,5},{9,10},{10,9},{11,12},{12,11},... | collective-permute-start | bytes 393224 | tf_op jit(solution)/shard_map/ppermute | solution.py:416
  101.9 0.7 collective-permute-done.24.lev_e
  102.6 0.6 collective-permute-start.31
  103.2 6.5 %collective-permute-done.25.lev_o = f32[8,32,128]{2,1,0:T(8,128)S(1)} collective-permute-done((f32[8,32,128]{2,1,0:T(8,128)S(1)}, f32[8,32,128]{2,1,0:T(8,128)S(1)}, u32[]{:S(2)}, u32[]{:S(2)}) %collective-permute-start.25) | collective-permute-done | bytes 131104 | tf_op jit(solution)/shard_map/ppermute | solution.py:416
  109.7 0.3 shard_map.61.after.npa
  110.0 4.3 %shard_map.62 = (f32[8,32,64,128]{3,2,1,0:T(8,128)}, f32[8,32,64,128]{3,2,1,0:T(8,128)S(1)}, f32[8,32,64,128]{3,2,1,0:T(8,128)S(1)}, f32[7,64,128]{2,1,0:T(8,128)S(1)}) custom-call(f32[8,32,64,128]{3,2,1,0:T(8,128)S(1)} %shard_map.59.rest_0_.u, f32[16,64,128]{2,1,0:T(8,128)S(1)} %shard_map.58.after.rest_1_.pa, ...), custom_call_target="tpu_custom_call", output_to_operand_aliasing={{1}: (7, {}), {2}: (8, {})} | custom-call | flops 20000000 | tf_op jit(solution)/shard_map/pallas_call | solution.py:486
  114.3 0.1 collective-permute-start.27
  114.4 1.5 %collective-permute-done.27.other = f32[7,64,128]{2,1,0:T(8,128)S(1)} collective-permute-done((f32[7,64,128]{2,1,0:T(8,128)S(1)}, f32[7,64,128]{2,1,0:T(8,128)S(1)}, u32[]{:S(2)}, u32[]{:S(2)}) %collective-permute-start.27) | collective-permute-done | bytes 229408 | tf_op jit(solution)/shard_map/ppermute | solution.py:432
  116.0 6.7 %collective-permute-done.28.refs_0_ = f32[7,32,128]{2,1,0:T(8,128)S(1)} collective-permute-done((f32[7,32,128]{2,1,0:T(8,128)S(1)}, f32[7,32,128]{2,1,0:T(8,128)S(1)}, u32[]{:S(2)}, u32[]{:S(2)}) %collective-permute-start.28) | collective-permute-done | bytes 114720 | tf_op jit(solution)/shard_map/ppermute | solution.py:432
  122.7 1.3 collective-permute-start.29
  124.0 5.4 %collective-permute-done.29.refs_1_ = f32[7,32,128]{2,1,0:T(8,128)S(1)} collective-permute-done((f32[7,32,128]{2,1,0:T(8,128)S(1)}, f32[7,32,128]{2,1,0:T(8,128)S(1)}, u32[]{:S(2)}, u32[]{:S(2)}) %collective-permute-start.29) | collective-permute-done | bytes 114720 | tf_op jit(solution)/shard_map/ppermute | solution.py:432
  129.5 0.4 shard_map.65
  129.9 0.6 collective-permute-start.32
  130.4 0.9 collective-permute-done.32.rest_0_
  131.3 0.3 collective-permute-start.33
  131.6 5.1 %collective-permute-done.33.rest_1_ = f32[64,128]{1,0:T(8,128)S(1)} collective-permute-done((f32[64,128]{1,0:T(8,128)S(1)}, f32[64,128]{1,0:T(8,128)S(1)}, u32[]{:S(2)}, u32[]{:S(2)}) %collective-permute-start.33) | collective-permute-done | bytes 32800 | tf_op jit(solution)/shard_map/ppermute | solution.py:432
  136.7 1.3 collective-permute-start.34
  138.0 1.3 shard_map.66.rest_3_
  139.3 2.0 %shard_map.67.rest_4_ = f32[8,32,64,128]{3,2,1,0:T(8,128)} custom-call(f32[8,32,64,128]{3,2,1,0:T(8,128)S(1)} %get-tuple-element.63.sums, f32[7,64,128]{2,1,0:T(8,128)S(1)} %collective-permute-done.27.other, f32[7,32,128]{2,1,0:T(8,128)S(1)} %shard_map.64.before, f32[64,128]{1,0:T(8,128)S(1)} %get-tuple-element.67.after), custom_call_target="tpu_custom_call" | custom-call | flops 1000000 | tf_op jit(solution)/shard_map/pallas_call | solution.py:525
  141.3 1.2 collective-permute-done.34.rest_2_
  142.5 2.6 %shard_map.68 = (f32[8,32,64,128]{3,2,1,0:T(8,128)}, f32[8,32,64,128]{3,2,1,0:T(8,128)}) custom-call(f32[8,32,64,128]{3,2,1,0:T(8,128)S(1)} %get-tuple-element.63.sums, f32[7,64,128]{2,1,0:T(8,128)S(1)} %collective-permute-done.27.other, f32[7,32,128]{2,1,0:T(8,128)S(1)} %collective-permute-done.30.before, ...), custom_call_target="tpu_custom_call", output_to_operand_aliasing={{0}: (9, {}), {1}: (10, {})} | custom-call | flops 1000000 | tf_op jit(solution)/shard_map/pallas_call | solution.py:535
  (30 shorter events, 0.4 us)
Async XLA Ops:
  1.7 21.0 %collective-permute-start.6 = (f32[16,64,128]{2,1,0:T(8,128)S(1)}, f32[16,64,128]{2,1,0:T(8,128)S(1)}, u32[]{:S(2)}, u32[]{:S(2)}) collective-permute-start(f32[16,64,128]{2,1,0:T(8,128)S(1)} %shard_map.51.pa), channel_id=1, source_target_pairs={{0,64},{64,0},{1,65},{65,1},{2,66},{66,2},{3,67},{67,3},{4,68},{68... | collective-permute-start | bytes 1572872 | tf_op jit(solution)/shard_map/ppermute | solution.py:439
  6.8 10.0 %collective-permute-start.2 = (f32[8,64,128]{2,1,0:T(8,128)S(1)}, f32[8,64,128]{2,1,0:T(8,128)S(1)}, u32[]{:S(2)}, u32[]{:S(2)}) collective-permute-start(f32[8,64,128]{2,1,0:T(8,128)S(1)} %get-tuple-element.40), channel_id=1, source_target_pairs={{24,56},{32,0},{25,57},{33,1},{26,58},{34,2},{27,59},{35,3},{28,60... | collective-permute-start | bytes 786440 | tf_op jit(solution)/shard_map/ppermute | solution.py:421
  9.1 28.9 %collective-permute-start.7 = (f32[16,64,128]{2,1,0:T(8,128)S(1)}, f32[16,64,128]{2,1,0:T(8,128)S(1)}, u32[]{:S(2)}, u32[]{:S(2)}) collective-permute-start(f32[16,64,128]{2,1,0:T(8,128)S(1)} %get-tuple-element.38.pb), channel_id=1, source_target_pairs={{0,64},{64,0},{1,65},{65,1},{2,66},{66,2},{3,67},{67,3},{4,68},{68... | collective-permute-start | bytes 1572872 | tf_op jit(solution)/shard_map/ppermute | solution.py:449
  10.7 5.4 %collective-permute-start.4 = (f32[8,32,128]{2,1,0:T(8,128)S(1)}, f32[8,32,128]{2,1,0:T(8,128)S(1)}, u32[]{:S(2)}, u32[]{:S(2)}) collective-permute-start(f32[8,32,128]{2,1,0:T(8,128)S(1)} %get-tuple-element.41), channel_id=1, source_target_pairs={{0,1},{1,0},{2,3},{3,2},{4,5},{5,4},{6,7},{7,6},{8,9},{9,8},{10,11... | collective-permute-start | bytes 393224 | tf_op jit(solution)/shard_map/ppermute | solution.py:416
  12.2 10.5 %collective-permute-start.5 = (f32[8,32,128]{2,1,0:T(8,128)S(1)}, f32[8,32,128]{2,1,0:T(8,128)S(1)}, u32[]{:S(2)}, u32[]{:S(2)}) collective-permute-start(f32[8,32,128]{2,1,0:T(8,128)S(1)} %get-tuple-element.42), channel_id=1, source_target_pairs={{1,2},{2,1},{3,4},{4,3},{5,6},{6,5},{9,10},{10,9},{11,12},{12,11},... | collective-permute-start | bytes 393224 | tf_op jit(solution)/shard_map/ppermute | solution.py:416
  16.0 7.6 %collective-permute-start.1 = (f32[8,64,128]{2,1,0:T(8,128)S(1)}, f32[8,64,128]{2,1,0:T(8,128)S(1)}, u32[]{:S(2)}, u32[]{:S(2)}) collective-permute-start(f32[8,64,128]{2,1,0:T(8,128)S(1)} %get-tuple-element.40), channel_id=1, source_target_pairs={{8,16},{16,8},{40,48},{48,40},{9,17},{17,9},{41,49},{49,41},{10,18... | collective-permute-start | bytes 786440 | tf_op jit(solution)/shard_map/ppermute | solution.py:422
  16.7 15.4 %collective-permute-start.3 = (f32[8,64,128]{2,1,0:T(8,128)S(1)}, f32[8,64,128]{2,1,0:T(8,128)S(1)}, u32[]{:S(2)}, u32[]{:S(2)}) collective-permute-start(f32[8,64,128]{2,1,0:T(8,128)S(1)} %collective-permute-done.2), channel_id=1, source_target_pairs={{56,32},{0,24},{57,33},{1,25},{58,34},{2,26},{59,35},{3,27},{60,36... | collective-permute-start | bytes 786440 | tf_op jit(solution)/shard_map/ppermute | solution.py:423
  22.7 9.4 %collective-permute-start = (f32[8,64,128]{2,1,0:T(8,128)S(1)}, f32[8,64,128]{2,1,0:T(8,128)S(1)}, u32[]{:S(2)}, u32[]{:S(2)}) collective-permute-start(f32[8,64,128]{2,1,0:T(8,128)S(1)} %get-tuple-element.39), channel_id=1, source_target_pairs={{0,8},{8,0},{16,24},{24,16},{32,40},{40,32},{48,56},{56,48},{1,9},... | collective-permute-start | bytes 786440 | tf_op jit(solution)/shard_map/ppermute | solution.py:422
  23.0 30.4 %collective-permute-start.12 = (f32[16,64,128]{2,1,0:T(8,128)S(1)}, f32[16,64,128]{2,1,0:T(8,128)S(1)}, u32[]{:S(2)}, u32[]{:S(2)}) collective-permute-start(f32[16,64,128]{2,1,0:T(8,128)S(1)} %shard_map.52.after.rest_1_.pa), channel_id=1, source_target_pairs={{0,64},{64,0},{1,65},{65,1},{2,66},{66,2},{3,67},{67,3},{4,68},{68... | collective-permute-start | bytes 1572872 | tf_op jit(solution)/shard_map/ppermute | solution.py:463
  38.6 25.6 %collective-permute-start.13 = (f32[16,64,128]{2,1,0:T(8,128)S(1)}, f32[16,64,128]{2,1,0:T(8,128)S(1)}, u32[]{:S(2)}, u32[]{:S(2)}) collective-permute-start(f32[16,64,128]{2,1,0:T(8,128)S(1)} %get-tuple-element.46.pb), channel_id=1, source_target_pairs={{0,64},{64,0},{1,65},{65,1},{2,66},{66,2},{3,67},{67,3},{4,68},{68... | collective-permute-start | bytes 1572872 | tf_op jit(solution)/shard_map/ppermute | solution.py:481
  40.5 7.0 %collective-permute-start.10 = (f32[8,32,128]{2,1,0:T(8,128)S(1)}, f32[8,32,128]{2,1,0:T(8,128)S(1)}, u32[]{:S(2)}, u32[]{:S(2)}) collective-permute-start(f32[8,32,128]{2,1,0:T(8,128)S(1)} %get-tuple-element.49), channel_id=1, source_target_pairs={{0,1},{1,0},{2,3},{3,2},{4,5},{5,4},{6,7},{7,6},{8,9},{9,8},{10,11... | collective-permute-start | bytes 393224 | tf_op jit(solution)/shard_map/ppermute | solution.py:416
  42.1 11.3 %collective-permute-start.11 = (f32[8,32,128]{2,1,0:T(8,128)S(1)}, f32[8,32,128]{2,1,0:T(8,128)S(1)}, u32[]{:S(2)}, u32[]{:S(2)}) collective-permute-start(f32[8,32,128]{2,1,0:T(8,128)S(1)} %get-tuple-element.50), channel_id=1, source_target_pairs={{1,2},{2,1},{3,4},{4,3},{5,6},{6,5},{9,10},{10,9},{11,12},{12,11},... | collective-permute-start | bytes 393224 | tf_op jit(solution)/shard_map/ppermute | solution.py:416
  46.1 7.7 %collective-permute-start.8 = (f32[8,64,128]{2,1,0:T(8,128)S(1)}, f32[8,64,128]{2,1,0:T(8,128)S(1)}, u32[]{:S(2)}, u32[]{:S(2)}) collective-permute-start(f32[8,64,128]{2,1,0:T(8,128)S(1)} %get-tuple-element.47), channel_id=1, source_target_pairs={{0,8},{8,0},{16,24},{24,16},{32,40},{40,32},{48,56},{56,48},{1,9},... | collective-permute-start | bytes 786440 | tf_op jit(solution)/shard_map/ppermute | solution.py:416
  47.5 12.9 %collective-permute-start.9 = (f32[8,64,128]{2,1,0:T(8,128)S(1)}, f32[8,64,128]{2,1,0:T(8,128)S(1)}, u32[]{:S(2)}, u32[]{:S(2)}) collective-permute-start(f32[8,64,128]{2,1,0:T(8,128)S(1)} %get-tuple-element.48), channel_id=1, source_target_pairs={{8,16},{16,8},{24,32},{32,24},{40,48},{48,40},{9,17},{17,9},{25,33... | collective-permute-start | bytes 786440 | tf_op jit(solution)/shard_map/ppermute | solution.py:416
  53.6 27.4 %collective-permute-start.20 = (f32[16,64,128]{2,1,0:T(8,128)S(1)}, f32[16,64,128]{2,1,0:T(8,128)S(1)}, u32[]{:S(2)}, u32[]{:S(2)}) collective-permute-start(f32[16,64,128]{2,1,0:T(8,128)S(1)} %shard_map.55.after.rest_1_.pa), channel_id=1, source_target_pairs={{0,64},{64,0},{1,65},{65,1},{2,66},{66,2},{3,67},{67,3},{4,68},{68... | collective-permute-start | bytes 1572872 | tf_op jit(solution)/shard_map/ppermute | solution.py:463
  64.8 9.4 %collective-permute-start.16 = (f32[8,64,128]{2,1,0:T(8,128)S(1)}, f32[8,64,128]{2,1,0:T(8,128)S(1)}, u32[]{:S(2)}, u32[]{:S(2)}) collective-permute-start(f32[8,64,128]{2,1,0:T(8,128)S(1)} %get-tuple-element.55), channel_id=1, source_target_pairs={{24,56},{32,0},{25,57},{33,1},{26,58},{34,2},{27,59},{35,3},{28,60... | collective-permute-start | bytes 786440 | tf_op jit(solution)/shard_map/ppermute | solution.py:421
  66.1 24.1 %collective-permute-start.21 = (f32[16,64,128]{2,1,0:T(8,128)S(1)}, f32[16,64,128]{2,1,0:T(8,128)S(1)}, u32[]{:S(2)}, u32[]{:S(2)}) collective-permute-start(f32[16,64,128]{2,1,0:T(8,128)S(1)} %get-tuple-element.53.pb), channel_id=1, source_target_pairs={{0,64},{64,0},{1,65},{65,1},{2,66},{66,2},{3,67},{67,3},{4,68},{68... | collective-permute-start | bytes 1572872 | tf_op jit(solution)/shard_map/ppermute | solution.py:481
  67.6 5.9 %collective-permute-start.18 = (f32[8,32,128]{2,1,0:T(8,128)S(1)}, f32[8,32,128]{2,1,0:T(8,128)S(1)}, u32[]{:S(2)}, u32[]{:S(2)}) collective-permute-start(f32[8,32,128]{2,1,0:T(8,128)S(1)} %get-tuple-element.56), channel_id=1, source_target_pairs={{0,1},{1,0},{2,3},{3,2},{4,5},{5,4},{6,7},{7,6},{8,9},{9,8},{10,11... | collective-permute-start | bytes 393224 | tf_op jit(solution)/shard_map/ppermute | solution.py:416
  69.2 11.7 %collective-permute-start.19 = (f32[8,32,128]{2,1,0:T(8,128)S(1)}, f32[8,32,128]{2,1,0:T(8,128)S(1)}, u32[]{:S(2)}, u32[]{:S(2)}) collective-permute-start(f32[8,32,128]{2,1,0:T(8,128)S(1)} %get-tuple-element.57), channel_id=1, source_target_pairs={{1,2},{2,1},{3,4},{4,3},{5,6},{6,5},{9,10},{10,9},{11,12},{12,11},... | collective-permute-start | bytes 393224 | tf_op jit(solution)/shard_map/ppermute | solution.py:416
  73.5 8.0 %collective-permute-start.15 = (f32[8,64,128]{2,1,0:T(8,128)S(1)}, f32[8,64,128]{2,1,0:T(8,128)S(1)}, u32[]{:S(2)}, u32[]{:S(2)}) collective-permute-start(f32[8,64,128]{2,1,0:T(8,128)S(1)} %get-tuple-element.55), channel_id=1, source_target_pairs={{8,16},{16,8},{40,48},{48,40},{9,17},{17,9},{41,49},{49,41},{10,18... | collective-permute-start | bytes 786440 | tf_op jit(solution)/shard_map/ppermute | solution.py:422
  74.2 12.0 %collective-permute-start.17 = (f32[8,64,128]{2,1,0:T(8,128)S(1)}, f32[8,64,128]{2,1,0:T(8,128)S(1)}, u32[]{:S(2)}, u32[]{:S(2)}) collective-permute-start(f32[8,64,128]{2,1,0:T(8,128)S(1)} %collective-permute-done.16), channel_id=1, source_target_pairs={{56,32},{0,24},{57,33},{1,25},{58,34},{2,26},{59,35},{3,27},{60,36... | collective-permute-start | bytes 786440 | tf_op jit(solution)/shard_map/ppermute | solution.py:423
  80.9 5.4 %collective-permute-start.14 = (f32[8,64,128]{2,1,0:T(8,128)S(1)}, f32[8,64,128]{2,1,0:T(8,128)S(1)}, u32[]{:S(2)}, u32[]{:S(2)}) collective-permute-start(f32[8,64,128]{2,1,0:T(8,128)S(1)} %get-tuple-element.54), channel_id=1, source_target_pairs={{0,8},{8,0},{16,24},{24,16},{32,40},{40,32},{48,56},{56,48},{1,9},... | collective-permute-start | bytes 786440 | tf_op jit(solution)/shard_map/ppermute | solution.py:422
  81.3 28.4 %collective-permute-start.26 = (f32[16,64,128]{2,1,0:T(8,128)S(1)}, f32[16,64,128]{2,1,0:T(8,128)S(1)}, u32[]{:S(2)}, u32[]{:S(2)}) collective-permute-start(f32[16,64,128]{2,1,0:T(8,128)S(1)} %shard_map.58.after.rest_1_.pa), channel_id=1, source_target_pairs={{0,64},{64,0},{1,65},{65,1},{2,66},{66,2},{3,67},{67,3},{4,68},{68... | collective-permute-start | bytes 1572872 | tf_op jit(solution)/shard_map/ppermute | solution.py:463
  90.7 19.3 %collective-permute-start.22 = (f32[8,64,128]{2,1,0:T(8,128)S(1)}, f32[8,64,128]{2,1,0:T(8,128)S(1)}, u32[]{:S(2)}, u32[]{:S(2)}) collective-permute-start(f32[8,64,128]{2,1,0:T(8,128)S(1)} %get-tuple-element.59), channel_id=1, source_target_pairs={{0,8},{8,0},{16,24},{24,16},{32,40},{40,32},{48,56},{56,48},{1,9},... | collective-permute-start | bytes 786440 | tf_op jit(solution)/shard_map/ppermute | solution.py:416
  91.4 18.6 %collective-permute-start.23 = (f32[8,64,128]{2,1,0:T(8,128)S(1)}, f32[8,64,128]{2,1,0:T(8,128)S(1)}, u32[]{:S(2)}, u32[]{:S(2)}) collective-permute-start(f32[8,64,128]{2,1,0:T(8,128)S(1)} %get-tuple-element.60), channel_id=1, source_target_pairs={{8,16},{16,8},{24,32},{32,24},{40,48},{48,40},{9,17},{17,9},{25,33... | collective-permute-start | bytes 786440 | tf_op jit(solution)/shard_map/ppermute | solution.py:416
  96.1 6.5 %collective-permute-start.24 = (f32[8,32,128]{2,1,0:T(8,128)S(1)}, f32[8,32,128]{2,1,0:T(8,128)S(1)}, u32[]{:S(2)}, u32[]{:S(2)}) collective-permute-start(f32[8,32,128]{2,1,0:T(8,128)S(1)} %get-tuple-element.61), channel_id=1, source_target_pairs={{0,1},{1,0},{2,3},{3,2},{4,5},{5,4},{6,7},{7,6},{8,9},{9,8},{10,11... | collective-permute-start | bytes 393224 | tf_op jit(solution)/shard_map/ppermute | solution.py:416
  98.3 11.4 %collective-permute-start.25 = (f32[8,32,128]{2,1,0:T(8,128)S(1)}, f32[8,32,128]{2,1,0:T(8,128)S(1)}, u32[]{:S(2)}, u32[]{:S(2)}) collective-permute-start(f32[8,32,128]{2,1,0:T(8,128)S(1)} %get-tuple-element.62), channel_id=1, source_target_pairs={{1,2},{2,1},{3,4},{4,3},{5,6},{6,5},{9,10},{10,9},{11,12},{12,11},... | collective-permute-start | bytes 393224 | tf_op jit(solution)/shard_map/ppermute | solution.py:416
  102.6 26.9 %collective-permute-start.31 = (f32[16,64,128]{2,1,0:T(8,128)S(1)}, f32[16,64,128]{2,1,0:T(8,128)S(1)}, u32[]{:S(2)}, u32[]{:S(2)}) collective-permute-start(f32[16,64,128]{2,1,0:T(8,128)S(1)} %get-tuple-element.58.pb), channel_id=1, source_target_pairs={{0,64},{64,0},{1,65},{65,1},{2,66},{66,2},{3,67},{67,3},{4,68},{68... | collective-permute-start | bytes 1572872 | tf_op jit(solution)/shard_map/ppermute | solution.py:481
  114.3 1.6 %collective-permute-start.27 = (f32[7,64,128]{2,1,0:T(8,128)S(1)}, f32[7,64,128]{2,1,0:T(8,128)S(1)}, u32[]{:S(2)}, u32[]{:S(2)}) collective-permute-start(f32[7,64,128]{2,1,0:T(8,128)S(1)} %get-tuple-element.64.total), channel_id=1, source_target_pairs={{0,8},{8,0},{16,24},{24,16},{32,40},{40,32},{48,56},{56,48},{1,9},... | collective-permute-start | bytes 688136 | tf_op jit(solution)/shard_map/ppermute | solution.py:432
  115.9 6.8 %collective-permute-start.28 = (f32[7,32,128]{2,1,0:T(8,128)S(1)}, f32[7,32,128]{2,1,0:T(8,128)S(1)}, u32[]{:S(2)}, u32[]{:S(2)}) collective-permute-start(f32[7,32,128]{2,1,0:T(8,128)S(1)} %shard_map.63), channel_id=1, source_target_pairs={{0,16},{8,24},{16,0},{24,8},{32,48},{40,56},{48,32},{56,40},{1,17}... | collective-permute-start | bytes 344072 | tf_op jit(solution)/shard_map/ppermute | solution.py:432
  122.7 6.7 %collective-permute-start.29 = (f32[7,32,128]{2,1,0:T(8,128)S(1)}, f32[7,32,128]{2,1,0:T(8,128)S(1)}, u32[]{:S(2)}, u32[]{:S(2)}) collective-permute-start(f32[7,32,128]{2,1,0:T(8,128)S(1)} %add.17), channel_id=1, source_target_pairs={{0,32},{8,40},{16,48},{24,56},{1,33},{9,41},{17,49},{25,57},{2,34}... | collective-permute-start | bytes 344072 | tf_op jit(solution)/shard_map/ppermute | solution.py:432
  129.4 13.1 %collective-permute-start.30 = (f32[7,32,128]{2,1,0:T(8,128)S(1)}, f32[7,32,128]{2,1,0:T(8,128)S(1)}, u32[]{:S(2)}, u32[]{:S(2)}) collective-permute-start(f32[7,32,128]{2,1,0:T(8,128)S(1)} %shard_map.64.before), channel_id=1, source_target_pairs={{0,8},{8,0},{16,24},{24,16},{32,40},{40,32},{48,56},{56,48},{1,9},... | collective-permute-start | bytes 344072 | tf_op jit(solution)/shard_map/ppermute | solution.py:513
  129.9 1.4 collective-permute-start.32
  131.3 5.4 %collective-permute-start.33 = (f32[64,128]{1,0:T(8,128)S(1)}, f32[64,128]{1,0:T(8,128)S(1)}, u32[]{:S(2)}, u32[]{:S(2)}) collective-permute-start(f32[64,128]{1,0:T(8,128)S(1)} %add.18), channel_id=1, source_target_pairs={{0,16},{8,24},{16,0},{24,8},{32,48},{40,56},{48,32},{56,40},{1,17}... | collective-permute-start | bytes 98312 | tf_op jit(solution)/shard_map/ppermute | solution.py:432
  136.7 5.8 %collective-permute-start.34 = (f32[64,128]{1,0:T(8,128)S(1)}, f32[64,128]{1,0:T(8,128)S(1)}, u32[]{:S(2)}, u32[]{:S(2)}) collective-permute-start(f32[64,128]{1,0:T(8,128)S(1)} %add.19), channel_id=1, source_target_pairs={{0,32},{8,40},{16,48},{24,56},{1,33},{9,41},{17,49},{25,57},{2,34}... | collective-permute-start | bytes 98312 | tf_op jit(solution)/shard_map/ppermute | solution.py:432

commit v12 on v11

--- a/solution.py
+++ b/solution.py
@@ -274,14 +274,20 @@
         copy_out(plane_at(depth, nj), depth).wait()
 
 
-def late_kernel(f, end_in, end, sem):
+def late_kernel(f, npa, npb, end_in, end, sem):
     del end_in
-    nj = f.shape[0]
-    copies = []
-    for p in range(LATE):
-        j = plane_at(nj - LATE + p, nj)
-        copies.append(pltpu.make_async_copy(f.at[j], end.at[j], sem.at[p]))
-        copies[-1].start()
+    nj, ni = f.shape[:2]
+    q = ni // 4
+    pj = plane_at(0, nj)
+    pairs = [(f.at[j], end.at[j]) for j in (plane_at(nj - LATE + p, nj) for p in range(LATE))]
+    pairs += [
+        (npb.at[pl.ds(0, q)], end.at[pj, pl.ds(0, q)]),
+        (npa, end.at[pj, pl.ds(q, 2 * q)]),
+        (npb.at[pl.ds(q, q)], end.at[pj, pl.ds(3 * q, q)]),
+    ]
+    copies = [pltpu.make_async_copy(source, target, sem.at[p]) for p, (source, target) in enumerate(pairs)]
+    for copy in copies:
+        copy.start()
     for copy in copies:
         copy.wait()
 
@@ -362,26 +368,18 @@
         copy.wait()
 
 
-def last_totals_kernel(scale, sums, other, before, npa, npb, edge_sums, *rest):
-    *others, _, _, end, out, stage, edge_stage, sem, edge_sem = rest
+def last_totals_kernel(scale, sums, other, before, edge_sums, *rest):
+    *others, _, out, stage, edge_stage, sem, edge_sem = rest
     nj, ni = sums.shape[:2]
-    q = ni // 4
     pj = plane_at(0, nj)
-    copies = [
-        pltpu.make_async_copy(npb.at[pl.ds(0, q)], end.at[pj, pl.ds(0, q)], edge_sem.at[0]),
-        pltpu.make_async_copy(npa, end.at[pj, pl.ds(q, 2 * q)], edge_sem.at[1]),
-        pltpu.make_async_copy(npb.at[pl.ds(q, q)], end.at[pj, pl.ds(3 * q, q)], edge_sem.at[2]),
-        pltpu.make_async_copy(edge_stage, out.at[pj], edge_sem.at[3]),
-    ]
-    for copy in copies[:3]:
-        copy.start()
-    copies += half_totals(scale, jnp.logical_not(odd("lon")), sums, other, before, out, stage, sem)
 
     def put(i, value):
         edge_stage[i] = value
 
     total_rows(scale, ni, lambda i: edge_sums[i], earlier([other[...] for other in others]), put)
-    copies[3].start()
+    copies = [pltpu.make_async_copy(edge_stage, out.at[pj], edge_sem)]
+    copies[0].start()
+    copies += half_totals(scale, jnp.logical_not(odd("lon")), sums, other, before, out, stage, sem)
     for copy in copies:
         copy.wait()
 
@@ -493,15 +491,6 @@
         flops=2 * 10**7,
     )(u, pa, pb, *lon, *lev, in_vmem(d), in_vmem(f), n_pa)
     other = partner(0, total)
-    end = call(
-        late_kernel,
-        H(nj, ni, nk, nm),
-        HBM,
-        (VMEM, HBM),
-        scratch=(pltpu.SemaphoreType.DMA((LATE,)),),
-        aliases={1: 0},
-        flops=10**5,
-    )(in_vmem(values), in_hbm(end))
     half_total = call(half_kernel, V(nj - 1, nk // 2, nm), VMEM, (VMEM,) * 2, flops=10**5)(
         in_vmem(total), in_vmem(other)
     )
@@ -521,6 +510,16 @@
         others.append(partner(bit, edge_total))
         edge_total = edge_total + others[-1]
     others = tuple(map(in_vmem, others))
+    n_pb = in_vmem(n_pb)
+    end = call(
+        late_kernel,
+        H(nj, ni, nk, nm),
+        HBM,
+        (VMEM,) * 3 + (HBM,),
+        scratch=(pltpu.SemaphoreType.DMA((LATE + 3,)),),
+        aliases={3: 0},
+        flops=10**5,
+    )(in_vmem(values), n_pa, n_pb, in_hbm(end))
     sums, other = in_vmem(sums), in_vmem(other)
     out = call(
         functools.partial(totals_kernel, scale),
@@ -531,22 +530,22 @@
         scratch=(V(nj - 1, ni, nk // 2, nm), pltpu.SemaphoreType.DMA((nj - 1,))),
         flops=10**6,
     )(sums, other, in_vmem(mine), edge_total_1)
-    n = 6 + bits
-    end, out = call(
+    n = 4 + bits
+    out = call(
         functools.partial(last_totals_kernel, scale),
-        (H(nj, ni, nk, nm),) * 2,
-        (HBM, HBM),
-        (VMEM,) * n + (HBM, HBM),
+        H(nj, ni, nk, nm),
+        HBM,
+        (VMEM,) * n + (HBM,),
         scratch=(
             V(nj - 1, ni, nk // 2, nm),
             V(ni, nk, nm),
             pltpu.SemaphoreType.DMA((nj - 1,)),
-            pltpu.SemaphoreType.DMA((4,)),
+            pltpu.SemaphoreType.DMA,
         ),
         limit=6,
-        aliases={n: 0, n + 1: 1},
+        aliases={n: 0},
         flops=10**6,
-    )(sums, other, in_vmem(back), n_pa, in_vmem(n_pb), in_vmem(edge_sums), *others, in_hbm(end), in_hbm(out))
+    )(sums, other, in_vmem(back), in_vmem(edge_sums), *others, in_hbm(out))
     return out, end
 
 

time: 147 us -> 147 us (level)
  no operation moved by 1% of the time
where the time goes in v12:
time: 147 us; the launch traced here: 145 us
  waiting for transfers between devices  61.9 us (42%)
  starting transfers between devices  49.3 us (34%)
  Pallas kernels  32.6 us (22%)
    ppermute x12, starting transfers between devices, exchange(): return (lax.ppermute(e, axis, swaps(0)), lax.ppermute(o, axis, swaps(1)))  30.8 us
    ppermute x12, waiting for transfers between devices, exchange(): return (lax.ppermute(e, axis, swaps(0)), lax.ppermute(o, axis, swaps(1)))  28.4 us
    ppermute x6, waiting for transfers between devices, partner(): return lax.ppermute(total, 'lon', pairs)  20.3 us
    ppermute x2, waiting for transfers between devices, lon_exchange(): return (e, o + lax.ppermute(relayed, 'lon', [(7, 4), (0, 3)]))  13.2 us
    pallas_call x2, Pallas kernels, per_device(): call(bulk_kernel, V(nj, ni, nk, nm), VMEM, (VMEM,) * 9 + (ANY,), flops=2...  7.75 us
    pallas_call x1, Pallas kernels, per_device(): call(first_bulk_kernel, (V(nj, ni, nk, nm),) * 3, (VMEM,) * 3, (VMEM,) *...  5.88 us
    pallas_call x1, Pallas kernels, per_device(): call(load_kernel, (V(nj, ni, nk, nm), V(half, nk, nm), V(ni, nk, nm), V(n...  4.43 us
    pallas_call x1, Pallas kernels, per_device(): call(last_bulk_kernel, (H(nj, ni, nk, nm), V(nj, ni, nk, nm), V(nj, ni, n...  4.28 us
  transfers between devices with their start and end apart: 35, of which 15 were waited for; matrix products, arithmetic and copies ran while one was open for 0% of the time, Pallas kernels for 20%

profile of v12, /device:TPU:98, one launch (start us, length us, event | category | flops | bytes accessed | tf_op | source)
XLA Modules:
  0.0 145.0 jit_solution(11126707503367194184)
XLA Ops:
  0.6 1.1 shard_map.51.pa
  1.7 0.6 collective-permute-start.6
  2.3 4.4 %shard_map.50 = (f32[8,32,64,128]{3,2,1,0:T(8,128)S(1)}, f32[16,64,128]{2,1,0:T(8,128)S(1)}, f32[32,64,128]{2,1,0:T(8,128)S(1)}, f32[32,64,128]{2,1,0:T(8,128)S(...) custom-call(f32[8,32,64,128]{3,2,1,0:T(8,128)} %u_in.3, ...), custom_call_target="tpu_custom_call" | custom-call | flops 1000000 | tf_op jit(solution)/shard_map/pallas_call | solution.py:438
  6.8 2.3 %collective-permute-start.2 = (f32[8,64,128]{2,1,0:T(8,128)S(1)}, f32[8,64,128]{2,1,0:T(8,128)S(1)}, u32[]{:S(2)}, u32[]{:S(2)}) collective-permute-start(f32[8,64,128]{2,1,0:T(8,128)S(1)} %get-tuple-element.38), channel_id=1, source_target_pairs={{24,56},{32,0},{25,57},{33,1},{26,58},{34,2},{27,59},{35,3},{28,60... | collective-permute-start | bytes 786440 | tf_op jit(solution)/shard_map/ppermute | solution.py:419
  9.1 1.6 %collective-permute-start.7 = (f32[16,64,128]{2,1,0:T(8,128)S(1)}, f32[16,64,128]{2,1,0:T(8,128)S(1)}, u32[]{:S(2)}, u32[]{:S(2)}) collective-permute-start(f32[16,64,128]{2,1,0:T(8,128)S(1)} %get-tuple-element.36.pb), channel_id=1, source_target_pairs={{0,64},{64,0},{1,65},{65,1},{2,66},{66,2},{3,67},{67,3},{4,68},{68... | collective-permute-start | bytes 1572872 | tf_op jit(solution)/shard_map/ppermute | solution.py:447
  10.7 1.6 %collective-permute-start.4 = (f32[8,32,128]{2,1,0:T(8,128)S(1)}, f32[8,32,128]{2,1,0:T(8,128)S(1)}, u32[]{:S(2)}, u32[]{:S(2)}) collective-permute-start(f32[8,32,128]{2,1,0:T(8,128)S(1)} %get-tuple-element.39), channel_id=1, source_target_pairs={{0,1},{1,0},{2,3},{3,2},{4,5},{5,4},{6,7},{7,6},{8,9},{9,8},{10,11... | collective-permute-start | bytes 393224 | tf_op jit(solution)/shard_map/ppermute | solution.py:414
  12.2 3.8 %collective-permute-start.5 = (f32[8,32,128]{2,1,0:T(8,128)S(1)}, f32[8,32,128]{2,1,0:T(8,128)S(1)}, u32[]{:S(2)}, u32[]{:S(2)}) collective-permute-start(f32[8,32,128]{2,1,0:T(8,128)S(1)} %get-tuple-element.40), channel_id=1, source_target_pairs={{1,2},{2,1},{3,4},{4,3},{5,6},{6,5},{9,10},{10,9},{11,12},{12,11},... | collective-permute-start | bytes 393224 | tf_op jit(solution)/shard_map/ppermute | solution.py:414
  16.0 0.7 collective-permute-start.1
  16.7 1.3 collective-permute-start.3
  18.0 4.7 %collective-permute-done.5.lev_o = f32[8,32,128]{2,1,0:T(8,128)S(1)} collective-permute-done((f32[8,32,128]{2,1,0:T(8,128)S(1)}, f32[8,32,128]{2,1,0:T(8,128)S(1)}, u32[]{:S(2)}, u32[]{:S(2)}) %collective-permute-start.5) | collective-permute-done | bytes 131104 | tf_op jit(solution)/shard_map/ppermute | solution.py:414
  22.7 0.3 shard_map.52.after.rest_1_.pa
  23.0 0.6 collective-permute-start.12
  23.6 8.5 %collective-permute-done.3 = f32[8,64,128]{2,1,0:T(8,128)S(1)} collective-permute-done((f32[8,64,128]{2,1,0:T(8,128)S(1)}, f32[8,64,128]{2,1,0:T(8,128)S(1)}, u32[]{:S(2)}, u32[]{:S(2)}) %collective-permute-start.3) | collective-permute-done | bytes 262176 | tf_op jit(solution)/shard_map/ppermute | solution.py:421
  32.1 5.9 %shard_map.53 = (f32[8,32,64,128]{3,2,1,0:T(8,128)S(1)}, f32[8,32,64,128]{3,2,1,0:T(8,128)S(1)}, f32[8,32,64,128]{3,2,1,0:T(8,128)S(1)}) custom-call(f32[8,32,64,128]{3,2,1,0:T(8,128)S(1)} %get-tuple-element.35.u, f32[16,64,128]{2,1,0:T(8,128)S(1)} %shard_map.51.pa, f32[16,64,128]{2,1,0:T(8,128)S(1)} %get-tuple-element.36.pb, ...), custom_call_target="tpu_custom_call" | custom-call | flops 20000000 | tf_op jit(solution)/shard_map/pallas_call | solution.py:463
  38.0 0.6 shard_map.54
  38.6 1.9 %collective-permute-start.13 = (f32[16,64,128]{2,1,0:T(8,128)S(1)}, f32[16,64,128]{2,1,0:T(8,128)S(1)}, u32[]{:S(2)}, u32[]{:S(2)}) collective-permute-start(f32[16,64,128]{2,1,0:T(8,128)S(1)} %get-tuple-element.44.pb), channel_id=1, source_target_pairs={{0,64},{64,0},{1,65},{65,1},{2,66},{66,2},{3,67},{67,3},{4,68},{68... | collective-permute-start | bytes 1572872 | tf_op jit(solution)/shard_map/ppermute | solution.py:479
  40.5 1.6 %collective-permute-start.10 = (f32[8,32,128]{2,1,0:T(8,128)S(1)}, f32[8,32,128]{2,1,0:T(8,128)S(1)}, u32[]{:S(2)}, u32[]{:S(2)}) collective-permute-start(f32[8,32,128]{2,1,0:T(8,128)S(1)} %get-tuple-element.47), channel_id=1, source_target_pairs={{0,1},{1,0},{2,3},{3,2},{4,5},{5,4},{6,7},{7,6},{8,9},{9,8},{10,11... | collective-permute-start | bytes 393224 | tf_op jit(solution)/shard_map/ppermute | solution.py:414
  42.1 4.1 %collective-permute-start.11 = (f32[8,32,128]{2,1,0:T(8,128)S(1)}, f32[8,32,128]{2,1,0:T(8,128)S(1)}, u32[]{:S(2)}, u32[]{:S(2)}) collective-permute-start(f32[8,32,128]{2,1,0:T(8,128)S(1)} %get-tuple-element.48), channel_id=1, source_target_pairs={{1,2},{2,1},{3,4},{4,3},{5,6},{6,5},{9,10},{10,9},{11,12},{12,11},... | collective-permute-start | bytes 393224 | tf_op jit(solution)/shard_map/ppermute | solution.py:414
  46.1 1.3 collective-permute-start.8
  47.5 1.9 %collective-permute-start.9 = (f32[8,64,128]{2,1,0:T(8,128)S(1)}, f32[8,64,128]{2,1,0:T(8,128)S(1)}, u32[]{:S(2)}, u32[]{:S(2)}) collective-permute-start(f32[8,64,128]{2,1,0:T(8,128)S(1)} %get-tuple-element.46), channel_id=1, source_target_pairs={{8,16},{16,8},{24,32},{32,24},{40,48},{48,40},{9,17},{17,9},{25,33... | collective-permute-start | bytes 786440 | tf_op jit(solution)/shard_map/ppermute | solution.py:414
  49.4 4.0 %collective-permute-done.11.lev_o = f32[8,32,128]{2,1,0:T(8,128)S(1)} collective-permute-done((f32[8,32,128]{2,1,0:T(8,128)S(1)}, f32[8,32,128]{2,1,0:T(8,128)S(1)}, u32[]{:S(2)}, u32[]{:S(2)}) %collective-permute-start.11) | collective-permute-done | bytes 131104 | tf_op jit(solution)/shard_map/ppermute | solution.py:414
  53.4 0.3 shard_map.55.after.rest_1_.pa
  53.6 0.2 collective-permute-start.20
  53.8 6.6 %collective-permute-done.9.lon_o = f32[8,64,128]{2,1,0:T(8,128)S(1)} collective-permute-done((f32[8,64,128]{2,1,0:T(8,128)S(1)}, f32[8,64,128]{2,1,0:T(8,128)S(1)}, u32[]{:S(2)}, u32[]{:S(2)}) %collective-permute-start.9) | collective-permute-done | bytes 262176 | tf_op jit(solution)/shard_map/ppermute | solution.py:414
  60.3 3.9 %shard_map.56.rest_0_.u = f32[8,32,64,128]{3,2,1,0:T(8,128)S(1)} custom-call(f32[8,32,64,128]{3,2,1,0:T(8,128)S(1)} %get-tuple-element.43.rest_0_.u, f32[16,64,128]{2,1,0:T(8,128)S(1)} %shard_map.52.after.rest_1_.pa, f32[16,64,128]{2,1,0:T(8,128)S(1)} %get-tuple-element.44.pb, f32[8,64,128]{2,1,0:T(8,128)S(1)} %collective-permute-done.8.lon_e, ...), custom_call_target="tpu_custom_call" | custom-call | flops 20000000 | tf_op jit(solution)/shard_map/pallas_call | solution.py:472
  64.2 0.6 shard_map.57
  64.8 1.3 collective-permute-start.16
  66.1 1.5 %collective-permute-start.21 = (f32[16,64,128]{2,1,0:T(8,128)S(1)}, f32[16,64,128]{2,1,0:T(8,128)S(1)}, u32[]{:S(2)}, u32[]{:S(2)}) collective-permute-start(f32[16,64,128]{2,1,0:T(8,128)S(1)} %get-tuple-element.51.pb), channel_id=1, source_target_pairs={{0,64},{64,0},{1,65},{65,1},{2,66},{66,2},{3,67},{67,3},{4,68},{68... | collective-permute-start | bytes 1572872 | tf_op jit(solution)/shard_map/ppermute | solution.py:479
  67.6 1.6 %collective-permute-start.18 = (f32[8,32,128]{2,1,0:T(8,128)S(1)}, f32[8,32,128]{2,1,0:T(8,128)S(1)}, u32[]{:S(2)}, u32[]{:S(2)}) collective-permute-start(f32[8,32,128]{2,1,0:T(8,128)S(1)} %get-tuple-element.54), channel_id=1, source_target_pairs={{0,1},{1,0},{2,3},{3,2},{4,5},{5,4},{6,7},{7,6},{8,9},{9,8},{10,11... | collective-permute-start | bytes 393224 | tf_op jit(solution)/shard_map/ppermute | solution.py:414
  69.2 3.8 %collective-permute-start.19 = (f32[8,32,128]{2,1,0:T(8,128)S(1)}, f32[8,32,128]{2,1,0:T(8,128)S(1)}, u32[]{:S(2)}, u32[]{:S(2)}) collective-permute-start(f32[8,32,128]{2,1,0:T(8,128)S(1)} %get-tuple-element.55), channel_id=1, source_target_pairs={{1,2},{2,1},{3,4},{4,3},{5,6},{6,5},{9,10},{10,9},{11,12},{12,11},... | collective-permute-start | bytes 393224 | tf_op jit(solution)/shard_map/ppermute | solution.py:414
  73.0 0.6 collective-permute-done.18.lev_e
  73.5 0.7 collective-permute-start.15
  74.2 1.3 collective-permute-start.17
  75.5 5.4 %collective-permute-done.19.lev_o = f32[8,32,128]{2,1,0:T(8,128)S(1)} collective-permute-done((f32[8,32,128]{2,1,0:T(8,128)S(1)}, f32[8,32,128]{2,1,0:T(8,128)S(1)}, u32[]{:S(2)}, u32[]{:S(2)}) %collective-permute-start.19) | collective-permute-done | bytes 131104 | tf_op jit(solution)/shard_map/ppermute | solution.py:414
  80.9 0.1 collective-permute-start.14
  81.0 0.3 shard_map.58.after.rest_1_.pa
  81.3 0.3 collective-permute-start.26
  81.5 4.7 %collective-permute-done.17 = f32[8,64,128]{2,1,0:T(8,128)S(1)} collective-permute-done((f32[8,64,128]{2,1,0:T(8,128)S(1)}, f32[8,64,128]{2,1,0:T(8,128)S(1)}, u32[]{:S(2)}, u32[]{:S(2)}) %collective-permute-start.17) | collective-permute-done | bytes 262176 | tf_op jit(solution)/shard_map/ppermute | solution.py:421
  86.3 3.9 %shard_map.59.rest_0_.u = f32[8,32,64,128]{3,2,1,0:T(8,128)S(1)} custom-call(f32[8,32,64,128]{3,2,1,0:T(8,128)S(1)} %shard_map.56.rest_0_.u, f32[16,64,128]{2,1,0:T(8,128)S(1)} %shard_map.55.after.rest_1_.pa, f32[16,64,128]{2,1,0:T(8,128)S(1)} %get-tuple-element.51.pb, f32[8,64,128]{2,1,0:T(8,128)S(1)} %collective-permute-done.14.lon_e, ...), custom_call_target="tpu_custom_call" | custom-call | flops 20000000 | tf_op jit(solution)/shard_map/pallas_call | solution.py:472
  90.2 0.6 shard_map.60
  90.7 0.6 collective-permute-start.22
  91.4 4.7 %collective-permute-start.23 = (f32[8,64,128]{2,1,0:T(8,128)S(1)}, f32[8,64,128]{2,1,0:T(8,128)S(1)}, u32[]{:S(2)}, u32[]{:S(2)}) collective-permute-start(f32[8,64,128]{2,1,0:T(8,128)S(1)} %get-tuple-element.58), channel_id=1, source_target_pairs={{8,16},{16,8},{24,32},{32,24},{40,48},{48,40},{9,17},{17,9},{25,33... | collective-permute-start | bytes 786440 | tf_op jit(solution)/shard_map/ppermute | solution.py:414
  96.1 2.2 %collective-permute-start.24 = (f32[8,32,128]{2,1,0:T(8,128)S(1)}, f32[8,32,128]{2,1,0:T(8,128)S(1)}, u32[]{:S(2)}, u32[]{:S(2)}) collective-permute-start(f32[8,32,128]{2,1,0:T(8,128)S(1)} %get-tuple-element.59), channel_id=1, source_target_pairs={{0,1},{1,0},{2,3},{3,2},{4,5},{5,4},{6,7},{7,6},{8,9},{9,8},{10,11... | collective-permute-start | bytes 393224 | tf_op jit(solution)/shard_map/ppermute | solution.py:414
  98.3 3.6 %collective-permute-start.25 = (f32[8,32,128]{2,1,0:T(8,128)S(1)}, f32[8,32,128]{2,1,0:T(8,128)S(1)}, u32[]{:S(2)}, u32[]{:S(2)}) collective-permute-start(f32[8,32,128]{2,1,0:T(8,128)S(1)} %get-tuple-element.60), channel_id=1, source_target_pairs={{1,2},{2,1},{3,4},{4,3},{5,6},{6,5},{9,10},{10,9},{11,12},{12,11},... | collective-permute-start | bytes 393224 | tf_op jit(solution)/shard_map/ppermute | solution.py:414
  101.9 0.7 collective-permute-done.24.lev_e
  102.6 0.6 collective-permute-start.31
  103.2 6.5 %collective-permute-done.25.lev_o = f32[8,32,128]{2,1,0:T(8,128)S(1)} collective-permute-done((f32[8,32,128]{2,1,0:T(8,128)S(1)}, f32[8,32,128]{2,1,0:T(8,128)S(1)}, u32[]{:S(2)}, u32[]{:S(2)}) %collective-permute-start.25) | collective-permute-done | bytes 131104 | tf_op jit(solution)/shard_map/ppermute | solution.py:414
  109.7 0.3 shard_map.61.after.npa
  110.0 4.3 %shard_map.62 = (f32[8,32,64,128]{3,2,1,0:T(8,128)}, f32[8,32,64,128]{3,2,1,0:T(8,128)S(1)}, f32[8,32,64,128]{3,2,1,0:T(8,128)S(1)}, f32[7,64,128]{2,1,0:T(8,128)S(1)}) custom-call(f32[8,32,64,128]{3,2,1,0:T(8,128)S(1)} %shard_map.59.rest_0_.u, f32[16,64,128]{2,1,0:T(8,128)S(1)} %shard_map.58.after.rest_1_.pa, ...), custom_call_target="tpu_custom_call", output_to_operand_aliasing={{1}: (7, {}), {2}: (8, {})} | custom-call | flops 20000000 | tf_op jit(solution)/shard_map/pallas_call | solution.py:484
  114.3 0.1 collective-permute-start.27
  114.4 1.5 %collective-permute-done.27.other = f32[7,64,128]{2,1,0:T(8,128)S(1)} collective-permute-done((f32[7,64,128]{2,1,0:T(8,128)S(1)}, f32[7,64,128]{2,1,0:T(8,128)S(1)}, u32[]{:S(2)}, u32[]{:S(2)}) %collective-permute-start.27) | collective-permute-done | bytes 229408 | tf_op jit(solution)/shard_map/ppermute | solution.py:430
  116.0 6.7 %collective-permute-done.28.refs_0_ = f32[7,32,128]{2,1,0:T(8,128)S(1)} collective-permute-done((f32[7,32,128]{2,1,0:T(8,128)S(1)}, f32[7,32,128]{2,1,0:T(8,128)S(1)}, u32[]{:S(2)}, u32[]{:S(2)}) %collective-permute-start.28) | collective-permute-done | bytes 114720 | tf_op jit(solution)/shard_map/ppermute | solution.py:430
  122.7 1.3 collective-permute-start.29
  124.0 5.4 %collective-permute-done.29.refs_1_ = f32[7,32,128]{2,1,0:T(8,128)S(1)} collective-permute-done((f32[7,32,128]{2,1,0:T(8,128)S(1)}, f32[7,32,128]{2,1,0:T(8,128)S(1)}, u32[]{:S(2)}, u32[]{:S(2)}) %collective-permute-start.29) | collective-permute-done | bytes 114720 | tf_op jit(solution)/shard_map/ppermute | solution.py:430
  129.5 0.4 shard_map.65
  129.9 0.6 collective-permute-start.32
  130.4 0.9 collective-permute-done.32.rest_0_
  131.3 0.3 collective-permute-start.33
  131.6 5.1 %collective-permute-done.33.rest_1_ = f32[64,128]{1,0:T(8,128)S(1)} collective-permute-done((f32[64,128]{1,0:T(8,128)S(1)}, f32[64,128]{1,0:T(8,128)S(1)}, u32[]{:S(2)}, u32[]{:S(2)}) %collective-permute-start.33) | collective-permute-done | bytes 32800 | tf_op jit(solution)/shard_map/ppermute | solution.py:430
  136.7 1.3 collective-permute-start.34
  138.0 1.7 %shard_map.68 = f32[8,32,64,128]{3,2,1,0:T(8,128)} custom-call(f32[8,32,64,128]{3,2,1,0:T(8,128)S(1)} %get-tuple-element.65.f, f32[16,64,128]{2,1,0:T(8,128)S(1)} %shard_map.61.after.npa, f32[16,64,128]{2,1,0:T(8,128)S(1)} %get-tuple-element.66.npb, f32[8,32,64,128]{3,2,1,0:T(8,128)} %get-tuple-element.67.end_in), custom_call_target="tpu_custom_call", output_to_operand_aliasing={{}: (3, {})} | custom-call | flops 100000 | tf_op jit(solution)/shard_map/pallas_call | solution.py:514
  139.7 2.0 %shard_map.66.rest_3_ = f32[8,32,64,128]{3,2,1,0:T(8,128)} custom-call(f32[8,32,64,128]{3,2,1,0:T(8,128)S(1)} %get-tuple-element.61.sums, f32[7,64,128]{2,1,0:T(8,128)S(1)} %collective-permute-done.27.other, f32[7,32,128]{2,1,0:T(8,128)S(1)} %shard_map.64.before, f32[64,128]{1,0:T(8,128)S(1)} %get-tuple-element.64.after), custom_call_target="tpu_custom_call" | custom-call | flops 1000000 | tf_op jit(solution)/shard_map/pallas_call | solution.py:524
  141.7 0.8 collective-permute-done.34.rest_2_
  142.5 2.3 %shard_map.67 = f32[8,32,64,128]{3,2,1,0:T(8,128)} custom-call(f32[8,32,64,128]{3,2,1,0:T(8,128)S(1)} %get-tuple-element.61.sums, f32[7,64,128]{2,1,0:T(8,128)S(1)} %collective-permute-done.27.other, f32[7,32,128]{2,1,0:T(8,128)S(1)} %collective-permute-done.30.before, ...), custom_call_target="tpu_custom_call", output_to_operand_aliasing={{}: (7, {})} | custom-call | flops 1000000 | tf_op jit(solution)/shard_map/pallas_call | solution.py:534
  (30 shorter events, 0.4 us)
Async XLA Ops:
  1.7 21.0 %collective-permute-start.6 = (f32[16,64,128]{2,1,0:T(8,128)S(1)}, f32[16,64,128]{2,1,0:T(8,128)S(1)}, u32[]{:S(2)}, u32[]{:S(2)}) collective-permute-start(f32[16,64,128]{2,1,0:T(8,128)S(1)} %shard_map.51.pa), channel_id=1, source_target_pairs={{0,64},{64,0},{1,65},{65,1},{2,66},{66,2},{3,67},{67,3},{4,68},{68... | collective-permute-start | bytes 1572872 | tf_op jit(solution)/shard_map/ppermute | solution.py:437
  6.8 10.0 %collective-permute-start.2 = (f32[8,64,128]{2,1,0:T(8,128)S(1)}, f32[8,64,128]{2,1,0:T(8,128)S(1)}, u32[]{:S(2)}, u32[]{:S(2)}) collective-permute-start(f32[8,64,128]{2,1,0:T(8,128)S(1)} %get-tuple-element.38), channel_id=1, source_target_pairs={{24,56},{32,0},{25,57},{33,1},{26,58},{34,2},{27,59},{35,3},{28,60... | collective-permute-start | bytes 786440 | tf_op jit(solution)/shard_map/ppermute | solution.py:419
  9.1 28.9 %collective-permute-start.7 = (f32[16,64,128]{2,1,0:T(8,128)S(1)}, f32[16,64,128]{2,1,0:T(8,128)S(1)}, u32[]{:S(2)}, u32[]{:S(2)}) collective-permute-start(f32[16,64,128]{2,1,0:T(8,128)S(1)} %get-tuple-element.36.pb), channel_id=1, source_target_pairs={{0,64},{64,0},{1,65},{65,1},{2,66},{66,2},{3,67},{67,3},{4,68},{68... | collective-permute-start | bytes 1572872 | tf_op jit(solution)/shard_map/ppermute | solution.py:447
  10.7 5.4 %collective-permute-start.4 = (f32[8,32,128]{2,1,0:T(8,128)S(1)}, f32[8,32,128]{2,1,0:T(8,128)S(1)}, u32[]{:S(2)}, u32[]{:S(2)}) collective-permute-start(f32[8,32,128]{2,1,0:T(8,128)S(1)} %get-tuple-element.39), channel_id=1, source_target_pairs={{0,1},{1,0},{2,3},{3,2},{4,5},{5,4},{6,7},{7,6},{8,9},{9,8},{10,11... | collective-permute-start | bytes 393224 | tf_op jit(solution)/shard_map/ppermute | solution.py:414
  12.2 10.5 %collective-permute-start.5 = (f32[8,32,128]{2,1,0:T(8,128)S(1)}, f32[8,32,128]{2,1,0:T(8,128)S(1)}, u32[]{:S(2)}, u32[]{:S(2)}) collective-permute-start(f32[8,32,128]{2,1,0:T(8,128)S(1)} %get-tuple-element.40), channel_id=1, source_target_pairs={{1,2},{2,1},{3,4},{4,3},{5,6},{6,5},{9,10},{10,9},{11,12},{12,11},... | collective-permute-start | bytes 393224 | tf_op jit(solution)/shard_map/ppermute | solution.py:414
  16.0 7.6 %collective-permute-start.1 = (f32[8,64,128]{2,1,0:T(8,128)S(1)}, f32[8,64,128]{2,1,0:T(8,128)S(1)}, u32[]{:S(2)}, u32[]{:S(2)}) collective-permute-start(f32[8,64,128]{2,1,0:T(8,128)S(1)} %get-tuple-element.38), channel_id=1, source_target_pairs={{8,16},{16,8},{40,48},{48,40},{9,17},{17,9},{41,49},{49,41},{10,18... | collective-permute-start | bytes 786440 | tf_op jit(solution)/shard_map/ppermute | solution.py:420
  16.7 15.4 %collective-permute-start.3 = (f32[8,64,128]{2,1,0:T(8,128)S(1)}, f32[8,64,128]{2,1,0:T(8,128)S(1)}, u32[]{:S(2)}, u32[]{:S(2)}) collective-permute-start(f32[8,64,128]{2,1,0:T(8,128)S(1)} %collective-permute-done.2), channel_id=1, source_target_pairs={{56,32},{0,24},{57,33},{1,25},{58,34},{2,26},{59,35},{3,27},{60,36... | collective-permute-start | bytes 786440 | tf_op jit(solution)/shard_map/ppermute | solution.py:421
  22.7 9.4 %collective-permute-start = (f32[8,64,128]{2,1,0:T(8,128)S(1)}, f32[8,64,128]{2,1,0:T(8,128)S(1)}, u32[]{:S(2)}, u32[]{:S(2)}) collective-permute-start(f32[8,64,128]{2,1,0:T(8,128)S(1)} %get-tuple-element.37), channel_id=1, source_target_pairs={{0,8},{8,0},{16,24},{24,16},{32,40},{40,32},{48,56},{56,48},{1,9},... | collective-permute-start | bytes 786440 | tf_op jit(solution)/shard_map/ppermute | solution.py:420
  23.0 30.4 %collective-permute-start.12 = (f32[16,64,128]{2,1,0:T(8,128)S(1)}, f32[16,64,128]{2,1,0:T(8,128)S(1)}, u32[]{:S(2)}, u32[]{:S(2)}) collective-permute-start(f32[16,64,128]{2,1,0:T(8,128)S(1)} %shard_map.52.after.rest_1_.pa), channel_id=1, source_target_pairs={{0,64},{64,0},{1,65},{65,1},{2,66},{66,2},{3,67},{67,3},{4,68},{68... | collective-permute-start | bytes 1572872 | tf_op jit(solution)/shard_map/ppermute | solution.py:461
  38.6 25.6 %collective-permute-start.13 = (f32[16,64,128]{2,1,0:T(8,128)S(1)}, f32[16,64,128]{2,1,0:T(8,128)S(1)}, u32[]{:S(2)}, u32[]{:S(2)}) collective-permute-start(f32[16,64,128]{2,1,0:T(8,128)S(1)} %get-tuple-element.44.pb), channel_id=1, source_target_pairs={{0,64},{64,0},{1,65},{65,1},{2,66},{66,2},{3,67},{67,3},{4,68},{68... | collective-permute-start | bytes 1572872 | tf_op jit(solution)/shard_map/ppermute | solution.py:479
  40.5 7.0 %collective-permute-start.10 = (f32[8,32,128]{2,1,0:T(8,128)S(1)}, f32[8,32,128]{2,1,0:T(8,128)S(1)}, u32[]{:S(2)}, u32[]{:S(2)}) collective-permute-start(f32[8,32,128]{2,1,0:T(8,128)S(1)} %get-tuple-element.47), channel_id=1, source_target_pairs={{0,1},{1,0},{2,3},{3,2},{4,5},{5,4},{6,7},{7,6},{8,9},{9,8},{10,11... | collective-permute-start | bytes 393224 | tf_op jit(solution)/shard_map/ppermute | solution.py:414
  42.1 11.3 %collective-permute-start.11 = (f32[8,32,128]{2,1,0:T(8,128)S(1)}, f32[8,32,128]{2,1,0:T(8,128)S(1)}, u32[]{:S(2)}, u32[]{:S(2)}) collective-permute-start(f32[8,32,128]{2,1,0:T(8,128)S(1)} %get-tuple-element.48), channel_id=1, source_target_pairs={{1,2},{2,1},{3,4},{4,3},{5,6},{6,5},{9,10},{10,9},{11,12},{12,11},... | collective-permute-start | bytes 393224 | tf_op jit(solution)/shard_map/ppermute | solution.py:414
  46.1 7.7 %collective-permute-start.8 = (f32[8,64,128]{2,1,0:T(8,128)S(1)}, f32[8,64,128]{2,1,0:T(8,128)S(1)}, u32[]{:S(2)}, u32[]{:S(2)}) collective-permute-start(f32[8,64,128]{2,1,0:T(8,128)S(1)} %get-tuple-element.45), channel_id=1, source_target_pairs={{0,8},{8,0},{16,24},{24,16},{32,40},{40,32},{48,56},{56,48},{1,9},... | collective-permute-start | bytes 786440 | tf_op jit(solution)/shard_map/ppermute | solution.py:414
  47.5 12.9 %collective-permute-start.9 = (f32[8,64,128]{2,1,0:T(8,128)S(1)}, f32[8,64,128]{2,1,0:T(8,128)S(1)}, u32[]{:S(2)}, u32[]{:S(2)}) collective-permute-start(f32[8,64,128]{2,1,0:T(8,128)S(1)} %get-tuple-element.46), channel_id=1, source_target_pairs={{8,16},{16,8},{24,32},{32,24},{40,48},{48,40},{9,17},{17,9},{25,33... | collective-permute-start | bytes 786440 | tf_op jit(solution)/shard_map/ppermute | solution.py:414
  53.6 27.4 %collective-permute-start.20 = (f32[16,64,128]{2,1,0:T(8,128)S(1)}, f32[16,64,128]{2,1,0:T(8,128)S(1)}, u32[]{:S(2)}, u32[]{:S(2)}) collective-permute-start(f32[16,64,128]{2,1,0:T(8,128)S(1)} %shard_map.55.after.rest_1_.pa), channel_id=1, source_target_pairs={{0,64},{64,0},{1,65},{65,1},{2,66},{66,2},{3,67},{67,3},{4,68},{68... | collective-permute-start | bytes 1572872 | tf_op jit(solution)/shard_map/ppermute | solution.py:461
  64.8 9.4 %collective-permute-start.16 = (f32[8,64,128]{2,1,0:T(8,128)S(1)}, f32[8,64,128]{2,1,0:T(8,128)S(1)}, u32[]{:S(2)}, u32[]{:S(2)}) collective-permute-start(f32[8,64,128]{2,1,0:T(8,128)S(1)} %get-tuple-element.53), channel_id=1, source_target_pairs={{24,56},{32,0},{25,57},{33,1},{26,58},{34,2},{27,59},{35,3},{28,60... | collective-permute-start | bytes 786440 | tf_op jit(solution)/shard_map/ppermute | solution.py:419
  66.1 24.1 %collective-permute-start.21 = (f32[16,64,128]{2,1,0:T(8,128)S(1)}, f32[16,64,128]{2,1,0:T(8,128)S(1)}, u32[]{:S(2)}, u32[]{:S(2)}) collective-permute-start(f32[16,64,128]{2,1,0:T(8,128)S(1)} %get-tuple-element.51.pb), channel_id=1, source_target_pairs={{0,64},{64,0},{1,65},{65,1},{2,66},{66,2},{3,67},{67,3},{4,68},{68... | collective-permute-start | bytes 1572872 | tf_op jit(solution)/shard_map/ppermute | solution.py:479
  67.6 5.9 %collective-permute-start.18 = (f32[8,32,128]{2,1,0:T(8,128)S(1)}, f32[8,32,128]{2,1,0:T(8,128)S(1)}, u32[]{:S(2)}, u32[]{:S(2)}) collective-permute-start(f32[8,32,128]{2,1,0:T(8,128)S(1)} %get-tuple-element.54), channel_id=1, source_target_pairs={{0,1},{1,0},{2,3},{3,2},{4,5},{5,4},{6,7},{7,6},{8,9},{9,8},{10,11... | collective-permute-start | bytes 393224 | tf_op jit(solution)/shard_map/ppermute | solution.py:414
  69.2 11.7 %collective-permute-start.19 = (f32[8,32,128]{2,1,0:T(8,128)S(1)}, f32[8,32,128]{2,1,0:T(8,128)S(1)}, u32[]{:S(2)}, u32[]{:S(2)}) collective-permute-start(f32[8,32,128]{2,1,0:T(8,128)S(1)} %get-tuple-element.55), channel_id=1, source_target_pairs={{1,2},{2,1},{3,4},{4,3},{5,6},{6,5},{9,10},{10,9},{11,12},{12,11},... | collective-permute-start | bytes 393224 | tf_op jit(solution)/shard_map/ppermute | solution.py:414
  73.5 8.0 %collective-permute-start.15 = (f32[8,64,128]{2,1,0:T(8,128)S(1)}, f32[8,64,128]{2,1,0:T(8,128)S(1)}, u32[]{:S(2)}, u32[]{:S(2)}) collective-permute-start(f32[8,64,128]{2,1,0:T(8,128)S(1)} %get-tuple-element.53), channel_id=1, source_target_pairs={{8,16},{16,8},{40,48},{48,40},{9,17},{17,9},{41,49},{49,41},{10,18... | collective-permute-start | bytes 786440 | tf_op jit(solution)/shard_map/ppermute | solution.py:420
  74.2 12.0 %collective-permute-start.17 = (f32[8,64,128]{2,1,0:T(8,128)S(1)}, f32[8,64,128]{2,1,0:T(8,128)S(1)}, u32[]{:S(2)}, u32[]{:S(2)}) collective-permute-start(f32[8,64,128]{2,1,0:T(8,128)S(1)} %collective-permute-done.16), channel_id=1, source_target_pairs={{56,32},{0,24},{57,33},{1,25},{58,34},{2,26},{59,35},{3,27},{60,36... | collective-permute-start | bytes 786440 | tf_op jit(solution)/shard_map/ppermute | solution.py:421
  80.9 5.4 %collective-permute-start.14 = (f32[8,64,128]{2,1,0:T(8,128)S(1)}, f32[8,64,128]{2,1,0:T(8,128)S(1)}, u32[]{:S(2)}, u32[]{:S(2)}) collective-permute-start(f32[8,64,128]{2,1,0:T(8,128)S(1)} %get-tuple-element.52), channel_id=1, source_target_pairs={{0,8},{8,0},{16,24},{24,16},{32,40},{40,32},{48,56},{56,48},{1,9},... | collective-permute-start | bytes 786440 | tf_op jit(solution)/shard_map/ppermute | solution.py:420
  81.3 28.4 %collective-permute-start.26 = (f32[16,64,128]{2,1,0:T(8,128)S(1)}, f32[16,64,128]{2,1,0:T(8,128)S(1)}, u32[]{:S(2)}, u32[]{:S(2)}) collective-permute-start(f32[16,64,128]{2,1,0:T(8,128)S(1)} %shard_map.58.after.rest_1_.pa), channel_id=1, source_target_pairs={{0,64},{64,0},{1,65},{65,1},{2,66},{66,2},{3,67},{67,3},{4,68},{68... | collective-permute-start | bytes 1572872 | tf_op jit(solution)/shard_map/ppermute | solution.py:461
  90.7 19.3 %collective-permute-start.22 = (f32[8,64,128]{2,1,0:T(8,128)S(1)}, f32[8,64,128]{2,1,0:T(8,128)S(1)}, u32[]{:S(2)}, u32[]{:S(2)}) collective-permute-start(f32[8,64,128]{2,1,0:T(8,128)S(1)} %get-tuple-element.57), channel_id=1, source_target_pairs={{0,8},{8,0},{16,24},{24,16},{32,40},{40,32},{48,56},{56,48},{1,9},... | collective-permute-start | bytes 786440 | tf_op jit(solution)/shard_map/ppermute | solution.py:414
  91.4 18.6 %collective-permute-start.23 = (f32[8,64,128]{2,1,0:T(8,128)S(1)}, f32[8,64,128]{2,1,0:T(8,128)S(1)}, u32[]{:S(2)}, u32[]{:S(2)}) collective-permute-start(f32[8,64,128]{2,1,0:T(8,128)S(1)} %get-tuple-element.58), channel_id=1, source_target_pairs={{8,16},{16,8},{24,32},{32,24},{40,48},{48,40},{9,17},{17,9},{25,33... | collective-permute-start | bytes 786440 | tf_op jit(solution)/shard_map/ppermute | solution.py:414
  96.1 6.5 %collective-permute-start.24 = (f32[8,32,128]{2,1,0:T(8,128)S(1)}, f32[8,32,128]{2,1,0:T(8,128)S(1)}, u32[]{:S(2)}, u32[]{:S(2)}) collective-permute-start(f32[8,32,128]{2,1,0:T(8,128)S(1)} %get-tuple-element.59), channel_id=1, source_target_pairs={{0,1},{1,0},{2,3},{3,2},{4,5},{5,4},{6,7},{7,6},{8,9},{9,8},{10,11... | collective-permute-start | bytes 393224 | tf_op jit(solution)/shard_map/ppermute | solution.py:414
  98.3 11.4 %collective-permute-start.25 = (f32[8,32,128]{2,1,0:T(8,128)S(1)}, f32[8,32,128]{2,1,0:T(8,128)S(1)}, u32[]{:S(2)}, u32[]{:S(2)}) collective-permute-start(f32[8,32,128]{2,1,0:T(8,128)S(1)} %get-tuple-element.60), channel_id=1, source_target_pairs={{1,2},{2,1},{3,4},{4,3},{5,6},{6,5},{9,10},{10,9},{11,12},{12,11},... | collective-permute-start | bytes 393224 | tf_op jit(solution)/shard_map/ppermute | solution.py:414
  102.6 26.9 %collective-permute-start.31 = (f32[16,64,128]{2,1,0:T(8,128)S(1)}, f32[16,64,128]{2,1,0:T(8,128)S(1)}, u32[]{:S(2)}, u32[]{:S(2)}) collective-permute-start(f32[16,64,128]{2,1,0:T(8,128)S(1)} %get-tuple-element.56.pb), channel_id=1, source_target_pairs={{0,64},{64,0},{1,65},{65,1},{2,66},{66,2},{3,67},{67,3},{4,68},{68... | collective-permute-start | bytes 1572872 | tf_op jit(solution)/shard_map/ppermute | solution.py:479
  114.3 1.6 %collective-permute-start.27 = (f32[7,64,128]{2,1,0:T(8,128)S(1)}, f32[7,64,128]{2,1,0:T(8,128)S(1)}, u32[]{:S(2)}, u32[]{:S(2)}) collective-permute-start(f32[7,64,128]{2,1,0:T(8,128)S(1)} %get-tuple-element.62.total), channel_id=1, source_target_pairs={{0,8},{8,0},{16,24},{24,16},{32,40},{40,32},{48,56},{56,48},{1,9},... | collective-permute-start | bytes 688136 | tf_op jit(solution)/shard_map/ppermute | solution.py:430
  115.9 6.8 %collective-permute-start.28 = (f32[7,32,128]{2,1,0:T(8,128)S(1)}, f32[7,32,128]{2,1,0:T(8,128)S(1)}, u32[]{:S(2)}, u32[]{:S(2)}) collective-permute-start(f32[7,32,128]{2,1,0:T(8,128)S(1)} %shard_map.63), channel_id=1, source_target_pairs={{0,16},{8,24},{16,0},{24,8},{32,48},{40,56},{48,32},{56,40},{1,17}... | collective-permute-start | bytes 344072 | tf_op jit(solution)/shard_map/ppermute | solution.py:430
  122.7 6.7 %collective-permute-start.29 = (f32[7,32,128]{2,1,0:T(8,128)S(1)}, f32[7,32,128]{2,1,0:T(8,128)S(1)}, u32[]{:S(2)}, u32[]{:S(2)}) collective-permute-start(f32[7,32,128]{2,1,0:T(8,128)S(1)} %add.17), channel_id=1, source_target_pairs={{0,32},{8,40},{16,48},{24,56},{1,33},{9,41},{17,49},{25,57},{2,34}... | collective-permute-start | bytes 344072 | tf_op jit(solution)/shard_map/ppermute | solution.py:430
  129.4 13.1 %collective-permute-start.30 = (f32[7,32,128]{2,1,0:T(8,128)S(1)}, f32[7,32,128]{2,1,0:T(8,128)S(1)}, u32[]{:S(2)}, u32[]{:S(2)}) collective-permute-start(f32[7,32,128]{2,1,0:T(8,128)S(1)} %shard_map.64.before), channel_id=1, source_target_pairs={{0,8},{8,0},{16,24},{24,16},{32,40},{40,32},{48,56},{56,48},{1,9},... | collective-permute-start | bytes 344072 | tf_op jit(solution)/shard_map/ppermute | solution.py:502
  129.9 1.4 collective-permute-start.32
  131.3 5.4 %collective-permute-start.33 = (f32[64,128]{1,0:T(8,128)S(1)}, f32[64,128]{1,0:T(8,128)S(1)}, u32[]{:S(2)}, u32[]{:S(2)}) collective-permute-start(f32[64,128]{1,0:T(8,128)S(1)} %add.18), channel_id=1, source_target_pairs={{0,16},{8,24},{16,0},{24,8},{32,48},{40,56},{48,32},{56,40},{1,17}... | collective-permute-start | bytes 98312 | tf_op jit(solution)/shard_map/ppermute | solution.py:430
  136.7 5.8 %collective-permute-start.34 = (f32[64,128]{1,0:T(8,128)S(1)}, f32[64,128]{1,0:T(8,128)S(1)}, u32[]{:S(2)}, u32[]{:S(2)}) collective-permute-start(f32[64,128]{1,0:T(8,128)S(1)} %add.19), channel_id=1, source_target_pairs={{0,32},{8,40},{16,48},{24,56},{1,33},{9,41},{17,49},{25,57},{2,34}... | collective-permute-start | bytes 98312 | tf_op jit(solution)/shard_map/ppermute | solution.py:430
